TPU v7x, 256 devices: a whole 4x4x8 slice. The times are simulated.
256 devices in a mesh: gx: 8 (over z), gy: 4 (over y), gz: 8 (over x, core).
Axes of the slice: x: 4, y: 4, z: 8, core: 2. Of those that a mesh axis runs over, the one named last changes fastest.
Arguments:
- point_data: float32 [1, 6, 131072], P(None, None, ('gx', 'gy', 'gz')), may hold values from -1 to 1
- neighbours: int32 [1, 64, 64, 64, 32], P(None, 'gx', 'gy', 'gz'), may hold values from 0 to 131071, as said below
- counts: int32 [1, 64, 64, 64], P(None, 'gx', 'gy', 'gz'), may hold values from 1 to 32, as said below
- kernel_in: bfloat16 [6, 80], replicated, may hold values from -2.5 to 2.5
- kernel_mid: bfloat16 [80, 80], replicated, may hold values from -0.625 to 0.625
- kernel_out: bfloat16 [80, 64], replicated, may hold values from -0.625 to 0.625
- spectral: bfloat16 [2, 16, 16, 16, 64, 64], P(None, 'gz', 'gx', 'gy'), may hold values from -48 to 48
- skip_weight: bfloat16 [64, 64], replicated, may hold values from -0.75 to 0.75
Outputs:
- latent_out: float32 [1, 64, 64, 64, 64], P(None, 'gx', 'gy', 'gz')
Inputs may be any that keep to these rules, and one draw needn't show every extreme that they name: `neighbours`: points are owned by location: point j of a geometry belongs to the device at position j // 512 in the order gx, gy, gz. Every neighbour of a node is owned by the node's own device or by a device whose gx, gy and gz indices each differ from it by at most one. Slots s >= counts of the node are padding that names some point all the same. `counts`: on every device some node of every geometry has all 32 slots valid.
All inputs are finite; a program needn't handle non-finite values.
Results may differ from a plain program's by a relative error of at most 0.02.
Values may be sent and summed in bfloat16 or wider, within the bound.
No kernel may reach another device: no remote copies, remote signals or barrier semaphores. Data moves between devices by JAX's collectives and lax.ppermute only.
A program may use at most 64 MiB of HBM per device.

v0:
```python
import math

import jax
import jax.numpy as jnp
from jax import lax
from jax.sharding import Mesh
from jax.sharding import PartitionSpec as P

GRID = 64
MODES = 16
NB = 32
GZ = ("gz_0", "gz_1")
GX_GY_GZ = ("gx", "gy", "gz_0", "gz_1")


HIGHEST = lax.Precision.HIGHEST
NORM_FLOOR = 1.0


def extended(cells, sides, width):
    for axis, dim in sides:
        count = lax.axis_size(axis)
        ends = count - 1
        head = lax.slice_in_dim(cells, 0, width, axis=dim)
        tail = lax.slice_in_dim(cells, cells.shape[dim] - width, cells.shape[dim], axis=dim)
        cells = jnp.concatenate(
            [
                lax.ppermute(tail, axis, [(i, (i + 1) % count) for i in range(ends)]),
                cells,
                lax.ppermute(head, axis, [((i + 1) % count, i) for i in range(ends)]),
            ],
            axis=dim,
        )
    return cells


def in_one_piece(arrays, axis, split_dim, concat_dim, along):
    both = jnp.concatenate(arrays, axis=along)
    result, at, done = (
        lax.all_to_all(both, axis, split_axis=split_dim, concat_axis=concat_dim, tiled=True),
        0,
        [],
    )
    for a in arrays:
        done.append(lax.slice_in_dim(result, at, at + a.shape[along], axis=along))
        at += a.shape[along]
    return tuple(done)


def all_in_one(x, axis):
    leaves = jax.tree.leaves(x)
    turns = sorted(range(len(leaves)), key=lambda k: -leaves[k].size)
    width = (1, *leaves[turns[0]].shape)[-1]
    lines = [
        jnp.pad(leaves[k].reshape(-1), (0, -leaves[k].size % width)).reshape(-1, width)
        for k in turns
    ]
    both, at, found = (lax.all_gather(jnp.concatenate(lines), axis), 0, {})
    for k, line in zip(turns, lines):
        share = both[:, at : at + len(line)].reshape(len(both), -1)
        found[k] = share[:, : leaves[k].size].reshape(-1, *leaves[k].shape)
        at += len(line)
    numbers = iter(range(len(leaves)))
    return jax.tree.map(lambda _: found[next(numbers)], x)


def merged_by_axis(x, axes, combine):
    for axis in axes:
        pieces = all_in_one(x, axis)
        x = jax.tree.map(lambda part: part[0], pieces)
        for k in range(1, lax.axis_size(axis)):
            x = combine(x, jax.tree.map(lambda part: part[k], pieces))
    return x


def tables(length, keep_count, centred):
    position = jnp.arange(length, dtype=jnp.int32)
    frequency = jnp.arange(keep_count, dtype=jnp.int32)
    if centred:
        frequency = jnp.where(
            frequency < keep_count // 2, frequency, frequency + length - keep_count
        )
    phases = frequency[:, None] * position[None, :] % length
    angles = phases.astype(jnp.float32) * (2.0 * math.pi / length)
    return (jnp.cos(angles), jnp.sin(angles))


def third_weights(cos_table, sin_table, length):
    factor = (
        jnp.where(jnp.arange(cos_table.shape[0]) == 0, 1.0, 2.0).astype(jnp.float32)[:, None]
        / length**3
    )
    return (cos_table * factor, sin_table * factor)


def contract(pattern, operand, table):
    return jnp.einsum(pattern, operand, table, precision=HIGHEST)


def forward_real(values, cos_table, sin_table, pattern):
    return (contract(pattern, values, cos_table), -contract(pattern, values, sin_table))


def forward_complex(real_part, imag_part, cos_table, sin_table, pattern):
    new_real = contract(pattern, real_part, cos_table) + contract(pattern, imag_part, sin_table)
    new_imag = contract(pattern, imag_part, cos_table) - contract(pattern, real_part, sin_table)
    return (new_real, new_imag)


def inverse_complex(real_part, imag_part, cos_table, sin_table, pattern):
    new_real = contract(pattern, real_part, cos_table) - contract(pattern, imag_part, sin_table)
    new_imag = contract(pattern, real_part, sin_table) + contract(pattern, imag_part, cos_table)
    return (new_real, new_imag)


def inverse_real(real_part, imag_part, cos_table, sin_table, pattern):
    return contract(pattern, real_part, cos_table) - contract(pattern, imag_part, sin_table)


def kernel_mean(pair, valid, kernel_in, kernel_mid, kernel_out):
    hidden_one = jax.nn.gelu(
        jnp.dot(kernel_in.T, pair, preferred_element_type=jnp.float32), approximate=True
    ).astype(jnp.bfloat16)
    hidden_two = jax.nn.gelu(
        jnp.dot(kernel_mid.T, hidden_one, preferred_element_type=jnp.float32), approximate=True
    ).astype(jnp.bfloat16)
    values = jnp.dot(kernel_out.T, hidden_two, preferred_element_type=jnp.float32)
    values = values.reshape(values.shape[0], -1, NB)
    slots = jnp.arange(NB, dtype=jnp.int32)
    used = (slots[None, :] < valid[:, None]).astype(jnp.float32)
    total = jnp.sum(values * used[None], axis=2)
    return (total / valid.astype(jnp.float32)[None]).T.astype(jnp.bfloat16)


def split_exact(values):
    upper = values.astype(jnp.bfloat16)
    rest = values - upper.astype(jnp.float32)
    middle = rest.astype(jnp.bfloat16)
    lower = (rest - middle.astype(jnp.float32)).astype(jnp.bfloat16)
    return jnp.stack([upper, middle, lower], axis=1)


def merge_moments(first, second):
    count_a, mean_a, square_a = first
    count_b, mean_b, square_b = second
    total = count_a + count_b
    delta = mean_b - mean_a
    return (
        total,
        mean_a + delta * (count_b / total),
        square_a + square_b + delta * delta * (count_a * count_b / total),
    )


def body(point_data, neighbours, counts, kernel_in, kernel_mid, kernel_out, spectral, skip_weight):
    count_y = lax.axis_size("gy")
    count_z = lax.axis_size(GZ)
    place_x = lax.axis_index("gx")
    place_y = lax.axis_index("gy")
    place_z = lax.axis_index(GZ)
    geometry_count, cells_x, cells_y, cells_z = neighbours.shape[0:4]
    per_device = point_data.shape[2]
    channels = skip_weight.shape[0]
    beside_all = extended(point_data[None, None, None], (("gx", 0), ("gy", 1), (GZ, 2)), 1)
    table = jnp.transpose(beside_all, (3, 4, 0, 1, 2, 5)).reshape(
        geometry_count, point_data.shape[1], 27, per_device
    )
    pieces = split_exact(table).reshape(geometry_count, 3 * point_data.shape[1] * 27, per_device)
    owner = neighbours // per_device
    offset_z = owner % count_z - place_z + 1
    offset_y = owner // count_z % count_y - place_y + 1
    offset_x = owner // (count_z * count_y) - place_x + 1
    block_index = (offset_x * 3 + offset_y) * 3 + offset_z
    slot_index = neighbours % per_device
    centre_y = (
        (place_y * cells_y + jnp.arange(cells_y, dtype=jnp.int32)).astype(jnp.float32) + 0.5
    ) / GRID
    centre_z = (
        (place_z * cells_z + jnp.arange(cells_z, dtype=jnp.int32)).astype(jnp.float32) + 0.5
    ) / GRID
    row_y = jnp.broadcast_to(centre_y[:, None, None], (cells_y, cells_z, NB)).reshape(1, -1)
    row_z = jnp.broadcast_to(centre_z[None, :, None], (cells_y, cells_z, NB)).reshape(1, -1)
    slot_ids = jnp.arange(per_device, dtype=jnp.int32)[:, None]
    block_ids = jnp.arange(27, dtype=jnp.int32)[:, None]

    def one_slab(step):
        geometry = step // cells_x
        slab = step % cells_x
        rows = lax.dynamic_index_in_dim(pieces, geometry, 0, keepdims=False)
        blocks = lax.dynamic_index_in_dim(
            lax.dynamic_index_in_dim(block_index, geometry, 0, keepdims=False),
            slab,
            0,
            keepdims=False,
        ).reshape(1, -1)
        slots = lax.dynamic_index_in_dim(
            lax.dynamic_index_in_dim(slot_index, geometry, 0, keepdims=False),
            slab,
            0,
            keepdims=False,
        ).reshape(1, -1)
        valid = lax.dynamic_index_in_dim(
            lax.dynamic_index_in_dim(counts, geometry, 0, keepdims=False), slab, 0, keepdims=False
        ).reshape(-1)
        slot_hot = (slots == slot_ids).astype(jnp.bfloat16)
        found = jnp.dot(rows, slot_hot, preferred_element_type=jnp.float32).reshape(3, 6, 27, -1)
        found = found[0] + found[1] + found[2]
        block_hot = (blocks == block_ids).astype(jnp.float32)
        picked = jnp.sum(found * block_hot[None], axis=1)
        row_x = ((place_x * cells_x + slab).astype(jnp.float32) + 0.5) / GRID
        pair = jnp.concatenate(
            [picked[0:1] - row_x, picked[1:2] - row_y, picked[2:3] - row_z, picked[3:6]], axis=0
        ).astype(jnp.bfloat16)
        return kernel_mean(pair, valid, kernel_in, kernel_mid, kernel_out)

    latent = lax.map(one_slab, jnp.arange(geometry_count * cells_x, dtype=jnp.int32))
    latent = latent.reshape(geometry_count, cells_x, cells_y, cells_z, channels)
    cos_centred, sin_centred = tables(GRID, MODES, True)
    cos_third, sin_third = tables(GRID, MODES, False)
    back_cos, back_sin = third_weights(cos_third, sin_third, GRID)
    depth_full = lax.all_to_all(latent, GZ, split_axis=4, concat_axis=3, tiled=True)
    real_part, imag_part = forward_real(
        depth_full.astype(jnp.float32), cos_third, sin_third, "gxyzc,kz->gxykc"
    )
    real_part, imag_part = in_one_piece((real_part, imag_part), "gy", 3, 2, 0)
    real_part, imag_part = forward_complex(
        real_part, imag_part, cos_centred, sin_centred, "gxykc,jy->gxjkc"
    )
    real_part, imag_part = in_one_piece((real_part, imag_part), "gx", 2, 1, 0)
    real_part, imag_part = forward_complex(
        real_part, imag_part, cos_centred, sin_centred, "gxjkc,ix->gijkc"
    )
    spec_real, spec_imag = in_one_piece((real_part, imag_part), GZ, 1, 4, 0)
    spec_real = spec_real.astype(jnp.bfloat16)
    spec_imag = spec_imag.astype(jnp.bfloat16)
    mixed_real = jnp.einsum(
        "gijkc,ijkco->gijko", spec_real, spectral[0], preferred_element_type=jnp.float32
    ) - jnp.einsum("gijkc,ijkco->gijko", spec_imag, spectral[1], preferred_element_type=jnp.float32)
    mixed_imag = jnp.einsum(
        "gijkc,ijkco->gijko", spec_real, spectral[1], preferred_element_type=jnp.float32
    ) + jnp.einsum("gijkc,ijkco->gijko", spec_imag, spectral[0], preferred_element_type=jnp.float32)
    mixed_real = mixed_real.astype(jnp.bfloat16)
    mixed_imag = mixed_imag.astype(jnp.bfloat16)
    real_part, imag_part = in_one_piece((mixed_real, mixed_imag), GZ, 4, 1, 0)
    real_part, imag_part = inverse_complex(
        real_part.astype(jnp.float32),
        imag_part.astype(jnp.float32),
        cos_centred,
        sin_centred,
        "gijkc,ix->gxjkc",
    )
    real_part, imag_part = in_one_piece((real_part, imag_part), "gx", 1, 2, 0)
    real_part, imag_part = inverse_complex(
        real_part, imag_part, cos_centred, sin_centred, "gxjkc,jy->gxykc"
    )
    real_part, imag_part = in_one_piece((real_part, imag_part), "gy", 2, 3, 0)
    depth_part = inverse_real(real_part, imag_part, back_cos, back_sin, "gxykc,kz->gxyzc")
    branch = lax.all_to_all(depth_part, GZ, split_axis=3, concat_axis=4, tiled=True)
    skip = jnp.einsum("gxyzc,co->gxyzo", latent, skip_weight, preferred_element_type=jnp.float32)
    cells_total = float(GRID**3)
    local_cells = float(branch.shape[1] * branch.shape[2] * branch.shape[3])
    local_mean = jnp.sum(branch, axis=(1, 2, 3)) / local_cells
    local_centred = branch - local_mean[:, None, None, None, :]
    local_square = jnp.sum(local_centred * local_centred, axis=(1, 2, 3))
    local_count = jnp.full(local_mean.shape, local_cells, jnp.float32)
    merged = merged_by_axis((local_count, local_mean, local_square), GX_GY_GZ, merge_moments)
    mean = merged[1]
    variance = merged[2] / cells_total
    centred_branch = branch - mean[:, None, None, None, :]
    normed = centred_branch / jnp.sqrt(variance + NORM_FLOOR)[:, None, None, None, :]
    return jax.nn.gelu(normed + skip, approximate=True)


def solution(mesh):
    split = Mesh(
        mesh.devices.reshape(mesh.shape["gx"], mesh.shape["gy"], 4, 2), ("gx", "gy", "gz_0", "gz_1")
    )
    return jax.shard_map(
        body,
        mesh=split,
        in_specs=(
            P(None, None, GX_GY_GZ),
            P(None, "gx", "gy", GZ, None),
            P(None, "gx", "gy", GZ),
            P(),
            P(),
            P(),
            P(None, GZ, "gx", "gy", None, None),
            P(),
        ),
        out_specs=P(None, "gx", "gy", GZ, None),
        check_vma=False,
    )
```

profile of v0, /device:TPU:1, one launch (start us, length us, event | category | flops | bytes accessed | tf_op | source)
XLA Modules:
  0.0 357.7 jit_solution(7783864194018625842)
XLA Ops:
  0.0 4.5 %collective-permute-start = (f32[1,1,1,1,6,512]{5,0,4,3,2,1:T(1,128)}, f32[1,1,1,1,6,512]{5,0,4,3,2,1:T(1,128)S(1)}, u32[]{:S(2)}, u32[]{:S(2)}) collective-permute-start(f32[1,1,1,1,6,512]{5,0,4,3,2,1:T(1,128)} %bitcast.912), channel_id=1, source_target_pairs={{0,32},{32,64},{64,96},{96,128},{128,160},{160,192},{192,224},{1,3... | collective-permute-start | bytes 36872 | tf_op jit(solution)/shard_map/ppermute | solution.py:28
  5.8 3.4 fusion.65
  10.1 3.2 collective-permute-start.2
  14.6 3.5 collective-permute-done.3
  18.9 6.4 %collective-permute-start.4 = (f32[3,3,1,1,6,512]{5,0,4,3,2,1:T(4,128)S(1)}, f32[3,3,1,1,6,512]{5,0,4,3,2,1:T(4,128)S(1)}, u32[]{:S(2)}, u32[]{:S(2)}) collective-permute-start(f32[3,3,1,1,6,512]{5,0,4,3,2,1:T(4,128)S(1)} %pad_maximum_fusion.3), channel_id=1, source_target_pairs={{0,1},{1,2},{2,3},{3,4},{4,5},{5,6},{6,7},{8,9},{9,10},{10,11},{11... | collective-permute-start | bytes 331784 | tf_op jit(solution)/shard_map/ppermute | solution.py:28
  27.3 4.4 %collective-permute-done.5 = f32[3,3,1,1,6,512]{5,0,4,3,2,1:T(4,128)S(1)} collective-permute-done((f32[3,3,1,1,6,512]{5,0,4,3,2,1:T(4,128)S(1)}, f32[3,3,1,1,6,512]{5,0,4,3,2,1:T(4,128)S(1)}, u32[]{:S(2)}, u32[]{:S(2)}) %collective-permute-start.5) | collective-permute-done | bytes 110624 | tf_op jit(solution)/shard_map/ppermute | solution.py:30
  33.6 3.7 %maximum_reduce_fusion = bf16[3,6,27,512]{3,2,1,0:T(8,128)(2,1)S(1)} fusion(bf16[1,1,6,27,512]{4,0,3,2,1:T(2,128)(2,1)S(1)} %get-tuple-element.357, bf16[1,1,6,27,512]{4,0,3,2,1:T(2,128)(2,1)S(1)} %get-tuple-element.356, bf16[1,1,6,27,512]{4,0,3,2,1:T(2,128)(2,1)S(1)} %convert_element_type.231), kind=kLoop, calls=%fused_computation.77 | loop fusion | flops 497664 | bytes 995328 | tf_op jit(solution)/shard_map/stack | solution.py:140
  38.3 135.5 %while.13 = (s32[]{:T(128)}, bf16[8,128,64]{2,1,0:T(8,128)(2,1)}, s32[8]{0:T(128)S(1)}, s32[1,8,16,8,32]{4,3,2,1,0:T(8,128)}, bf16[1,486,512]{2,1,0:T(8,128)(2,1...) while((s32[]{:T(128)}, bf16[8,128,64]{2,1,0:T(8,128)(2,1)}, ...), condition=%wide.region_3.4_spmd.clone, body=%wide.region_0.3_spmd.clone.sunk | while | flops 2148343808 | bytes 34155936 | solution.py:216
  41.7 3.5 fusion.355
  58.6 3.5 fusion.355
  75.6 3.5 fusion.355
  92.5 3.5 fusion.355
  109.5 3.5 fusion.355
  126.4 3.5 fusion.355
  143.3 3.5 fusion.355
  160.3 3.5 fusion.355
  177.6 9.4 %all_to_all.123 = bf16[8,2,4096]{2,1,0:T(2,128)(2,1)S(1)} all-to-all(bf16[8,2,4096]{2,1,0:T(2,128)(2,1)S(1)} %reshape.2088), channel_id=1, replica_groups=mesh['gx'=8,'gy'=4,'gz_0'=4,'gz_1'=2] {'gz_0','gz_1'}, dimensions={0} | all-to-all | bytes 262144 | tf_op jit(solution)/shard_map/all_to_all | solution.py:221
  194.7 3.9 %all-to-all-start.1 = ((f32[4,1,8192]{2,1,0:T(1,128)}), f32[4,1,8192]{2,1,0:T(1,128)S(1)}, u32[]{:S(2)}, u32[]{:S(2)}) async-start(f32[4,1,8192]{2,1,0:T(1,128)} %reshape.2090), calls=%async_computation.1 | async-start | bytes 262144 | tf_op jit(solution)/shard_map/all_to_all | solution.py:40
  198.6 4.8 %all-to-all-done.1 = f32[4,1,8192]{2,1,0:T(1,128)S(1)} async-done(((f32[4,1,8192]{2,1,0:T(1,128)}), f32[4,1,8192]{2,1,0:T(1,128)S(1)}, u32[]{:S(2)}, u32[]{:S(2)}) %all-to-all-start.1) | async-done | bytes 131104 | tf_op jit(solution)/shard_map/all_to_all | solution.py:40
  209.3 15.8 %all_to_all.124 = f32[8,1,1024]{2,1,0:T(1,128)S(1)} all-to-all(f32[8,1,1024]{2,1,0:T(1,128)S(1)} %reshape.2092), channel_id=1, replica_groups=mesh['gx'=8,'gy'=4,'gz_0'=4,'gz_1'=2] {'gx'}, dimensions={0} | all-to-all | bytes 65536 | tf_op jit(solution)/shard_map/all_to_all | solution.py:40
  228.6 10.7 %all_to_all.125 = bf16[8,2,128]{2,1,0:T(2,128)(2,1)S(1)} all-to-all(bf16[8,2,128]{2,1,0:T(2,128)(2,1)S(1)} %reshape.2094), channel_id=1, replica_groups=mesh['gx'=8,'gy'=4,'gz_0'=4,'gz_1'=2] {'gz_0','gz_1'}, dimensions={0} | all-to-all | bytes 8192 | tf_op jit(solution)/shard_map/all_to_all | solution.py:40
  240.8 8.1 %all_to_all.126 = bf16[8,2,128]{2,1,0:T(2,128)(2,1)S(1)} all-to-all(bf16[8,2,128]{2,1,0:T(2,128)(2,1)S(1)} %reshape.2096), channel_id=1, replica_groups=mesh['gx'=8,'gy'=4,'gz_0'=4,'gz_1'=2] {'gz_0','gz_1'}, dimensions={0} | all-to-all | bytes 8192 | tf_op jit(solution)/shard_map/all_to_all | solution.py:40
  251.9 9.3 %all_to_all.127 = f32[8,1,1024]{2,1,0:T(1,128)S(1)} all-to-all(f32[8,1,1024]{2,1,0:T(1,128)S(1)} %reshape.2098), channel_id=1, replica_groups=mesh['gx'=8,'gy'=4,'gz_0'=4,'gz_1'=2] {'gx'}, dimensions={0} | all-to-all | bytes 65536 | tf_op jit(solution)/shard_map/all_to_all | solution.py:40
  267.1 3.1 reshape.2100
  270.2 3.5 all-to-all-start.6
  273.7 4.8 %all-to-all-done.6 = f32[4,1,8192]{2,1,0:T(1,128)S(1)} async-done(((f32[4,1,8192]{2,1,0:T(1,128)}), f32[4,1,8192]{2,1,0:T(1,128)S(1)}, u32[]{:S(2)}, u32[]{:S(2)}) %all-to-all-start.6) | async-done | bytes 131104 | tf_op jit(solution)/shard_map/all_to_all | solution.py:40
  289.0 6.3 %all-to-all-start.7 = ((f32[8,1,8192]{2,1,0:T(1,128)}), f32[8,1,8192]{2,1,0:T(1,128)S(1)}, u32[]{:S(2)}, u32[]{:S(2)}) async-start(f32[8,1,8192]{2,1,0:T(1,128)} %reshape.2102), calls=%async_computation.7 | async-start | bytes 524288 | tf_op jit(solution)/shard_map/all_to_all | solution.py:258
  295.3 6.5 %all-to-all-done.7 = f32[8,1,8192]{2,1,0:T(1,128)S(1)} async-done(((f32[8,1,8192]{2,1,0:T(1,128)}), f32[8,1,8192]{2,1,0:T(1,128)S(1)}, u32[]{:S(2)}, u32[]{:S(2)}) %all-to-all-start.7) | async-done | bytes 262176 | tf_op jit(solution)/shard_map/all_to_all | solution.py:258
  309.4 15.6 %all-gather.4 = f32[8,3,64]{2,1,0:T(4,128)S(1)} all-gather(f32[1,3,64]{2,1,0:T(4,128)S(1)} %maximum_bitcast_fusion.1), channel_id=2, replica_groups=mesh['gx'=8,'gy'=4,'gz_0'=4,'gz_1'=2] {'gx'}, dimensions={0}, use_global_device_ids=true | all-gather | bytes 6912 | tf_op jit(solution)/shard_map/all_gather | solution.py:58
  325.0 8.1 %all-gather.5 = f32[4,3,64]{2,1,0:T(4,128)S(1)} all-gather(f32[1,3,64]{2,1,0:T(4,128)S(1)} %maximum_bitcast_fusion.2), channel_id=3, replica_groups=mesh['gx'=8,'gy'=4,'gz_0'=4,'gz_1'=2] {'gy'}, dimensions={0}, use_global_device_ids=true | all-gather | bytes 3840 | tf_op jit(solution)/shard_map/all_gather | solution.py:58
  333.2 8.1 %all-gather.6 = f32[4,3,64]{2,1,0:T(4,128)S(1)} all-gather(f32[1,3,64]{2,1,0:T(4,128)S(1)} %maximum_bitcast_fusion.3), channel_id=4, replica_groups=mesh['gx'=8,'gy'=4,'gz_0'=4,'gz_1'=2] {'gz_0'}, dimensions={0}, use_global_device_ids=true | all-gather | bytes 3840 | tf_op jit(solution)/shard_map/all_gather | solution.py:58
  341.4 12.6 %all-gather.7 = f32[2,3,64]{2,1,0:T(4,128)S(1)} all-gather(f32[1,3,64]{2,1,0:T(4,128)S(1)} %maximum_bitcast_fusion.4), channel_id=5, replica_groups=mesh['gx'=8,'gy'=4,'gz_0'=4,'gz_1'=2] {'gz_1'}, dimensions={0}, use_global_device_ids=true | all-gather | bytes 2304 | tf_op jit(solution)/shard_map/all_gather | solution.py:58
  (347 shorter events, 153.0 us)
Async XLA Ops:
  0.0 356.2 %copy-start = (bf16[64,64]{1,0:T(8,128)(2,1)S(1)}, bf16[64,64]{1,0:T(8,128)(2,1)}, u32[]{:S(2)}) copy-start(bf16[64,64]{1,0:T(8,128)(2,1)} %param.17) | copy-start | bytes 24580
  0.0 9.2 %collective-permute-start = (f32[1,1,1,1,6,512]{5,0,4,3,2,1:T(1,128)}, f32[1,1,1,1,6,512]{5,0,4,3,2,1:T(1,128)S(1)}, u32[]{:S(2)}, u32[]{:S(2)}) collective-permute-start(f32[1,1,1,1,6,512]{5,0,4,3,2,1:T(1,128)} %bitcast.912), channel_id=1, source_target_pairs={{0,32},{32,64},{64,96},{96,128},{128,160},{160,192},{192,224},{1,3... | collective-permute-start | bytes 36872 | tf_op jit(solution)/shard_map/ppermute | solution.py:28
  4.5 4.8 %collective-permute-start.1 = (f32[1,1,1,1,6,512]{5,0,4,3,2,1:T(1,128)}, f32[1,1,1,1,6,512]{5,0,4,3,2,1:T(1,128)S(1)}, u32[]{:S(2)}, u32[]{:S(2)}) collective-permute-start(f32[1,1,1,1,6,512]{5,0,4,3,2,1:T(1,128)} %bitcast.913), channel_id=1, source_target_pairs={{32,0},{64,32},{96,64},{128,96},{160,128},{192,160},{224,192},{33,... | collective-permute-start | bytes 36872 | tf_op jit(solution)/shard_map/ppermute | solution.py:30
  10.1 4.5 %collective-permute-start.2 = (f32[3,1,1,1,6,512]{5,0,4,3,2,1:T(4,128)S(1)}, f32[3,1,1,1,6,512]{5,0,4,3,2,1:T(4,128)S(1)}, u32[]{:S(2)}, u32[]{:S(2)}) collective-permute-start(f32[3,1,1,1,6,512]{5,0,4,3,2,1:T(4,128)S(1)} %pad_maximum_fusion.6), channel_id=1, source_target_pairs={{0,8},{8,16},{16,24},{1,9},{9,17},{17,25},{2,10},{10,18},{18,26},{... | collective-permute-start | bytes 110600 | tf_op jit(solution)/shard_map/ppermute | solution.py:28
  13.3 4.8 %collective-permute-start.3 = (f32[3,1,1,1,6,512]{5,0,4,3,2,1:T(4,128)S(1)}, f32[3,1,1,1,6,512]{5,0,4,3,2,1:T(4,128)S(1)}, u32[]{:S(2)}, u32[]{:S(2)}) collective-permute-start(f32[3,1,1,1,6,512]{5,0,4,3,2,1:T(4,128)S(1)} %pad_maximum_fusion.6), channel_id=1, source_target_pairs={{8,0},{16,8},{24,16},{9,1},{17,9},{25,17},{10,2},{18,10},{26,18},{... | collective-permute-start | bytes 110600 | tf_op jit(solution)/shard_map/ppermute | solution.py:30
  18.9 8.4 %collective-permute-start.4 = (f32[3,3,1,1,6,512]{5,0,4,3,2,1:T(4,128)S(1)}, f32[3,3,1,1,6,512]{5,0,4,3,2,1:T(4,128)S(1)}, u32[]{:S(2)}, u32[]{:S(2)}) collective-permute-start(f32[3,3,1,1,6,512]{5,0,4,3,2,1:T(4,128)S(1)} %pad_maximum_fusion.3), channel_id=1, source_target_pairs={{0,1},{1,2},{2,3},{3,4},{4,5},{5,6},{6,7},{8,9},{9,10},{10,11},{11... | collective-permute-start | bytes 331784 | tf_op jit(solution)/shard_map/ppermute | solution.py:28
  25.3 6.5 %collective-permute-start.5 = (f32[3,3,1,1,6,512]{5,0,4,3,2,1:T(4,128)S(1)}, f32[3,3,1,1,6,512]{5,0,4,3,2,1:T(4,128)S(1)}, u32[]{:S(2)}, u32[]{:S(2)}) collective-permute-start(f32[3,3,1,1,6,512]{5,0,4,3,2,1:T(4,128)S(1)} %pad_maximum_fusion.3), channel_id=1, source_target_pairs={{1,0},{2,1},{3,2},{4,3},{5,4},{6,5},{7,6},{9,8},{10,9},{11,10},{12... | collective-permute-start | bytes 331784 | tf_op jit(solution)/shard_map/ppermute | solution.py:30
  32.9 5.3 %copy-start.1 = (bf16[80,64]{0,1:T(8,128)(2,1)S(1)}, bf16[80,64]{0,1:T(8,128)(2,1)}, u32[]{:S(2)}) copy-start(bf16[80,64]{0,1:T(8,128)(2,1)} %param.15) | copy-start | bytes 30724
  32.9 5.3 %copy-start.4 = (bf16[80,80]{1,0:T(8,128)(2,1)S(1)}, bf16[80,80]{1,0:T(8,128)(2,1)}, u32[]{:S(2)}) copy-start(bf16[80,80]{1,0:T(8,128)(2,1)} %param.14) | copy-start | bytes 38404
  32.9 5.3 %copy-start.5 = (bf16[6,80]{1,0:T(8,128)(2,1)S(1)}, bf16[6,80]{1,0:T(8,128)(2,1)}, u32[]{:S(2)}) copy-start(bf16[6,80]{1,0:T(8,128)(2,1)} %param.13) | copy-start | bytes 2884
  194.7 8.7 %all-to-all-start.1 = ((f32[4,1,8192]{2,1,0:T(1,128)}), f32[4,1,8192]{2,1,0:T(1,128)S(1)}, u32[]{:S(2)}, u32[]{:S(2)}) async-start(f32[4,1,8192]{2,1,0:T(1,128)} %reshape.2090), calls=%async_computation.1 | async-start | bytes 262144 | tf_op jit(solution)/shard_map/all_to_all | solution.py:40
  226.5 13.1 %copy-start.3 = (bf16[2,2,2,4,64,64]{5,4,3,2,1,0:T(8,128)(2,1)S(1)}, bf16[2,2,2,4,64,64]{5,4,3,2,1,0:T(8,128)(2,1)}, u32[]{:S(2)}) copy-start(bf16[2,2,2,4,64,64]{5,4,3,2,1,0:T(8,128)(2,1)} %param.16) | copy-start | bytes 786436
  270.2 8.3 %all-to-all-start.6 = ((f32[4,1,8192]{2,1,0:T(1,128)}), f32[4,1,8192]{2,1,0:T(1,128)S(1)}, u32[]{:S(2)}, u32[]{:S(2)}) async-start(f32[4,1,8192]{2,1,0:T(1,128)} %reshape.2100), calls=%async_computation.6 | async-start | bytes 262144 | tf_op jit(solution)/shard_map/all_to_all | solution.py:40
  289.0 12.8 %all-to-all-start.7 = ((f32[8,1,8192]{2,1,0:T(1,128)}), f32[8,1,8192]{2,1,0:T(1,128)S(1)}, u32[]{:S(2)}, u32[]{:S(2)}) async-start(f32[8,1,8192]{2,1,0:T(1,128)} %reshape.2102), calls=%async_computation.7 | async-start | bytes 524288 | tf_op jit(solution)/shard_map/all_to_all | solution.py:258
  309.2 47.0 %copy-start.2 = (bf16[8,128,64]{2,1,0:T(8,128)(2,1)S(1)}, bf16[8,128,64]{2,1,0:T(8,128)(2,1)}, u32[]{:S(2)}) copy-start(bf16[8,128,64]{2,1,0:T(8,128)(2,1)} %get-tuple-element.193) | copy-start | bytes 393220
where the time goes:
time: 363 us; the launch traced here: 358 us
  blocking collectives  97.5 us (27%)
  local copies, waits for them, and re-layouts  83.7 us (23%)
  matrix products  51.6 us (14%)
  other arithmetic  51.4 us (14%)
  starting transfers between devices  32.3 us (9%)
  waiting for transfers between devices  24.2 us (7%)
  loops' own time  16 us (4%)
    all_gather x4, blocking collectives, all_in_one(): both, at, found = (lax.all_gather(jnp.concatenate(lines), axis), 0, {})  44.4 us
    all_to_all x4, blocking collectives, in_one_piece(): lax.all_to_all(both, axis, split_axis=split_dim, concat_axis=concat_dim,...  43.7 us
    dot_general x8, matrix products, one_slab(): jnp.dot(rows, slot_hot, preferred_element_type=jnp.float32)  28.3 us
    add x8, other arithmetic, one_slab(): found = found[0] + found[1] + found[2]  18.1 us
    add x8, local copies, waits for them, and re-layouts, one_slab(): found = found[0] + found[1] + found[2]  17 us
    another operation x1, loops' own time, body(): lax.map(one_slab, jnp.arange(geometry_count * cells_x, dtype=jnp.int32))  16 us
    unnamed x30, local copies, waits for them, and re-layouts  15.6 us
    ppermute x3, starting transfers between devices, extended(): lax.ppermute(tail, axis, [(i, (i + 1) % count) for i in range(ends)])  14 us
  transfers between devices with their start and end apart: 9, of which 7 were waited for; matrix products, arithmetic and copies ran while one was open for 1% of the time, Pallas kernels for 0%

commit v1 on v0

v1 whole, which is shorter than its diff:
```python
import math

import jax
import jax.numpy as jnp
import numpy as np
from jax import lax
from jax.experimental import pallas as pl
from jax.experimental.pallas import tpu as pltpu
from jax.sharding import Mesh
from jax.sharding import PartitionSpec as P

f32 = jnp.float32
bf16 = jnp.bfloat16
i32 = jnp.int32

GRID = 64
NB = 32
CELLS = float(GRID**3)
NORM_FLOOR = 1.0
GZ = ("gz_0", "gz_1")
ALL = ("gx", "gy", "gz_0", "gz_1")
C0 = math.sqrt(2.0 / math.pi)
C1 = C0 * 0.044715
VMEM = pl.BlockSpec(memory_space=pltpu.VMEM)
SMEM = pl.BlockSpec(memory_space=pltpu.SMEM)


def freq(n):
    return np.where(n < 8, n, n - 16)


def angle(f, m):
    return 2.0 * math.pi * ((f * m) % GRID) / GRID


def split_two(a):
    hi = a.astype(bf16)
    lo = (a - hi.astype(a.dtype)).astype(bf16)
    return hi, lo


def third_forward():
    kh, r, kl, c = np.meshgrid(*map(np.arange, (4, 2, 4, 8)), indexing="ij")
    k, r, c = (4 * kh + kl).reshape(-1, 1), r.reshape(-1, 1), c.reshape(-1, 1)
    z = np.repeat(np.arange(64), 8)[None, :]
    cc = np.tile(np.arange(8), 64)[None, :]
    a = angle(k, z)
    v = np.where(r == 0, np.cos(a), -np.sin(a)) * (c == cc)
    return split_two(v)


def third_inverse():
    z = np.repeat(np.arange(64), 8)[:, None]
    o = np.tile(np.arange(8), 64)[:, None]
    s, kh, kl, r, oo = (
        a.reshape(1, -1) for a in np.meshgrid(*map(np.arange, (2, 4, 4, 2, 8)), indexing="ij")
    )
    k = 4 * kh + kl
    a = angle(k, z)
    w = np.where(k == 0, 1.0, 2.0) / CELLS
    cos, sin = np.cos(a), np.sin(a)
    v = np.where(s == 0, np.where(r == 0, cos, -sin), np.where(r == 0, -sin, -cos))
    return (v * w * (o == oo)).astype(bf16)


def plane_tables():
    jl, il, jh, ih = (a.reshape(-1) for a in np.meshgrid(*map(np.arange, (2, 2, 8, 8)), indexing="ij"))
    fwd = freq(2 * ih + il), freq(2 * jh + jl)
    il, jh, ih, jl = (a.reshape(-1) for a in np.meshgrid(*map(np.arange, (2, 8, 8, 2)), indexing="ij"))
    inv = freq(2 * ih + il), freq(2 * jh + jl)
    return fwd, inv, np.repeat(np.arange(8), 16), np.tile(np.arange(16), 8)


def partner_table():
    _, (fi, fj), _, _ = plane_tables()
    hit = (fi[:, None] == -fi[None, :]) & (fj[:, None] == -fj[None, :])
    return hit.astype(np.float32).astype(bf16)


def mode_masks():
    jl, il, kl = (a.reshape(-1, 1) for a in np.meshgrid(*map(np.arange, (2, 2, 4)), indexing="ij"))
    jc, ic, _, kc, _ = (
        a.reshape(1, -1) for a in np.meshgrid(*map(np.arange, (2, 2, 2, 4, 8)), indexing="ij")
    )
    own = ((jl == jc) & (il == ic) & (kl == kc)).astype(np.float32)
    _, ib, kb, _, _ = (
        a.reshape(1, -1) for a in np.meshgrid(*map(np.arange, (8, 2, 4, 2, 8)), indexing="ij")
    )
    place = ((il == ib) & (kl == kb)).astype(np.float32)
    half = np.zeros((8, 16), np.float32)
    half[jl[:, 0], np.arange(16)] = 1.0
    return own, place, half.astype(bf16)


def placing():
    ro, oh, ol = (a.reshape(-1, 1) for a in np.meshgrid(*map(np.arange, (2, 8, 8)), indexing="ij"))
    oc, _, _, rc, lc = (
        a.reshape(1, -1) for a in np.meshgrid(*map(np.arange, (8, 2, 4, 2, 8)), indexing="ij")
    )
    return ((ro == rc) & (oh == oc) & (ol == lc)).astype(np.float32).astype(bf16)


def dot(a, b):
    return jnp.dot(a, b, preferred_element_type=f32)


def dot_t(a, b):
    return lax.dot_general(a, b, (((1,), (1,)), ((), ())), preferred_element_type=f32)


def gelu_twice(v):
    return v * jnp.tanh(v * (v * v * C1 + C0)) + v


def encoder_kernel(
    place_ref, below_ref, own_ref, above_ref, nb_ref, cnt_ref, ki_ref, km_ref, ko_ref, out_ref, turn, acc_ref
):
    px, py, pz = place_ref[0], place_ref[1], place_ref[2]
    lane = lax.broadcasted_iota(i32, (8, 128), 1)
    row = lax.broadcasted_iota(i32, (8, 128), 0)
    centres = (
        ((px * 8 + (lane >> 4)).astype(f32) + 0.5) / GRID,
        ((py * 16 + (lane & 15)).astype(f32) + 0.5) / GRID,
        ((pz * 8 + row).astype(f32) + 0.5) / GRID,
    )
    counts = cnt_ref[...]
    turn[...] = jnp.zeros(turn.shape, f32)
    acc_ref[...] = jnp.zeros(acc_ref.shape, f32)
    parts = (below_ref, own_ref, above_ref)

    def gather(s):
        j = nb_ref[s]
        owner = j >> 9
        dz = (owner & 7) - pz + 1
        dy = ((owner >> 3) & 3) - py + 1
        dx = (owner >> 5) - px + 1
        chunk = ((dz * 3 + dy) * 3 + dx) * 4 + ((j >> 7) & 3)
        at = j & 127
        bits = [((chunk >> b) & 1) == 1 for b in range(7)]
        valid = counts > s
        for c in range(6):

            def pick(lo, level):
                if lo >= 108:
                    return None
                if level == 0:
                    line = jnp.broadcast_to(parts[lo // 36][lo % 36, c : c + 1, :], (8, 128))
                    return jnp.take_along_axis(line, at, axis=1, mode="promise_in_bounds")
                first = pick(lo, level - 1)
                second = pick(lo + (1 << (level - 1)), level - 1)
                return first if second is None else jnp.where(bits[level - 1], second, first)

            value = pick(0, 7)
            if c < 3:
                value = value - centres[c]
            turn[c] = jnp.where(valid, value, 0.0)
        return jnp.concatenate([turn[:, z, :] for z in range(8)], axis=1)

    def step(s, pair):
        following = gather(jnp.minimum(s + 1, NB - 1))
        hidden = gelu_twice(dot(ki_ref[...], pair.astype(bf16))).astype(bf16)
        acc_ref[...] += gelu_twice(dot(km_ref[...], hidden))
        return following

    lax.fori_loop(0, NB, step, gather(0))
    inverse = 0.5 / counts.astype(f32)
    total = acc_ref[...] * jnp.concatenate([inverse[z : z + 1, :] for z in range(8)], axis=1)
    upper = total.astype(bf16)
    lower = (total - upper.astype(f32)).astype(bf16)
    latent = dot(ko_ref[...], upper) + dot(ko_ref[...], lower)
    out_ref[...] = latent.astype(bf16).reshape(8, 8, 1024)


def forward_kernel(m_ref, ahi_ref, alo_ref, whi_ref, wlo_ref, out_ref):
    rows = [
        m_ref[s].astype(f32)[:, z * 128 : (z + 1) * 128] for s in range(8) for z in range(8)
    ]
    cells = jnp.concatenate(rows, axis=0).astype(bf16)
    z = dot(ahi_ref[...], cells) + dot(alo_ref[...], cells)
    right = []
    for kh in range(4):
        right += [z[kh * 64 + 32 : kh * 64 + 64], -z[kh * 64 : kh * 64 + 32]]
    both = jnp.concatenate([z, jnp.concatenate(right, axis=0)], axis=1).astype(bf16)
    p = dot_t(whi_ref[...], both) + dot_t(wlo_ref[...], both)
    for kh in range(4):
        for h in range(2):
            line = jnp.concatenate(
                [p[q * 64 : (q + 1) * 64, kh * 64 : (kh + 1) * 64] for q in (2 * h, 2 * h + 1)], axis=1
            )
            for jh in range(8):
                out_ref[pl.ds(((jh * 4 + kh) * 8) * 2 + h, 8, stride=2), :] = line[jh * 8 : jh * 8 + 8]


def mix_kernel(r_ref, w_ref, own_ref, sel_ref, place_ref, half_ref, out_ref):
    s = jnp.sum(r_ref[...], axis=0)
    s = s.astype(bf16).astype(f32)
    own = own_ref[...]
    g = jnp.zeros((16, 128), f32)
    for ch in range(8):
        line = jnp.concatenate([s[2 * ch : 2 * ch + 1], s[2 * ch + 1 : 2 * ch + 2]], axis=1)
        g = g + dot((line * own).astype(bf16), w_ref[ch])
    spread = dot(g.astype(bf16), sel_ref[...]) * place_ref[...]
    d = dot(half_ref[...], spread.astype(bf16))
    d = jnp.concatenate([d[0:2, oh * 128 : (oh + 1) * 128] for oh in range(8)], axis=0).astype(bf16)
    for n in range(32):
        out_ref[n] = d


def inverse_kernel(q_ref, v_ref, bc_ref, bs_ref, partner_ref, out_ref):
    blocks = []
    for kh in range(4):
        rows = jnp.concatenate([q_ref[jh, kh] for jh in range(8)], axis=0).astype(f32)
        blocks.append(jnp.concatenate([rows[:, 0:64], rows[:, 64:128]], axis=0))
    x = jnp.concatenate(blocks, axis=1)
    row = lax.broadcasted_iota(i32, (256, 256), 0)
    lane = lax.broadcasted_iota(i32, (256, 256), 1)
    x = jnp.where((row == 0) & (lane < 8), 0.0, x)
    xb = x.astype(bf16)
    twin = dot(partner_ref[...], xb[:, 0:128])
    low = lane[0:1, 0:128]
    side = jnp.where(low < 8, 0.5, jnp.where(low < 16, -0.5, 0.0))
    weight = jnp.where(lane[0:1, :] < 16, 0.5, 2.0)
    power = jnp.sum(x * x, axis=0, keepdims=True) * weight
    cross = jnp.sum(x[:, 0:128] * twin, axis=0, keepdims=True) * side
    power = jnp.broadcast_to(power[:, 0:128] + power[:, 128:256] + cross, (8, 128))
    for shift in (8, 16, 32, 64):
        power = power + pltpu.roll(power, shift, 1)
    scale = lax.rsqrt(power * (1.0 / (CELLS * CELLS)) + NORM_FLOOR)[0:1]
    scale = jnp.concatenate([scale, scale], axis=1)
    g = (dot(v_ref[...], xb) * scale).astype(bf16)
    out = dot_t(bc_ref[...], g[0:128]) + dot_t(bs_ref[...], g[128:256])
    out_ref[...] = out.astype(bf16).reshape(8, 8, 8, 128)


def output_kernel(y_ref, lat_ref, w_ref, out_ref):
    for z in range(8):
        y = jnp.concatenate([y_ref[s, z].astype(f32) for s in range(8)], axis=0)
        lat = jnp.concatenate(
            [lat_ref[s].astype(f32)[:, z * 128 : (z + 1) * 128] for s in range(8)], axis=0
        )
        both = jnp.concatenate([lat, y], axis=0).T.astype(bf16)
        v = dot(both, w_ref[...])
        out_ref[:, z, :] = 0.5 * gelu_twice(v)


def call(kernel, name, shape, dtype, *args, scratch=(), smem=0):
    return pl.pallas_call(
        kernel,
        out_shape=jax.ShapeDtypeStruct(shape, dtype),
        in_specs=[SMEM] * smem + [VMEM] * (len(args) - smem),
        out_specs=VMEM,
        scratch_shapes=list(scratch),
        compiler_params=pltpu.CompilerParams(vmem_limit_bytes=48 * 1024 * 1024),
        name=name,
    )(*args)


def beside(cells, axis):
    count = lax.axis_size(axis)
    ends = count - 1
    return (
        lax.ppermute(cells, axis, [(i, i + 1) for i in range(ends)]),
        cells,
        lax.ppermute(cells, axis, [(i + 1, i) for i in range(ends)]),
    )


def turned(cos, sin, phase):
    c, s = jnp.cos(phase), jnp.sin(phase)
    return cos * c - sin * s, sin * c + cos * s


def body(point_data, neighbours, counts, kernel_in, kernel_mid, kernel_out, spectral, skip_weight):
    gx = lax.axis_index("gx")
    gy = lax.axis_index("gy")
    gz = lax.axis_index(GZ)
    place = jnp.stack([gx, gy, gz]).astype(i32)

    own = jnp.pad(point_data[0].reshape(6, 4, 128).transpose(1, 0, 2), ((0, 0), (0, 2), (0, 0)))
    line = jnp.concatenate(beside(own, "gx"), axis=0)
    plane = jnp.concatenate(beside(line, "gy"), axis=0)
    below, same, above = beside(plane, GZ)

    near = neighbours[0].transpose(3, 2, 0, 1).reshape(NB, 8, 128)
    valid = counts[0].transpose(2, 0, 1).reshape(8, 128)
    ki = jnp.pad(kernel_in.T, ((0, 0), (0, 2)))
    km = kernel_mid.T * jnp.bfloat16(0.5)
    latent = call(
        encoder_kernel,
        "encoder",
        (8, 8, 1024),
        bf16,
        place,
        below,
        same,
        above,
        near,
        valid,
        ki,
        km,
        kernel_out.T,
        scratch=(pltpu.VMEM((8, 8, 128), f32), pltpu.VMEM((80, 1024), f32)),
        smem=1,
    )

    (ffi, ffj), (ifi, ifj), xl, yl = plane_tables()
    local = angle(1, ffi[:, None] * xl[None, :] + ffj[:, None] * yl[None, :])
    phase = ((jnp.asarray(ffi, i32) * 8 * gx + jnp.asarray(ffj, i32) * 16 * gy) % GRID).astype(f32)
    cos, sin = turned(
        np.cos(local).astype(np.float32),
        np.sin(local).astype(np.float32),
        (phase * (2.0 * math.pi / GRID))[:, None],
    )
    whi, wlo = split_two(jnp.concatenate([cos, sin], axis=1))
    local = angle(1, ifi[None, :] * xl[:, None] + ifj[None, :] * yl[:, None])
    phase = ((jnp.asarray(ifi, i32) * 8 * gx + jnp.asarray(ifj, i32) * 16 * gy) % GRID).astype(f32)
    cos, sin = turned(
        np.cos(local).astype(np.float32),
        np.sin(local).astype(np.float32),
        (phase * (2.0 * math.pi / GRID))[None, :],
    )
    back = jnp.concatenate([cos, sin], axis=0).astype(bf16)

    w = spectral.reshape(2, 2, 2, 4, 8, 8, 64).transpose(0, 4, 2, 1, 3, 5, 6)
    wr, wi = w[0], w[1]
    mixing = jnp.stack(
        [jnp.concatenate([wr, wi], axis=-1), jnp.concatenate([-wi, wr], axis=-1)], axis=3
    ).reshape(8, 256, 128)
    joint = jnp.concatenate([skip_weight, jnp.eye(64, dtype=bf16)], axis=0)

    depth = lax.all_to_all(latent, GZ, split_axis=0, concat_axis=0)
    ahi, alo = third_forward()
    partial = call(forward_kernel, "forward", (512, 128), f32, depth, ahi, alo, whi, wlo)
    partial = lax.all_to_all(partial.reshape(256, 2, 128), ALL, split_axis=0, concat_axis=0)
    own_mask, place_mask, half = mode_masks()
    mixed = call(
        mix_kernel,
        "mix",
        (32, 16, 128),
        bf16,
        partial.reshape(32, 16, 128),
        mixing,
        own_mask,
        placing(),
        place_mask,
        half,
    )
    mixed = lax.all_to_all(mixed.reshape(256, 2, 128), ALL, split_axis=0, concat_axis=0)
    third = third_inverse()
    branch = call(
        inverse_kernel,
        "inverse",
        (8, 8, 8, 128),
        bf16,
        mixed.reshape(8, 4, 16, 128),
        back,
        third[:, :256],
        third[:, 256:],
        partner_table(),
    )
    branch = lax.all_to_all(branch, GZ, split_axis=0, concat_axis=0)
    out = call(output_kernel, "output", (128, 8, 64), f32, branch, latent, joint)
    return out.reshape(1, 8, 16, 8, 64)


def solution(mesh):
    split = Mesh(
        mesh.devices.reshape(mesh.shape["gx"], mesh.shape["gy"], 4, 2), ("gx", "gy", "gz_0", "gz_1")
    )
    return jax.shard_map(
        body,
        mesh=split,
        in_specs=(
            P(None, None, ALL),
            P(None, "gx", "gy", GZ, None),
            P(None, "gx", "gy", GZ),
            P(),
            P(),
            P(),
            P(None, GZ, "gx", "gy", None, None),
            P(),
        ),
        out_specs=P(None, "gx", "gy", GZ, None),
        check_vma=False,
    )
```

time: 363 us -> 132 us (0.36); the launches traced: 358 us -> 132 us
  blocking collectives: 97.5 us -> 0 us
  local copies, waits for them, and re-layouts: 83.7 us -> 4.3 us
  matrix products: 51.6 us -> 0 us
  other arithmetic: 51.4 us -> 0.76 us
  Pallas kernels: 0 us -> 35.3 us
  waiting for transfers between devices: 24.2 us -> 45.7 us
  loops' own time: 16 us -> 0 us
  starting transfers between devices: 32.3 us -> 45 us
    all_to_all x5 -> x0, blocking collectives: 53.1 us -> none  [the longest x4 43.7 us: in_one_piece(): lax.all_to_all(both, axis, split_axis=split_dim, concat_axis=concat_dim,...]
    dot_general x33 -> x0, matrix products: 46.5 us -> none  [the longest x8 28.3 us: one_slab(): jnp.dot(rows, slot_hot, preferred_element_type=jnp.float32)]
    all_gather x4 -> x0, blocking collectives: 44.4 us -> none  [all_in_one(): both, at, found = (lax.all_gather(jnp.concatenate(lines), axis), 0, {})]
    pallas_call x0 -> x5, Pallas kernels: none -> 35.3 us  [call(): pl.pallas_call(kernel, out_shape=jax.ShapeDtypeStruct(shape, dtype), in_s...]
    add x19 -> x0, other arithmetic: 21.8 us -> none  [the longest x8 18.1 us: one_slab(): found = found[0] + found[1] + found[2]]
    all_to_all x3 -> x4, waiting for transfers between devices: 16.1 us -> 37.4 us  [the longest x1 14.7 us: body(): lax.all_to_all(partial.reshape(256, 2, 128), ALL, split_axis=0, concat_ax...]
    dynamic_slice x32 -> x0, local copies, waits for them, and re-layouts: 18 us -> none  [the longest x8 7.09 us: one_slab(): lax.dynamic_index_in_dim(lax.dynamic_index_in_dim(block_index, geometry,...]
    add x8 -> x0, local copies, waits for them, and re-layouts: 17 us -> none  [one_slab(): found = found[0] + found[1] + found[2]]
  transfers between devices with their start and end apart: 9 -> 10, of which waited for: 7 -> 7; matrix products, arithmetic and copies ran while one was open for 1% -> 1% of each run, Pallas kernels for 0% -> 0%
where the time goes in v1:
time: 132 us
  waiting for transfers between devices  45.7 us (35%)
  starting transfers between devices  45 us (34%)
  Pallas kernels  35.3 us (27%)
  local copies, waits for them, and re-layouts  4.3 us (3%)
    pallas_call x5, Pallas kernels, call(): pl.pallas_call(kernel, out_shape=jax.ShapeDtypeStruct(shape, dtype), in_s...  35.3 us
    all_to_all x1, waiting for transfers between devices, body(): lax.all_to_all(partial.reshape(256, 2, 128), ALL, split_axis=0, concat_ax...  14.7 us
    ppermute x3, starting transfers between devices, beside(): lax.ppermute(cells, axis, [(i, i + 1) for i in range(ends)])  13.9 us
    all_to_all x1, waiting for transfers between devices, body(): lax.all_to_all(mixed.reshape(256, 2, 128), ALL, split_axis=0, concat_axis=0)  12.9 us
    all_to_all x1, starting transfers between devices, body(): lax.all_to_all(partial.reshape(256, 2, 128), ALL, split_axis=0, concat_ax...  12.7 us
    ppermute x3, waiting for transfers between devices, beside(): lax.ppermute(cells, axis, [(i + 1, i) for i in range(ends)])  8.26 us
    all_to_all x1, starting transfers between devices, body(): lax.all_to_all(mixed.reshape(256, 2, 128), ALL, split_axis=0, concat_axis=0)  5.89 us
    all_to_all x1, waiting for transfers between devices, body(): depth = lax.all_to_all(latent, GZ, split_axis=0, concat_axis=0)  5.22 us
  transfers between devices with their start and end apart: 10, of which 7 were waited for; matrix products, arithmetic and copies ran while one was open for 1% of the time, Pallas kernels for 0%

profile of v1, /device:TPU:1, one launch (start us, length us, event | category | flops | bytes accessed | tf_op | source)
XLA Modules:
  0.0 131.6 jit_solution(15374650573101380815)
XLA Ops:
  0.0 0.8 copy.44
  0.8 4.3 %collective-permute-start = (f32[4,8,128]{2,1,0:T(8,128)S(1)}, f32[4,8,128]{2,1,0:T(8,128)S(1)}, u32[]{:S(2)}, u32[]{:S(2)}) collective-permute-start(f32[4,8,128]{2,1,0:T(8,128)S(1)} %pad.8), channel_id=1, source_target_pairs={{0,32},{32,64},{64,96},{96,128},{128,160},{160,192},{192,224},{1,3... | collective-permute-start | bytes 49160 | tf_op jit(solution)/shard_map/ppermute | solution.py:262
  5.1 1.3 collective-permute-start.1
  6.5 0.6 copy-done.23
  7.3 0.1 copy_bitcast_fusion
  7.5 0.7 copy-done.14
  8.3 0.1 multiply_subtract_fusion
  8.5 1.3 collective-permute-done.1
  9.8 3.2 %collective-permute-start.2 = (f32[12,8,128]{2,1,0:T(8,128)S(1)}, f32[12,8,128]{2,1,0:T(8,128)S(1)}, u32[]{:S(2)}, u32[]{:S(2)}) collective-permute-start(f32[12,8,128]{2,1,0:T(8,128)S(1)} %pad_maximum_fusion.3), channel_id=1, source_target_pairs={{0,8},{8,16},{16,24},{1,9},{9,17},{17,25},{2,10},{10,18},{18,26},{... | collective-permute-start | bytes 147464 | tf_op jit(solution)/shard_map/ppermute | solution.py:262
  13.0 1.3 collective-permute-start.3
  14.4 3.5 %collective-permute-done.3 = f32[12,8,128]{2,1,0:T(8,128)S(1)} collective-permute-done((f32[12,8,128]{2,1,0:T(8,128)S(1)}, f32[12,8,128]{2,1,0:T(8,128)S(1)}, u32[]{:S(2)}, u32[]{:S(2)}) %collective-permute-start.3) | collective-permute-done | bytes 49184 | tf_op jit(solution)/shard_map/ppermute | solution.py:264
  17.9 6.3 %collective-permute-start.4 = (f32[36,8,128]{2,1,0:T(8,128)S(1)}, f32[36,8,128]{2,1,0:T(8,128)S(1)}, u32[]{:S(2)}, u32[]{:S(2)}) collective-permute-start(f32[36,8,128]{2,1,0:T(8,128)S(1)} %constant_dynamic-update-slice_fusion.own_ref), channel_id=1, source_target_pairs={{0,1},{1,2},{2,3},{3,4},{4,5},{5,6},{6,7},{8,9},{9,10},{10,11},{11... | collective-permute-start | bytes 442376 | tf_op jit(solution)/shard_map/ppermute | solution.py:262
  24.2 1.9 %collective-permute-start.5 = (f32[36,8,128]{2,1,0:T(8,128)S(1)}, f32[36,8,128]{2,1,0:T(8,128)S(1)}, u32[]{:S(2)}, u32[]{:S(2)}) collective-permute-start(f32[36,8,128]{2,1,0:T(8,128)S(1)} %constant_dynamic-update-slice_fusion.own_ref), channel_id=1, source_target_pairs={{1,0},{2,1},{3,2},{4,3},{5,4},{6,5},{7,6},{9,8},{10,9},{11,10},{12... | collective-permute-start | bytes 442376 | tf_op jit(solution)/shard_map/ppermute | solution.py:264
  26.2 0.2 copy.37.nb_ref
  26.5 0.5 copy-done.19
  26.9 0.1 copy.35
  27.2 3.5 %collective-permute-done.5.above_ref = f32[36,8,128]{2,1,0:T(8,128)S(1)} collective-permute-done((f32[36,8,128]{2,1,0:T(8,128)S(1)}, f32[36,8,128]{2,1,0:T(8,128)S(1)}, u32[]{:S(2)}, u32[]{:S(2)}) %collective-permute-start.5) | collective-permute-done | bytes 147488 | tf_op jit(solution)/shard_map/ppermute | solution.py:264
  30.7 28.9 %encoder.1.lat_ref = bf16[8,8,1024]{2,1,0:T(8,128)(2,1)} custom-call(s32[3]{0:T(128)S(1)} %pad_add_fusion.place_ref, f32[36,8,128]{2,1,0:T(8,128)S(1)} %collective-permute-done.4.below_ref, f32[36,8,128]{2,1,0:T(8,128)S(1)} %constant_dynamic-update-slice_fusion.own_ref, f32[36,8,128]{2,1,0:T(8,128)S(1)} %collective-permute-done.5.above_ref, ...), custom_call_target="tpu_custom_call" | custom-call | tf_op jit(solution)/shard_map/encoder/pallas_call | solution.py:247
  59.6 4.3 %all-to-all-start = ((bf16[8,8,1024]{2,1,0:T(8,128)(2,1)}), bf16[8,8,1024]{2,1,0:T(8,128)(2,1)S(1)}, u32[]{:S(2)}, u32[]{:S(2)}) async-start(bf16[8,8,1024]{2,1,0:T(8,128)(2,1)} %encoder.1.lat_ref), calls=%async_computation | async-start | bytes 262144 | tf_op jit(solution)/shard_map/all_to_all | solution.py:331
  63.8 5.2 %all-to-all-done.m_ref = bf16[8,8,1024]{2,1,0:T(8,128)(2,1)S(1)} async-done(((bf16[8,8,1024]{2,1,0:T(8,128)(2,1)}), bf16[8,8,1024]{2,1,0:T(8,128)(2,1)S(1)}, u32[]{:S(2)}, u32[]{:S(2)}) %all-to-all-start) | async-done | bytes 131104 | tf_op jit(solution)/shard_map/all_to_all | solution.py:331
  69.1 1.4 %forward.1 = f32[512,128]{1,0:T(8,128)} custom-call(bf16[8,8,1024]{2,1,0:T(8,128)(2,1)S(1)} %all-to-all-done.m_ref, bf16[256,512]{1,0:T(8,128)(2,1)S(1)} %copy-done.4, bf16[256,512]{1,0:T(8,128)(2,1)S(1)} %copy-done.5, bf16[256,256]{1,0:T(8,128)(2,1)S(1)} %fusion.whi_ref, bf16[256,256]{1,0:T(8,128)(2,1)S(1)} %subtract_convert_fusion.wlo_ref), custom_call_target="tpu_custom_call" | custom-call | tf_op jit(solution)/shard_map/forward/pallas_call | solution.py:247
  70.5 12.7 %all-to-all-start.1 = ((f32[256,2,128]{2,1,0:T(2,128)}), f32[256,2,128]{2,1,0:T(2,128)S(1)}, u32[]{:S(2)}, u32[]{:S(2)}) async-start(f32[256,2,128]{2,1,0:T(2,128)} %bitcast.13), calls=%async_computation.1 | async-start | bytes 524288 | tf_op jit(solution)/shard_map/all_to_all | solution.py:334
  83.3 0.3 maximum_bitcast_fusion
  83.7 14.7 %all-to-all-done.1 = f32[256,2,128]{2,1,0:T(2,128)S(1)} async-done(((f32[256,2,128]{2,1,0:T(2,128)}), f32[256,2,128]{2,1,0:T(2,128)S(1)}, u32[]{:S(2)}, u32[]{:S(2)}) %all-to-all-start.1) | async-done | bytes 262176 | tf_op jit(solution)/shard_map/all_to_all | solution.py:334
  98.5 1.1 mix.1
  99.6 5.9 %all-to-all-start.2 = ((bf16[256,2,128]{2,1,0:T(2,128)(2,1)}), bf16[256,2,128]{2,1,0:T(2,128)(2,1)S(1)}, u32[]{:S(2)}, u32[]{:S(2)}) async-start(bf16[256,2,128]{2,1,0:T(2,128)(2,1)} %bitcast.23), calls=%async_computation.2 | async-start | bytes 262144 | tf_op jit(solution)/shard_map/all_to_all | solution.py:348
  105.7 12.9 %all-to-all-done.2 = bf16[256,2,128]{2,1,0:T(2,128)(2,1)S(1)} async-done(((bf16[256,2,128]{2,1,0:T(2,128)(2,1)}), bf16[256,2,128]{2,1,0:T(2,128)(2,1)S(1)}, u32[]{:S(2)}, u32[]{:S(2)}) %all-to-all-start.2) | async-done | bytes 131104 | tf_op jit(solution)/shard_map/all_to_all | solution.py:348
  118.6 1.6 %inverse.1 = bf16[8,8,8,128]{3,2,1,0:T(8,128)(2,1)} custom-call(bf16[8,4,16,128]{3,2,1,0:T(8,128)(2,1)S(1)} %bitcast.44, bf16[256,256]{1,0:T(8,128)(2,1)S(1)} %pad_maximum_fusion.2.v_ref, bf16[512,256]{1,0:T(8,128)(2,1)S(1)} %copy-done.3, bf16[512,256]{1,0:T(8,128)(2,1)S(1)} %copy-done.2, bf16[256,256]{1,0:T(8,128)(2,1)S(1)} %copy-done.6), custom_call_target="tpu_custom_call" | custom-call | tf_op jit(solution)/shard_map/inverse/pallas_call | solution.py:247
  120.2 3.8 %all-to-all-start.3 = ((bf16[8,8,8,128]{3,2,1,0:T(8,128)(2,1)}), bf16[8,8,8,128]{3,2,1,0:T(8,128)(2,1)S(1)}, u32[]{:S(2)}, u32[]{:S(2)}) async-start(bf16[8,8,8,128]{3,2,1,0:T(8,128)(2,1)} %inverse.1), calls=%async_computation.3 | async-start | bytes 262144 | tf_op jit(solution)/shard_map/all_to_all | solution.py:361
  124.0 0.7 copy-done.18
  124.7 4.5 %all-to-all-done.3.y_ref = bf16[8,8,8,128]{3,2,1,0:T(8,128)(2,1)S(1)} async-done(((bf16[8,8,8,128]{3,2,1,0:T(8,128)(2,1)}), bf16[8,8,8,128]{3,2,1,0:T(8,128)(2,1)S(1)}, u32[]{:S(2)}, u32[]{:S(2)}) %all-to-all-start.3) | async-done | bytes 131104 | tf_op jit(solution)/shard_map/all_to_all | solution.py:361
  129.3 2.3 %output.1 = f32[128,8,64]{2,1,0:T(8,128)} custom-call(bf16[8,8,8,128]{3,2,1,0:T(8,128)(2,1)S(1)} %all-to-all-done.3.y_ref, bf16[8,8,1024]{2,1,0:T(8,128)(2,1)} %encoder.1.lat_ref, bf16[128,64]{1,0:T(8,128)(2,1)S(1)} %pad_maximum_fusion.4.w_ref), custom_call_target="tpu_custom_call" | custom-call | tf_op jit(solution)/shard_map/output/pallas_call | solution.py:247
  (72 shorter events, 0.9 us)
Async XLA Ops:
  0.0 7.3 %copy-start = (bf16[2,2,2,4,64,64]{5,4,3,2,1,0:T(8,128)(2,1)S(1)}, bf16[2,2,2,4,64,64]{5,4,3,2,1,0:T(8,128)(2,1)}, u32[]{:S(2)}) copy-start(bf16[2,2,2,4,64,64]{5,4,3,2,1,0:T(8,128)(2,1)} %param.31) | copy-start | bytes 786436
  0.8 7.7 %collective-permute-start = (f32[4,8,128]{2,1,0:T(8,128)S(1)}, f32[4,8,128]{2,1,0:T(8,128)S(1)}, u32[]{:S(2)}, u32[]{:S(2)}) collective-permute-start(f32[4,8,128]{2,1,0:T(8,128)S(1)} %pad.8), channel_id=1, source_target_pairs={{0,32},{32,64},{64,96},{96,128},{128,160},{160,192},{192,224},{1,3... | collective-permute-start | bytes 49160 | tf_op jit(solution)/shard_map/ppermute | solution.py:262
  5.1 4.7 %collective-permute-start.1 = (f32[4,8,128]{2,1,0:T(8,128)S(1)}, f32[4,8,128]{2,1,0:T(8,128)S(1)}, u32[]{:S(2)}, u32[]{:S(2)}) collective-permute-start(f32[4,8,128]{2,1,0:T(8,128)S(1)} %pad.8), channel_id=1, source_target_pairs={{32,0},{64,32},{96,64},{128,96},{160,128},{192,160},{224,192},{33,... | collective-permute-start | bytes 49160 | tf_op jit(solution)/shard_map/ppermute | solution.py:264
  6.5 0.7 copy-start.21
  6.5 0.7 copy-start.22
  6.5 0.7 copy-start.20
  7.3 0.9 copy-start.14
  7.3 1.0 copy-start.15
  7.3 1.1 copy-start.17
  7.5 18.8 %copy-start.11 = (s32[1,8,16,8,32]{4,3,2,1,0:T(8,128)S(1)}, s32[1,8,16,8,32]{4,3,2,1,0:T(8,128)}, u32[]{:S(2)}) copy-start(s32[1,8,16,8,32]{4,3,2,1,0:T(8,128)} %param.26) | copy-start | bytes 393220
  9.8 4.5 %collective-permute-start.2 = (f32[12,8,128]{2,1,0:T(8,128)S(1)}, f32[12,8,128]{2,1,0:T(8,128)S(1)}, u32[]{:S(2)}, u32[]{:S(2)}) collective-permute-start(f32[12,8,128]{2,1,0:T(8,128)S(1)} %pad_maximum_fusion.3), channel_id=1, source_target_pairs={{0,8},{8,16},{16,24},{1,9},{9,17},{17,25},{2,10},{10,18},{18,26},{... | collective-permute-start | bytes 147464 | tf_op jit(solution)/shard_map/ppermute | solution.py:262
  13.0 4.8 %collective-permute-start.3 = (f32[12,8,128]{2,1,0:T(8,128)S(1)}, f32[12,8,128]{2,1,0:T(8,128)S(1)}, u32[]{:S(2)}, u32[]{:S(2)}) collective-permute-start(f32[12,8,128]{2,1,0:T(8,128)S(1)} %pad_maximum_fusion.3), channel_id=1, source_target_pairs={{8,0},{16,8},{24,16},{9,1},{17,9},{25,17},{10,2},{18,10},{26,18},{... | collective-permute-start | bytes 147464 | tf_op jit(solution)/shard_map/ppermute | solution.py:264
  17.9 9.3 %collective-permute-start.4 = (f32[36,8,128]{2,1,0:T(8,128)S(1)}, f32[36,8,128]{2,1,0:T(8,128)S(1)}, u32[]{:S(2)}, u32[]{:S(2)}) collective-permute-start(f32[36,8,128]{2,1,0:T(8,128)S(1)} %constant_dynamic-update-slice_fusion.own_ref), channel_id=1, source_target_pairs={{0,1},{1,2},{2,3},{3,4},{4,5},{5,6},{6,7},{8,9},{9,10},{10,11},{11... | collective-permute-start | bytes 442376 | tf_op jit(solution)/shard_map/ppermute | solution.py:262
  24.2 6.5 %collective-permute-start.5 = (f32[36,8,128]{2,1,0:T(8,128)S(1)}, f32[36,8,128]{2,1,0:T(8,128)S(1)}, u32[]{:S(2)}, u32[]{:S(2)}) collective-permute-start(f32[36,8,128]{2,1,0:T(8,128)S(1)} %constant_dynamic-update-slice_fusion.own_ref), channel_id=1, source_target_pairs={{1,0},{2,1},{3,2},{4,3},{5,4},{6,5},{7,6},{9,8},{10,9},{11,10},{12... | collective-permute-start | bytes 442376 | tf_op jit(solution)/shard_map/ppermute | solution.py:264
  26.2 0.8 copy-start.16
  27.1 3.5 %copy-start.9 = (bf16[80,64]{0,1:T(8,128)(2,1)S(1)}, bf16[80,64]{0,1:T(8,128)(2,1)}, u32[]{:S(2)}) copy-start(bf16[80,64]{0,1:T(8,128)(2,1)} %param.30) | copy-start | bytes 30724
  59.6 9.5 %copy-start.5 = (bf16[256,512]{1,0:T(8,128)(2,1)S(1)}, bf16[256,512]{1,0:T(8,128)(2,1)}, u32[]{:S(2)}) copy-start(bf16[256,512]{1,0:T(8,128)(2,1)} %constant.94.clone.alo_ref) | copy-start | bytes 786436
  59.6 9.5 %all-to-all-start = ((bf16[8,8,1024]{2,1,0:T(8,128)(2,1)}), bf16[8,8,1024]{2,1,0:T(8,128)(2,1)S(1)}, u32[]{:S(2)}, u32[]{:S(2)}) async-start(bf16[8,8,1024]{2,1,0:T(8,128)(2,1)} %encoder.1.lat_ref), calls=%async_computation | async-start | bytes 262144 | tf_op jit(solution)/shard_map/all_to_all | solution.py:331
  63.8 5.2 %copy-start.4 = (bf16[256,512]{1,0:T(8,128)(2,1)S(1)}, bf16[256,512]{1,0:T(8,128)(2,1)}, u32[]{:S(2)}) copy-start(bf16[256,512]{1,0:T(8,128)(2,1)} %constant.93.clone.ahi_ref) | copy-start | bytes 786436
  70.5 28.0 %all-to-all-start.1 = ((f32[256,2,128]{2,1,0:T(2,128)}), f32[256,2,128]{2,1,0:T(2,128)S(1)}, u32[]{:S(2)}, u32[]{:S(2)}) async-start(f32[256,2,128]{2,1,0:T(2,128)} %bitcast.13), calls=%async_computation.1 | async-start | bytes 524288 | tf_op jit(solution)/shard_map/all_to_all | solution.py:334
  83.6 14.9 %copy-start.1 = (bf16[128,1024]{1,0:T(8,128)(2,1)S(1)}, bf16[128,1024]{1,0:T(8,128)(2,1)}, u32[]{:S(2)}) copy-start(bf16[128,1024]{1,0:T(8,128)(2,1)} %constant.96.clone.sel_ref) | copy-start | bytes 786436
  83.7 14.8 %copy-start.7 = (f32[16,1024]{1,0:T(8,128)S(1)}, f32[16,1024]{1,0:T(8,128)}, u32[]{:S(2)}) copy-start(f32[16,1024]{1,0:T(8,128)} %constant.97.clone.place_ref) | copy-start | bytes 196612
  83.7 14.8 %copy-start.8 = (f32[16,256]{1,0:T(8,128)S(1)}, f32[16,256]{1,0:T(8,128)}, u32[]{:S(2)}) copy-start(f32[16,256]{1,0:T(8,128)} %constant.95.clone.own_ref) | copy-start | bytes 49156
  83.7 14.8 %copy-start.10 = (bf16[8,16]{1,0:T(8,128)(2,1)S(1)}, bf16[8,16]{1,0:T(8,128)(2,1)}, u32[]{:S(2)}) copy-start(bf16[8,16]{1,0:T(8,128)(2,1)} %constant.98.clone.half_ref) | copy-start | bytes 772
  99.6 5.9 %copy-start.12 = (f32[128,256]{1,0:T(8,128)S(1)}, f32[128,256]{1,0:T(8,128)}, u32[]{:S(2)}) copy-start(f32[128,256]{1,0:T(8,128)} %constant.91.clone) | copy-start | bytes 393220
  99.6 5.9 %copy-start.13 = (f32[128,256]{1,0:T(8,128)S(1)}, f32[128,256]{1,0:T(8,128)}, u32[]{:S(2)}) copy-start(f32[128,256]{1,0:T(8,128)} %constant.92.clone) | copy-start | bytes 393220
  99.6 19.0 %all-to-all-start.2 = ((bf16[256,2,128]{2,1,0:T(2,128)(2,1)}), bf16[256,2,128]{2,1,0:T(2,128)(2,1)S(1)}, u32[]{:S(2)}, u32[]{:S(2)}) async-start(bf16[256,2,128]{2,1,0:T(2,128)(2,1)} %bitcast.23), calls=%async_computation.2 | async-start | bytes 262144 | tf_op jit(solution)/shard_map/all_to_all | solution.py:348
  105.6 13.0 %copy-start.2 = (bf16[512,256]{1,0:T(8,128)(2,1)S(1)}, bf16[512,256]{1,0:T(8,128)(2,1)}, u32[]{:S(2)}) copy-start(bf16[512,256]{1,0:T(8,128)(2,1)} %constant.100.clone.bs_ref) | copy-start | bytes 786436
  105.6 13.0 %copy-start.3 = (bf16[512,256]{1,0:T(8,128)(2,1)S(1)}, bf16[512,256]{1,0:T(8,128)(2,1)}, u32[]{:S(2)}) copy-start(bf16[512,256]{1,0:T(8,128)(2,1)} %constant.99.clone.bc_ref) | copy-start | bytes 786436
  105.6 13.0 %copy-start.6 = (bf16[256,256]{1,0:T(8,128)(2,1)S(1)}, bf16[256,256]{1,0:T(8,128)(2,1)}, u32[]{:S(2)}) copy-start(bf16[256,256]{1,0:T(8,128)(2,1)} %constant.101.clone.partner_ref) | copy-start | bytes 393220
  120.2 9.0 %all-to-all-start.3 = ((bf16[8,8,8,128]{3,2,1,0:T(8,128)(2,1)}), bf16[8,8,8,128]{3,2,1,0:T(8,128)(2,1)S(1)}, u32[]{:S(2)}, u32[]{:S(2)}) async-start(bf16[8,8,8,128]{3,2,1,0:T(8,128)(2,1)} %inverse.1), calls=%async_computation.3 | async-start | bytes 262144 | tf_op jit(solution)/shard_map/all_to_all | solution.py:361
  124.0 0.7 copy-start.18
  (2 other events, 1.4 us)

commit v2 on v1

--- a/solution.py
+++ b/solution.py
@@ -112,66 +112,159 @@
     return v * jnp.tanh(v * (v * v * C1 + C0)) + v
 
 
+def column(line):
+    return jnp.broadcast_to(line, (128, 128)).T
+
+
+def rank_rows(rank, first, count):
+    r = lax.broadcasted_iota(i32, (count, 1024), 0) + first
+    return jnp.where(r == rank, 1.0, 0.0).astype(bf16)
+
+
+def sort_kernel(place_ref, nb_ref, cnt_ref, code_ref, cnt8_ref, cen_ref, rank_ref, scnt_ref, steps_ref):
+    px, py, pz = place_ref[0], place_ref[1], place_ref[2]
+    j = nb_ref[...]
+    owner = j >> 9
+    dz = (owner & 7) - pz + 1
+    dy = ((owner >> 3) & 3) - py + 1
+    dx = (owner >> 5) - px + 1
+    chunk = (((dz * 3 + dy) * 3 + dx) * 4 + ((j >> 7) & 3)) & 127
+    chunk = chunk.astype(f32)
+    lane = (j & 127).astype(f32)
+    counts = cnt_ref[...].astype(f32)
+    row8 = lax.broadcasted_iota(i32, (8, 128), 0)
+    lane8 = lax.broadcasted_iota(i32, (8, 128), 1)
+    key = counts * 1024.0 - (row8 * 128 + lane8).astype(f32)
+    flat = [key[z : z + 1] for z in range(8)]
+    ranks = [jnp.zeros((128, 128), f32) for _ in range(8)]
+    for z in range(8):
+        own = column(flat[z])
+        ranks = [r + jnp.where(own > line, 1.0, 0.0) for r, line in zip(ranks, flat)]
+    rank = jnp.concatenate([jnp.sum(r, axis=0, keepdims=True) for r in ranks], axis=1).astype(i32)
+    rank_ref[...] = jnp.broadcast_to(rank, (8, 1024))
+    flat = [
+        jnp.concatenate([a[:, z, :] for z in range(8)], axis=1) for a in (chunk, lane)
+    ]
+    node = lax.broadcasted_iota(i32, (8, 1024), 1)
+    wide = lax.broadcasted_iota(i32, (8, 1024), 0)
+    line = jnp.concatenate([counts[z : z + 1] for z in range(8)], axis=1)
+    tail = jnp.where(
+        wide == 0,
+        line,
+        jnp.where(wide == 1, (node >> 7).astype(f32), (node & 127).astype(f32)),
+    )
+    rows = jnp.concatenate(flat + [tail], axis=0).astype(bf16)
+    odd = (row8 & 1) == 1
+    for t in range(4):
+        found = dot_t(rows, rank_rows(rank, t * 256, 256))
+        code = (found[0:32] * 128.0 + found[32:64]).astype(i32)
+        for s in range(4):
+            for h in range(2):
+                code_ref[t, pl.ds(s * 16 + h, 8, stride=2), :] = code[
+                    s * 8 : s * 8 + 8, h * 128 : h * 128 + 128
+                ]
+        tail = found[64:72]
+
+        def both(n):
+            return jnp.where(odd, tail[n : n + 1, 128:256], tail[n : n + 1, 0:128])
+
+        cnt8_ref[t] = both(0).astype(i32)
+        cell = both(2).astype(i32)
+        cen_ref[t, 0] = ((px * 8 + (cell >> 4)).astype(f32) + 0.5) / GRID
+        cen_ref[t, 1] = ((py * 16 + (cell & 15)).astype(f32) + 0.5) / GRID
+        cen_ref[t, 2] = ((pz * 8).astype(f32) + both(1) + 0.5) / GRID
+        scnt_ref[:, t * 256 : t * 256 + 256] = jnp.broadcast_to(tail[0:1], (8, 256))
+        steps_ref[t] = (jnp.max(tail[0:1]).astype(i32) + 3) >> 2
+
+
 def encoder_kernel(
-    place_ref, below_ref, own_ref, above_ref, nb_ref, cnt_ref, ki_ref, km_ref, ko_ref, out_ref, turn, acc_ref
+    steps_ref,
+    below_ref,
+    own_ref,
+    above_ref,
+    code_ref,
+    cnt8_ref,
+    cen_ref,
+    rank_ref,
+    scnt_ref,
+    ki_ref,
+    km_ref,
+    ko_ref,
+    out_ref,
+    words,
+    off_ref,
+    turn,
+    acc_ref,
 ):
-    px, py, pz = place_ref[0], place_ref[1], place_ref[2]
-    lane = lax.broadcasted_iota(i32, (8, 128), 1)
-    row = lax.broadcasted_iota(i32, (8, 128), 0)
-    centres = (
-        ((px * 8 + (lane >> 4)).astype(f32) + 0.5) / GRID,
-        ((py * 16 + (lane & 15)).astype(f32) + 0.5) / GRID,
-        ((pz * 8 + row).astype(f32) + 0.5) / GRID,
-    )
-    counts = cnt_ref[...]
+    parts = (below_ref, own_ref, above_ref)
+    most = jnp.zeros((8, 128), f32)
+    for part in parts:
+        most = jnp.maximum(most, jnp.max(jnp.abs(part[...]), axis=0))
+    most = jnp.maximum(jnp.max(most, axis=1, keepdims=True), 1e-30)
+    scale = jnp.broadcast_to(32767.0 / most, (8, 128))
+    unit = jnp.broadcast_to(most * (1.0 / 32767.0), (8, 128))
+    for n in range(108):
+        q = (parts[n // 36][n % 36] * scale + 32768.5).astype(i32)
+        words[n] = (q << 16) | pltpu.roll(q, 5, 0)
+    units = [jnp.broadcast_to(unit[c : c + 1], (8, 128)) for c in range(6)]
+    for t in range(4):
+        for c in range(3):
+            off_ref[t, c] = cen_ref[t, c] + 32768.0 * units[c]
     turn[...] = jnp.zeros(turn.shape, f32)
     acc_ref[...] = jnp.zeros(acc_ref.shape, f32)
-    parts = (below_ref, own_ref, above_ref)
-
-    def gather(s):
-        j = nb_ref[s]
-        owner = j >> 9
-        dz = (owner & 7) - pz + 1
-        dy = ((owner >> 3) & 3) - py + 1
-        dx = (owner >> 5) - px + 1
-        chunk = ((dz * 3 + dy) * 3 + dx) * 4 + ((j >> 7) & 3)
-        at = j & 127
-        bits = [((chunk >> b) & 1) == 1 for b in range(7)]
-        valid = counts > s
-        for c in range(6):
+    slot = lax.broadcasted_iota(i32, (8, 128), 0) >> 1
+
+    def gather(t, b):
+        code = code_ref[t, pl.ds(pl.multiple_of(b * 8, 8), 8), :]
+        at = code & 127
+        bits = [(code & (128 << n)) != 0 for n in range(7)]
+        valid = cnt8_ref[t] > slot + b * 4
+        for c in range(3):
 
             def pick(lo, level):
                 if lo >= 108:
                     return None
                 if level == 0:
-                    line = jnp.broadcast_to(parts[lo // 36][lo % 36, c : c + 1, :], (8, 128))
+                    line = jnp.broadcast_to(words[lo, c : c + 1, :], (8, 128))
                     return jnp.take_along_axis(line, at, axis=1, mode="promise_in_bounds")
                 first = pick(lo, level - 1)
                 second = pick(lo + (1 << (level - 1)), level - 1)
                 return first if second is None else jnp.where(bits[level - 1], second, first)
 
-            value = pick(0, 7)
-            if c < 3:
-                value = value - centres[c]
-            turn[c] = jnp.where(valid, value, 0.0)
-        return jnp.concatenate([turn[:, z, :] for z in range(8)], axis=1)
-
-    def step(s, pair):
-        following = gather(jnp.minimum(s + 1, NB - 1))
+            word = pick(0, 7)
+            place = lax.shift_right_logical(word, 16).astype(f32) * units[c] - off_ref[t, c]
+            normal = ((word & 65535) - 32768).astype(f32) * units[c + 3]
+            turn[c] = jnp.where(valid, place, 0.0)
+            turn[c + 3] = jnp.where(valid, normal, 0.0)
+        return jnp.concatenate([turn[:, n, :] for n in range(8)], axis=1)
+
+    def step(_, carry):
+        t, b, pair = carry
+        last = b + 1 >= steps_ref[t]
+        nt = jnp.where(last, jnp.minimum(t + 1, 3), t)
+        nb = jnp.where(last, 0, b + 1)
+        following = gather(nt, nb)
         hidden = gelu_twice(dot(ki_ref[...], pair.astype(bf16))).astype(bf16)
-        acc_ref[...] += gelu_twice(dot(km_ref[...], hidden))
-        return following
-
-    lax.fori_loop(0, NB, step, gather(0))
-    inverse = 0.5 / counts.astype(f32)
-    total = acc_ref[...] * jnp.concatenate([inverse[z : z + 1, :] for z in range(8)], axis=1)
-    upper = total.astype(bf16)
-    lower = (total - upper.astype(f32)).astype(bf16)
-    latent = dot(ko_ref[...], upper) + dot(ko_ref[...], lower)
-    out_ref[...] = latent.astype(bf16).reshape(8, 8, 1024)
-
-
-def forward_kernel(m_ref, ahi_ref, alo_ref, whi_ref, wlo_ref, out_ref):
+        hidden = gelu_twice(dot(km_ref[...], hidden))
+        acc_ref[t] += (
+            hidden[:, 0:256] + hidden[:, 256:512] + hidden[:, 512:768] + hidden[:, 768:1024]
+        )
+        return nt, nb, following
+
+    total = steps_ref[0] + steps_ref[1] + steps_ref[2] + steps_ref[3]
+    lax.fori_loop(0, total, step, (jnp.int32(0), jnp.int32(0), gather(0, 0)))
+    mean = jnp.concatenate([acc_ref[t] for t in range(4)], axis=1) * (0.5 / scnt_ref[0:1])
+    upper = mean.astype(bf16)
+    lower = (mean - upper.astype(f32)).astype(bf16)
+    latent = (dot(ko_ref[...], upper) + dot(ko_ref[...], lower)).astype(bf16)
+    rank = rank_ref[0:1]
+    spread = jnp.zeros((64, 1024), f32)
+    for t in range(4):
+        spread = spread + dot(latent[:, t * 256 : t * 256 + 256], rank_rows(rank, t * 256, 256))
+    out_ref[...] = spread.astype(bf16).reshape(8, 8, 1024)
+
+
+def forward_kernel(m_ref, ahi_ref, alo_ref, whi_ref, wlo_ref, out_ref, wide):
     rows = [
         m_ref[s].astype(f32)[:, z * 128 : (z + 1) * 128] for s in range(8) for z in range(8)
     ]
@@ -188,11 +281,12 @@
                 [p[q * 64 : (q + 1) * 64, kh * 64 : (kh + 1) * 64] for q in (2 * h, 2 * h + 1)], axis=1
             )
             for jh in range(8):
-                out_ref[pl.ds(((jh * 4 + kh) * 8) * 2 + h, 8, stride=2), :] = line[jh * 8 : jh * 8 + 8]
+                wide[pl.ds(((jh * 4 + kh) * 8) * 2 + h, 8, stride=2), :] = line[jh * 8 : jh * 8 + 8]
+    out_ref[...] = wide[...].astype(bf16)
 
 
 def mix_kernel(r_ref, w_ref, own_ref, sel_ref, place_ref, half_ref, out_ref):
-    s = jnp.sum(r_ref[...], axis=0)
+    s = jnp.sum(r_ref[...].astype(f32), axis=0)
     s = s.astype(bf16).astype(f32)
     own = own_ref[...]
     g = jnp.zeros((16, 128), f32)
@@ -255,6 +349,47 @@
     )(*args)
 
 
+def sorted_nodes(place, near, valid):
+    shapes = (
+        ((4, 64, 128), i32),
+        ((4, 8, 128), i32),
+        ((4, 3, 8, 128), f32),
+        ((8, 1024), i32),
+        ((8, 1024), f32),
+        ((4,), i32),
+    )
+    return pl.pallas_call(
+        sort_kernel,
+        out_shape=[jax.ShapeDtypeStruct(*s) for s in shapes],
+        in_specs=[SMEM, VMEM, VMEM],
+        out_specs=[VMEM] * 5 + [SMEM],
+        compiler_params=pltpu.CompilerParams(vmem_limit_bytes=48 * 1024 * 1024),
+        name="sort",
+    )(place, near, valid)
+
+
+def encode(steps, tables, pieces, ki, km, ko):
+    return call(
+        encoder_kernel,
+        "encoder",
+        (8, 8, 1024),
+        bf16,
+        steps,
+        *pieces,
+        *tables,
+        ki,
+        km,
+        ko,
+        scratch=(
+            pltpu.VMEM((108, 8, 128), i32),
+            pltpu.VMEM((4, 3, 8, 128), f32),
+            pltpu.VMEM((8, 8, 128), f32),
+            pltpu.VMEM((4, 80, 256), f32),
+        ),
+        smem=1,
+    )
+
+
 def beside(cells, axis):
     count = lax.axis_size(axis)
     ends = count - 1
@@ -285,23 +420,8 @@
     valid = counts[0].transpose(2, 0, 1).reshape(8, 128)
     ki = jnp.pad(kernel_in.T, ((0, 0), (0, 2)))
     km = kernel_mid.T * jnp.bfloat16(0.5)
-    latent = call(
-        encoder_kernel,
-        "encoder",
-        (8, 8, 1024),
-        bf16,
-        place,
-        below,
-        same,
-        above,
-        near,
-        valid,
-        ki,
-        km,
-        kernel_out.T,
-        scratch=(pltpu.VMEM((8, 8, 128), f32), pltpu.VMEM((80, 1024), f32)),
-        smem=1,
-    )
+    *tables, steps = sorted_nodes(place, near, valid)
+    latent = encode(steps, tables, (below, same, above), ki, km, kernel_out.T)
 
     (ffi, ffj), (ifi, ifj), xl, yl = plane_tables()
     local = angle(1, ffi[:, None] * xl[None, :] + ffj[:, None] * yl[None, :])
@@ -330,7 +450,7 @@
 
     depth = lax.all_to_all(latent, GZ, split_axis=0, concat_axis=0)
     ahi, alo = third_forward()
-    partial = call(forward_kernel, "forward", (512, 128), f32, depth, ahi, alo, whi, wlo)
+    partial = call(forward_kernel, "forward", (512, 128), bf16, depth, ahi, alo, whi, wlo, scratch=(pltpu.VMEM((512, 128), f32),))
     partial = lax.all_to_all(partial.reshape(256, 2, 128), ALL, split_axis=0, concat_axis=0)
     own_mask, place_mask, half = mode_masks()
     mixed = call(

time: 132 us -> 116 us (0.88)
  Pallas kernels: 35.3 us -> 21.6 us
  waiting for transfers between devices: 45.7 us -> 40 us
  starting transfers between devices: 45 us -> 46.6 us
    pallas_call x5, Pallas kernels: 35.3 us -> 19 us  [call(): pl.pallas_call(kernel, out_shape=jax.ShapeDtypeStruct(shape, dtype), in_s...]
    ppermute x3, waiting for transfers between devices: 8.26 us -> 4.83 us  [beside(): lax.ppermute(cells, axis, [(i + 1, i) for i in range(ends)])]
    pallas_call x0 -> x1, Pallas kernels: none -> 2.61 us  [sorted_nodes(): pl.pallas_call(sort_kernel, out_shape=[jax.ShapeDtypeStruct(*s) for s in...]
    all_to_all x1, waiting for transfers between devices: 14.7 us -> 12.4 us  [body(): lax.all_to_all(partial.reshape(256, 2, 128), ALL, split_axis=0, concat_ax...]
    all_to_all x1, starting transfers between devices: 4.25 us -> 6.04 us  [body(): depth = lax.all_to_all(latent, GZ, split_axis=0, concat_axis=0)]
  transfers between devices with their start and end apart: 10 -> 10, of which waited for: 7 -> 7; matrix products, arithmetic and copies ran while one was open for 1% -> 1% of each run, Pallas kernels for 0% -> 2%
where the time goes in v2:
time: 116 us; the launch traced here: 115 us
  starting transfers between devices  46.6 us (40%)
  waiting for transfers between devices  40 us (34%)
  Pallas kernels  21.6 us (19%)
  local copies, waits for them, and re-layouts  5.53 us (5%)
    pallas_call x5, Pallas kernels, call(): pl.pallas_call(kernel, out_shape=jax.ShapeDtypeStruct(shape, dtype), in_s...  19 us
    ppermute x3, starting transfers between devices, beside(): lax.ppermute(cells, axis, [(i, i + 1) for i in range(ends)])  13.9 us
    all_to_all x1, waiting for transfers between devices, body(): lax.all_to_all(mixed.reshape(256, 2, 128), ALL, split_axis=0, concat_axis=0)  12.9 us
    all_to_all x1, starting transfers between devices, body(): lax.all_to_all(partial.reshape(256, 2, 128), ALL, split_axis=0, concat_ax...  12.7 us
    all_to_all x1, waiting for transfers between devices, body(): lax.all_to_all(partial.reshape(256, 2, 128), ALL, split_axis=0, concat_ax...  12.4 us
    all_to_all x1, starting transfers between devices, body(): depth = lax.all_to_all(latent, GZ, split_axis=0, concat_axis=0)  6.04 us
    all_to_all x1, starting transfers between devices, body(): lax.all_to_all(mixed.reshape(256, 2, 128), ALL, split_axis=0, concat_axis=0)  5.64 us
    all_to_all x1, waiting for transfers between devices, body(): depth = lax.all_to_all(latent, GZ, split_axis=0, concat_axis=0)  5.22 us
  transfers between devices with their start and end apart: 10, of which 7 were waited for; matrix products, arithmetic and copies ran while one was open for 1% of the time, Pallas kernels for 2%

profile of v2, /device:TPU:1, one launch (start us, length us, event | category | flops | bytes accessed | tf_op | source)
XLA Modules:
  0.0 114.9 jit_solution(10753169145086462942)
XLA Ops:
  0.0 0.8 copy.44
  0.8 4.3 %collective-permute-start = (f32[4,8,128]{2,1,0:T(8,128)S(1)}, f32[4,8,128]{2,1,0:T(8,128)S(1)}, u32[]{:S(2)}, u32[]{:S(2)}) collective-permute-start(f32[4,8,128]{2,1,0:T(8,128)S(1)} %pad.8), channel_id=1, source_target_pairs={{0,32},{32,64},{64,96},{96,128},{128,160},{160,192},{192,224},{1,3... | collective-permute-start | bytes 49160 | tf_op jit(solution)/shard_map/ppermute | solution.py:397
  5.1 1.3 %collective-permute-start.1 = (f32[4,8,128]{2,1,0:T(8,128)S(1)}, f32[4,8,128]{2,1,0:T(8,128)S(1)}, u32[]{:S(2)}, u32[]{:S(2)}) collective-permute-start(f32[4,8,128]{2,1,0:T(8,128)S(1)} %pad.8), channel_id=1, source_target_pairs={{32,0},{64,32},{96,64},{128,96},{160,128},{192,160},{224,192},{33,... | collective-permute-start | bytes 49160 | tf_op jit(solution)/shard_map/ppermute | solution.py:399
  6.5 0.6 copy-done.23
  7.5 0.8 copy-done.14
  8.7 1.1 collective-permute-done.1
  9.8 3.2 %collective-permute-start.2 = (f32[12,8,128]{2,1,0:T(8,128)S(1)}, f32[12,8,128]{2,1,0:T(8,128)S(1)}, u32[]{:S(2)}, u32[]{:S(2)}) collective-permute-start(f32[12,8,128]{2,1,0:T(8,128)S(1)} %pad_maximum_fusion.3), channel_id=1, source_target_pairs={{0,8},{8,16},{16,24},{1,9},{9,17},{17,25},{2,10},{10,18},{18,26},{... | collective-permute-start | bytes 147464 | tf_op jit(solution)/shard_map/ppermute | solution.py:397
  13.0 1.3 %collective-permute-start.3 = (f32[12,8,128]{2,1,0:T(8,128)S(1)}, f32[12,8,128]{2,1,0:T(8,128)S(1)}, u32[]{:S(2)}, u32[]{:S(2)}) collective-permute-start(f32[12,8,128]{2,1,0:T(8,128)S(1)} %pad_maximum_fusion.3), channel_id=1, source_target_pairs={{8,0},{16,8},{24,16},{9,1},{17,9},{25,17},{10,2},{18,10},{26,18},{... | collective-permute-start | bytes 147464 | tf_op jit(solution)/shard_map/ppermute | solution.py:399
  14.4 3.5 %collective-permute-done.3 = f32[12,8,128]{2,1,0:T(8,128)S(1)} collective-permute-done((f32[12,8,128]{2,1,0:T(8,128)S(1)}, f32[12,8,128]{2,1,0:T(8,128)S(1)}, u32[]{:S(2)}, u32[]{:S(2)}) %collective-permute-start.3) | collective-permute-done | bytes 49184 | tf_op jit(solution)/shard_map/ppermute | solution.py:399
  17.9 6.3 %collective-permute-start.4 = (f32[36,8,128]{2,1,0:T(8,128)S(1)}, f32[36,8,128]{2,1,0:T(8,128)S(1)}, u32[]{:S(2)}, u32[]{:S(2)}) collective-permute-start(f32[36,8,128]{2,1,0:T(8,128)S(1)} %constant_dynamic-update-slice_fusion.own_ref), channel_id=1, source_target_pairs={{0,1},{1,2},{2,3},{3,4},{4,5},{5,6},{6,7},{8,9},{9,10},{10,11},{11... | collective-permute-start | bytes 442376 | tf_op jit(solution)/shard_map/ppermute | solution.py:397
  24.2 1.9 %collective-permute-start.5 = (f32[36,8,128]{2,1,0:T(8,128)S(1)}, f32[36,8,128]{2,1,0:T(8,128)S(1)}, u32[]{:S(2)}, u32[]{:S(2)}) collective-permute-start(f32[36,8,128]{2,1,0:T(8,128)S(1)} %constant_dynamic-update-slice_fusion.own_ref), channel_id=1, source_target_pairs={{1,0},{2,1},{3,2},{4,3},{5,4},{6,5},{7,6},{9,8},{10,9},{11,10},{12... | collective-permute-start | bytes 442376 | tf_op jit(solution)/shard_map/ppermute | solution.py:399
  26.2 0.2 copy.34.nb_ref
  26.5 0.5 copy-done.16
  27.1 0.6 copy-done.19
  27.8 2.6 %sort.1 = (s32[4,64,128]{2,1,0:T(8,128)S(1)}, s32[4,8,128]{2,1,0:T(8,128)S(1)}, f32[4,3,8,128]{3,2,1,0:T(8,128)S(1)}, s32[8,1024]{1,0:T(8,128)S(1)}, f32[8,1024]{1,0:T(8,128)S(1)}, /*index=5*/s32[4]{0:T(128)S(1)}) custom-call(s32[3]{0:T(128)S(1)} %pad_add_fusion.place_ref, s32[32,8,128]{2,1,0:T(8,128)S(1)} %copy.34.nb_ref, s32[8,128]{1,0:T(8,128)S(1)} %reshape.36.cnt_ref), custom_call_target="tpu_custom_call" | custom-call | tf_op jit(solution)/shard_map/sort/pallas_call | solution.py:361
  30.5 0.2 collective-permute-done.5.above_ref
  30.7 0.5 copy-done.8
  31.1 12.6 %encoder.1.lat_ref = bf16[8,8,1024]{2,1,0:T(8,128)(2,1)} custom-call(s32[4]{0:T(128)S(1)} %get-tuple-element.11.steps_ref, f32[36,8,128]{2,1,0:T(8,128)S(1)} %collective-permute-done.4.below_ref, f32[36,8,128]{2,1,0:T(8,128)S(1)} %constant_dynamic-update-slice_fusion.own_ref, f32[36,8,128]{2,1,0:T(8,128)S(1)} %collective-permute-done.5.above_ref, ...), custom_call_target="tpu_custom_call" | custom-call | tf_op jit(solution)/shard_map/encoder/pallas_call | solution.py:341
  43.7 6.0 %all-to-all-start = ((bf16[8,8,1024]{2,1,0:T(8,128)(2,1)}), bf16[8,8,1024]{2,1,0:T(8,128)(2,1)S(1)}, u32[]{:S(2)}, u32[]{:S(2)}) async-start(bf16[8,8,1024]{2,1,0:T(8,128)(2,1)} %encoder.1.lat_ref), calls=%async_computation | async-start | bytes 262144 | tf_op jit(solution)/shard_map/all_to_all | solution.py:451
  49.8 5.2 %all-to-all-done.m_ref = bf16[8,8,1024]{2,1,0:T(8,128)(2,1)S(1)} async-done(((bf16[8,8,1024]{2,1,0:T(8,128)(2,1)}), bf16[8,8,1024]{2,1,0:T(8,128)(2,1)S(1)}, u32[]{:S(2)}, u32[]{:S(2)}) %all-to-all-start) | async-done | bytes 131104 | tf_op jit(solution)/shard_map/all_to_all | solution.py:451
  55.0 1.4 %forward.1 = bf16[512,128]{1,0:T(8,128)(2,1)} custom-call(bf16[8,8,1024]{2,1,0:T(8,128)(2,1)S(1)} %all-to-all-done.m_ref, bf16[256,512]{1,0:T(8,128)(2,1)S(1)} %copy-done.4, bf16[256,512]{1,0:T(8,128)(2,1)S(1)} %copy-done.5, bf16[256,256]{1,0:T(8,128)(2,1)S(1)} %fusion.whi_ref, bf16[256,256]{1,0:T(8,128)(2,1)S(1)} %subtract_convert_fusion.wlo_ref), custom_call_target="tpu_custom_call" | custom-call | tf_op jit(solution)/shard_map/forward/pallas_call | solution.py:341
  56.4 12.7 %all-to-all-start.1 = ((bf16[256,2,128]{2,1,0:T(2,128)(2,1)}), bf16[256,2,128]{2,1,0:T(2,128)(2,1)S(1)}, u32[]{:S(2)}, u32[]{:S(2)}) async-start(bf16[256,2,128]{2,1,0:T(2,128)(2,1)} %bitcast.13), calls=%async_computation.1 | async-start | bytes 262144 | tf_op jit(solution)/shard_map/all_to_all | solution.py:454
  69.2 0.3 maximum_bitcast_fusion
  69.6 12.4 %all-to-all-done.1 = bf16[256,2,128]{2,1,0:T(2,128)(2,1)S(1)} async-done(((bf16[256,2,128]{2,1,0:T(2,128)(2,1)}), bf16[256,2,128]{2,1,0:T(2,128)(2,1)S(1)}, u32[]{:S(2)}, u32[]{:S(2)}) %all-to-all-start.1) | async-done | bytes 131104 | tf_op jit(solution)/shard_map/all_to_all | solution.py:454
  82.1 1.1 mix.1
  83.2 5.6 %all-to-all-start.2 = ((bf16[256,2,128]{2,1,0:T(2,128)(2,1)}), bf16[256,2,128]{2,1,0:T(2,128)(2,1)S(1)}, u32[]{:S(2)}, u32[]{:S(2)}) async-start(bf16[256,2,128]{2,1,0:T(2,128)(2,1)} %bitcast.23), calls=%async_computation.2 | async-start | bytes 262144 | tf_op jit(solution)/shard_map/all_to_all | solution.py:468
  89.0 12.9 %all-to-all-done.2 = bf16[256,2,128]{2,1,0:T(2,128)(2,1)S(1)} async-done(((bf16[256,2,128]{2,1,0:T(2,128)(2,1)}), bf16[256,2,128]{2,1,0:T(2,128)(2,1)S(1)}, u32[]{:S(2)}, u32[]{:S(2)}) %all-to-all-start.2) | async-done | bytes 131104 | tf_op jit(solution)/shard_map/all_to_all | solution.py:468
  101.9 1.6 %inverse.1 = bf16[8,8,8,128]{3,2,1,0:T(8,128)(2,1)} custom-call(bf16[8,4,16,128]{3,2,1,0:T(8,128)(2,1)S(1)} %bitcast.44, bf16[256,256]{1,0:T(8,128)(2,1)S(1)} %pad_maximum_fusion.2.v_ref, bf16[512,256]{1,0:T(8,128)(2,1)S(1)} %copy-done.3, bf16[512,256]{1,0:T(8,128)(2,1)S(1)} %copy-done.2, bf16[256,256]{1,0:T(8,128)(2,1)S(1)} %copy-done.6), custom_call_target="tpu_custom_call" | custom-call | tf_op jit(solution)/shard_map/inverse/pallas_call | solution.py:341
  103.6 3.8 %all-to-all-start.3 = ((bf16[8,8,8,128]{3,2,1,0:T(8,128)(2,1)}), bf16[8,8,8,128]{3,2,1,0:T(8,128)(2,1)S(1)}, u32[]{:S(2)}, u32[]{:S(2)}) async-start(bf16[8,8,8,128]{3,2,1,0:T(8,128)(2,1)} %inverse.1), calls=%async_computation.3 | async-start | bytes 262144 | tf_op jit(solution)/shard_map/all_to_all | solution.py:481
  107.3 0.7 copy-done.18
  108.1 4.5 %all-to-all-done.3.y_ref = bf16[8,8,8,128]{3,2,1,0:T(8,128)(2,1)S(1)} async-done(((bf16[8,8,8,128]{3,2,1,0:T(8,128)(2,1)}), bf16[8,8,8,128]{3,2,1,0:T(8,128)(2,1)S(1)}, u32[]{:S(2)}, u32[]{:S(2)}) %all-to-all-start.3) | async-done | bytes 131104 | tf_op jit(solution)/shard_map/all_to_all | solution.py:481
  112.6 2.3 %output.1 = f32[128,8,64]{2,1,0:T(8,128)} custom-call(bf16[8,8,8,128]{3,2,1,0:T(8,128)(2,1)S(1)} %all-to-all-done.3.y_ref, bf16[8,8,1024]{2,1,0:T(8,128)(2,1)} %encoder.1.lat_ref, bf16[128,64]{1,0:T(8,128)(2,1)S(1)} %pad_maximum_fusion.4.w_ref), custom_call_target="tpu_custom_call" | custom-call | tf_op jit(solution)/shard_map/output/pallas_call | solution.py:341
  (73 shorter events, 1.3 us)
Async XLA Ops:
  0.0 7.3 %copy-start = (bf16[2,2,2,4,64,64]{5,4,3,2,1,0:T(8,128)(2,1)S(1)}, bf16[2,2,2,4,64,64]{5,4,3,2,1,0:T(8,128)(2,1)}, u32[]{:S(2)}) copy-start(bf16[2,2,2,4,64,64]{5,4,3,2,1,0:T(8,128)(2,1)} %param.31) | copy-start | bytes 786436
  0.8 7.9 %collective-permute-start = (f32[4,8,128]{2,1,0:T(8,128)S(1)}, f32[4,8,128]{2,1,0:T(8,128)S(1)}, u32[]{:S(2)}, u32[]{:S(2)}) collective-permute-start(f32[4,8,128]{2,1,0:T(8,128)S(1)} %pad.8), channel_id=1, source_target_pairs={{0,32},{32,64},{64,96},{96,128},{128,160},{160,192},{192,224},{1,3... | collective-permute-start | bytes 49160 | tf_op jit(solution)/shard_map/ppermute | solution.py:397
  5.1 4.7 %collective-permute-start.1 = (f32[4,8,128]{2,1,0:T(8,128)S(1)}, f32[4,8,128]{2,1,0:T(8,128)S(1)}, u32[]{:S(2)}, u32[]{:S(2)}) collective-permute-start(f32[4,8,128]{2,1,0:T(8,128)S(1)} %pad.8), channel_id=1, source_target_pairs={{32,0},{64,32},{96,64},{128,96},{160,128},{192,160},{224,192},{33,... | collective-permute-start | bytes 49160 | tf_op jit(solution)/shard_map/ppermute | solution.py:399
  6.5 0.7 copy-start.21
  6.5 0.7 copy-start.22
  6.5 0.7 copy-start.20
  7.4 0.9 copy-start.14
  7.4 1.0 copy-start.15
  7.5 1.1 copy-start.17
  7.5 18.7 %copy-start.11 = (s32[1,8,16,8,32]{4,3,2,1,0:T(8,128)S(1)}, s32[1,8,16,8,32]{4,3,2,1,0:T(8,128)}, u32[]{:S(2)}) copy-start(s32[1,8,16,8,32]{4,3,2,1,0:T(8,128)} %param.26) | copy-start | bytes 393220
  9.8 4.5 %collective-permute-start.2 = (f32[12,8,128]{2,1,0:T(8,128)S(1)}, f32[12,8,128]{2,1,0:T(8,128)S(1)}, u32[]{:S(2)}, u32[]{:S(2)}) collective-permute-start(f32[12,8,128]{2,1,0:T(8,128)S(1)} %pad_maximum_fusion.3), channel_id=1, source_target_pairs={{0,8},{8,16},{16,24},{1,9},{9,17},{17,25},{2,10},{10,18},{18,26},{... | collective-permute-start | bytes 147464 | tf_op jit(solution)/shard_map/ppermute | solution.py:397
  13.0 4.8 %collective-permute-start.3 = (f32[12,8,128]{2,1,0:T(8,128)S(1)}, f32[12,8,128]{2,1,0:T(8,128)S(1)}, u32[]{:S(2)}, u32[]{:S(2)}) collective-permute-start(f32[12,8,128]{2,1,0:T(8,128)S(1)} %pad_maximum_fusion.3), channel_id=1, source_target_pairs={{8,0},{16,8},{24,16},{9,1},{17,9},{25,17},{10,2},{18,10},{26,18},{... | collective-permute-start | bytes 147464 | tf_op jit(solution)/shard_map/ppermute | solution.py:399
  17.9 12.6 %collective-permute-start.4 = (f32[36,8,128]{2,1,0:T(8,128)S(1)}, f32[36,8,128]{2,1,0:T(8,128)S(1)}, u32[]{:S(2)}, u32[]{:S(2)}) collective-permute-start(f32[36,8,128]{2,1,0:T(8,128)S(1)} %constant_dynamic-update-slice_fusion.own_ref), channel_id=1, source_target_pairs={{0,1},{1,2},{2,3},{3,4},{4,5},{5,6},{6,7},{8,9},{9,10},{10,11},{11... | collective-permute-start | bytes 442376 | tf_op jit(solution)/shard_map/ppermute | solution.py:397
  24.2 6.5 %collective-permute-start.5 = (f32[36,8,128]{2,1,0:T(8,128)S(1)}, f32[36,8,128]{2,1,0:T(8,128)S(1)}, u32[]{:S(2)}, u32[]{:S(2)}) collective-permute-start(f32[36,8,128]{2,1,0:T(8,128)S(1)} %constant_dynamic-update-slice_fusion.own_ref), channel_id=1, source_target_pairs={{1,0},{2,1},{3,2},{4,3},{5,4},{6,5},{7,6},{9,8},{10,9},{11,10},{12... | collective-permute-start | bytes 442376 | tf_op jit(solution)/shard_map/ppermute | solution.py:399
  26.2 0.8 copy-start.16
  30.4 0.7 copy-start.8
  43.7 11.3 %copy-start.5 = (bf16[256,512]{1,0:T(8,128)(2,1)S(1)}, bf16[256,512]{1,0:T(8,128)(2,1)}, u32[]{:S(2)}) copy-start(bf16[256,512]{1,0:T(8,128)(2,1)} %constant.94.clone.alo_ref) | copy-start | bytes 786436
  43.7 11.3 %all-to-all-start = ((bf16[8,8,1024]{2,1,0:T(8,128)(2,1)}), bf16[8,8,1024]{2,1,0:T(8,128)(2,1)S(1)}, u32[]{:S(2)}, u32[]{:S(2)}) async-start(bf16[8,8,1024]{2,1,0:T(8,128)(2,1)} %encoder.1.lat_ref), calls=%async_computation | async-start | bytes 262144 | tf_op jit(solution)/shard_map/all_to_all | solution.py:451
  49.8 5.2 %copy-start.4 = (bf16[256,512]{1,0:T(8,128)(2,1)S(1)}, bf16[256,512]{1,0:T(8,128)(2,1)}, u32[]{:S(2)}) copy-start(bf16[256,512]{1,0:T(8,128)(2,1)} %constant.93.clone.ahi_ref) | copy-start | bytes 786436
  56.4 25.7 %all-to-all-start.1 = ((bf16[256,2,128]{2,1,0:T(2,128)(2,1)}), bf16[256,2,128]{2,1,0:T(2,128)(2,1)S(1)}, u32[]{:S(2)}, u32[]{:S(2)}) async-start(bf16[256,2,128]{2,1,0:T(2,128)(2,1)} %bitcast.13), calls=%async_computation.1 | async-start | bytes 262144 | tf_op jit(solution)/shard_map/all_to_all | solution.py:454
  69.5 12.5 %copy-start.1 = (bf16[128,1024]{1,0:T(8,128)(2,1)S(1)}, bf16[128,1024]{1,0:T(8,128)(2,1)}, u32[]{:S(2)}) copy-start(bf16[128,1024]{1,0:T(8,128)(2,1)} %constant.96.clone.sel_ref) | copy-start | bytes 786436
  69.5 12.5 %copy-start.7 = (f32[16,1024]{1,0:T(8,128)S(1)}, f32[16,1024]{1,0:T(8,128)}, u32[]{:S(2)}) copy-start(f32[16,1024]{1,0:T(8,128)} %constant.97.clone.place_ref) | copy-start | bytes 196612
  69.5 12.5 %copy-start.9 = (f32[16,256]{1,0:T(8,128)S(1)}, f32[16,256]{1,0:T(8,128)}, u32[]{:S(2)}) copy-start(f32[16,256]{1,0:T(8,128)} %constant.95.clone.own_ref) | copy-start | bytes 49156
  69.6 12.4 %copy-start.10 = (bf16[8,16]{1,0:T(8,128)(2,1)S(1)}, bf16[8,16]{1,0:T(8,128)(2,1)}, u32[]{:S(2)}) copy-start(bf16[8,16]{1,0:T(8,128)(2,1)} %constant.98.clone.half_ref) | copy-start | bytes 772
  83.2 5.7 %copy-start.12 = (f32[128,256]{1,0:T(8,128)S(1)}, f32[128,256]{1,0:T(8,128)}, u32[]{:S(2)}) copy-start(f32[128,256]{1,0:T(8,128)} %constant.91.clone) | copy-start | bytes 393220
  83.2 5.7 %copy-start.13 = (f32[128,256]{1,0:T(8,128)S(1)}, f32[128,256]{1,0:T(8,128)}, u32[]{:S(2)}) copy-start(f32[128,256]{1,0:T(8,128)} %constant.92.clone) | copy-start | bytes 393220
  83.2 18.7 %all-to-all-start.2 = ((bf16[256,2,128]{2,1,0:T(2,128)(2,1)}), bf16[256,2,128]{2,1,0:T(2,128)(2,1)S(1)}, u32[]{:S(2)}, u32[]{:S(2)}) async-start(bf16[256,2,128]{2,1,0:T(2,128)(2,1)} %bitcast.23), calls=%async_computation.2 | async-start | bytes 262144 | tf_op jit(solution)/shard_map/all_to_all | solution.py:468
  88.9 13.0 %copy-start.2 = (bf16[512,256]{1,0:T(8,128)(2,1)S(1)}, bf16[512,256]{1,0:T(8,128)(2,1)}, u32[]{:S(2)}) copy-start(bf16[512,256]{1,0:T(8,128)(2,1)} %constant.100.clone.bs_ref) | copy-start | bytes 786436
  88.9 13.0 %copy-start.3 = (bf16[512,256]{1,0:T(8,128)(2,1)S(1)}, bf16[512,256]{1,0:T(8,128)(2,1)}, u32[]{:S(2)}) copy-start(bf16[512,256]{1,0:T(8,128)(2,1)} %constant.99.clone.bc_ref) | copy-start | bytes 786436
  89.0 13.0 %copy-start.6 = (bf16[256,256]{1,0:T(8,128)(2,1)S(1)}, bf16[256,256]{1,0:T(8,128)(2,1)}, u32[]{:S(2)}) copy-start(bf16[256,256]{1,0:T(8,128)(2,1)} %constant.101.clone.partner_ref) | copy-start | bytes 393220
  103.6 9.0 %all-to-all-start.3 = ((bf16[8,8,8,128]{3,2,1,0:T(8,128)(2,1)}), bf16[8,8,8,128]{3,2,1,0:T(8,128)(2,1)S(1)}, u32[]{:S(2)}, u32[]{:S(2)}) async-start(bf16[8,8,8,128]{3,2,1,0:T(8,128)(2,1)} %inverse.1), calls=%async_computation.3 | async-start | bytes 262144 | tf_op jit(solution)/shard_map/all_to_all | solution.py:481
  107.3 0.7 copy-start.18
  (2 other events, 1.4 us)

commit v3 on v2

--- a/solution.py
+++ b/solution.py
@@ -15,6 +15,7 @@
 
 GRID = 64
 NB = 32
+NEAR_EARLY = True
 CELLS = float(GRID**3)
 NORM_FLOOR = 1.0
 GZ = ("gz_0", "gz_1")
@@ -121,20 +122,46 @@
     return jnp.where(r == rank, 1.0, 0.0).astype(bf16)
 
 
-def sort_kernel(place_ref, nb_ref, cnt_ref, code_ref, cnt8_ref, cen_ref, rank_ref, scnt_ref, steps_ref):
+def sort_kernel(
+    place_ref, nb_ref, cnt_ref, far_ref, near_ref, far8_ref, near8_ref, cen_ref, rank_ref, scnt_ref, steps_ref, lists
+):
     px, py, pz = place_ref[0], place_ref[1], place_ref[2]
-    j = nb_ref[...]
-    owner = j >> 9
-    dz = (owner & 7) - pz + 1
-    dy = ((owner >> 3) & 3) - py + 1
-    dx = (owner >> 5) - px + 1
-    chunk = (((dz * 3 + dy) * 3 + dx) * 4 + ((j >> 7) & 3)) & 127
-    chunk = chunk.astype(f32)
-    lane = (j & 127).astype(f32)
-    counts = cnt_ref[...].astype(f32)
+    me = (px * 4 + py) * 8 + pz
+    counts = cnt_ref[...]
+    nothing = jnp.full((8, 128), -1, i32)
+    far = jnp.zeros((8, 128), i32)
+    near = jnp.zeros((8, 128), i32)
+    codes, far_at, near_at = [], [], []
+    for s in range(NB):
+        j = nb_ref[s]
+        owner = j >> 9
+        dz = (owner & 7) - pz + 1
+        dy = ((owner >> 3) & 3) - py + 1
+        dx = (owner >> 5) - px + 1
+        chunk = (((dz * 3 + dy) * 3 + dx) * 4 + ((j >> 7) & 3)) & 127
+        codes.append(chunk * 128 + (j & 127))
+        valid = counts > s
+        mine = owner == me
+        is_far = valid & jnp.logical_not(mine)
+        is_near = valid & mine
+        far_at.append(jnp.where(is_far, far, nothing))
+        near_at.append(jnp.where(is_near, near, nothing))
+        far = far + is_far.astype(i32)
+        near = near + is_near.astype(i32)
+    for p in range(NB):
+        first = jnp.zeros((8, 128), i32)
+        second = jnp.zeros((8, 128), i32)
+        for s in range(p, NB):
+            first = jnp.where(far_at[s] == p, codes[s], first)
+            second = jnp.where(near_at[s] == p, codes[s], second)
+        lists[p] = (first >> 7).astype(f32)
+        lists[NB + p] = (first & 127).astype(f32)
+        lists[2 * NB + p] = ((second >> 7) & 3).astype(f32)
+        lists[3 * NB + p] = (second & 127).astype(f32)
+    far, near = far.astype(f32), near.astype(f32)
     row8 = lax.broadcasted_iota(i32, (8, 128), 0)
     lane8 = lax.broadcasted_iota(i32, (8, 128), 1)
-    key = counts * 1024.0 - (row8 * 128 + lane8).astype(f32)
+    key = far * 1024.0 - (row8 * 128 + lane8).astype(f32)
     flat = [key[z : z + 1] for z in range(8)]
     ranks = [jnp.zeros((128, 128), f32) for _ in range(8)]
     for z in range(8):
@@ -142,39 +169,84 @@
         ranks = [r + jnp.where(own > line, 1.0, 0.0) for r, line in zip(ranks, flat)]
     rank = jnp.concatenate([jnp.sum(r, axis=0, keepdims=True) for r in ranks], axis=1).astype(i32)
     rank_ref[...] = jnp.broadcast_to(rank, (8, 1024))
-    flat = [
-        jnp.concatenate([a[:, z, :] for z in range(8)], axis=1) for a in (chunk, lane)
-    ]
     node = lax.broadcasted_iota(i32, (8, 1024), 1)
     wide = lax.broadcasted_iota(i32, (8, 1024), 0)
-    line = jnp.concatenate([counts[z : z + 1] for z in range(8)], axis=1)
-    tail = jnp.where(
-        wide == 0,
-        line,
-        jnp.where(wide == 1, (node >> 7).astype(f32), (node & 127).astype(f32)),
-    )
-    rows = jnp.concatenate(flat + [tail], axis=0).astype(bf16)
+    far = jnp.concatenate([far[z : z + 1] for z in range(8)], axis=1)
+    near = jnp.concatenate([near[z : z + 1] for z in range(8)], axis=1)
+    tail = jnp.where(wide == 2, (node >> 7).astype(f32), (node & 127).astype(f32))
+    tail = jnp.where(wide == 0, far, jnp.where(wide == 1, near, tail))
+    rows = jnp.concatenate([lists[:, z, :] for z in range(8)], axis=1)
+    rows = jnp.concatenate([rows, tail], axis=0).astype(bf16)
     odd = (row8 & 1) == 1
     for t in range(4):
         found = dot_t(rows, rank_rows(rank, t * 256, 256))
-        code = (found[0:32] * 128.0 + found[32:64]).astype(i32)
-        for s in range(4):
-            for h in range(2):
-                code_ref[t, pl.ds(s * 16 + h, 8, stride=2), :] = code[
-                    s * 8 : s * 8 + 8, h * 128 : h * 128 + 128
-                ]
-        tail = found[64:72]
+        for ref, at in ((far_ref, 0), (near_ref, 2 * NB)):
+            code = (found[at : at + 32] * 128.0 + found[at + 32 : at + 64]).astype(i32)
+            for s in range(4):
+                for h in range(2):
+                    ref[t, pl.ds(s * 16 + h, 8, stride=2), :] = code[
+                        s * 8 : s * 8 + 8, h * 128 : h * 128 + 128
+                    ]
+        tail = found[4 * NB : 4 * NB + 8]
 
         def both(n):
             return jnp.where(odd, tail[n : n + 1, 128:256], tail[n : n + 1, 0:128])
 
-        cnt8_ref[t] = both(0).astype(i32)
-        cell = both(2).astype(i32)
+        far8_ref[t] = both(0).astype(i32)
+        near8_ref[t] = both(1).astype(i32)
+        cell = both(3).astype(i32)
         cen_ref[t, 0] = ((px * 8 + (cell >> 4)).astype(f32) + 0.5) / GRID
         cen_ref[t, 1] = ((py * 16 + (cell & 15)).astype(f32) + 0.5) / GRID
-        cen_ref[t, 2] = ((pz * 8).astype(f32) + both(1) + 0.5) / GRID
-        scnt_ref[:, t * 256 : t * 256 + 256] = jnp.broadcast_to(tail[0:1], (8, 256))
-        steps_ref[t] = (jnp.max(tail[0:1]).astype(i32) + 3) >> 2
+        cen_ref[t, 2] = ((pz * 8).astype(f32) + both(2) + 0.5) / GRID
+        scnt_ref[:, t * 256 : t * 256 + 256] = jnp.broadcast_to(tail[0:1] + tail[1:2], (8, 256))
+        steps_ref[t] = jnp.maximum((jnp.max(tail[0:1]).astype(i32) + 3) >> 2, 1)
+        steps_ref[4 + t] = jnp.maximum((jnp.max(tail[1:2]).astype(i32) + 3) >> 2, 1)
+
+
+def pair_sums(steps_ref, at, gather, ki_ref, km_ref, acc_ref):
+    def step(_, carry):
+        t, b, pair = carry
+        last = b + 1 >= steps_ref[at + t]
+        nt = jnp.where(last, jnp.minimum(t + 1, 3), t)
+        nb = jnp.where(last, 0, b + 1)
+        following = gather(nt, nb)
+        hidden = gelu_twice(dot(ki_ref[...], pair.astype(bf16))).astype(bf16)
+        hidden = gelu_twice(dot(km_ref[...], hidden))
+        acc_ref[t] += (
+            hidden[:, 0:256] + hidden[:, 256:512] + hidden[:, 512:768] + hidden[:, 768:1024]
+        )
+        return nt, nb, following
+
+    total = steps_ref[at] + steps_ref[at + 1] + steps_ref[at + 2] + steps_ref[at + 3]
+    lax.fori_loop(0, total, step, (jnp.int32(0), jnp.int32(0), gather(0, 0)))
+
+
+def near_kernel(steps_ref, own_ref, code_ref, cnt8_ref, cen_ref, ki_ref, km_ref, acc_ref, turn):
+    turn[...] = jnp.zeros(turn.shape, f32)
+    acc_ref[...] = jnp.zeros(acc_ref.shape, f32)
+    slot = lax.broadcasted_iota(i32, (8, 128), 0) >> 1
+
+    def gather(t, b):
+        code = code_ref[t, pl.ds(pl.multiple_of(b * 8, 8), 8), :]
+        at = code & 127
+        low, high = (code & 128) != 0, (code & 256) != 0
+        valid = cnt8_ref[t] > slot + b * 4
+        for c in range(6):
+            found = [
+                jnp.take_along_axis(
+                    jnp.broadcast_to(own_ref[n, c : c + 1, :], (8, 128)), at, axis=1, mode="promise_in_bounds"
+                )
+                for n in range(4)
+            ]
+            value = jnp.where(
+                high, jnp.where(low, found[3], found[2]), jnp.where(low, found[1], found[0])
+            )
+            if c < 3:
+                value = value - cen_ref[t, c]
+            turn[c] = jnp.where(valid, value, 0.0)
+        return jnp.concatenate([turn[:, n, :] for n in range(8)], axis=1)
+
+    pair_sums(steps_ref, 4, gather, ki_ref, km_ref, acc_ref)
 
 
 def encoder_kernel(
@@ -187,6 +259,7 @@
     cen_ref,
     rank_ref,
     scnt_ref,
+    sum_ref,
     ki_ref,
     km_ref,
     ko_ref,
@@ -211,7 +284,7 @@
         for c in range(3):
             off_ref[t, c] = cen_ref[t, c] + 32768.0 * units[c]
     turn[...] = jnp.zeros(turn.shape, f32)
-    acc_ref[...] = jnp.zeros(acc_ref.shape, f32)
+    acc_ref[...] = sum_ref[...]
     slot = lax.broadcasted_iota(i32, (8, 128), 0) >> 1
 
     def gather(t, b):
@@ -238,21 +311,7 @@
             turn[c + 3] = jnp.where(valid, normal, 0.0)
         return jnp.concatenate([turn[:, n, :] for n in range(8)], axis=1)
 
-    def step(_, carry):
-        t, b, pair = carry
-        last = b + 1 >= steps_ref[t]
-        nt = jnp.where(last, jnp.minimum(t + 1, 3), t)
-        nb = jnp.where(last, 0, b + 1)
-        following = gather(nt, nb)
-        hidden = gelu_twice(dot(ki_ref[...], pair.astype(bf16))).astype(bf16)
-        hidden = gelu_twice(dot(km_ref[...], hidden))
-        acc_ref[t] += (
-            hidden[:, 0:256] + hidden[:, 256:512] + hidden[:, 512:768] + hidden[:, 768:1024]
-        )
-        return nt, nb, following
-
-    total = steps_ref[0] + steps_ref[1] + steps_ref[2] + steps_ref[3]
-    lax.fori_loop(0, total, step, (jnp.int32(0), jnp.int32(0), gather(0, 0)))
+    pair_sums(steps_ref, 0, gather, ki_ref, km_ref, acc_ref)
     mean = jnp.concatenate([acc_ref[t] for t in range(4)], axis=1) * (0.5 / scnt_ref[0:1])
     upper = mean.astype(bf16)
     lower = (mean - upper.astype(f32)).astype(bf16)
@@ -352,34 +411,93 @@
 def sorted_nodes(place, near, valid):
     shapes = (
         ((4, 64, 128), i32),
+        ((4, 64, 128), i32),
+        ((4, 8, 128), i32),
         ((4, 8, 128), i32),
         ((4, 3, 8, 128), f32),
         ((8, 1024), i32),
         ((8, 1024), f32),
-        ((4,), i32),
+        ((8,), i32),
     )
     return pl.pallas_call(
         sort_kernel,
         out_shape=[jax.ShapeDtypeStruct(*s) for s in shapes],
         in_specs=[SMEM, VMEM, VMEM],
-        out_specs=[VMEM] * 5 + [SMEM],
+        out_specs=[VMEM] * 7 + [SMEM],
+        scratch_shapes=[pltpu.VMEM((4 * NB, 8, 128), f32)],
         compiler_params=pltpu.CompilerParams(vmem_limit_bytes=48 * 1024 * 1024),
         name="sort",
     )(place, near, valid)
 
 
-def encode(steps, tables, pieces, ki, km, ko):
-    return call(
+def beside(cells, axis):
+    count = lax.axis_size(axis)
+    ends = count - 1
+    return (
+        lax.ppermute(cells, axis, [(i, i + 1) for i in range(ends)]),
+        cells,
+        lax.ppermute(cells, axis, [(i + 1, i) for i in range(ends)]),
+    )
+
+
+def turned(cos, sin, phase):
+    c, s = jnp.cos(phase), jnp.sin(phase)
+    return cos * c - sin * s, sin * c + cos * s
+
+
+def body(point_data, neighbours, counts, kernel_in, kernel_mid, kernel_out, spectral, skip_weight):
+    gx = lax.axis_index("gx")
+    gy = lax.axis_index("gy")
+    gz = lax.axis_index(GZ)
+    place = jnp.stack([gx, gy, gz]).astype(i32)
+
+    own = jnp.pad(point_data[0].reshape(6, 4, 128).transpose(1, 0, 2), ((0, 0), (0, 2), (0, 0)))
+    near = neighbours[0].transpose(3, 2, 0, 1).reshape(NB, 8, 128)
+    valid = counts[0].transpose(2, 0, 1).reshape(8, 128)
+    ki = jnp.pad(kernel_in.T, ((0, 0), (0, 2)))
+    km = kernel_mid.T * jnp.bfloat16(0.5)
+
+    line = jnp.concatenate(beside(own, "gx"), axis=0)
+    tables = sorted_nodes(place, near, valid)
+    line, tables = lax.optimization_barrier((line, tables))
+    far_code, near_code, far8, near8, centres, rank, sorted_counts, steps = tables
+    plane = jnp.concatenate(beside(line, "gy"), axis=0)
+    sums = call(
+        near_kernel,
+        "near",
+        (4, 80, 256),
+        f32,
+        steps,
+        own,
+        near_code,
+        near8,
+        centres,
+        ki,
+        km,
+        scratch=(pltpu.VMEM((8, 8, 128), f32),),
+        smem=1,
+    )
+    if NEAR_EARLY:
+        plane, sums = lax.optimization_barrier((plane, sums))
+    below, same, above = beside(plane, GZ)
+    latent = call(
         encoder_kernel,
         "encoder",
         (8, 8, 1024),
         bf16,
         steps,
-        *pieces,
-        *tables,
+        below,
+        same,
+        above,
+        far_code,
+        far8,
+        centres,
+        rank,
+        sorted_counts,
+        sums,
         ki,
         km,
-        ko,
+        kernel_out.T,
         scratch=(
             pltpu.VMEM((108, 8, 128), i32),
             pltpu.VMEM((4, 3, 8, 128), f32),
@@ -388,40 +506,6 @@
         ),
         smem=1,
     )
-
-
-def beside(cells, axis):
-    count = lax.axis_size(axis)
-    ends = count - 1
-    return (
-        lax.ppermute(cells, axis, [(i, i + 1) for i in range(ends)]),
-        cells,
-        lax.ppermute(cells, axis, [(i + 1, i) for i in range(ends)]),
-    )
-
-
-def turned(cos, sin, phase):
-    c, s = jnp.cos(phase), jnp.sin(phase)
-    return cos * c - sin * s, sin * c + cos * s
-
-
-def body(point_data, neighbours, counts, kernel_in, kernel_mid, kernel_out, spectral, skip_weight):
-    gx = lax.axis_index("gx")
-    gy = lax.axis_index("gy")
-    gz = lax.axis_index(GZ)
-    place = jnp.stack([gx, gy, gz]).astype(i32)
-
-    own = jnp.pad(point_data[0].reshape(6, 4, 128).transpose(1, 0, 2), ((0, 0), (0, 2), (0, 0)))
-    line = jnp.concatenate(beside(own, "gx"), axis=0)
-    plane = jnp.concatenate(beside(line, "gy"), axis=0)
-    below, same, above = beside(plane, GZ)
-
-    near = neighbours[0].transpose(3, 2, 0, 1).reshape(NB, 8, 128)
-    valid = counts[0].transpose(2, 0, 1).reshape(8, 128)
-    ki = jnp.pad(kernel_in.T, ((0, 0), (0, 2)))
-    km = kernel_mid.T * jnp.bfloat16(0.5)
-    *tables, steps = sorted_nodes(place, near, valid)
-    latent = encode(steps, tables, (below, same, above), ki, km, kernel_out.T)
 
     (ffi, ffj), (ifi, ifj), xl, yl = plane_tables()
     local = angle(1, ffi[:, None] * xl[None, :] + ffj[:, None] * yl[None, :])

time: 116 us -> 120 us (1.034)
  Pallas kernels: 21.6 us -> 28.9 us
  local copies, waits for them, and re-layouts: 5.53 us -> 3.81 us
    pallas_call x5 -> x6, Pallas kernels: 19 us -> 25.6 us  [call(): pl.pallas_call(kernel, out_shape=jax.ShapeDtypeStruct(shape, dtype), in_s...]
    all_to_all x1, starting transfers between devices: 12.7 us -> 16.6 us  [body(): lax.all_to_all(partial.reshape(256, 2, 128), ALL, split_axis=0, concat_ax...]
    all_to_all x1, starting transfers between devices: 6.04 us -> 3.45 us  [body(): depth = lax.all_to_all(latent, GZ, split_axis=0, concat_axis=0)]
    ppermute x3, starting transfers between devices: 13.9 us -> 11.9 us  [beside(): lax.ppermute(cells, axis, [(i, i + 1) for i in range(ends)])]
    unnamed x54 -> x50, local copies, waits for them, and re-layouts: 4.19 us -> 2.48 us
  transfers between devices with their start and end apart: 10 -> 10, of which waited for: 7 -> 5; matrix products, arithmetic and copies ran while one was open for 1% -> 1% of each run, Pallas kernels for 2% -> 12%
where the time goes in v3:
time: 120 us; the launch traced here: 119 us
  starting transfers between devices  46 us (38%)
  waiting for transfers between devices  38.9 us (32%)
  Pallas kernels  28.9 us (24%)
  local copies, waits for them, and re-layouts  3.81 us (3%)
    pallas_call x6, Pallas kernels, call(): pl.pallas_call(kernel, out_shape=jax.ShapeDtypeStruct(shape, dtype), in_s...  25.6 us
    all_to_all x1, starting transfers between devices, body(): lax.all_to_all(partial.reshape(256, 2, 128), ALL, split_axis=0, concat_ax...  16.6 us
    all_to_all x1, waiting for transfers between devices, body(): lax.all_to_all(mixed.reshape(256, 2, 128), ALL, split_axis=0, concat_axis=0)  12.9 us
    all_to_all x1, waiting for transfers between devices, body(): lax.all_to_all(partial.reshape(256, 2, 128), ALL, split_axis=0, concat_ax...  12.4 us
    ppermute x3, starting transfers between devices, beside(): lax.ppermute(cells, axis, [(i, i + 1) for i in range(ends)])  11.9 us
    all_to_all x1, starting transfers between devices, body(): lax.all_to_all(mixed.reshape(256, 2, 128), ALL, split_axis=0, concat_axis=0)  5.64 us
    all_to_all x1, waiting for transfers between devices, body(): depth = lax.all_to_all(latent, GZ, split_axis=0, concat_axis=0)  4.65 us
    all_to_all x1, waiting for transfers between devices, body(): branch = lax.all_to_all(branch, GZ, split_axis=0, concat_axis=0)  4.54 us
  transfers between devices with their start and end apart: 10, of which 5 were waited for; matrix products, arithmetic and copies ran while one was open for 1% of the time, Pallas kernels for 12%

profile of v3, /device:TPU:1, one launch (start us, length us, event | category | flops | bytes accessed | tf_op | source)
XLA Modules:
  0.0 118.8 jit_solution(3629822252383383153)
XLA Ops:
  0.0 0.8 copy.44
  0.8 4.4 %collective-permute-start = (f32[4,8,128]{2,1,0:T(8,128)S(1)}, f32[4,8,128]{2,1,0:T(8,128)S(1)}, u32[]{:S(2)}, u32[]{:S(2)}) collective-permute-start(f32[4,8,128]{2,1,0:T(8,128)S(1)} %pad.8.own_ref), channel_id=1, source_target_pairs={{0,32},{32,64},{64,96},{96,128},{128,160},{160,192},{192,224},{1,3... | collective-permute-start | bytes 49160 | tf_op jit(solution)/shard_map/ppermute | solution.py:437
  5.1 1.3 %collective-permute-start.1 = (f32[4,8,128]{2,1,0:T(8,128)S(1)}, f32[4,8,128]{2,1,0:T(8,128)S(1)}, u32[]{:S(2)}, u32[]{:S(2)}) collective-permute-start(f32[4,8,128]{2,1,0:T(8,128)S(1)} %pad.8.own_ref), channel_id=1, source_target_pairs={{32,0},{64,32},{96,64},{128,96},{160,128},{192,160},{224,192},{33,... | collective-permute-start | bytes 49160 | tf_op jit(solution)/shard_map/ppermute | solution.py:439
  6.5 0.1 copy.37
  6.6 0.1 copy_bitcast_fusion
  6.9 0.9 copy-done.11
  7.8 0.2 copy.35.nb_ref
  8.0 0.5 copy-done.16
  8.6 3.3 %sort.1 = (s32[4,64,128]{2,1,0:T(8,128)S(1)}, s32[4,64,128]{2,1,0:T(8,128)S(1)}, s32[4,8,128]{2,1,0:T(8,128)S(1)}, s32[4,8,128]{2,1,0:T(8,128)S(1)}, f32[4,3,8,1...) custom-call(s32[3]{0:T(128)S(1)} %pad_add_fusion.place_ref, ...), custom_call_target="tpu_custom_call" | custom-call | tf_op jit(solution)/shard_map/sort/pallas_call | solution.py:422
  12.0 3.2 %collective-permute-start.2 = (f32[12,8,128]{2,1,0:T(8,128)S(1)}, f32[12,8,128]{2,1,0:T(8,128)S(1)}, u32[]{:S(2)}, u32[]{:S(2)}) collective-permute-start(f32[12,8,128]{2,1,0:T(8,128)S(1)} %pad_maximum_fusion.4), channel_id=1, source_target_pairs={{0,8},{8,16},{16,24},{1,9},{9,17},{17,25},{2,10},{10,18},{18,26},{... | collective-permute-start | bytes 147464 | tf_op jit(solution)/shard_map/ppermute | solution.py:437
  15.2 1.3 %collective-permute-start.3 = (f32[12,8,128]{2,1,0:T(8,128)S(1)}, f32[12,8,128]{2,1,0:T(8,128)S(1)}, u32[]{:S(2)}, u32[]{:S(2)}) collective-permute-start(f32[12,8,128]{2,1,0:T(8,128)S(1)} %pad_maximum_fusion.4), channel_id=1, source_target_pairs={{8,0},{16,8},{24,16},{9,1},{17,9},{25,17},{10,2},{18,10},{26,18},{... | collective-permute-start | bytes 147464 | tf_op jit(solution)/shard_map/ppermute | solution.py:439
  16.6 0.1 copy.36
  16.8 11.0 %near.1.sum_ref = f32[4,80,256]{2,1,0:T(8,128)S(1)} custom-call(s32[8]{0:T(128)S(1)} %get-tuple-element.32.steps_ref, f32[4,8,128]{2,1,0:T(8,128)S(1)} %pad.8.own_ref, s32[4,64,128]{2,1,0:T(8,128)S(1)} %get-tuple-element.34.code_ref, s32[4,8,128]{2,1,0:T(8,128)S(1)} %get-tuple-element.35.cnt8_ref, f32[4,3,8,128]{3,2,1,0:T(8,128)S(1)} %get-tuple-element.36.cen_ref, ...), custom_call_target="tpu_custom_call" | custom-call | tf_op jit(solution)/shard_map/near/pallas_call | solution.py:400
  27.8 4.4 %collective-permute-start.4 = (f32[36,8,128]{2,1,0:T(8,128)S(1)}, f32[36,8,128]{2,1,0:T(8,128)S(1)}, u32[]{:S(2)}, u32[]{:S(2)}) collective-permute-start(f32[36,8,128]{2,1,0:T(8,128)S(1)} %pad_maximum_fusion.2.own_ref), channel_id=1, source_target_pairs={{0,1},{1,2},{2,3},{3,4},{4,5},{5,6},{6,7},{8,9},{9,10},{10,11},{11... | collective-permute-start | bytes 442376 | tf_op jit(solution)/shard_map/ppermute | solution.py:437
  32.2 1.9 %collective-permute-start.5 = (f32[36,8,128]{2,1,0:T(8,128)S(1)}, f32[36,8,128]{2,1,0:T(8,128)S(1)}, u32[]{:S(2)}, u32[]{:S(2)}) collective-permute-start(f32[36,8,128]{2,1,0:T(8,128)S(1)} %pad_maximum_fusion.2.own_ref), channel_id=1, source_target_pairs={{1,0},{2,1},{3,2},{4,3},{5,4},{6,5},{7,6},{9,8},{10,9},{11,10},{12... | collective-permute-start | bytes 442376 | tf_op jit(solution)/shard_map/ppermute | solution.py:439
  34.1 0.1 multiply_subtract_fusion
  34.3 4.3 %collective-permute-done.5.above_ref = f32[36,8,128]{2,1,0:T(8,128)S(1)} collective-permute-done((f32[36,8,128]{2,1,0:T(8,128)S(1)}, f32[36,8,128]{2,1,0:T(8,128)S(1)}, u32[]{:S(2)}, u32[]{:S(2)}) %collective-permute-start.5) | collective-permute-done | bytes 147488 | tf_op jit(solution)/shard_map/ppermute | solution.py:439
  38.7 8.2 %encoder.1.lat_ref = bf16[8,8,1024]{2,1,0:T(8,128)(2,1)} custom-call(s32[8]{0:T(128)S(1)} %get-tuple-element.32.steps_ref, f32[36,8,128]{2,1,0:T(8,128)S(1)} %collective-permute-done.4.below_ref, f32[36,8,128]{2,1,0:T(8,128)S(1)} %pad_maximum_fusion.2.own_ref, f32[36,8,128]{2,1,0:T(8,128)S(1)} %collective-permute-done.5.above_ref, ...), custom_call_target="tpu_custom_call" | custom-call | tf_op jit(solution)/shard_map/encoder/pallas_call | solution.py:400
  46.9 3.5 %all-to-all-start = ((bf16[8,8,1024]{2,1,0:T(8,128)(2,1)}), bf16[8,8,1024]{2,1,0:T(8,128)(2,1)S(1)}, u32[]{:S(2)}, u32[]{:S(2)}) async-start(bf16[8,8,1024]{2,1,0:T(8,128)(2,1)} %encoder.1.lat_ref), calls=%async_computation | async-start | bytes 262144 | tf_op jit(solution)/shard_map/all_to_all | solution.py:535
  50.4 4.6 %all-to-all-done.m_ref = bf16[8,8,1024]{2,1,0:T(8,128)(2,1)S(1)} async-done(((bf16[8,8,1024]{2,1,0:T(8,128)(2,1)}), bf16[8,8,1024]{2,1,0:T(8,128)(2,1)S(1)}, u32[]{:S(2)}, u32[]{:S(2)}) %all-to-all-start) | async-done | bytes 131104 | tf_op jit(solution)/shard_map/all_to_all | solution.py:535
  55.0 1.4 %forward.1 = bf16[512,128]{1,0:T(8,128)(2,1)} custom-call(bf16[8,8,1024]{2,1,0:T(8,128)(2,1)S(1)} %all-to-all-done.m_ref, bf16[256,512]{1,0:T(8,128)(2,1)S(1)} %copy-done.4, bf16[256,512]{1,0:T(8,128)(2,1)S(1)} %copy-done.5, bf16[256,256]{1,0:T(8,128)(2,1)S(1)} %fusion.whi_ref, bf16[256,256]{1,0:T(8,128)(2,1)S(1)} %subtract_convert_fusion.wlo_ref), custom_call_target="tpu_custom_call" | custom-call | tf_op jit(solution)/shard_map/forward/pallas_call | solution.py:400
  56.4 16.6 %all-to-all-start.1 = ((bf16[256,2,128]{2,1,0:T(2,128)(2,1)}), bf16[256,2,128]{2,1,0:T(2,128)(2,1)S(1)}, u32[]{:S(2)}, u32[]{:S(2)}) async-start(bf16[256,2,128]{2,1,0:T(2,128)(2,1)} %bitcast.13), calls=%async_computation.1 | async-start | bytes 262144 | tf_op jit(solution)/shard_map/all_to_all | solution.py:538
  73.2 0.3 maximum_bitcast_fusion
  73.6 12.4 %all-to-all-done.1 = bf16[256,2,128]{2,1,0:T(2,128)(2,1)S(1)} async-done(((bf16[256,2,128]{2,1,0:T(2,128)(2,1)}), bf16[256,2,128]{2,1,0:T(2,128)(2,1)S(1)}, u32[]{:S(2)}, u32[]{:S(2)}) %all-to-all-start.1) | async-done | bytes 131104 | tf_op jit(solution)/shard_map/all_to_all | solution.py:538
  86.0 1.1 mix.1
  87.2 5.6 %all-to-all-start.2 = ((bf16[256,2,128]{2,1,0:T(2,128)(2,1)}), bf16[256,2,128]{2,1,0:T(2,128)(2,1)S(1)}, u32[]{:S(2)}, u32[]{:S(2)}) async-start(bf16[256,2,128]{2,1,0:T(2,128)(2,1)} %bitcast.23), calls=%async_computation.2 | async-start | bytes 262144 | tf_op jit(solution)/shard_map/all_to_all | solution.py:552
  92.9 12.9 %all-to-all-done.2 = bf16[256,2,128]{2,1,0:T(2,128)(2,1)S(1)} async-done(((bf16[256,2,128]{2,1,0:T(2,128)(2,1)}), bf16[256,2,128]{2,1,0:T(2,128)(2,1)S(1)}, u32[]{:S(2)}, u32[]{:S(2)}) %all-to-all-start.2) | async-done | bytes 131104 | tf_op jit(solution)/shard_map/all_to_all | solution.py:552
  105.9 1.6 %inverse.1 = bf16[8,8,8,128]{3,2,1,0:T(8,128)(2,1)} custom-call(bf16[8,4,16,128]{3,2,1,0:T(8,128)(2,1)S(1)} %bitcast.44, bf16[256,256]{1,0:T(8,128)(2,1)S(1)} %pad_maximum_fusion.3.v_ref, bf16[512,256]{1,0:T(8,128)(2,1)S(1)} %copy-done.3, bf16[512,256]{1,0:T(8,128)(2,1)S(1)} %copy-done.2, bf16[256,256]{1,0:T(8,128)(2,1)S(1)} %copy-done.6), custom_call_target="tpu_custom_call" | custom-call | tf_op jit(solution)/shard_map/inverse/pallas_call | solution.py:400
  107.5 3.8 %all-to-all-start.3 = ((bf16[8,8,8,128]{3,2,1,0:T(8,128)(2,1)}), bf16[8,8,8,128]{3,2,1,0:T(8,128)(2,1)S(1)}, u32[]{:S(2)}, u32[]{:S(2)}) async-start(bf16[8,8,8,128]{3,2,1,0:T(8,128)(2,1)} %inverse.1), calls=%async_computation.3 | async-start | bytes 262144 | tf_op jit(solution)/shard_map/all_to_all | solution.py:565
  111.3 0.7 copy-done.18
  112.0 4.5 %all-to-all-done.3.y_ref = bf16[8,8,8,128]{3,2,1,0:T(8,128)(2,1)S(1)} async-done(((bf16[8,8,8,128]{3,2,1,0:T(8,128)(2,1)}), bf16[8,8,8,128]{3,2,1,0:T(8,128)(2,1)S(1)}, u32[]{:S(2)}, u32[]{:S(2)}) %all-to-all-start.3) | async-done | bytes 131104 | tf_op jit(solution)/shard_map/all_to_all | solution.py:565
  116.5 2.3 %output.1 = f32[128,8,64]{2,1,0:T(8,128)} custom-call(bf16[8,8,8,128]{3,2,1,0:T(8,128)(2,1)S(1)} %all-to-all-done.3.y_ref, bf16[8,8,1024]{2,1,0:T(8,128)(2,1)} %encoder.1.lat_ref, bf16[128,64]{1,0:T(8,128)(2,1)S(1)} %pad_maximum_fusion.5.w_ref), custom_call_target="tpu_custom_call" | custom-call | tf_op jit(solution)/shard_map/output/pallas_call | solution.py:400
  (70 shorter events, 0.7 us)
Async XLA Ops:
  0.0 6.6 %copy-start = (bf16[2,2,2,4,64,64]{5,4,3,2,1,0:T(8,128)(2,1)S(1)}, bf16[2,2,2,4,64,64]{5,4,3,2,1,0:T(8,128)(2,1)}, u32[]{:S(2)}) copy-start(bf16[2,2,2,4,64,64]{5,4,3,2,1,0:T(8,128)(2,1)} %param.31) | copy-start | bytes 786436
  0.8 5.7 %copy-start.17 = (bf16[80,80]{1,0:T(8,128)(2,1)S(1)}, bf16[80,80]{1,0:T(8,128)(2,1)}, u32[]{:S(2)}) copy-start(bf16[80,80]{1,0:T(8,128)(2,1)} %param.29) | copy-start | bytes 38404
  0.8 11.1 %collective-permute-start = (f32[4,8,128]{2,1,0:T(8,128)S(1)}, f32[4,8,128]{2,1,0:T(8,128)S(1)}, u32[]{:S(2)}, u32[]{:S(2)}) collective-permute-start(f32[4,8,128]{2,1,0:T(8,128)S(1)} %pad.8.own_ref), channel_id=1, source_target_pairs={{0,32},{32,64},{64,96},{96,128},{128,160},{160,192},{192,224},{1,3... | collective-permute-start | bytes 49160 | tf_op jit(solution)/shard_map/ppermute | solution.py:437
  5.1 6.8 %collective-permute-start.1 = (f32[4,8,128]{2,1,0:T(8,128)S(1)}, f32[4,8,128]{2,1,0:T(8,128)S(1)}, u32[]{:S(2)}, u32[]{:S(2)}) collective-permute-start(f32[4,8,128]{2,1,0:T(8,128)S(1)} %pad.8.own_ref), channel_id=1, source_target_pairs={{32,0},{64,32},{96,64},{128,96},{160,128},{192,160},{224,192},{33,... | collective-permute-start | bytes 49160 | tf_op jit(solution)/shard_map/ppermute | solution.py:439
  6.7 1.0 copy-start.11
  11.9 4.6 %copy-start.21 = (s32[256]{0:T(256)S(1)}, s32[256]{0:T(256)}, u32[]{:S(2)}) copy-start(s32[256]{0:T(256)} %constant.86.clone) | copy-start | bytes 3076
  11.9 4.6 %copy-start.22 = (s32[256]{0:T(256)S(1)}, s32[256]{0:T(256)}, u32[]{:S(2)}) copy-start(s32[256]{0:T(256)} %constant.89.clone) | copy-start | bytes 3076
  11.9 4.6 %copy-start.23 = (s32[256]{0:T(256)S(1)}, s32[256]{0:T(256)}, u32[]{:S(2)}) copy-start(s32[256]{0:T(256)} %constant.90.clone) | copy-start | bytes 3076
  12.0 4.6 %copy-start.20 = (s32[256]{0:T(256)S(1)}, s32[256]{0:T(256)}, u32[]{:S(2)}) copy-start(s32[256]{0:T(256)} %constant.85.clone) | copy-start | bytes 3076
  12.0 4.6 %copy-start.19 = (bf16[6,80]{1,0:T(8,128)(2,1)S(1)}, bf16[6,80]{1,0:T(8,128)(2,1)}, u32[]{:S(2)}) copy-start(bf16[6,80]{1,0:T(8,128)(2,1)} %param.28) | copy-start | bytes 2884
  12.0 15.8 %collective-permute-start.2 = (f32[12,8,128]{2,1,0:T(8,128)S(1)}, f32[12,8,128]{2,1,0:T(8,128)S(1)}, u32[]{:S(2)}, u32[]{:S(2)}) collective-permute-start(f32[12,8,128]{2,1,0:T(8,128)S(1)} %pad_maximum_fusion.4), channel_id=1, source_target_pairs={{0,8},{8,16},{16,24},{1,9},{9,17},{17,25},{2,10},{10,18},{18,26},{... | collective-permute-start | bytes 147464 | tf_op jit(solution)/shard_map/ppermute | solution.py:437
  15.2 12.6 %collective-permute-start.3 = (f32[12,8,128]{2,1,0:T(8,128)S(1)}, f32[12,8,128]{2,1,0:T(8,128)S(1)}, u32[]{:S(2)}, u32[]{:S(2)}) collective-permute-start(f32[12,8,128]{2,1,0:T(8,128)S(1)} %pad_maximum_fusion.4), channel_id=1, source_target_pairs={{8,0},{16,8},{24,16},{9,1},{17,9},{25,17},{10,2},{18,10},{26,18},{... | collective-permute-start | bytes 147464 | tf_op jit(solution)/shard_map/ppermute | solution.py:439
  27.8 6.4 %copy-start.14 = (f32[256,128]{1,0:T(8,128)S(1)}, f32[256,128]{1,0:T(8,128)}, u32[]{:S(2)}) copy-start(f32[256,128]{1,0:T(8,128)} %constant.87.clone) | copy-start | bytes 393220
  27.8 6.4 %copy-start.15 = (f32[256,128]{1,0:T(8,128)S(1)}, f32[256,128]{1,0:T(8,128)}, u32[]{:S(2)}) copy-start(f32[256,128]{1,0:T(8,128)} %constant.88.clone) | copy-start | bytes 393220
  27.8 6.5 %collective-permute-start.4 = (f32[36,8,128]{2,1,0:T(8,128)S(1)}, f32[36,8,128]{2,1,0:T(8,128)S(1)}, u32[]{:S(2)}, u32[]{:S(2)}) collective-permute-start(f32[36,8,128]{2,1,0:T(8,128)S(1)} %pad_maximum_fusion.2.own_ref), channel_id=1, source_target_pairs={{0,1},{1,2},{2,3},{3,4},{4,5},{5,6},{6,7},{8,9},{9,10},{10,11},{11... | collective-permute-start | bytes 442376 | tf_op jit(solution)/shard_map/ppermute | solution.py:437
  32.2 6.5 %collective-permute-start.5 = (f32[36,8,128]{2,1,0:T(8,128)S(1)}, f32[36,8,128]{2,1,0:T(8,128)S(1)}, u32[]{:S(2)}, u32[]{:S(2)}) collective-permute-start(f32[36,8,128]{2,1,0:T(8,128)S(1)} %pad_maximum_fusion.2.own_ref), channel_id=1, source_target_pairs={{1,0},{2,1},{3,2},{4,3},{5,4},{6,5},{7,6},{9,8},{10,9},{11,10},{12... | collective-permute-start | bytes 442376 | tf_op jit(solution)/shard_map/ppermute | solution.py:439
  34.3 4.4 %copy-start.8 = (bf16[80,64]{0,1:T(8,128)(2,1)S(1)}, bf16[80,64]{0,1:T(8,128)(2,1)}, u32[]{:S(2)}) copy-start(bf16[80,64]{0,1:T(8,128)(2,1)} %param.30) | copy-start | bytes 30724
  46.9 8.2 %copy-start.5 = (bf16[256,512]{1,0:T(8,128)(2,1)S(1)}, bf16[256,512]{1,0:T(8,128)(2,1)}, u32[]{:S(2)}) copy-start(bf16[256,512]{1,0:T(8,128)(2,1)} %constant.94.clone.alo_ref) | copy-start | bytes 786436
  46.9 8.1 %all-to-all-start = ((bf16[8,8,1024]{2,1,0:T(8,128)(2,1)}), bf16[8,8,1024]{2,1,0:T(8,128)(2,1)S(1)}, u32[]{:S(2)}, u32[]{:S(2)}) async-start(bf16[8,8,1024]{2,1,0:T(8,128)(2,1)} %encoder.1.lat_ref), calls=%async_computation | async-start | bytes 262144 | tf_op jit(solution)/shard_map/all_to_all | solution.py:535
  50.4 4.7 %copy-start.4 = (bf16[256,512]{1,0:T(8,128)(2,1)S(1)}, bf16[256,512]{1,0:T(8,128)(2,1)}, u32[]{:S(2)}) copy-start(bf16[256,512]{1,0:T(8,128)(2,1)} %constant.93.clone.ahi_ref) | copy-start | bytes 786436
  56.4 29.6 %all-to-all-start.1 = ((bf16[256,2,128]{2,1,0:T(2,128)(2,1)}), bf16[256,2,128]{2,1,0:T(2,128)(2,1)S(1)}, u32[]{:S(2)}, u32[]{:S(2)}) async-start(bf16[256,2,128]{2,1,0:T(2,128)(2,1)} %bitcast.13), calls=%async_computation.1 | async-start | bytes 262144 | tf_op jit(solution)/shard_map/all_to_all | solution.py:538
  73.5 12.5 %copy-start.1 = (bf16[128,1024]{1,0:T(8,128)(2,1)S(1)}, bf16[128,1024]{1,0:T(8,128)(2,1)}, u32[]{:S(2)}) copy-start(bf16[128,1024]{1,0:T(8,128)(2,1)} %constant.96.clone.sel_ref) | copy-start | bytes 786436
  73.5 12.5 %copy-start.7 = (f32[16,1024]{1,0:T(8,128)S(1)}, f32[16,1024]{1,0:T(8,128)}, u32[]{:S(2)}) copy-start(f32[16,1024]{1,0:T(8,128)} %constant.97.clone.place_ref) | copy-start | bytes 196612
  73.5 12.5 %copy-start.9 = (f32[16,256]{1,0:T(8,128)S(1)}, f32[16,256]{1,0:T(8,128)}, u32[]{:S(2)}) copy-start(f32[16,256]{1,0:T(8,128)} %constant.95.clone.own_ref) | copy-start | bytes 49156
  73.6 12.4 %copy-start.10 = (bf16[8,16]{1,0:T(8,128)(2,1)S(1)}, bf16[8,16]{1,0:T(8,128)(2,1)}, u32[]{:S(2)}) copy-start(bf16[8,16]{1,0:T(8,128)(2,1)} %constant.98.clone.half_ref) | copy-start | bytes 772
  87.2 5.7 %copy-start.12 = (f32[128,256]{1,0:T(8,128)S(1)}, f32[128,256]{1,0:T(8,128)}, u32[]{:S(2)}) copy-start(f32[128,256]{1,0:T(8,128)} %constant.91.clone) | copy-start | bytes 393220
  87.2 5.7 %copy-start.13 = (f32[128,256]{1,0:T(8,128)S(1)}, f32[128,256]{1,0:T(8,128)}, u32[]{:S(2)}) copy-start(f32[128,256]{1,0:T(8,128)} %constant.92.clone) | copy-start | bytes 393220
  87.2 18.7 %all-to-all-start.2 = ((bf16[256,2,128]{2,1,0:T(2,128)(2,1)}), bf16[256,2,128]{2,1,0:T(2,128)(2,1)S(1)}, u32[]{:S(2)}, u32[]{:S(2)}) async-start(bf16[256,2,128]{2,1,0:T(2,128)(2,1)} %bitcast.23), calls=%async_computation.2 | async-start | bytes 262144 | tf_op jit(solution)/shard_map/all_to_all | solution.py:552
  92.8 13.0 %copy-start.2 = (bf16[512,256]{1,0:T(8,128)(2,1)S(1)}, bf16[512,256]{1,0:T(8,128)(2,1)}, u32[]{:S(2)}) copy-start(bf16[512,256]{1,0:T(8,128)(2,1)} %constant.100.clone.bs_ref) | copy-start | bytes 786436
  92.8 13.0 %copy-start.3 = (bf16[512,256]{1,0:T(8,128)(2,1)S(1)}, bf16[512,256]{1,0:T(8,128)(2,1)}, u32[]{:S(2)}) copy-start(bf16[512,256]{1,0:T(8,128)(2,1)} %constant.99.clone.bc_ref) | copy-start | bytes 786436
  92.9 13.0 %copy-start.6 = (bf16[256,256]{1,0:T(8,128)(2,1)S(1)}, bf16[256,256]{1,0:T(8,128)(2,1)}, u32[]{:S(2)}) copy-start(bf16[256,256]{1,0:T(8,128)(2,1)} %constant.101.clone.partner_ref) | copy-start | bytes 393220
  107.5 9.0 %all-to-all-start.3 = ((bf16[8,8,8,128]{3,2,1,0:T(8,128)(2,1)}), bf16[8,8,8,128]{3,2,1,0:T(8,128)(2,1)S(1)}, u32[]{:S(2)}, u32[]{:S(2)}) async-start(bf16[8,8,8,128]{3,2,1,0:T(8,128)(2,1)} %inverse.1), calls=%async_computation.3 | async-start | bytes 262144 | tf_op jit(solution)/shard_map/all_to_all | solution.py:565
  (2 other events, 1.5 us)

commit v4 on v3

--- a/solution.py
+++ b/solution.py
@@ -16,6 +16,8 @@
 GRID = 64
 NB = 32
 NEAR_EARLY = True
+ROWS = 8 * NB + 32
+LAST = ROWS
 CELLS = float(GRID**3)
 NORM_FLOOR = 1.0
 GZ = ("gz_0", "gz_1")
@@ -122,9 +124,7 @@
     return jnp.where(r == rank, 1.0, 0.0).astype(bf16)
 
 
-def sort_kernel(
-    place_ref, nb_ref, cnt_ref, far_ref, near_ref, far8_ref, near8_ref, cen_ref, rank_ref, scnt_ref, steps_ref, lists
-):
+def sort_kernel(place_ref, nb_ref, cnt_ref, far_ref, near_ref, rank_ref, scnt_ref, tile_ref, lists):
     px, py, pz = place_ref[0], place_ref[1], place_ref[2]
     me = (px * 4 + py) * 8 + pz
     counts = cnt_ref[...]
@@ -161,7 +161,7 @@
     far, near = far.astype(f32), near.astype(f32)
     row8 = lax.broadcasted_iota(i32, (8, 128), 0)
     lane8 = lax.broadcasted_iota(i32, (8, 128), 1)
-    key = far * 1024.0 - (row8 * 128 + lane8).astype(f32)
+    key = counts.astype(f32) * 1024.0 - (row8 * 128 + lane8).astype(f32)
     flat = [key[z : z + 1] for z in range(8)]
     ranks = [jnp.zeros((128, 128), f32) for _ in range(8)]
     for z in range(8):
@@ -177,86 +177,101 @@
     tail = jnp.where(wide == 0, far, jnp.where(wide == 1, near, tail))
     rows = jnp.concatenate([lists[:, z, :] for z in range(8)], axis=1)
     rows = jnp.concatenate([rows, tail], axis=0).astype(bf16)
-    odd = (row8 & 1) == 1
+    slot = lax.broadcasted_iota(i32, (NB, 128), 0)
+    ends = [0, 0]
     for t in range(4):
         found = dot_t(rows, rank_rows(rank, t * 256, 256))
-        for ref, at in ((far_ref, 0), (near_ref, 2 * NB)):
-            code = (found[at : at + 32] * 128.0 + found[at + 32 : at + 64]).astype(i32)
-            for s in range(4):
-                for h in range(2):
-                    ref[t, pl.ds(s * 16 + h, 8, stride=2), :] = code[
-                        s * 8 : s * 8 + 8, h * 128 : h * 128 + 128
-                    ]
         tail = found[4 * NB : 4 * NB + 8]
-
-        def both(n):
-            return jnp.where(odd, tail[n : n + 1, 128:256], tail[n : n + 1, 0:128])
-
-        far8_ref[t] = both(0).astype(i32)
-        near8_ref[t] = both(1).astype(i32)
-        cell = both(3).astype(i32)
-        cen_ref[t, 0] = ((px * 8 + (cell >> 4)).astype(f32) + 0.5) / GRID
-        cen_ref[t, 1] = ((py * 16 + (cell & 15)).astype(f32) + 0.5) / GRID
-        cen_ref[t, 2] = ((pz * 8).astype(f32) + both(2) + 0.5) / GRID
         scnt_ref[:, t * 256 : t * 256 + 256] = jnp.broadcast_to(tail[0:1] + tail[1:2], (8, 256))
-        steps_ref[t] = jnp.maximum((jnp.max(tail[0:1]).astype(i32) + 3) >> 2, 1)
-        steps_ref[4 + t] = jnp.maximum((jnp.max(tail[1:2]).astype(i32) + 3) >> 2, 1)
-
-
-def pair_sums(steps_ref, at, gather, ki_ref, km_ref, acc_ref):
-    def step(_, carry):
-        t, b, pair = carry
-        last = b + 1 >= steps_ref[at + t]
-        nt = jnp.where(last, jnp.minimum(t + 1, 3), t)
-        nb = jnp.where(last, 0, b + 1)
-        following = gather(nt, nb)
+        for h in range(2):
+            part = found[:, h * 128 : h * 128 + 128]
+            cell = (tail[2:3] * 128.0 + tail[3:4])[:, h * 128 : h * 128 + 128] * 16384.0
+            for n, ref in enumerate((far_ref, near_ref)):
+                word = (part[2 * n * NB : (2 * n + 1) * NB] * 128.0 + part[(2 * n + 1) * NB : (2 * n + 2) * NB] + cell).astype(i32)
+                length = tail[n : n + 1, h * 128 : h * 128 + 128].astype(i32)
+                start = ends[n]
+                ref[pl.ds(start, NB), :] = jnp.where(slot < length, word, -1)
+                most = jnp.max(length)
+
+                def mark(r, carry):
+                    tile_ref[n, start + r] = 2 * t + h
+                    return carry
+
+                lax.fori_loop(0, most, mark, 0)
+                ends[n] = start + most
+    for n, ref in enumerate((far_ref, near_ref)):
+        ref[pl.ds(ends[n], 16), :] = jnp.full((16, 128), -1, i32)
+        for r in range(16):
+            tile_ref[n, ends[n] + r] = 0
+        tile_ref[n, LAST] = jnp.maximum((ends[n] + 15) >> 4, 1)
+
+
+def pair_sums(place_ref, tile_ref, at, code_ref, look_up, ki_ref, km_ref, turn, acc_ref):
+    px, py, pz = place_ref[0], place_ref[1], place_ref[2]
+    x0 = px.astype(f32) * 8.0 + 0.5
+    y0 = py.astype(f32) * 16.0 + 0.5
+    z0 = pz.astype(f32) * 8.0 + 0.5
+    turn[...] = jnp.zeros(turn.shape, f32)
+    steps = tile_ref[at, LAST]
+
+    def gather(b):
+        lines = []
+        for half in range(2):
+            code = code_ref[pl.ds(pl.multiple_of(b * 16 + half * 8, 8), 8), :]
+            cell = code >> 14
+            centres = (
+                (((cell >> 4) & 7).astype(f32) + x0) * (1.0 / GRID),
+                ((cell & 15).astype(f32) + y0) * (1.0 / GRID),
+                ((cell >> 7).astype(f32) + z0) * (1.0 / GRID),
+            )
+            values = look_up(code)
+            for c in range(6):
+                value = values[c]
+                if c < 3:
+                    value = value - centres[c]
+                turn[half, c] = jnp.where(code >= 0, value, 0.0)
+            lines += [turn[half, :, n, :] for n in range(8)]
+        return jnp.concatenate(lines, axis=1)
+
+    def step(b, pair):
+        following = gather(jnp.minimum(b + 1, steps - 1))
         hidden = gelu_twice(dot(ki_ref[...], pair.astype(bf16))).astype(bf16)
         hidden = gelu_twice(dot(km_ref[...], hidden))
-        acc_ref[t] += (
-            hidden[:, 0:256] + hidden[:, 256:512] + hidden[:, 512:768] + hidden[:, 768:1024]
-        )
-        return nt, nb, following
-
-    total = steps_ref[at] + steps_ref[at + 1] + steps_ref[at + 2] + steps_ref[at + 3]
-    lax.fori_loop(0, total, step, (jnp.int32(0), jnp.int32(0), gather(0, 0)))
-
-
-def near_kernel(steps_ref, own_ref, code_ref, cnt8_ref, cen_ref, ki_ref, km_ref, acc_ref, turn):
-    turn[...] = jnp.zeros(turn.shape, f32)
+        for r in range(16):
+            acc_ref[tile_ref[at, b * 16 + r]] += hidden[:, r * 128 : r * 128 + 128]
+        return following
+
+    lax.fori_loop(0, steps, step, gather(0))
+
+
+def lane_gather(line, at):
+    return jnp.take_along_axis(jnp.broadcast_to(line, (8, 128)), at, axis=1, mode="promise_in_bounds")
+
+
+def near_kernel(place_ref, tile_ref, own_ref, code_ref, ki_ref, km_ref, acc_ref, turn):
     acc_ref[...] = jnp.zeros(acc_ref.shape, f32)
-    slot = lax.broadcasted_iota(i32, (8, 128), 0) >> 1
-
-    def gather(t, b):
-        code = code_ref[t, pl.ds(pl.multiple_of(b * 8, 8), 8), :]
+
+    def look_up(code):
         at = code & 127
         low, high = (code & 128) != 0, (code & 256) != 0
-        valid = cnt8_ref[t] > slot + b * 4
+        values = []
         for c in range(6):
-            found = [
-                jnp.take_along_axis(
-                    jnp.broadcast_to(own_ref[n, c : c + 1, :], (8, 128)), at, axis=1, mode="promise_in_bounds"
-                )
-                for n in range(4)
-            ]
-            value = jnp.where(
-                high, jnp.where(low, found[3], found[2]), jnp.where(low, found[1], found[0])
+            found = [lane_gather(own_ref[n, c : c + 1, :], at) for n in range(4)]
+            values.append(
+                jnp.where(high, jnp.where(low, found[3], found[2]), jnp.where(low, found[1], found[0]))
             )
-            if c < 3:
-                value = value - cen_ref[t, c]
-            turn[c] = jnp.where(valid, value, 0.0)
-        return jnp.concatenate([turn[:, n, :] for n in range(8)], axis=1)
-
-    pair_sums(steps_ref, 4, gather, ki_ref, km_ref, acc_ref)
+        return values
+
+    pair_sums(place_ref, tile_ref, 1, code_ref, look_up, ki_ref, km_ref, turn, acc_ref)
 
 
 def encoder_kernel(
-    steps_ref,
+    place_ref,
+    tile_ref,
     below_ref,
     own_ref,
     above_ref,
     code_ref,
-    cnt8_ref,
-    cen_ref,
     rank_ref,
     scnt_ref,
     sum_ref,
@@ -265,7 +280,6 @@
     ko_ref,
     out_ref,
     words,
-    off_ref,
     turn,
     acc_ref,
 ):
@@ -280,39 +294,30 @@
         q = (parts[n // 36][n % 36] * scale + 32768.5).astype(i32)
         words[n] = (q << 16) | pltpu.roll(q, 5, 0)
     units = [jnp.broadcast_to(unit[c : c + 1], (8, 128)) for c in range(6)]
-    for t in range(4):
-        for c in range(3):
-            off_ref[t, c] = cen_ref[t, c] + 32768.0 * units[c]
-    turn[...] = jnp.zeros(turn.shape, f32)
     acc_ref[...] = sum_ref[...]
-    slot = lax.broadcasted_iota(i32, (8, 128), 0) >> 1
-
-    def gather(t, b):
-        code = code_ref[t, pl.ds(pl.multiple_of(b * 8, 8), 8), :]
+
+    def look_up(code):
         at = code & 127
         bits = [(code & (128 << n)) != 0 for n in range(7)]
-        valid = cnt8_ref[t] > slot + b * 4
+        values = [None] * 6
         for c in range(3):
 
             def pick(lo, level):
                 if lo >= 108:
                     return None
                 if level == 0:
-                    line = jnp.broadcast_to(words[lo, c : c + 1, :], (8, 128))
-                    return jnp.take_along_axis(line, at, axis=1, mode="promise_in_bounds")
+                    return lane_gather(words[lo, c : c + 1, :], at)
                 first = pick(lo, level - 1)
                 second = pick(lo + (1 << (level - 1)), level - 1)
                 return first if second is None else jnp.where(bits[level - 1], second, first)
 
             word = pick(0, 7)
-            place = lax.shift_right_logical(word, 16).astype(f32) * units[c] - off_ref[t, c]
-            normal = ((word & 65535) - 32768).astype(f32) * units[c + 3]
-            turn[c] = jnp.where(valid, place, 0.0)
-            turn[c + 3] = jnp.where(valid, normal, 0.0)
-        return jnp.concatenate([turn[:, n, :] for n in range(8)], axis=1)
-
-    pair_sums(steps_ref, 0, gather, ki_ref, km_ref, acc_ref)
-    mean = jnp.concatenate([acc_ref[t] for t in range(4)], axis=1) * (0.5 / scnt_ref[0:1])
+            values[c] = (lax.shift_right_logical(word, 16) - 32768).astype(f32) * units[c]
+            values[c + 3] = ((word & 65535) - 32768).astype(f32) * units[c + 3]
+        return values
+
+    pair_sums(place_ref, tile_ref, 0, code_ref, look_up, ki_ref, km_ref, turn, acc_ref)
+    mean = jnp.concatenate([acc_ref[t] for t in range(8)], axis=1) * (0.5 / scnt_ref[0:1])
     upper = mean.astype(bf16)
     lower = (mean - upper.astype(f32)).astype(bf16)
     latent = (dot(ko_ref[...], upper) + dot(ko_ref[...], lower)).astype(bf16)
@@ -410,20 +415,17 @@
 
 def sorted_nodes(place, near, valid):
     shapes = (
-        ((4, 64, 128), i32),
-        ((4, 64, 128), i32),
-        ((4, 8, 128), i32),
-        ((4, 8, 128), i32),
-        ((4, 3, 8, 128), f32),
+        ((ROWS, 128), i32),
+        ((ROWS, 128), i32),
         ((8, 1024), i32),
         ((8, 1024), f32),
-        ((8,), i32),
+        ((2, LAST + 1), i32),
     )
     return pl.pallas_call(
         sort_kernel,
         out_shape=[jax.ShapeDtypeStruct(*s) for s in shapes],
         in_specs=[SMEM, VMEM, VMEM],
-        out_specs=[VMEM] * 7 + [SMEM],
+        out_specs=[VMEM] * 4 + [SMEM],
         scratch_shapes=[pltpu.VMEM((4 * NB, 8, 128), f32)],
         compiler_params=pltpu.CompilerParams(vmem_limit_bytes=48 * 1024 * 1024),
         name="sort",
@@ -460,22 +462,21 @@
     line = jnp.concatenate(beside(own, "gx"), axis=0)
     tables = sorted_nodes(place, near, valid)
     line, tables = lax.optimization_barrier((line, tables))
-    far_code, near_code, far8, near8, centres, rank, sorted_counts, steps = tables
+    far_code, near_code, rank, sorted_counts, tiles = tables
     plane = jnp.concatenate(beside(line, "gy"), axis=0)
     sums = call(
         near_kernel,
         "near",
-        (4, 80, 256),
+        (8, 80, 128),
         f32,
-        steps,
+        place,
+        tiles,
         own,
         near_code,
-        near8,
-        centres,
         ki,
         km,
-        scratch=(pltpu.VMEM((8, 8, 128), f32),),
-        smem=1,
+        scratch=(pltpu.VMEM((2, 8, 8, 128), f32),),
+        smem=2,
     )
     if NEAR_EARLY:
         plane, sums = lax.optimization_barrier((plane, sums))
@@ -485,13 +486,12 @@
         "encoder",
         (8, 8, 1024),
         bf16,
-        steps,
+        place,
+        tiles,
         below,
         same,
         above,
         far_code,
-        far8,
-        centres,
         rank,
         sorted_counts,
         sums,
@@ -500,11 +500,10 @@
         kernel_out.T,
         scratch=(
             pltpu.VMEM((108, 8, 128), i32),
-            pltpu.VMEM((4, 3, 8, 128), f32),
-            pltpu.VMEM((8, 8, 128), f32),
-            pltpu.VMEM((4, 80, 256), f32),
+            pltpu.VMEM((2, 8, 8, 128), f32),
+            pltpu.VMEM((8, 80, 128), f32),
         ),
-        smem=1,
+        smem=2,
     )
 
     (ffi, ffj), (ifi, ifj), xl, yl = plane_tables()

time: 120 us -> 121 us (level)
    pallas_call x1, Pallas kernels: 3.26 us -> 8.61 us  [sorted_nodes(): pl.pallas_call(sort_kernel, out_shape=[jax.ShapeDtypeStruct(*s) for s in...]
    pallas_call x6, Pallas kernels: 25.6 us -> 20.8 us  [call(): pl.pallas_call(kernel, out_shape=jax.ShapeDtypeStruct(shape, dtype), in_s...]
where the time goes in v4:
time: 121 us; the launch traced here: 120 us
  starting transfers between devices  46.3 us (38%)
  waiting for transfers between devices  39.4 us (33%)
  Pallas kernels  29.4 us (24%)
  local copies, waits for them, and re-layouts  3.81 us (3%)
    pallas_call x6, Pallas kernels, call(): pl.pallas_call(kernel, out_shape=jax.ShapeDtypeStruct(shape, dtype), in_s...  20.8 us
    all_to_all x1, starting transfers between devices, body(): lax.all_to_all(partial.reshape(256, 2, 128), ALL, split_axis=0, concat_ax...  17.1 us
    all_to_all x1, waiting for transfers between devices, body(): lax.all_to_all(mixed.reshape(256, 2, 128), ALL, split_axis=0, concat_axis=0)  12.9 us
    all_to_all x1, waiting for transfers between devices, body(): lax.all_to_all(partial.reshape(256, 2, 128), ALL, split_axis=0, concat_ax...  12.4 us
    ppermute x3, starting transfers between devices, beside(): lax.ppermute(cells, axis, [(i, i + 1) for i in range(ends)])  11.9 us
    pallas_call x1, Pallas kernels, sorted_nodes(): pl.pallas_call(sort_kernel, out_shape=[jax.ShapeDtypeStruct(*s) for s in...  8.61 us
    all_to_all x1, starting transfers between devices, body(): lax.all_to_all(mixed.reshape(256, 2, 128), ALL, split_axis=0, concat_axis=0)  5.64 us
    all_to_all x1, waiting for transfers between devices, body(): depth = lax.all_to_all(latent, GZ, split_axis=0, concat_axis=0)  5.14 us
  transfers between devices with their start and end apart: 10, of which 5 were waited for; matrix products, arithmetic and copies ran while one was open for 1% of the time, Pallas kernels for 12%

profile of v4, /device:TPU:1, one launch (start us, length us, event | category | flops | bytes accessed | tf_op | source)
XLA Modules:
  0.0 120.2 jit_solution(3984559290346480202)
XLA Ops:
  0.0 0.8 copy.44
  0.8 4.4 %collective-permute-start = (f32[4,8,128]{2,1,0:T(8,128)S(1)}, f32[4,8,128]{2,1,0:T(8,128)S(1)}, u32[]{:S(2)}, u32[]{:S(2)}) collective-permute-start(f32[4,8,128]{2,1,0:T(8,128)S(1)} %pad.8.own_ref), channel_id=1, source_target_pairs={{0,32},{32,64},{64,96},{96,128},{128,160},{160,192},{192,224},{1,3... | collective-permute-start | bytes 49160 | tf_op jit(solution)/shard_map/ppermute | solution.py:439
  5.1 1.3 %collective-permute-start.1 = (f32[4,8,128]{2,1,0:T(8,128)S(1)}, f32[4,8,128]{2,1,0:T(8,128)S(1)}, u32[]{:S(2)}, u32[]{:S(2)}) collective-permute-start(f32[4,8,128]{2,1,0:T(8,128)S(1)} %pad.8.own_ref), channel_id=1, source_target_pairs={{32,0},{64,32},{96,64},{128,96},{160,128},{192,160},{224,192},{33,... | collective-permute-start | bytes 49160 | tf_op jit(solution)/shard_map/ppermute | solution.py:441
  6.5 0.1 copy.37
  6.6 0.1 copy_bitcast_fusion
  6.9 0.9 copy-done.11
  7.8 0.2 copy.35.nb_ref
  8.0 0.5 copy-done.16
  8.6 8.6 %sort.1 = (s32[288,128]{1,0:T(8,128)S(1)}, s32[288,128]{1,0:T(8,128)S(1)}, s32[8,1024]{1,0:T(8,128)S(1)}, f32[8,1024]{1,0:T(8,128)S(1)}, s32[2,289]{1,0:T(2,128)S(1)}) custom-call(s32[3]{0:T(128)S(1)} %pad_add_fusion.place_ref, s32[32,8,128]{2,1,0:T(8,128)S(1)} %copy.35.nb_ref, s32[8,128]{1,0:T(8,128)S(1)} %reshape.36.cnt_ref), custom_call_target="tpu_custom_call" | custom-call | tf_op jit(solution)/shard_map/sort/pallas_call | solution.py:424
  17.3 3.2 %collective-permute-start.2 = (f32[12,8,128]{2,1,0:T(8,128)S(1)}, f32[12,8,128]{2,1,0:T(8,128)S(1)}, u32[]{:S(2)}, u32[]{:S(2)}) collective-permute-start(f32[12,8,128]{2,1,0:T(8,128)S(1)} %pad_maximum_fusion.4), channel_id=1, source_target_pairs={{0,8},{8,16},{16,24},{1,9},{9,17},{17,25},{2,10},{10,18},{18,26},{... | collective-permute-start | bytes 147464 | tf_op jit(solution)/shard_map/ppermute | solution.py:439
  20.5 1.3 %collective-permute-start.3 = (f32[12,8,128]{2,1,0:T(8,128)S(1)}, f32[12,8,128]{2,1,0:T(8,128)S(1)}, u32[]{:S(2)}, u32[]{:S(2)}) collective-permute-start(f32[12,8,128]{2,1,0:T(8,128)S(1)} %pad_maximum_fusion.4), channel_id=1, source_target_pairs={{8,0},{16,8},{24,16},{9,1},{17,9},{25,17},{10,2},{18,10},{26,18},{... | collective-permute-start | bytes 147464 | tf_op jit(solution)/shard_map/ppermute | solution.py:441
  21.9 0.1 copy.36
  22.1 5.5 %near.1.sum_ref = f32[8,80,128]{2,1,0:T(8,128)S(1)} custom-call(s32[3]{0:T(128)S(1)} %pad_add_fusion.place_ref, s32[2,289]{1,0:T(2,128)S(1)} %get-tuple-element.23.tile_ref, f32[4,8,128]{2,1,0:T(8,128)S(1)} %pad.8.own_ref, s32[288,128]{1,0:T(8,128)S(1)} %get-tuple-element.25.code_ref, bf16[80,8]{1,0:T(8,128)(2,1)S(1)} %pad.9.ki_ref, ...), custom_call_target="tpu_custom_call" | custom-call | tf_op jit(solution)/shard_map/near/pallas_call | solution.py:405
  27.7 4.4 %collective-permute-start.4 = (f32[36,8,128]{2,1,0:T(8,128)S(1)}, f32[36,8,128]{2,1,0:T(8,128)S(1)}, u32[]{:S(2)}, u32[]{:S(2)}) collective-permute-start(f32[36,8,128]{2,1,0:T(8,128)S(1)} %pad_maximum_fusion.2.own_ref), channel_id=1, source_target_pairs={{0,1},{1,2},{2,3},{3,4},{4,5},{5,6},{6,7},{8,9},{9,10},{10,11},{11... | collective-permute-start | bytes 442376 | tf_op jit(solution)/shard_map/ppermute | solution.py:439
  32.1 1.9 %collective-permute-start.5 = (f32[36,8,128]{2,1,0:T(8,128)S(1)}, f32[36,8,128]{2,1,0:T(8,128)S(1)}, u32[]{:S(2)}, u32[]{:S(2)}) collective-permute-start(f32[36,8,128]{2,1,0:T(8,128)S(1)} %pad_maximum_fusion.2.own_ref), channel_id=1, source_target_pairs={{1,0},{2,1},{3,2},{4,3},{5,4},{6,5},{7,6},{9,8},{10,9},{11,10},{12... | collective-permute-start | bytes 442376 | tf_op jit(solution)/shard_map/ppermute | solution.py:441
  34.0 0.1 multiply_subtract_fusion
  34.2 4.3 %collective-permute-done.5.above_ref = f32[36,8,128]{2,1,0:T(8,128)S(1)} collective-permute-done((f32[36,8,128]{2,1,0:T(8,128)S(1)}, f32[36,8,128]{2,1,0:T(8,128)S(1)}, u32[]{:S(2)}, u32[]{:S(2)}) %collective-permute-start.5) | collective-permute-done | bytes 147488 | tf_op jit(solution)/shard_map/ppermute | solution.py:441
  38.5 8.8 %encoder.1.lat_ref = bf16[8,8,1024]{2,1,0:T(8,128)(2,1)} custom-call(s32[3]{0:T(128)S(1)} %pad_add_fusion.place_ref, s32[2,289]{1,0:T(2,128)S(1)} %get-tuple-element.23.tile_ref, f32[36,8,128]{2,1,0:T(8,128)S(1)} %collective-permute-done.4.below_ref, f32[36,8,128]{2,1,0:T(8,128)S(1)} %pad_maximum_fusion.2.own_ref, ...), custom_call_target="tpu_custom_call" | custom-call | tf_op jit(solution)/shard_map/encoder/pallas_call | solution.py:405
  47.4 3.5 %all-to-all-start = ((bf16[8,8,1024]{2,1,0:T(8,128)(2,1)}), bf16[8,8,1024]{2,1,0:T(8,128)(2,1)S(1)}, u32[]{:S(2)}, u32[]{:S(2)}) async-start(bf16[8,8,1024]{2,1,0:T(8,128)(2,1)} %encoder.1.lat_ref), calls=%async_computation | async-start | bytes 262144 | tf_op jit(solution)/shard_map/all_to_all | solution.py:534
  50.9 5.1 %all-to-all-done.m_ref = bf16[8,8,1024]{2,1,0:T(8,128)(2,1)S(1)} async-done(((bf16[8,8,1024]{2,1,0:T(8,128)(2,1)}), bf16[8,8,1024]{2,1,0:T(8,128)(2,1)S(1)}, u32[]{:S(2)}, u32[]{:S(2)}) %all-to-all-start) | async-done | bytes 131104 | tf_op jit(solution)/shard_map/all_to_all | solution.py:534
  56.0 1.4 %forward.1 = bf16[512,128]{1,0:T(8,128)(2,1)} custom-call(bf16[8,8,1024]{2,1,0:T(8,128)(2,1)S(1)} %all-to-all-done.m_ref, bf16[256,512]{1,0:T(8,128)(2,1)S(1)} %copy-done.4, bf16[256,512]{1,0:T(8,128)(2,1)S(1)} %copy-done.5, bf16[256,256]{1,0:T(8,128)(2,1)S(1)} %fusion.whi_ref, bf16[256,256]{1,0:T(8,128)(2,1)S(1)} %subtract_convert_fusion.wlo_ref), custom_call_target="tpu_custom_call" | custom-call | tf_op jit(solution)/shard_map/forward/pallas_call | solution.py:405
  57.4 17.1 %all-to-all-start.1 = ((bf16[256,2,128]{2,1,0:T(2,128)(2,1)}), bf16[256,2,128]{2,1,0:T(2,128)(2,1)S(1)}, u32[]{:S(2)}, u32[]{:S(2)}) async-start(bf16[256,2,128]{2,1,0:T(2,128)(2,1)} %bitcast.13), calls=%async_computation.1 | async-start | bytes 262144 | tf_op jit(solution)/shard_map/all_to_all | solution.py:537
  74.5 0.3 maximum_bitcast_fusion
  74.9 12.4 %all-to-all-done.1 = bf16[256,2,128]{2,1,0:T(2,128)(2,1)S(1)} async-done(((bf16[256,2,128]{2,1,0:T(2,128)(2,1)}), bf16[256,2,128]{2,1,0:T(2,128)(2,1)S(1)}, u32[]{:S(2)}, u32[]{:S(2)}) %all-to-all-start.1) | async-done | bytes 131104 | tf_op jit(solution)/shard_map/all_to_all | solution.py:537
  87.4 1.1 mix.1
  88.5 5.6 %all-to-all-start.2 = ((bf16[256,2,128]{2,1,0:T(2,128)(2,1)}), bf16[256,2,128]{2,1,0:T(2,128)(2,1)S(1)}, u32[]{:S(2)}, u32[]{:S(2)}) async-start(bf16[256,2,128]{2,1,0:T(2,128)(2,1)} %bitcast.23), calls=%async_computation.2 | async-start | bytes 262144 | tf_op jit(solution)/shard_map/all_to_all | solution.py:551
  94.3 12.9 %all-to-all-done.2 = bf16[256,2,128]{2,1,0:T(2,128)(2,1)S(1)} async-done(((bf16[256,2,128]{2,1,0:T(2,128)(2,1)}), bf16[256,2,128]{2,1,0:T(2,128)(2,1)S(1)}, u32[]{:S(2)}, u32[]{:S(2)}) %all-to-all-start.2) | async-done | bytes 131104 | tf_op jit(solution)/shard_map/all_to_all | solution.py:551
  107.3 1.6 %inverse.1 = bf16[8,8,8,128]{3,2,1,0:T(8,128)(2,1)} custom-call(bf16[8,4,16,128]{3,2,1,0:T(8,128)(2,1)S(1)} %bitcast.44, bf16[256,256]{1,0:T(8,128)(2,1)S(1)} %pad_maximum_fusion.3.v_ref, bf16[512,256]{1,0:T(8,128)(2,1)S(1)} %copy-done.3, bf16[512,256]{1,0:T(8,128)(2,1)S(1)} %copy-done.2, bf16[256,256]{1,0:T(8,128)(2,1)S(1)} %copy-done.6), custom_call_target="tpu_custom_call" | custom-call | tf_op jit(solution)/shard_map/inverse/pallas_call | solution.py:405
  108.9 3.8 %all-to-all-start.3 = ((bf16[8,8,8,128]{3,2,1,0:T(8,128)(2,1)}), bf16[8,8,8,128]{3,2,1,0:T(8,128)(2,1)S(1)}, u32[]{:S(2)}, u32[]{:S(2)}) async-start(bf16[8,8,8,128]{3,2,1,0:T(8,128)(2,1)} %inverse.1), calls=%async_computation.3 | async-start | bytes 262144 | tf_op jit(solution)/shard_map/all_to_all | solution.py:564
  112.7 0.7 copy-done.18
  113.4 4.5 %all-to-all-done.3.y_ref = bf16[8,8,8,128]{3,2,1,0:T(8,128)(2,1)S(1)} async-done(((bf16[8,8,8,128]{3,2,1,0:T(8,128)(2,1)}), bf16[8,8,8,128]{3,2,1,0:T(8,128)(2,1)S(1)}, u32[]{:S(2)}, u32[]{:S(2)}) %all-to-all-start.3) | async-done | bytes 131104 | tf_op jit(solution)/shard_map/all_to_all | solution.py:564
  117.9 2.3 %output.1 = f32[128,8,64]{2,1,0:T(8,128)} custom-call(bf16[8,8,8,128]{3,2,1,0:T(8,128)(2,1)S(1)} %all-to-all-done.3.y_ref, bf16[8,8,1024]{2,1,0:T(8,128)(2,1)} %encoder.1.lat_ref, bf16[128,64]{1,0:T(8,128)(2,1)S(1)} %pad_maximum_fusion.5.w_ref), custom_call_target="tpu_custom_call" | custom-call | tf_op jit(solution)/shard_map/output/pallas_call | solution.py:405
  (70 shorter events, 0.7 us)
Async XLA Ops:
  0.0 6.6 %copy-start = (bf16[2,2,2,4,64,64]{5,4,3,2,1,0:T(8,128)(2,1)S(1)}, bf16[2,2,2,4,64,64]{5,4,3,2,1,0:T(8,128)(2,1)}, u32[]{:S(2)}) copy-start(bf16[2,2,2,4,64,64]{5,4,3,2,1,0:T(8,128)(2,1)} %param.31) | copy-start | bytes 786436
  0.8 5.7 %copy-start.17 = (bf16[80,80]{1,0:T(8,128)(2,1)S(1)}, bf16[80,80]{1,0:T(8,128)(2,1)}, u32[]{:S(2)}) copy-start(bf16[80,80]{1,0:T(8,128)(2,1)} %param.29) | copy-start | bytes 38404
  0.8 16.5 %collective-permute-start = (f32[4,8,128]{2,1,0:T(8,128)S(1)}, f32[4,8,128]{2,1,0:T(8,128)S(1)}, u32[]{:S(2)}, u32[]{:S(2)}) collective-permute-start(f32[4,8,128]{2,1,0:T(8,128)S(1)} %pad.8.own_ref), channel_id=1, source_target_pairs={{0,32},{32,64},{64,96},{96,128},{128,160},{160,192},{192,224},{1,3... | collective-permute-start | bytes 49160 | tf_op jit(solution)/shard_map/ppermute | solution.py:439
  5.1 12.1 %collective-permute-start.1 = (f32[4,8,128]{2,1,0:T(8,128)S(1)}, f32[4,8,128]{2,1,0:T(8,128)S(1)}, u32[]{:S(2)}, u32[]{:S(2)}) collective-permute-start(f32[4,8,128]{2,1,0:T(8,128)S(1)} %pad.8.own_ref), channel_id=1, source_target_pairs={{32,0},{64,32},{96,64},{128,96},{160,128},{192,160},{224,192},{33,... | collective-permute-start | bytes 49160 | tf_op jit(solution)/shard_map/ppermute | solution.py:441
  6.7 1.0 copy-start.11
  17.3 4.5 %copy-start.21 = (s32[256]{0:T(256)S(1)}, s32[256]{0:T(256)}, u32[]{:S(2)}) copy-start(s32[256]{0:T(256)} %constant.86.clone) | copy-start | bytes 3076
  17.3 4.5 %copy-start.22 = (s32[256]{0:T(256)S(1)}, s32[256]{0:T(256)}, u32[]{:S(2)}) copy-start(s32[256]{0:T(256)} %constant.89.clone) | copy-start | bytes 3076
  17.3 4.5 %copy-start.23 = (s32[256]{0:T(256)S(1)}, s32[256]{0:T(256)}, u32[]{:S(2)}) copy-start(s32[256]{0:T(256)} %constant.90.clone) | copy-start | bytes 3076
  17.3 4.5 %copy-start.20 = (s32[256]{0:T(256)S(1)}, s32[256]{0:T(256)}, u32[]{:S(2)}) copy-start(s32[256]{0:T(256)} %constant.85.clone) | copy-start | bytes 3076
  17.3 4.6 %copy-start.19 = (bf16[6,80]{1,0:T(8,128)(2,1)S(1)}, bf16[6,80]{1,0:T(8,128)(2,1)}, u32[]{:S(2)}) copy-start(bf16[6,80]{1,0:T(8,128)(2,1)} %param.28) | copy-start | bytes 2884
  17.3 10.3 %collective-permute-start.2 = (f32[12,8,128]{2,1,0:T(8,128)S(1)}, f32[12,8,128]{2,1,0:T(8,128)S(1)}, u32[]{:S(2)}, u32[]{:S(2)}) collective-permute-start(f32[12,8,128]{2,1,0:T(8,128)S(1)} %pad_maximum_fusion.4), channel_id=1, source_target_pairs={{0,8},{8,16},{16,24},{1,9},{9,17},{17,25},{2,10},{10,18},{18,26},{... | collective-permute-start | bytes 147464 | tf_op jit(solution)/shard_map/ppermute | solution.py:439
  20.5 7.2 %collective-permute-start.3 = (f32[12,8,128]{2,1,0:T(8,128)S(1)}, f32[12,8,128]{2,1,0:T(8,128)S(1)}, u32[]{:S(2)}, u32[]{:S(2)}) collective-permute-start(f32[12,8,128]{2,1,0:T(8,128)S(1)} %pad_maximum_fusion.4), channel_id=1, source_target_pairs={{8,0},{16,8},{24,16},{9,1},{17,9},{25,17},{10,2},{18,10},{26,18},{... | collective-permute-start | bytes 147464 | tf_op jit(solution)/shard_map/ppermute | solution.py:441
  27.6 6.4 %copy-start.14 = (f32[256,128]{1,0:T(8,128)S(1)}, f32[256,128]{1,0:T(8,128)}, u32[]{:S(2)}) copy-start(f32[256,128]{1,0:T(8,128)} %constant.87.clone) | copy-start | bytes 393220
  27.6 6.4 %copy-start.15 = (f32[256,128]{1,0:T(8,128)S(1)}, f32[256,128]{1,0:T(8,128)}, u32[]{:S(2)}) copy-start(f32[256,128]{1,0:T(8,128)} %constant.88.clone) | copy-start | bytes 393220
  27.7 6.5 %collective-permute-start.4 = (f32[36,8,128]{2,1,0:T(8,128)S(1)}, f32[36,8,128]{2,1,0:T(8,128)S(1)}, u32[]{:S(2)}, u32[]{:S(2)}) collective-permute-start(f32[36,8,128]{2,1,0:T(8,128)S(1)} %pad_maximum_fusion.2.own_ref), channel_id=1, source_target_pairs={{0,1},{1,2},{2,3},{3,4},{4,5},{5,6},{6,7},{8,9},{9,10},{10,11},{11... | collective-permute-start | bytes 442376 | tf_op jit(solution)/shard_map/ppermute | solution.py:439
  32.1 6.5 %collective-permute-start.5 = (f32[36,8,128]{2,1,0:T(8,128)S(1)}, f32[36,8,128]{2,1,0:T(8,128)S(1)}, u32[]{:S(2)}, u32[]{:S(2)}) collective-permute-start(f32[36,8,128]{2,1,0:T(8,128)S(1)} %pad_maximum_fusion.2.own_ref), channel_id=1, source_target_pairs={{1,0},{2,1},{3,2},{4,3},{5,4},{6,5},{7,6},{9,8},{10,9},{11,10},{12... | collective-permute-start | bytes 442376 | tf_op jit(solution)/shard_map/ppermute | solution.py:441
  34.1 4.4 %copy-start.8 = (bf16[80,64]{0,1:T(8,128)(2,1)S(1)}, bf16[80,64]{0,1:T(8,128)(2,1)}, u32[]{:S(2)}) copy-start(bf16[80,64]{0,1:T(8,128)(2,1)} %param.30) | copy-start | bytes 30724
  47.4 8.6 %copy-start.5 = (bf16[256,512]{1,0:T(8,128)(2,1)S(1)}, bf16[256,512]{1,0:T(8,128)(2,1)}, u32[]{:S(2)}) copy-start(bf16[256,512]{1,0:T(8,128)(2,1)} %constant.94.clone.alo_ref) | copy-start | bytes 786436
  47.4 8.6 %all-to-all-start = ((bf16[8,8,1024]{2,1,0:T(8,128)(2,1)}), bf16[8,8,1024]{2,1,0:T(8,128)(2,1)S(1)}, u32[]{:S(2)}, u32[]{:S(2)}) async-start(bf16[8,8,1024]{2,1,0:T(8,128)(2,1)} %encoder.1.lat_ref), calls=%async_computation | async-start | bytes 262144 | tf_op jit(solution)/shard_map/all_to_all | solution.py:534
  50.8 5.2 %copy-start.4 = (bf16[256,512]{1,0:T(8,128)(2,1)S(1)}, bf16[256,512]{1,0:T(8,128)(2,1)}, u32[]{:S(2)}) copy-start(bf16[256,512]{1,0:T(8,128)(2,1)} %constant.93.clone.ahi_ref) | copy-start | bytes 786436
  57.4 30.0 %all-to-all-start.1 = ((bf16[256,2,128]{2,1,0:T(2,128)(2,1)}), bf16[256,2,128]{2,1,0:T(2,128)(2,1)S(1)}, u32[]{:S(2)}, u32[]{:S(2)}) async-start(bf16[256,2,128]{2,1,0:T(2,128)(2,1)} %bitcast.13), calls=%async_computation.1 | async-start | bytes 262144 | tf_op jit(solution)/shard_map/all_to_all | solution.py:537
  74.8 12.5 %copy-start.1 = (bf16[128,1024]{1,0:T(8,128)(2,1)S(1)}, bf16[128,1024]{1,0:T(8,128)(2,1)}, u32[]{:S(2)}) copy-start(bf16[128,1024]{1,0:T(8,128)(2,1)} %constant.96.clone.sel_ref) | copy-start | bytes 786436
  74.8 12.5 %copy-start.7 = (f32[16,1024]{1,0:T(8,128)S(1)}, f32[16,1024]{1,0:T(8,128)}, u32[]{:S(2)}) copy-start(f32[16,1024]{1,0:T(8,128)} %constant.97.clone.place_ref) | copy-start | bytes 196612
  74.9 12.5 %copy-start.9 = (f32[16,256]{1,0:T(8,128)S(1)}, f32[16,256]{1,0:T(8,128)}, u32[]{:S(2)}) copy-start(f32[16,256]{1,0:T(8,128)} %constant.95.clone.own_ref) | copy-start | bytes 49156
  74.9 12.4 %copy-start.10 = (bf16[8,16]{1,0:T(8,128)(2,1)S(1)}, bf16[8,16]{1,0:T(8,128)(2,1)}, u32[]{:S(2)}) copy-start(bf16[8,16]{1,0:T(8,128)(2,1)} %constant.98.clone.half_ref) | copy-start | bytes 772
  88.5 5.7 %copy-start.12 = (f32[128,256]{1,0:T(8,128)S(1)}, f32[128,256]{1,0:T(8,128)}, u32[]{:S(2)}) copy-start(f32[128,256]{1,0:T(8,128)} %constant.91.clone) | copy-start | bytes 393220
  88.5 5.7 %copy-start.13 = (f32[128,256]{1,0:T(8,128)S(1)}, f32[128,256]{1,0:T(8,128)}, u32[]{:S(2)}) copy-start(f32[128,256]{1,0:T(8,128)} %constant.92.clone) | copy-start | bytes 393220
  88.5 18.7 %all-to-all-start.2 = ((bf16[256,2,128]{2,1,0:T(2,128)(2,1)}), bf16[256,2,128]{2,1,0:T(2,128)(2,1)S(1)}, u32[]{:S(2)}, u32[]{:S(2)}) async-start(bf16[256,2,128]{2,1,0:T(2,128)(2,1)} %bitcast.23), calls=%async_computation.2 | async-start | bytes 262144 | tf_op jit(solution)/shard_map/all_to_all | solution.py:551
  94.2 13.0 %copy-start.2 = (bf16[512,256]{1,0:T(8,128)(2,1)S(1)}, bf16[512,256]{1,0:T(8,128)(2,1)}, u32[]{:S(2)}) copy-start(bf16[512,256]{1,0:T(8,128)(2,1)} %constant.100.clone.bs_ref) | copy-start | bytes 786436
  94.2 13.0 %copy-start.3 = (bf16[512,256]{1,0:T(8,128)(2,1)S(1)}, bf16[512,256]{1,0:T(8,128)(2,1)}, u32[]{:S(2)}) copy-start(bf16[512,256]{1,0:T(8,128)(2,1)} %constant.99.clone.bc_ref) | copy-start | bytes 786436
  94.3 13.0 %copy-start.6 = (bf16[256,256]{1,0:T(8,128)(2,1)S(1)}, bf16[256,256]{1,0:T(8,128)(2,1)}, u32[]{:S(2)}) copy-start(bf16[256,256]{1,0:T(8,128)(2,1)} %constant.101.clone.partner_ref) | copy-start | bytes 393220
  108.9 9.0 %all-to-all-start.3 = ((bf16[8,8,8,128]{3,2,1,0:T(8,128)(2,1)}), bf16[8,8,8,128]{3,2,1,0:T(8,128)(2,1)S(1)}, u32[]{:S(2)}, u32[]{:S(2)}) async-start(bf16[8,8,8,128]{3,2,1,0:T(8,128)(2,1)} %inverse.1), calls=%async_computation.3 | async-start | bytes 262144 | tf_op jit(solution)/shard_map/all_to_all | solution.py:564
  (2 other events, 1.5 us)

commit v5 on v4

--- a/solution.py
+++ b/solution.py
@@ -15,9 +15,7 @@
 
 GRID = 64
 NB = 32
-NEAR_EARLY = True
 ROWS = 8 * NB + 32
-LAST = ROWS
 CELLS = float(GRID**3)
 NORM_FLOOR = 1.0
 GZ = ("gz_0", "gz_1")
@@ -126,7 +124,6 @@
 
 def sort_kernel(place_ref, nb_ref, cnt_ref, far_ref, near_ref, rank_ref, scnt_ref, tile_ref, lists):
     px, py, pz = place_ref[0], place_ref[1], place_ref[2]
-    me = (px * 4 + py) * 8 + pz
     counts = cnt_ref[...]
     nothing = jnp.full((8, 128), -1, i32)
     far = jnp.zeros((8, 128), i32)
@@ -138,10 +135,10 @@
         dz = (owner & 7) - pz + 1
         dy = ((owner >> 3) & 3) - py + 1
         dx = (owner >> 5) - px + 1
-        chunk = (((dz * 3 + dy) * 3 + dx) * 4 + ((j >> 7) & 3)) & 127
+        chunk = ((dz >> 1) * 36 + (dy * 3 + dx) * 4 + ((j >> 7) & 3)) & 127
         codes.append(chunk * 128 + (j & 127))
         valid = counts > s
-        mine = owner == me
+        mine = dz == 1
         is_far = valid & jnp.logical_not(mine)
         is_near = valid & mine
         far_at.append(jnp.where(is_far, far, nothing))
@@ -156,7 +153,7 @@
             second = jnp.where(near_at[s] == p, codes[s], second)
         lists[p] = (first >> 7).astype(f32)
         lists[NB + p] = (first & 127).astype(f32)
-        lists[2 * NB + p] = ((second >> 7) & 3).astype(f32)
+        lists[2 * NB + p] = (second >> 7).astype(f32)
         lists[3 * NB + p] = (second & 127).astype(f32)
     far, near = far.astype(f32), near.astype(f32)
     row8 = lax.broadcasted_iota(i32, (8, 128), 0)
@@ -178,32 +175,28 @@
     rows = jnp.concatenate([lists[:, z, :] for z in range(8)], axis=1)
     rows = jnp.concatenate([rows, tail], axis=0).astype(bf16)
     slot = lax.broadcasted_iota(i32, (NB, 128), 0)
-    ends = [0, 0]
+    words, most = [], []
     for t in range(4):
         found = dot_t(rows, rank_rows(rank, t * 256, 256))
         tail = found[4 * NB : 4 * NB + 8]
         scnt_ref[:, t * 256 : t * 256 + 256] = jnp.broadcast_to(tail[0:1] + tail[1:2], (8, 256))
+        cell = (tail[2:3] * 128.0 + tail[3:4]) * 16384.0
         for h in range(2):
-            part = found[:, h * 128 : h * 128 + 128]
-            cell = (tail[2:3] * 128.0 + tail[3:4])[:, h * 128 : h * 128 + 128] * 16384.0
-            for n, ref in enumerate((far_ref, near_ref)):
-                word = (part[2 * n * NB : (2 * n + 1) * NB] * 128.0 + part[(2 * n + 1) * NB : (2 * n + 2) * NB] + cell).astype(i32)
-                length = tail[n : n + 1, h * 128 : h * 128 + 128].astype(i32)
-                start = ends[n]
-                ref[pl.ds(start, NB), :] = jnp.where(slot < length, word, -1)
-                most = jnp.max(length)
-
-                def mark(r, carry):
-                    tile_ref[n, start + r] = 2 * t + h
-                    return carry
-
-                lax.fori_loop(0, most, mark, 0)
-                ends[n] = start + most
+            at = slice(h * 128, h * 128 + 128)
+            for n in range(2):
+                upper, lower = found[2 * n * NB : (2 * n + 1) * NB], found[(2 * n + 1) * NB : (2 * n + 2) * NB]
+                word = (upper[:, at] * 128.0 + lower[:, at] + cell[:, at]).astype(i32)
+                length = tail[n : n + 1, at].astype(i32)
+                words.append(jnp.where(slot < length, word, -1))
+                most.append(jnp.max(length))
     for n, ref in enumerate((far_ref, near_ref)):
-        ref[pl.ds(ends[n], 16), :] = jnp.full((16, 128), -1, i32)
-        for r in range(16):
-            tile_ref[n, ends[n] + r] = 0
-        tile_ref[n, LAST] = jnp.maximum((ends[n] + 15) >> 4, 1)
+        end = 0
+        for t in range(8):
+            ref[pl.ds(end, NB), :] = words[2 * t + n]
+            end = end + most[2 * t + n]
+            tile_ref[n, t] = end
+        ref[pl.ds(end, 16), :] = jnp.full((16, 128), -1, i32)
+        tile_ref[n, 8] = jnp.maximum((end + 15) >> 4, 1)
 
 
 def pair_sums(place_ref, tile_ref, at, code_ref, look_up, ki_ref, km_ref, turn, acc_ref):
@@ -212,7 +205,8 @@
     y0 = py.astype(f32) * 16.0 + 0.5
     z0 = pz.astype(f32) * 8.0 + 0.5
     turn[...] = jnp.zeros(turn.shape, f32)
-    steps = tile_ref[at, LAST]
+    steps = tile_ref[at, 8]
+    ends = [tile_ref[at, t] for t in range(7)]
 
     def gather(b):
         lines = []
@@ -233,35 +227,68 @@
             lines += [turn[half, :, n, :] for n in range(8)]
         return jnp.concatenate(lines, axis=1)
 
-    def step(b, pair):
-        following = gather(jnp.minimum(b + 1, steps - 1))
+    def add(b, pair):
         hidden = gelu_twice(dot(ki_ref[...], pair.astype(bf16))).astype(bf16)
         hidden = gelu_twice(dot(km_ref[...], hidden))
         for r in range(16):
-            acc_ref[tile_ref[at, b * 16 + r]] += hidden[:, r * 128 : r * 128 + 128]
+            tile = sum((b * 16 + r >= end).astype(i32) for end in ends)
+            acc_ref[tile] += hidden[:, r * 128 : r * 128 + 128]
+
+    def step(b, pair):
+        following = gather(b + 1)
+        add(b, pair)
         return following
 
-    lax.fori_loop(0, steps, step, gather(0))
+    add(steps - 1, lax.fori_loop(0, steps - 1, step, gather(0)))
 
 
 def lane_gather(line, at):
     return jnp.take_along_axis(jnp.broadcast_to(line, (8, 128)), at, axis=1, mode="promise_in_bounds")
 
 
-def near_kernel(place_ref, tile_ref, own_ref, code_ref, ki_ref, km_ref, acc_ref, turn):
-    acc_ref[...] = jnp.zeros(acc_ref.shape, f32)
+def packed(parts, words):
+    most = jnp.zeros((8, 128), f32)
+    for part in parts:
+        most = jnp.maximum(most, jnp.max(jnp.abs(part[...]), axis=0))
+    most = jnp.maximum(jnp.max(most, axis=1, keepdims=True), 1e-30)
+    scale = jnp.broadcast_to(32767.0 / most, (8, 128))
+    unit = jnp.broadcast_to(most * (1.0 / 32767.0), (8, 128))
+    for n in range(36 * len(parts)):
+        q = (parts[n // 36][n % 36] * scale + 32768.5).astype(i32)
+        words[n] = (q << 16) | pltpu.roll(q, 5, 0)
+    return [jnp.broadcast_to(unit[c : c + 1], (8, 128)) for c in range(6)]
+
+
+def looking_up(words, units, count):
+    levels = (count - 1).bit_length()
 
     def look_up(code):
         at = code & 127
-        low, high = (code & 128) != 0, (code & 256) != 0
-        values = []
-        for c in range(6):
-            found = [lane_gather(own_ref[n, c : c + 1, :], at) for n in range(4)]
-            values.append(
-                jnp.where(high, jnp.where(low, found[3], found[2]), jnp.where(low, found[1], found[0]))
-            )
+        bits = [(code & (128 << n)) != 0 for n in range(levels)]
+        values = [None] * 6
+        for c in range(3):
+
+            def pick(lo, level):
+                if lo >= count:
+                    return None
+                if level == 0:
+                    return lane_gather(words[lo, c : c + 1, :], at)
+                first = pick(lo, level - 1)
+                second = pick(lo + (1 << (level - 1)), level - 1)
+                return first if second is None else jnp.where(bits[level - 1], second, first)
+
+            word = pick(0, levels)
+            values[c] = (lax.shift_right_logical(word, 16) - 32768).astype(f32) * units[c]
+            values[c + 3] = ((word & 65535) - 32768).astype(f32) * units[c + 3]
         return values
 
+    return look_up
+
+
+def near_kernel(place_ref, tile_ref, same_ref, code_ref, ki_ref, km_ref, acc_ref, words, turn):
+    units = packed((same_ref,), words)
+    acc_ref[...] = jnp.zeros(acc_ref.shape, f32)
+    look_up = looking_up(words, units, 36)
     pair_sums(place_ref, tile_ref, 1, code_ref, look_up, ki_ref, km_ref, turn, acc_ref)
 
 
@@ -269,7 +296,6 @@
     place_ref,
     tile_ref,
     below_ref,
-    own_ref,
     above_ref,
     code_ref,
     rank_ref,
@@ -283,39 +309,9 @@
     turn,
     acc_ref,
 ):
-    parts = (below_ref, own_ref, above_ref)
-    most = jnp.zeros((8, 128), f32)
-    for part in parts:
-        most = jnp.maximum(most, jnp.max(jnp.abs(part[...]), axis=0))
-    most = jnp.maximum(jnp.max(most, axis=1, keepdims=True), 1e-30)
-    scale = jnp.broadcast_to(32767.0 / most, (8, 128))
-    unit = jnp.broadcast_to(most * (1.0 / 32767.0), (8, 128))
-    for n in range(108):
-        q = (parts[n // 36][n % 36] * scale + 32768.5).astype(i32)
-        words[n] = (q << 16) | pltpu.roll(q, 5, 0)
-    units = [jnp.broadcast_to(unit[c : c + 1], (8, 128)) for c in range(6)]
+    units = packed((below_ref, above_ref), words)
     acc_ref[...] = sum_ref[...]
-
-    def look_up(code):
-        at = code & 127
-        bits = [(code & (128 << n)) != 0 for n in range(7)]
-        values = [None] * 6
-        for c in range(3):
-
-            def pick(lo, level):
-                if lo >= 108:
-                    return None
-                if level == 0:
-                    return lane_gather(words[lo, c : c + 1, :], at)
-                first = pick(lo, level - 1)
-                second = pick(lo + (1 << (level - 1)), level - 1)
-                return first if second is None else jnp.where(bits[level - 1], second, first)
-
-            word = pick(0, 7)
-            values[c] = (lax.shift_right_logical(word, 16) - 32768).astype(f32) * units[c]
-            values[c + 3] = ((word & 65535) - 32768).astype(f32) * units[c + 3]
-        return values
-
+    look_up = looking_up(words, units, 72)
     pair_sums(place_ref, tile_ref, 0, code_ref, look_up, ki_ref, km_ref, turn, acc_ref)
     mean = jnp.concatenate([acc_ref[t] for t in range(8)], axis=1) * (0.5 / scnt_ref[0:1])
     upper = mean.astype(bf16)
@@ -401,7 +397,7 @@
         out_ref[:, z, :] = 0.5 * gelu_twice(v)
 
 
-def call(kernel, name, shape, dtype, *args, scratch=(), smem=0):
+def call(kernel, shape, dtype, *args, scratch=(), smem=0):
     return pl.pallas_call(
         kernel,
         out_shape=jax.ShapeDtypeStruct(shape, dtype),
@@ -409,7 +405,6 @@
         out_specs=VMEM,
         scratch_shapes=list(scratch),
         compiler_params=pltpu.CompilerParams(vmem_limit_bytes=48 * 1024 * 1024),
-        name=name,
     )(*args)
 
 
@@ -419,7 +414,7 @@
         ((ROWS, 128), i32),
         ((8, 1024), i32),
         ((8, 1024), f32),
-        ((2, LAST + 1), i32),
+        ((2, 9), i32),
     )
     return pl.pallas_call(
         sort_kernel,
@@ -435,11 +430,9 @@
 def beside(cells, axis):
     count = lax.axis_size(axis)
     ends = count - 1
-    return (
-        lax.ppermute(cells, axis, [(i, i + 1) for i in range(ends)]),
-        cells,
-        lax.ppermute(cells, axis, [(i + 1, i) for i in range(ends)]),
-    )
+    lower = lax.ppermute(cells, axis, [(i, i + 1) for i in range(ends)])
+    upper = lax.ppermute(cells, axis, [(i + 1, i) for i in range(ends)])
+    return lower, cells, upper
 
 
 def turned(cos, sin, phase):
@@ -447,7 +440,7 @@
     return cos * c - sin * s, sin * c + cos * s
 
 
-def body(point_data, neighbours, counts, kernel_in, kernel_mid, kernel_out, spectral, skip_weight):
+def layer(point_data, neighbours, counts, kernel_in, kernel_mid, kernel_out, spectral, skip_weight):
     gx = lax.axis_index("gx")
     gy = lax.axis_index("gy")
     gz = lax.axis_index(GZ)
@@ -460,36 +453,31 @@
     km = kernel_mid.T * jnp.bfloat16(0.5)
 
     line = jnp.concatenate(beside(own, "gx"), axis=0)
+    plane = jnp.concatenate(beside(line, "gy"), axis=0)
     tables = sorted_nodes(place, near, valid)
-    line, tables = lax.optimization_barrier((line, tables))
+    plane, tables = lax.optimization_barrier((plane, tables))
     far_code, near_code, rank, sorted_counts, tiles = tables
-    plane = jnp.concatenate(beside(line, "gy"), axis=0)
+    below, same, above = beside(plane, GZ)
     sums = call(
         near_kernel,
-        "near",
         (8, 80, 128),
         f32,
         place,
         tiles,
-        own,
+        same,
         near_code,
         ki,
         km,
-        scratch=(pltpu.VMEM((2, 8, 8, 128), f32),),
+        scratch=(pltpu.VMEM((36, 8, 128), i32), pltpu.VMEM((2, 8, 8, 128), f32)),
         smem=2,
     )
-    if NEAR_EARLY:
-        plane, sums = lax.optimization_barrier((plane, sums))
-    below, same, above = beside(plane, GZ)
     latent = call(
         encoder_kernel,
-        "encoder",
         (8, 8, 1024),
         bf16,
         place,
         tiles,
         below,
-        same,
         above,
         far_code,
         rank,
@@ -499,7 +487,7 @@
         km,
         kernel_out.T,
         scratch=(
-            pltpu.VMEM((108, 8, 128), i32),
+            pltpu.VMEM((72, 8, 128), i32),
             pltpu.VMEM((2, 8, 8, 128), f32),
             pltpu.VMEM((8, 80, 128), f32),
         ),
@@ -533,26 +521,16 @@
 
     depth = lax.all_to_all(latent, GZ, split_axis=0, concat_axis=0)
     ahi, alo = third_forward()
-    partial = call(forward_kernel, "forward", (512, 128), bf16, depth, ahi, alo, whi, wlo, scratch=(pltpu.VMEM((512, 128), f32),))
+    partial = call(forward_kernel, (512, 128), bf16, depth, ahi, alo, whi, wlo, scratch=(pltpu.VMEM((512, 128), f32),))
     partial = lax.all_to_all(partial.reshape(256, 2, 128), ALL, split_axis=0, concat_axis=0)
     own_mask, place_mask, half = mode_masks()
     mixed = call(
-        mix_kernel,
-        "mix",
-        (32, 16, 128),
-        bf16,
-        partial.reshape(32, 16, 128),
-        mixing,
-        own_mask,
-        placing(),
-        place_mask,
-        half,
+        mix_kernel, (32, 16, 128), bf16, partial.reshape(32, 16, 128), mixing, own_mask, placing(), place_mask, half
     )
     mixed = lax.all_to_all(mixed.reshape(256, 2, 128), ALL, split_axis=0, concat_axis=0)
     third = third_inverse()
     branch = call(
         inverse_kernel,
-        "inverse",
         (8, 8, 8, 128),
         bf16,
         mixed.reshape(8, 4, 16, 128),
@@ -562,7 +540,7 @@
         partner_table(),
     )
     branch = lax.all_to_all(branch, GZ, split_axis=0, concat_axis=0)
-    out = call(output_kernel, "output", (128, 8, 64), f32, branch, latent, joint)
+    out = call(output_kernel, (128, 8, 64), f32, branch, latent, joint)
     return out.reshape(1, 8, 16, 8, 64)
 
 
@@ -571,7 +549,7 @@
         mesh.devices.reshape(mesh.shape["gx"], mesh.shape["gy"], 4, 2), ("gx", "gy", "gz_0", "gz_1")
     )
     return jax.shard_map(
-        body,
+        layer,
         mesh=split,
         in_specs=(
             P(None, None, ALL),

time: 121 us -> 118 us (0.975)
  Pallas kernels: 29.4 us -> 23.8 us
  local copies, waits for them, and re-layouts: 3.81 us -> 5.12 us
    pallas_call x1, Pallas kernels: 8.61 us -> 3.35 us  [sorted_nodes(): pl.pallas_call(sort_kernel, out_shape=[jax.ShapeDtypeStruct(*s) for s in...]
    ppermute x6, starting transfers between devices: 16.4 us -> 18.5 us  [the longest x3 14 us: beside(): lower = lax.ppermute(cells, axis, [(i, i + 1) for i in range(ends)])]
    unnamed x50 -> x54, local copies, waits for them, and re-layouts: 2.48 us -> 3.78 us
  transfers between devices with their start and end apart: 10 -> 10, of which waited for: 5 -> 6; matrix products, arithmetic and copies ran while one was open for 1% -> 1% of each run, Pallas kernels for 12% -> 9%
where the time goes in v5:
time: 118 us; the launch traced here: 117 us
  starting transfers between devices  47.4 us (40%)
  waiting for transfers between devices  39.9 us (34%)
  Pallas kernels  23.8 us (20%)
  local copies, waits for them, and re-layouts  5.12 us (4%)
    pallas_call x6, Pallas kernels, call(): pl.pallas_call(kernel, out_shape=jax.ShapeDtypeStruct(shape, dtype), in_s...  20.4 us
    ppermute x3, starting transfers between devices, beside(): lower = lax.ppermute(cells, axis, [(i, i + 1) for i in range(ends)])  14 us
    all_to_all x1, waiting for transfers between devices, layer(): lax.all_to_all(mixed.reshape(256, 2, 128), ALL, split_axis=0, concat_axis=0)  12.9 us
    all_to_all x1, starting transfers between devices, layer(): lax.all_to_all(partial.reshape(256, 2, 128), ALL, split_axis=0, concat_ax...  12.7 us
    all_to_all x1, waiting for transfers between devices, layer(): lax.all_to_all(partial.reshape(256, 2, 128), ALL, split_axis=0, concat_ax...  12.4 us
    all_to_all x1, starting transfers between devices, layer(): depth = lax.all_to_all(latent, GZ, split_axis=0, concat_axis=0)  6.74 us
    all_to_all x1, starting transfers between devices, layer(): lax.all_to_all(mixed.reshape(256, 2, 128), ALL, split_axis=0, concat_axis=0)  5.64 us
    all_to_all x1, waiting for transfers between devices, layer(): depth = lax.all_to_all(latent, GZ, split_axis=0, concat_axis=0)  5.22 us
  transfers between devices with their start and end apart: 10, of which 6 were waited for; matrix products, arithmetic and copies ran while one was open for 1% of the time, Pallas kernels for 9%

profile of v5, /device:TPU:1, one launch (start us, length us, event | category | flops | bytes accessed | tf_op | source)
XLA Modules:
  0.0 117.4 jit_solution(5115501133089013477)
XLA Ops:
  0.0 0.8 copy.44
  0.8 4.3 %collective-permute-start = (f32[4,8,128]{2,1,0:T(8,128)S(1)}, f32[4,8,128]{2,1,0:T(8,128)S(1)}, u32[]{:S(2)}, u32[]{:S(2)}) collective-permute-start(f32[4,8,128]{2,1,0:T(8,128)S(1)} %pad.8), channel_id=1, source_target_pairs={{0,32},{32,64},{64,96},{96,128},{128,160},{160,192},{192,224},{1,3... | collective-permute-start | bytes 49160 | tf_op jit(solution)/shard_map/ppermute | solution.py:433
  5.1 1.3 %collective-permute-start.1 = (f32[4,8,128]{2,1,0:T(8,128)S(1)}, f32[4,8,128]{2,1,0:T(8,128)S(1)}, u32[]{:S(2)}, u32[]{:S(2)}) collective-permute-start(f32[4,8,128]{2,1,0:T(8,128)S(1)} %pad.8), channel_id=1, source_target_pairs={{32,0},{64,32},{96,64},{128,96},{160,128},{192,160},{224,192},{33,... | collective-permute-start | bytes 49160 | tf_op jit(solution)/shard_map/ppermute | solution.py:434
  6.5 0.6 copy-done.23
  7.5 0.8 copy-done.14
  8.4 0.1 multiply_subtract_fusion
  8.6 1.2 %collective-permute-done.1 = f32[4,8,128]{2,1,0:T(8,128)S(1)} collective-permute-done((f32[4,8,128]{2,1,0:T(8,128)S(1)}, f32[4,8,128]{2,1,0:T(8,128)S(1)}, u32[]{:S(2)}, u32[]{:S(2)}) %collective-permute-start.1) | collective-permute-done | bytes 16416 | tf_op jit(solution)/shard_map/ppermute | solution.py:434
  9.8 3.2 %collective-permute-start.2 = (f32[12,8,128]{2,1,0:T(8,128)S(1)}, f32[12,8,128]{2,1,0:T(8,128)S(1)}, u32[]{:S(2)}, u32[]{:S(2)}) collective-permute-start(f32[12,8,128]{2,1,0:T(8,128)S(1)} %pad_maximum_fusion.3), channel_id=1, source_target_pairs={{0,8},{8,16},{16,24},{1,9},{9,17},{17,25},{2,10},{10,18},{18,26},{... | collective-permute-start | bytes 147464 | tf_op jit(solution)/shard_map/ppermute | solution.py:433
  13.1 0.2 copy.35.nb_ref
  13.3 0.5 copy-done.16
  13.9 0.6 copy-done.17
  14.7 3.4 %sort.1 = (s32[288,128]{1,0:T(8,128)S(1)}, s32[288,128]{1,0:T(8,128)S(1)}, s32[8,1024]{1,0:T(8,128)S(1)}, f32[8,1024]{1,0:T(8,128)S(1)}, s32[2,9]{1,0:T(2,128)S(1)}) custom-call(s32[3]{0:T(128)S(1)} %pad_add_fusion.place_ref, s32[32,8,128]{2,1,0:T(8,128)S(1)} %copy.35.nb_ref, s32[8,128]{1,0:T(8,128)S(1)} %reshape.36.cnt_ref), custom_call_target="tpu_custom_call" | custom-call | tf_op jit(solution)/shard_map/sort/pallas_call | solution.py:419
  18.0 1.3 %collective-permute-start.3 = (f32[12,8,128]{2,1,0:T(8,128)S(1)}, f32[12,8,128]{2,1,0:T(8,128)S(1)}, u32[]{:S(2)}, u32[]{:S(2)}) collective-permute-start(f32[12,8,128]{2,1,0:T(8,128)S(1)} %pad_maximum_fusion.3), channel_id=1, source_target_pairs={{8,0},{16,8},{24,16},{9,1},{17,9},{25,17},{10,2},{18,10},{26,18},{... | collective-permute-start | bytes 147464 | tf_op jit(solution)/shard_map/ppermute | solution.py:434
  19.4 3.5 %collective-permute-done.3 = f32[12,8,128]{2,1,0:T(8,128)S(1)} collective-permute-done((f32[12,8,128]{2,1,0:T(8,128)S(1)}, f32[12,8,128]{2,1,0:T(8,128)S(1)}, u32[]{:S(2)}, u32[]{:S(2)}) %collective-permute-start.3) | collective-permute-done | bytes 49184 | tf_op jit(solution)/shard_map/ppermute | solution.py:434
  22.9 6.5 %collective-permute-start.4 = (f32[36,8,128]{2,1,0:T(8,128)S(1)}, f32[36,8,128]{2,1,0:T(8,128)S(1)}, u32[]{:S(2)}, u32[]{:S(2)}) collective-permute-start(f32[36,8,128]{2,1,0:T(8,128)S(1)} %constant_dynamic-update-slice_fusion.same_ref), channel_id=1, source_target_pairs={{0,1},{1,2},{2,3},{3,4},{4,5},{5,6},{6,7},{8,9},{9,10},{10,11},{11... | collective-permute-start | bytes 442376 | tf_op jit(solution)/shard_map/ppermute | solution.py:433
  29.4 1.9 %collective-permute-start.5 = (f32[36,8,128]{2,1,0:T(8,128)S(1)}, f32[36,8,128]{2,1,0:T(8,128)S(1)}, u32[]{:S(2)}, u32[]{:S(2)}) collective-permute-start(f32[36,8,128]{2,1,0:T(8,128)S(1)} %constant_dynamic-update-slice_fusion.same_ref), channel_id=1, source_target_pairs={{1,0},{2,1},{3,2},{4,3},{5,4},{6,5},{7,6},{9,8},{10,9},{11,10},{12... | collective-permute-start | bytes 442376 | tf_op jit(solution)/shard_map/ppermute | solution.py:434
  31.5 7.3 %shard_map.235.sum_ref = f32[8,80,128]{2,1,0:T(8,128)S(1)} custom-call(s32[3]{0:T(128)S(1)} %pad_add_fusion.place_ref, s32[2,9]{1,0:T(2,128)S(1)} %get-tuple-element.21.tile_ref, f32[36,8,128]{2,1,0:T(8,128)S(1)} %constant_dynamic-update-slice_fusion.same_ref, s32[288,128]{1,0:T(8,128)S(1)} %get-tuple-element.26.code_ref, bf16[80,8]{1,0:T(8,128)(2,1)S(1)} %pad.9.ki_ref, ...), custom_call_target="tpu_custom_call" | custom-call | tf_op jit(solution)/shard_map/pallas_call | solution.py:401
  38.9 6.7 %shard_map.236.lat_ref = bf16[8,8,1024]{2,1,0:T(8,128)(2,1)} custom-call(s32[3]{0:T(128)S(1)} %pad_add_fusion.place_ref, s32[2,9]{1,0:T(2,128)S(1)} %get-tuple-element.21.tile_ref, f32[36,8,128]{2,1,0:T(8,128)S(1)} %collective-permute-done.4.below_ref, f32[36,8,128]{2,1,0:T(8,128)S(1)} %collective-permute-done.5.above_ref, ...), custom_call_target="tpu_custom_call" | custom-call | tf_op jit(solution)/shard_map/pallas_call | solution.py:401
  45.5 6.7 %all-to-all-start = ((bf16[8,8,1024]{2,1,0:T(8,128)(2,1)}), bf16[8,8,1024]{2,1,0:T(8,128)(2,1)S(1)}, u32[]{:S(2)}, u32[]{:S(2)}) async-start(bf16[8,8,1024]{2,1,0:T(8,128)(2,1)} %shard_map.236.lat_ref), calls=%async_computation | async-start | bytes 262144 | tf_op jit(solution)/shard_map/all_to_all | solution.py:522
  52.3 5.2 %all-to-all-done.m_ref = bf16[8,8,1024]{2,1,0:T(8,128)(2,1)S(1)} async-done(((bf16[8,8,1024]{2,1,0:T(8,128)(2,1)}), bf16[8,8,1024]{2,1,0:T(8,128)(2,1)S(1)}, u32[]{:S(2)}, u32[]{:S(2)}) %all-to-all-start) | async-done | bytes 131104 | tf_op jit(solution)/shard_map/all_to_all | solution.py:522
  57.5 1.4 %shard_map.237 = bf16[512,128]{1,0:T(8,128)(2,1)} custom-call(bf16[8,8,1024]{2,1,0:T(8,128)(2,1)S(1)} %all-to-all-done.m_ref, bf16[256,512]{1,0:T(8,128)(2,1)S(1)} %copy-done.4, bf16[256,512]{1,0:T(8,128)(2,1)S(1)} %copy-done.5, bf16[256,256]{1,0:T(8,128)(2,1)S(1)} %fusion.whi_ref, bf16[256,256]{1,0:T(8,128)(2,1)S(1)} %subtract_convert_fusion.wlo_ref), custom_call_target="tpu_custom_call" | custom-call | tf_op jit(solution)/shard_map/pallas_call | solution.py:401
  58.9 12.7 %all-to-all-start.1 = ((bf16[256,2,128]{2,1,0:T(2,128)(2,1)}), bf16[256,2,128]{2,1,0:T(2,128)(2,1)S(1)}, u32[]{:S(2)}, u32[]{:S(2)}) async-start(bf16[256,2,128]{2,1,0:T(2,128)(2,1)} %bitcast.13), calls=%async_computation.1 | async-start | bytes 262144 | tf_op jit(solution)/shard_map/all_to_all | solution.py:525
  71.7 0.3 maximum_bitcast_fusion
  72.1 12.4 %all-to-all-done.1 = bf16[256,2,128]{2,1,0:T(2,128)(2,1)S(1)} async-done(((bf16[256,2,128]{2,1,0:T(2,128)(2,1)}), bf16[256,2,128]{2,1,0:T(2,128)(2,1)S(1)}, u32[]{:S(2)}, u32[]{:S(2)}) %all-to-all-start.1) | async-done | bytes 131104 | tf_op jit(solution)/shard_map/all_to_all | solution.py:525
  84.6 1.1 shard_map.238
  85.7 5.6 %all-to-all-start.2 = ((bf16[256,2,128]{2,1,0:T(2,128)(2,1)}), bf16[256,2,128]{2,1,0:T(2,128)(2,1)S(1)}, u32[]{:S(2)}, u32[]{:S(2)}) async-start(bf16[256,2,128]{2,1,0:T(2,128)(2,1)} %bitcast.23), calls=%async_computation.2 | async-start | bytes 262144 | tf_op jit(solution)/shard_map/all_to_all | solution.py:530
  91.5 12.9 %all-to-all-done.2 = bf16[256,2,128]{2,1,0:T(2,128)(2,1)S(1)} async-done(((bf16[256,2,128]{2,1,0:T(2,128)(2,1)}), bf16[256,2,128]{2,1,0:T(2,128)(2,1)S(1)}, u32[]{:S(2)}, u32[]{:S(2)}) %all-to-all-start.2) | async-done | bytes 131104 | tf_op jit(solution)/shard_map/all_to_all | solution.py:530
  104.4 1.6 %shard_map.239 = bf16[8,8,8,128]{3,2,1,0:T(8,128)(2,1)} custom-call(bf16[8,4,16,128]{3,2,1,0:T(8,128)(2,1)S(1)} %bitcast.44, bf16[256,256]{1,0:T(8,128)(2,1)S(1)} %pad_maximum_fusion.2.v_ref, bf16[512,256]{1,0:T(8,128)(2,1)S(1)} %copy-done.3, bf16[512,256]{1,0:T(8,128)(2,1)S(1)} %copy-done.2, bf16[256,256]{1,0:T(8,128)(2,1)S(1)} %copy-done.6), custom_call_target="tpu_custom_call" | custom-call | tf_op jit(solution)/shard_map/pallas_call | solution.py:401
  106.0 3.8 %all-to-all-start.3 = ((bf16[8,8,8,128]{3,2,1,0:T(8,128)(2,1)}), bf16[8,8,8,128]{3,2,1,0:T(8,128)(2,1)S(1)}, u32[]{:S(2)}, u32[]{:S(2)}) async-start(bf16[8,8,8,128]{3,2,1,0:T(8,128)(2,1)} %shard_map.239), calls=%async_computation.3 | async-start | bytes 262144 | tf_op jit(solution)/shard_map/all_to_all | solution.py:542
  109.8 0.7 copy-done.18
  110.5 4.5 %all-to-all-done.3.y_ref = bf16[8,8,8,128]{3,2,1,0:T(8,128)(2,1)S(1)} async-done(((bf16[8,8,8,128]{3,2,1,0:T(8,128)(2,1)}), bf16[8,8,8,128]{3,2,1,0:T(8,128)(2,1)S(1)}, u32[]{:S(2)}, u32[]{:S(2)}) %all-to-all-start.3) | async-done | bytes 131104 | tf_op jit(solution)/shard_map/all_to_all | solution.py:542
  115.1 2.3 %shard_map.240 = f32[128,8,64]{2,1,0:T(8,128)} custom-call(bf16[8,8,8,128]{3,2,1,0:T(8,128)(2,1)S(1)} %all-to-all-done.3.y_ref, bf16[8,8,1024]{2,1,0:T(8,128)(2,1)} %shard_map.236.lat_ref, bf16[128,64]{1,0:T(8,128)(2,1)S(1)} %pad_maximum_fusion.4.w_ref), custom_call_target="tpu_custom_call" | custom-call | tf_op jit(solution)/shard_map/pallas_call | solution.py:401
  (74 shorter events, 1.2 us)
Async XLA Ops:
  0.0 7.3 %copy-start = (bf16[2,2,2,4,64,64]{5,4,3,2,1,0:T(8,128)(2,1)S(1)}, bf16[2,2,2,4,64,64]{5,4,3,2,1,0:T(8,128)(2,1)}, u32[]{:S(2)}) copy-start(bf16[2,2,2,4,64,64]{5,4,3,2,1,0:T(8,128)(2,1)} %param.31) | copy-start | bytes 786436
  0.8 7.8 %collective-permute-start = (f32[4,8,128]{2,1,0:T(8,128)S(1)}, f32[4,8,128]{2,1,0:T(8,128)S(1)}, u32[]{:S(2)}, u32[]{:S(2)}) collective-permute-start(f32[4,8,128]{2,1,0:T(8,128)S(1)} %pad.8), channel_id=1, source_target_pairs={{0,32},{32,64},{64,96},{96,128},{128,160},{160,192},{192,224},{1,3... | collective-permute-start | bytes 49160 | tf_op jit(solution)/shard_map/ppermute | solution.py:433
  5.1 4.7 %collective-permute-start.1 = (f32[4,8,128]{2,1,0:T(8,128)S(1)}, f32[4,8,128]{2,1,0:T(8,128)S(1)}, u32[]{:S(2)}, u32[]{:S(2)}) collective-permute-start(f32[4,8,128]{2,1,0:T(8,128)S(1)} %pad.8), channel_id=1, source_target_pairs={{32,0},{64,32},{96,64},{128,96},{160,128},{192,160},{224,192},{33,... | collective-permute-start | bytes 49160 | tf_op jit(solution)/shard_map/ppermute | solution.py:434
  6.5 0.7 copy-start.22
  6.5 0.7 copy-start.20
  7.4 0.9 copy-start.14
  7.4 1.0 copy-start.15
  7.5 5.6 %copy-start.11 = (s32[1,8,16,8,32]{4,3,2,1,0:T(8,128)S(1)}, s32[1,8,16,8,32]{4,3,2,1,0:T(8,128)}, u32[]{:S(2)}) copy-start(s32[1,8,16,8,32]{4,3,2,1,0:T(8,128)} %param.26) | copy-start | bytes 393220
  9.8 9.5 %collective-permute-start.2 = (f32[12,8,128]{2,1,0:T(8,128)S(1)}, f32[12,8,128]{2,1,0:T(8,128)S(1)}, u32[]{:S(2)}, u32[]{:S(2)}) collective-permute-start(f32[12,8,128]{2,1,0:T(8,128)S(1)} %pad_maximum_fusion.3), channel_id=1, source_target_pairs={{0,8},{8,16},{16,24},{1,9},{9,17},{17,25},{2,10},{10,18},{18,26},{... | collective-permute-start | bytes 147464 | tf_op jit(solution)/shard_map/ppermute | solution.py:433
  13.1 0.8 copy-start.16
  13.9 0.7 copy-start.17
  18.0 4.8 %collective-permute-start.3 = (f32[12,8,128]{2,1,0:T(8,128)S(1)}, f32[12,8,128]{2,1,0:T(8,128)S(1)}, u32[]{:S(2)}, u32[]{:S(2)}) collective-permute-start(f32[12,8,128]{2,1,0:T(8,128)S(1)} %pad_maximum_fusion.3), channel_id=1, source_target_pairs={{8,0},{16,8},{24,16},{9,1},{17,9},{25,17},{10,2},{18,10},{26,18},{... | collective-permute-start | bytes 147464 | tf_op jit(solution)/shard_map/ppermute | solution.py:434
  22.9 8.4 %copy-start.19 = (bf16[6,80]{1,0:T(8,128)(2,1)S(1)}, bf16[6,80]{1,0:T(8,128)(2,1)}, u32[]{:S(2)}) copy-start(bf16[6,80]{1,0:T(8,128)(2,1)} %param.28) | copy-start | bytes 2884
  22.9 15.9 %collective-permute-start.4 = (f32[36,8,128]{2,1,0:T(8,128)S(1)}, f32[36,8,128]{2,1,0:T(8,128)S(1)}, u32[]{:S(2)}, u32[]{:S(2)}) collective-permute-start(f32[36,8,128]{2,1,0:T(8,128)S(1)} %constant_dynamic-update-slice_fusion.same_ref), channel_id=1, source_target_pairs={{0,1},{1,2},{2,3},{3,4},{4,5},{5,6},{6,7},{8,9},{9,10},{10,11},{11... | collective-permute-start | bytes 442376 | tf_op jit(solution)/shard_map/ppermute | solution.py:433
  29.4 9.5 %collective-permute-start.5 = (f32[36,8,128]{2,1,0:T(8,128)S(1)}, f32[36,8,128]{2,1,0:T(8,128)S(1)}, u32[]{:S(2)}, u32[]{:S(2)}) collective-permute-start(f32[36,8,128]{2,1,0:T(8,128)S(1)} %constant_dynamic-update-slice_fusion.same_ref), channel_id=1, source_target_pairs={{1,0},{2,1},{3,2},{4,3},{5,4},{6,5},{7,6},{9,8},{10,9},{11,10},{12... | collective-permute-start | bytes 442376 | tf_op jit(solution)/shard_map/ppermute | solution.py:434
  31.5 7.4 %copy-start.8 = (bf16[80,64]{0,1:T(8,128)(2,1)S(1)}, bf16[80,64]{0,1:T(8,128)(2,1)}, u32[]{:S(2)}) copy-start(bf16[80,64]{0,1:T(8,128)(2,1)} %param.30) | copy-start | bytes 30724
  45.5 12.0 %copy-start.5 = (bf16[256,512]{1,0:T(8,128)(2,1)S(1)}, bf16[256,512]{1,0:T(8,128)(2,1)}, u32[]{:S(2)}) copy-start(bf16[256,512]{1,0:T(8,128)(2,1)} %constant.94.clone.alo_ref) | copy-start | bytes 786436
  45.5 12.0 %all-to-all-start = ((bf16[8,8,1024]{2,1,0:T(8,128)(2,1)}), bf16[8,8,1024]{2,1,0:T(8,128)(2,1)S(1)}, u32[]{:S(2)}, u32[]{:S(2)}) async-start(bf16[8,8,1024]{2,1,0:T(8,128)(2,1)} %shard_map.236.lat_ref), calls=%async_computation | async-start | bytes 262144 | tf_op jit(solution)/shard_map/all_to_all | solution.py:522
  52.3 5.2 %copy-start.4 = (bf16[256,512]{1,0:T(8,128)(2,1)S(1)}, bf16[256,512]{1,0:T(8,128)(2,1)}, u32[]{:S(2)}) copy-start(bf16[256,512]{1,0:T(8,128)(2,1)} %constant.93.clone.ahi_ref) | copy-start | bytes 786436
  58.9 25.6 %all-to-all-start.1 = ((bf16[256,2,128]{2,1,0:T(2,128)(2,1)}), bf16[256,2,128]{2,1,0:T(2,128)(2,1)S(1)}, u32[]{:S(2)}, u32[]{:S(2)}) async-start(bf16[256,2,128]{2,1,0:T(2,128)(2,1)} %bitcast.13), calls=%async_computation.1 | async-start | bytes 262144 | tf_op jit(solution)/shard_map/all_to_all | solution.py:525
  72.0 12.5 %copy-start.1 = (bf16[128,1024]{1,0:T(8,128)(2,1)S(1)}, bf16[128,1024]{1,0:T(8,128)(2,1)}, u32[]{:S(2)}) copy-start(bf16[128,1024]{1,0:T(8,128)(2,1)} %constant.96.clone.sel_ref) | copy-start | bytes 786436
  72.0 12.5 %copy-start.7 = (f32[16,1024]{1,0:T(8,128)S(1)}, f32[16,1024]{1,0:T(8,128)}, u32[]{:S(2)}) copy-start(f32[16,1024]{1,0:T(8,128)} %constant.97.clone.place_ref) | copy-start | bytes 196612
  72.0 12.5 %copy-start.9 = (f32[16,256]{1,0:T(8,128)S(1)}, f32[16,256]{1,0:T(8,128)}, u32[]{:S(2)}) copy-start(f32[16,256]{1,0:T(8,128)} %constant.95.clone.own_ref) | copy-start | bytes 49156
  72.1 12.5 %copy-start.10 = (bf16[8,16]{1,0:T(8,128)(2,1)S(1)}, bf16[8,16]{1,0:T(8,128)(2,1)}, u32[]{:S(2)}) copy-start(bf16[8,16]{1,0:T(8,128)(2,1)} %constant.98.clone.half_ref) | copy-start | bytes 772
  85.7 5.7 %copy-start.12 = (f32[128,256]{1,0:T(8,128)S(1)}, f32[128,256]{1,0:T(8,128)}, u32[]{:S(2)}) copy-start(f32[128,256]{1,0:T(8,128)} %constant.91.clone) | copy-start | bytes 393220
  85.7 5.7 %copy-start.13 = (f32[128,256]{1,0:T(8,128)S(1)}, f32[128,256]{1,0:T(8,128)}, u32[]{:S(2)}) copy-start(f32[128,256]{1,0:T(8,128)} %constant.92.clone) | copy-start | bytes 393220
  85.7 18.7 %all-to-all-start.2 = ((bf16[256,2,128]{2,1,0:T(2,128)(2,1)}), bf16[256,2,128]{2,1,0:T(2,128)(2,1)S(1)}, u32[]{:S(2)}, u32[]{:S(2)}) async-start(bf16[256,2,128]{2,1,0:T(2,128)(2,1)} %bitcast.23), calls=%async_computation.2 | async-start | bytes 262144 | tf_op jit(solution)/shard_map/all_to_all | solution.py:530
  91.4 13.0 %copy-start.2 = (bf16[512,256]{1,0:T(8,128)(2,1)S(1)}, bf16[512,256]{1,0:T(8,128)(2,1)}, u32[]{:S(2)}) copy-start(bf16[512,256]{1,0:T(8,128)(2,1)} %constant.100.clone.bs_ref) | copy-start | bytes 786436
  91.4 13.0 %copy-start.3 = (bf16[512,256]{1,0:T(8,128)(2,1)S(1)}, bf16[512,256]{1,0:T(8,128)(2,1)}, u32[]{:S(2)}) copy-start(bf16[512,256]{1,0:T(8,128)(2,1)} %constant.99.clone.bc_ref) | copy-start | bytes 786436
  91.4 13.0 %copy-start.6 = (bf16[256,256]{1,0:T(8,128)(2,1)S(1)}, bf16[256,256]{1,0:T(8,128)(2,1)}, u32[]{:S(2)}) copy-start(bf16[256,256]{1,0:T(8,128)(2,1)} %constant.101.clone.partner_ref) | copy-start | bytes 393220
  106.0 9.0 %all-to-all-start.3 = ((bf16[8,8,8,128]{3,2,1,0:T(8,128)(2,1)}), bf16[8,8,8,128]{3,2,1,0:T(8,128)(2,1)S(1)}, u32[]{:S(2)}, u32[]{:S(2)}) async-start(bf16[8,8,8,128]{3,2,1,0:T(8,128)(2,1)} %shard_map.239), calls=%async_computation.3 | async-start | bytes 262144 | tf_op jit(solution)/shard_map/all_to_all | solution.py:542
  109.8 0.7 copy-start.18
  (2 other events, 1.4 us)

commit v6 on v5

--- a/solution.py
+++ b/solution.py
@@ -122,43 +122,20 @@
     return jnp.where(r == rank, 1.0, 0.0).astype(bf16)
 
 
-def sort_kernel(place_ref, nb_ref, cnt_ref, far_ref, near_ref, rank_ref, scnt_ref, tile_ref, lists):
+def sort_kernel(place_ref, nb_ref, cnt_ref, code_ref, rank_ref, scnt_ref, tile_ref):
     px, py, pz = place_ref[0], place_ref[1], place_ref[2]
-    counts = cnt_ref[...]
-    nothing = jnp.full((8, 128), -1, i32)
-    far = jnp.zeros((8, 128), i32)
-    near = jnp.zeros((8, 128), i32)
-    codes, far_at, near_at = [], [], []
-    for s in range(NB):
-        j = nb_ref[s]
-        owner = j >> 9
-        dz = (owner & 7) - pz + 1
-        dy = ((owner >> 3) & 3) - py + 1
-        dx = (owner >> 5) - px + 1
-        chunk = ((dz >> 1) * 36 + (dy * 3 + dx) * 4 + ((j >> 7) & 3)) & 127
-        codes.append(chunk * 128 + (j & 127))
-        valid = counts > s
-        mine = dz == 1
-        is_far = valid & jnp.logical_not(mine)
-        is_near = valid & mine
-        far_at.append(jnp.where(is_far, far, nothing))
-        near_at.append(jnp.where(is_near, near, nothing))
-        far = far + is_far.astype(i32)
-        near = near + is_near.astype(i32)
-    for p in range(NB):
-        first = jnp.zeros((8, 128), i32)
-        second = jnp.zeros((8, 128), i32)
-        for s in range(p, NB):
-            first = jnp.where(far_at[s] == p, codes[s], first)
-            second = jnp.where(near_at[s] == p, codes[s], second)
-        lists[p] = (first >> 7).astype(f32)
-        lists[NB + p] = (first & 127).astype(f32)
-        lists[2 * NB + p] = (second >> 7).astype(f32)
-        lists[3 * NB + p] = (second & 127).astype(f32)
-    far, near = far.astype(f32), near.astype(f32)
+    j = nb_ref[...]
+    owner = j >> 9
+    dz = (owner & 7) - pz + 1
+    dy = ((owner >> 3) & 3) - py + 1
+    dx = (owner >> 5) - px + 1
+    group = jnp.where(dz == 1, 72, (dz >> 1) * 36)
+    chunk = ((group + (dy * 3 + dx) * 4 + ((j >> 7) & 3)) & 127).astype(f32)
+    lane = (j & 127).astype(f32)
+    counts = cnt_ref[...].astype(f32)
     row8 = lax.broadcasted_iota(i32, (8, 128), 0)
     lane8 = lax.broadcasted_iota(i32, (8, 128), 1)
-    key = counts.astype(f32) * 1024.0 - (row8 * 128 + lane8).astype(f32)
+    key = counts * 1024.0 - (row8 * 128 + lane8).astype(f32)
     flat = [key[z : z + 1] for z in range(8)]
     ranks = [jnp.zeros((128, 128), f32) for _ in range(8)]
     for z in range(8):
@@ -168,45 +145,41 @@
     rank_ref[...] = jnp.broadcast_to(rank, (8, 1024))
     node = lax.broadcasted_iota(i32, (8, 1024), 1)
     wide = lax.broadcasted_iota(i32, (8, 1024), 0)
-    far = jnp.concatenate([far[z : z + 1] for z in range(8)], axis=1)
-    near = jnp.concatenate([near[z : z + 1] for z in range(8)], axis=1)
-    tail = jnp.where(wide == 2, (node >> 7).astype(f32), (node & 127).astype(f32))
-    tail = jnp.where(wide == 0, far, jnp.where(wide == 1, near, tail))
-    rows = jnp.concatenate([lists[:, z, :] for z in range(8)], axis=1)
-    rows = jnp.concatenate([rows, tail], axis=0).astype(bf16)
+    line = jnp.concatenate([counts[z : z + 1] for z in range(8)], axis=1)
+    tail = jnp.where(wide == 1, (node >> 7).astype(f32), (node & 127).astype(f32))
+    tail = jnp.where(wide == 0, line, tail)
+    rows = [jnp.concatenate([a[:, z, :] for z in range(8)], axis=1) for a in (chunk, lane)]
+    rows = jnp.concatenate(rows + [tail], axis=0).astype(bf16)
     slot = lax.broadcasted_iota(i32, (NB, 128), 0)
     words, most = [], []
     for t in range(4):
         found = dot_t(rows, rank_rows(rank, t * 256, 256))
-        tail = found[4 * NB : 4 * NB + 8]
-        scnt_ref[:, t * 256 : t * 256 + 256] = jnp.broadcast_to(tail[0:1] + tail[1:2], (8, 256))
-        cell = (tail[2:3] * 128.0 + tail[3:4]) * 16384.0
+        tail = found[2 * NB : 2 * NB + 8]
+        scnt_ref[:, t * 256 : t * 256 + 256] = jnp.broadcast_to(tail[0:1], (8, 256))
+        cell = (tail[1:2] * 128.0 + tail[2:3]) * 16384.0
+        word = (found[0:NB] * 128.0 + found[NB : 2 * NB] + cell).astype(i32)
+        length = tail[0:1].astype(i32)
         for h in range(2):
             at = slice(h * 128, h * 128 + 128)
-            for n in range(2):
-                upper, lower = found[2 * n * NB : (2 * n + 1) * NB], found[(2 * n + 1) * NB : (2 * n + 2) * NB]
-                word = (upper[:, at] * 128.0 + lower[:, at] + cell[:, at]).astype(i32)
-                length = tail[n : n + 1, at].astype(i32)
-                words.append(jnp.where(slot < length, word, -1))
-                most.append(jnp.max(length))
-    for n, ref in enumerate((far_ref, near_ref)):
-        end = 0
-        for t in range(8):
-            ref[pl.ds(end, NB), :] = words[2 * t + n]
-            end = end + most[2 * t + n]
-            tile_ref[n, t] = end
-        ref[pl.ds(end, 16), :] = jnp.full((16, 128), -1, i32)
-        tile_ref[n, 8] = jnp.maximum((end + 15) >> 4, 1)
-
-
-def pair_sums(place_ref, tile_ref, at, code_ref, look_up, ki_ref, km_ref, turn, acc_ref):
+            words.append(jnp.where(slot < length[:, at], word[:, at], -1))
+            most.append(jnp.max(length[:, at]))
+    end = 0
+    for t in range(8):
+        code_ref[pl.ds(end, NB), :] = words[t]
+        end = end + most[t]
+        tile_ref[t] = end
+    code_ref[pl.ds(end, 16), :] = jnp.full((16, 128), -1, i32)
+    tile_ref[8] = (end + 15) >> 4
+
+
+def pair_sums(place_ref, tile_ref, code_ref, look_up, ki_ref, km_ref, turn, acc_ref):
     px, py, pz = place_ref[0], place_ref[1], place_ref[2]
     x0 = px.astype(f32) * 8.0 + 0.5
     y0 = py.astype(f32) * 16.0 + 0.5
     z0 = pz.astype(f32) * 8.0 + 0.5
     turn[...] = jnp.zeros(turn.shape, f32)
-    steps = tile_ref[at, 8]
-    ends = [tile_ref[at, t] for t in range(7)]
+    steps = tile_ref[8]
+    ends = [tile_ref[t] for t in range(7)]
 
     def gather(b):
         lines = []
@@ -218,7 +191,7 @@
                 ((cell & 15).astype(f32) + y0) * (1.0 / GRID),
                 ((cell >> 7).astype(f32) + z0) * (1.0 / GRID),
             )
-            values = look_up(code)
+            values = look_up(code, b * 2 + half)
             for c in range(6):
                 value = values[c]
                 if c < 3:
@@ -256,40 +229,41 @@
     for n in range(36 * len(parts)):
         q = (parts[n // 36][n % 36] * scale + 32768.5).astype(i32)
         words[n] = (q << 16) | pltpu.roll(q, 5, 0)
+    return unit
+
+
+def rows_of(unit):
     return [jnp.broadcast_to(unit[c : c + 1], (8, 128)) for c in range(6)]
 
 
-def looking_up(words, units, count):
+def pick_word(words, c, code, count):
     levels = (count - 1).bit_length()
-
-    def look_up(code):
-        at = code & 127
-        bits = [(code & (128 << n)) != 0 for n in range(levels)]
-        values = [None] * 6
-        for c in range(3):
-
-            def pick(lo, level):
-                if lo >= count:
-                    return None
-                if level == 0:
-                    return lane_gather(words[lo, c : c + 1, :], at)
-                first = pick(lo, level - 1)
-                second = pick(lo + (1 << (level - 1)), level - 1)
-                return first if second is None else jnp.where(bits[level - 1], second, first)
-
-            word = pick(0, levels)
-            values[c] = (lax.shift_right_logical(word, 16) - 32768).astype(f32) * units[c]
-            values[c + 3] = ((word & 65535) - 32768).astype(f32) * units[c + 3]
-        return values
-
-    return look_up
-
-
-def near_kernel(place_ref, tile_ref, same_ref, code_ref, ki_ref, km_ref, acc_ref, words, turn):
-    units = packed((same_ref,), words)
-    acc_ref[...] = jnp.zeros(acc_ref.shape, f32)
-    look_up = looking_up(words, units, 36)
-    pair_sums(place_ref, tile_ref, 1, code_ref, look_up, ki_ref, km_ref, turn, acc_ref)
+    at = code & 127
+    bits = [(code & (128 << n)) != 0 for n in range(levels)]
+
+    def pick(lo, level):
+        if lo >= count:
+            return None
+        if level == 0:
+            return lane_gather(words[lo, c : c + 1, :], at)
+        first = pick(lo, level - 1)
+        second = pick(lo + (1 << (level - 1)), level - 1)
+        return first if second is None else jnp.where(bits[level - 1], second, first)
+
+    return pick(0, levels)
+
+
+def near_kernel(tile_ref, same_ref, code_ref, out_ref, unit_ref, words):
+    unit_ref[...] = packed((same_ref,), words)
+
+    def step(b, carry):
+        for half in range(2):
+            code = code_ref[pl.ds(pl.multiple_of(b * 16 + half * 8, 8), 8), :] - 72 * 128
+            for c in range(3):
+                out_ref[b * 2 + half, c] = pick_word(words, c, code, 36)
+        return carry
+
+    lax.fori_loop(0, tile_ref[8], step, 0)
 
 
 def encoder_kernel(
@@ -298,9 +272,10 @@
     below_ref,
     above_ref,
     code_ref,
+    near_ref,
+    unit_ref,
     rank_ref,
     scnt_ref,
-    sum_ref,
     ki_ref,
     km_ref,
     ko_ref,
@@ -309,10 +284,22 @@
     turn,
     acc_ref,
 ):
-    units = packed((below_ref, above_ref), words)
-    acc_ref[...] = sum_ref[...]
-    look_up = looking_up(words, units, 72)
-    pair_sums(place_ref, tile_ref, 0, code_ref, look_up, ki_ref, km_ref, turn, acc_ref)
+    far_units = rows_of(packed((below_ref, above_ref), words))
+    near_units = rows_of(unit_ref[...])
+    acc_ref[...] = jnp.zeros(acc_ref.shape, f32)
+
+    def look_up(code, block):
+        near = (code & 16383) >= 72 * 128
+        values = [None] * 6
+        for c in range(3):
+            word = jnp.where(near, near_ref[block, c], pick_word(words, c, code, 72))
+            upper = jnp.where(near, near_units[c], far_units[c])
+            lower = jnp.where(near, near_units[c + 3], far_units[c + 3])
+            values[c] = (lax.shift_right_logical(word, 16) - 32768).astype(f32) * upper
+            values[c + 3] = ((word & 65535) - 32768).astype(f32) * lower
+        return values
+
+    pair_sums(place_ref, tile_ref, code_ref, look_up, ki_ref, km_ref, turn, acc_ref)
     mean = jnp.concatenate([acc_ref[t] for t in range(8)], axis=1) * (0.5 / scnt_ref[0:1])
     upper = mean.astype(bf16)
     lower = (mean - upper.astype(f32)).astype(bf16)
@@ -411,20 +398,31 @@
 def sorted_nodes(place, near, valid):
     shapes = (
         ((ROWS, 128), i32),
-        ((ROWS, 128), i32),
         ((8, 1024), i32),
         ((8, 1024), f32),
-        ((2, 9), i32),
+        ((9,), i32),
     )
     return pl.pallas_call(
         sort_kernel,
         out_shape=[jax.ShapeDtypeStruct(*s) for s in shapes],
         in_specs=[SMEM, VMEM, VMEM],
-        out_specs=[VMEM] * 4 + [SMEM],
-        scratch_shapes=[pltpu.VMEM((4 * NB, 8, 128), f32)],
+        out_specs=[VMEM] * 3 + [SMEM],
         compiler_params=pltpu.CompilerParams(vmem_limit_bytes=48 * 1024 * 1024),
         name="sort",
     )(place, near, valid)
+
+
+def near_words(tiles, same, code):
+    shapes = (((ROWS // 8, 3, 8, 128), i32), ((8, 128), f32))
+    return pl.pallas_call(
+        near_kernel,
+        out_shape=[jax.ShapeDtypeStruct(*s) for s in shapes],
+        in_specs=[SMEM, VMEM, VMEM],
+        out_specs=[VMEM] * 2,
+        scratch_shapes=[pltpu.VMEM((36, 8, 128), i32)],
+        compiler_params=pltpu.CompilerParams(vmem_limit_bytes=48 * 1024 * 1024),
+        name="near",
+    )(tiles, same, code)
 
 
 def beside(cells, axis):
@@ -456,21 +454,9 @@
     plane = jnp.concatenate(beside(line, "gy"), axis=0)
     tables = sorted_nodes(place, near, valid)
     plane, tables = lax.optimization_barrier((plane, tables))
-    far_code, near_code, rank, sorted_counts, tiles = tables
+    code, rank, sorted_counts, tiles = tables
     below, same, above = beside(plane, GZ)
-    sums = call(
-        near_kernel,
-        (8, 80, 128),
-        f32,
-        place,
-        tiles,
-        same,
-        near_code,
-        ki,
-        km,
-        scratch=(pltpu.VMEM((36, 8, 128), i32), pltpu.VMEM((2, 8, 8, 128), f32)),
-        smem=2,
-    )
+    words, units = near_words(tiles, same, code)
     latent = call(
         encoder_kernel,
         (8, 8, 1024),
@@ -479,10 +465,11 @@
         tiles,
         below,
         above,
-        far_code,
+        code,
+        words,
+        units,
         rank,
         sorted_counts,
-        sums,
         ki,
         km,
         kernel_out.T,
@@ -525,7 +512,15 @@
     partial = lax.all_to_all(partial.reshape(256, 2, 128), ALL, split_axis=0, concat_axis=0)
     own_mask, place_mask, half = mode_masks()
     mixed = call(
-        mix_kernel, (32, 16, 128), bf16, partial.reshape(32, 16, 128), mixing, own_mask, placing(), place_mask, half
+        mix_kernel,
+        (32, 16, 128),
+        bf16,
+        partial.reshape(32, 16, 128),
+        mixing,
+        own_mask,
+        placing(),
+        place_mask,
+        half,
     )
     mixed = lax.all_to_all(mixed.reshape(256, 2, 128), ALL, split_axis=0, concat_axis=0)
     third = third_inverse()

time: 118 us -> 116 us (0.983)
  starting transfers between devices: 47.4 us -> 45.1 us
    pallas_call x0 -> x1, Pallas kernels: none -> 3.71 us  [near_words(): pl.pallas_call(near_kernel, out_shape=[jax.ShapeDtypeStruct(*s) for s in...]
    pallas_call x6 -> x5, Pallas kernels: 20.4 us -> 17.1 us  [call(): pl.pallas_call(kernel, out_shape=jax.ShapeDtypeStruct(shape, dtype), in_s...]
    all_to_all x1, starting transfers between devices: 6.74 us -> 4.47 us  [layer(): depth = lax.all_to_all(latent, GZ, split_axis=0, concat_axis=0)]
  transfers between devices with their start and end apart: 10 -> 10, of which waited for: 6 -> 7; matrix products, arithmetic and copies ran while one was open for 1% -> 1% of each run, Pallas kernels for 9% -> 6%
where the time goes in v6:
time: 116 us
  starting transfers between devices  45.1 us (39%)
  waiting for transfers between devices  40.5 us (35%)
  Pallas kernels  23.6 us (20%)
  local copies, waits for them, and re-layouts  5.12 us (4%)
    pallas_call x5, Pallas kernels, call(): pl.pallas_call(kernel, out_shape=jax.ShapeDtypeStruct(shape, dtype), in_s...  17.1 us
    ppermute x3, starting transfers between devices, beside(): lower = lax.ppermute(cells, axis, [(i, i + 1) for i in range(ends)])  14 us
    all_to_all x1, waiting for transfers between devices, layer(): lax.all_to_all(mixed.reshape(256, 2, 128), ALL, split_axis=0, concat_axis=0)  12.9 us
    all_to_all x1, starting transfers between devices, layer(): lax.all_to_all(partial.reshape(256, 2, 128), ALL, split_axis=0, concat_ax...  12.7 us
    all_to_all x1, waiting for transfers between devices, layer(): lax.all_to_all(partial.reshape(256, 2, 128), ALL, split_axis=0, concat_ax...  12.4 us
    all_to_all x1, starting transfers between devices, layer(): lax.all_to_all(mixed.reshape(256, 2, 128), ALL, split_axis=0, concat_axis=0)  5.64 us
    ppermute x3, waiting for transfers between devices, beside(): upper = lax.ppermute(cells, axis, [(i + 1, i) for i in range(ends)])  5.34 us
    all_to_all x1, waiting for transfers between devices, layer(): depth = lax.all_to_all(latent, GZ, split_axis=0, concat_axis=0)  5.22 us
  transfers between devices with their start and end apart: 10, of which 7 were waited for; matrix products, arithmetic and copies ran while one was open for 1% of the time, Pallas kernels for 6%

profile of v6, /device:TPU:1, one launch (start us, length us, event | category | flops | bytes accessed | tf_op | source)
XLA Modules:
  0.0 115.5 jit_solution(2550967857442032152)
XLA Ops:
  0.0 0.8 copy.44
  0.8 4.3 %collective-permute-start = (f32[4,8,128]{2,1,0:T(8,128)S(1)}, f32[4,8,128]{2,1,0:T(8,128)S(1)}, u32[]{:S(2)}, u32[]{:S(2)}) collective-permute-start(f32[4,8,128]{2,1,0:T(8,128)S(1)} %pad.8), channel_id=1, source_target_pairs={{0,32},{32,64},{64,96},{96,128},{128,160},{160,192},{192,224},{1,3... | collective-permute-start | bytes 49160 | tf_op jit(solution)/shard_map/ppermute | solution.py:431
  5.1 1.3 %collective-permute-start.1 = (f32[4,8,128]{2,1,0:T(8,128)S(1)}, f32[4,8,128]{2,1,0:T(8,128)S(1)}, u32[]{:S(2)}, u32[]{:S(2)}) collective-permute-start(f32[4,8,128]{2,1,0:T(8,128)S(1)} %pad.8), channel_id=1, source_target_pairs={{32,0},{64,32},{96,64},{128,96},{160,128},{192,160},{224,192},{33,... | collective-permute-start | bytes 49160 | tf_op jit(solution)/shard_map/ppermute | solution.py:432
  6.5 0.6 copy-done.23
  7.5 0.8 copy-done.14
  8.6 1.2 %collective-permute-done.1 = f32[4,8,128]{2,1,0:T(8,128)S(1)} collective-permute-done((f32[4,8,128]{2,1,0:T(8,128)S(1)}, f32[4,8,128]{2,1,0:T(8,128)S(1)}, u32[]{:S(2)}, u32[]{:S(2)}) %collective-permute-start.1) | collective-permute-done | bytes 16416 | tf_op jit(solution)/shard_map/ppermute | solution.py:432
  9.8 3.2 %collective-permute-start.2 = (f32[12,8,128]{2,1,0:T(8,128)S(1)}, f32[12,8,128]{2,1,0:T(8,128)S(1)}, u32[]{:S(2)}, u32[]{:S(2)}) collective-permute-start(f32[12,8,128]{2,1,0:T(8,128)S(1)} %pad_maximum_fusion.3), channel_id=1, source_target_pairs={{0,8},{8,16},{16,24},{1,9},{9,17},{17,25},{2,10},{10,18},{18,26},{... | collective-permute-start | bytes 147464 | tf_op jit(solution)/shard_map/ppermute | solution.py:431
  13.1 0.2 copy.35.nb_ref
  13.3 0.5 copy-done.16
  13.9 0.6 copy-done.17
  14.7 2.7 %sort.1 = (s32[288,128]{1,0:T(8,128)S(1)}, s32[8,1024]{1,0:T(8,128)S(1)}, f32[8,1024]{1,0:T(8,128)S(1)}, s32[9]{0:T(128)S(1)}) custom-call(s32[3]{0:T(128)S(1)} %pad_add_fusion.place_ref, s32[32,8,128]{2,1,0:T(8,128)S(1)} %copy.35.nb_ref, s32[8,128]{1,0:T(8,128)S(1)} %reshape.36.cnt_ref), custom_call_target="tpu_custom_call" | custom-call | tf_op jit(solution)/shard_map/sort/pallas_call | solution.py:405
  17.4 1.3 %collective-permute-start.3 = (f32[12,8,128]{2,1,0:T(8,128)S(1)}, f32[12,8,128]{2,1,0:T(8,128)S(1)}, u32[]{:S(2)}, u32[]{:S(2)}) collective-permute-start(f32[12,8,128]{2,1,0:T(8,128)S(1)} %pad_maximum_fusion.3), channel_id=1, source_target_pairs={{8,0},{16,8},{24,16},{9,1},{17,9},{25,17},{10,2},{18,10},{26,18},{... | collective-permute-start | bytes 147464 | tf_op jit(solution)/shard_map/ppermute | solution.py:432
  18.8 3.5 %collective-permute-done.3 = f32[12,8,128]{2,1,0:T(8,128)S(1)} collective-permute-done((f32[12,8,128]{2,1,0:T(8,128)S(1)}, f32[12,8,128]{2,1,0:T(8,128)S(1)}, u32[]{:S(2)}, u32[]{:S(2)}) %collective-permute-start.3) | collective-permute-done | bytes 49184 | tf_op jit(solution)/shard_map/ppermute | solution.py:432
  22.3 6.5 %collective-permute-start.4 = (f32[36,8,128]{2,1,0:T(8,128)S(1)}, f32[36,8,128]{2,1,0:T(8,128)S(1)}, u32[]{:S(2)}, u32[]{:S(2)}) collective-permute-start(f32[36,8,128]{2,1,0:T(8,128)S(1)} %constant_dynamic-update-slice_fusion.same_ref), channel_id=1, source_target_pairs={{0,1},{1,2},{2,3},{3,4},{4,5},{5,6},{6,7},{8,9},{9,10},{10,11},{11... | collective-permute-start | bytes 442376 | tf_op jit(solution)/shard_map/ppermute | solution.py:431
  28.8 1.9 %collective-permute-start.5 = (f32[36,8,128]{2,1,0:T(8,128)S(1)}, f32[36,8,128]{2,1,0:T(8,128)S(1)}, u32[]{:S(2)}, u32[]{:S(2)}) collective-permute-start(f32[36,8,128]{2,1,0:T(8,128)S(1)} %constant_dynamic-update-slice_fusion.same_ref), channel_id=1, source_target_pairs={{1,0},{2,1},{3,2},{4,3},{5,4},{6,5},{7,6},{9,8},{10,9},{11,10},{12... | collective-permute-start | bytes 442376 | tf_op jit(solution)/shard_map/ppermute | solution.py:432
  30.9 3.7 %near.1 = (s32[36,3,8,128]{3,2,1,0:T(8,128)S(1)}, f32[8,128]{1,0:T(8,128)S(1)}) custom-call(s32[9]{0:T(128)S(1)} %get-tuple-element.20.tile_ref, f32[36,8,128]{2,1,0:T(8,128)S(1)} %constant_dynamic-update-slice_fusion.same_ref, s32[288,128]{1,0:T(8,128)S(1)} %get-tuple-element.22.code_ref), custom_call_target="tpu_custom_call" | custom-call | tf_op jit(solution)/shard_map/near/pallas_call | solution.py:417
  34.6 0.6 collective-permute-done.5.above_ref
  35.2 10.7 %shard_map.235.lat_ref = bf16[8,8,1024]{2,1,0:T(8,128)(2,1)} custom-call(s32[3]{0:T(128)S(1)} %pad_add_fusion.place_ref, s32[9]{0:T(128)S(1)} %get-tuple-element.20.tile_ref, f32[36,8,128]{2,1,0:T(8,128)S(1)} %collective-permute-done.4.below_ref, f32[36,8,128]{2,1,0:T(8,128)S(1)} %collective-permute-done.5.above_ref, ...), custom_call_target="tpu_custom_call" | custom-call | tf_op jit(solution)/shard_map/pallas_call | solution.py:388
  45.9 4.5 %all-to-all-start = ((bf16[8,8,1024]{2,1,0:T(8,128)(2,1)}), bf16[8,8,1024]{2,1,0:T(8,128)(2,1)S(1)}, u32[]{:S(2)}, u32[]{:S(2)}) async-start(bf16[8,8,1024]{2,1,0:T(8,128)(2,1)} %shard_map.235.lat_ref), calls=%async_computation | async-start | bytes 262144 | tf_op jit(solution)/shard_map/all_to_all | solution.py:509
  50.4 5.2 %all-to-all-done.m_ref = bf16[8,8,1024]{2,1,0:T(8,128)(2,1)S(1)} async-done(((bf16[8,8,1024]{2,1,0:T(8,128)(2,1)}), bf16[8,8,1024]{2,1,0:T(8,128)(2,1)S(1)}, u32[]{:S(2)}, u32[]{:S(2)}) %all-to-all-start) | async-done | bytes 131104 | tf_op jit(solution)/shard_map/all_to_all | solution.py:509
  55.6 1.4 %shard_map.236 = bf16[512,128]{1,0:T(8,128)(2,1)} custom-call(bf16[8,8,1024]{2,1,0:T(8,128)(2,1)S(1)} %all-to-all-done.m_ref, bf16[256,512]{1,0:T(8,128)(2,1)S(1)} %copy-done.4, bf16[256,512]{1,0:T(8,128)(2,1)S(1)} %copy-done.5, bf16[256,256]{1,0:T(8,128)(2,1)S(1)} %fusion.whi_ref, bf16[256,256]{1,0:T(8,128)(2,1)S(1)} %subtract_convert_fusion.wlo_ref), custom_call_target="tpu_custom_call" | custom-call | tf_op jit(solution)/shard_map/pallas_call | solution.py:388
  57.0 12.7 %all-to-all-start.1 = ((bf16[256,2,128]{2,1,0:T(2,128)(2,1)}), bf16[256,2,128]{2,1,0:T(2,128)(2,1)S(1)}, u32[]{:S(2)}, u32[]{:S(2)}) async-start(bf16[256,2,128]{2,1,0:T(2,128)(2,1)} %bitcast.13), calls=%async_computation.1 | async-start | bytes 262144 | tf_op jit(solution)/shard_map/all_to_all | solution.py:512
  69.8 0.3 maximum_bitcast_fusion
  70.2 12.4 %all-to-all-done.1 = bf16[256,2,128]{2,1,0:T(2,128)(2,1)S(1)} async-done(((bf16[256,2,128]{2,1,0:T(2,128)(2,1)}), bf16[256,2,128]{2,1,0:T(2,128)(2,1)S(1)}, u32[]{:S(2)}, u32[]{:S(2)}) %all-to-all-start.1) | async-done | bytes 131104 | tf_op jit(solution)/shard_map/all_to_all | solution.py:512
  82.7 1.1 shard_map.237
  83.8 5.6 %all-to-all-start.2 = ((bf16[256,2,128]{2,1,0:T(2,128)(2,1)}), bf16[256,2,128]{2,1,0:T(2,128)(2,1)S(1)}, u32[]{:S(2)}, u32[]{:S(2)}) async-start(bf16[256,2,128]{2,1,0:T(2,128)(2,1)} %bitcast.23), calls=%async_computation.2 | async-start | bytes 262144 | tf_op jit(solution)/shard_map/all_to_all | solution.py:525
  89.6 12.9 %all-to-all-done.2 = bf16[256,2,128]{2,1,0:T(2,128)(2,1)S(1)} async-done(((bf16[256,2,128]{2,1,0:T(2,128)(2,1)}), bf16[256,2,128]{2,1,0:T(2,128)(2,1)S(1)}, u32[]{:S(2)}, u32[]{:S(2)}) %all-to-all-start.2) | async-done | bytes 131104 | tf_op jit(solution)/shard_map/all_to_all | solution.py:525
  102.6 1.6 %shard_map.238 = bf16[8,8,8,128]{3,2,1,0:T(8,128)(2,1)} custom-call(bf16[8,4,16,128]{3,2,1,0:T(8,128)(2,1)S(1)} %bitcast.44, bf16[256,256]{1,0:T(8,128)(2,1)S(1)} %pad_maximum_fusion.2.v_ref, bf16[512,256]{1,0:T(8,128)(2,1)S(1)} %copy-done.3, bf16[512,256]{1,0:T(8,128)(2,1)S(1)} %copy-done.2, bf16[256,256]{1,0:T(8,128)(2,1)S(1)} %copy-done.6), custom_call_target="tpu_custom_call" | custom-call | tf_op jit(solution)/shard_map/pallas_call | solution.py:388
  104.2 3.8 %all-to-all-start.3 = ((bf16[8,8,8,128]{3,2,1,0:T(8,128)(2,1)}), bf16[8,8,8,128]{3,2,1,0:T(8,128)(2,1)S(1)}, u32[]{:S(2)}, u32[]{:S(2)}) async-start(bf16[8,8,8,128]{3,2,1,0:T(8,128)(2,1)} %shard_map.238), calls=%async_computation.3 | async-start | bytes 262144 | tf_op jit(solution)/shard_map/all_to_all | solution.py:537
  108.0 0.7 copy-done.18
  108.7 4.5 %all-to-all-done.3.y_ref = bf16[8,8,8,128]{3,2,1,0:T(8,128)(2,1)S(1)} async-done(((bf16[8,8,8,128]{3,2,1,0:T(8,128)(2,1)}), bf16[8,8,8,128]{3,2,1,0:T(8,128)(2,1)S(1)}, u32[]{:S(2)}, u32[]{:S(2)}) %all-to-all-start.3) | async-done | bytes 131104 | tf_op jit(solution)/shard_map/all_to_all | solution.py:537
  113.2 2.3 %shard_map.239 = f32[128,8,64]{2,1,0:T(8,128)} custom-call(bf16[8,8,8,128]{3,2,1,0:T(8,128)(2,1)S(1)} %all-to-all-done.3.y_ref, bf16[8,8,1024]{2,1,0:T(8,128)(2,1)} %shard_map.235.lat_ref, bf16[128,64]{1,0:T(8,128)(2,1)S(1)} %pad_maximum_fusion.4.w_ref), custom_call_target="tpu_custom_call" | custom-call | tf_op jit(solution)/shard_map/pallas_call | solution.py:388
  (74 shorter events, 1.3 us)
Async XLA Ops:
  0.0 7.3 %copy-start = (bf16[2,2,2,4,64,64]{5,4,3,2,1,0:T(8,128)(2,1)S(1)}, bf16[2,2,2,4,64,64]{5,4,3,2,1,0:T(8,128)(2,1)}, u32[]{:S(2)}) copy-start(bf16[2,2,2,4,64,64]{5,4,3,2,1,0:T(8,128)(2,1)} %param.31) | copy-start | bytes 786436
  0.8 7.8 %collective-permute-start = (f32[4,8,128]{2,1,0:T(8,128)S(1)}, f32[4,8,128]{2,1,0:T(8,128)S(1)}, u32[]{:S(2)}, u32[]{:S(2)}) collective-permute-start(f32[4,8,128]{2,1,0:T(8,128)S(1)} %pad.8), channel_id=1, source_target_pairs={{0,32},{32,64},{64,96},{96,128},{128,160},{160,192},{192,224},{1,3... | collective-permute-start | bytes 49160 | tf_op jit(solution)/shard_map/ppermute | solution.py:431
  5.1 4.7 %collective-permute-start.1 = (f32[4,8,128]{2,1,0:T(8,128)S(1)}, f32[4,8,128]{2,1,0:T(8,128)S(1)}, u32[]{:S(2)}, u32[]{:S(2)}) collective-permute-start(f32[4,8,128]{2,1,0:T(8,128)S(1)} %pad.8), channel_id=1, source_target_pairs={{32,0},{64,32},{96,64},{128,96},{160,128},{192,160},{224,192},{33,... | collective-permute-start | bytes 49160 | tf_op jit(solution)/shard_map/ppermute | solution.py:432
  6.5 0.7 copy-start.22
  6.5 0.7 copy-start.20
  7.4 0.9 copy-start.14
  7.4 1.0 copy-start.15
  7.5 5.6 %copy-start.11 = (s32[1,8,16,8,32]{4,3,2,1,0:T(8,128)S(1)}, s32[1,8,16,8,32]{4,3,2,1,0:T(8,128)}, u32[]{:S(2)}) copy-start(s32[1,8,16,8,32]{4,3,2,1,0:T(8,128)} %param.26) | copy-start | bytes 393220
  9.8 8.9 %collective-permute-start.2 = (f32[12,8,128]{2,1,0:T(8,128)S(1)}, f32[12,8,128]{2,1,0:T(8,128)S(1)}, u32[]{:S(2)}, u32[]{:S(2)}) collective-permute-start(f32[12,8,128]{2,1,0:T(8,128)S(1)} %pad_maximum_fusion.3), channel_id=1, source_target_pairs={{0,8},{8,16},{16,24},{1,9},{9,17},{17,25},{2,10},{10,18},{18,26},{... | collective-permute-start | bytes 147464 | tf_op jit(solution)/shard_map/ppermute | solution.py:431
  13.1 0.8 copy-start.16
  13.9 0.7 copy-start.17
  17.4 4.8 %collective-permute-start.3 = (f32[12,8,128]{2,1,0:T(8,128)S(1)}, f32[12,8,128]{2,1,0:T(8,128)S(1)}, u32[]{:S(2)}, u32[]{:S(2)}) collective-permute-start(f32[12,8,128]{2,1,0:T(8,128)S(1)} %pad_maximum_fusion.3), channel_id=1, source_target_pairs={{8,0},{16,8},{24,16},{9,1},{17,9},{25,17},{10,2},{18,10},{26,18},{... | collective-permute-start | bytes 147464 | tf_op jit(solution)/shard_map/ppermute | solution.py:432
  22.3 8.4 %copy-start.19 = (bf16[6,80]{1,0:T(8,128)(2,1)S(1)}, bf16[6,80]{1,0:T(8,128)(2,1)}, u32[]{:S(2)}) copy-start(bf16[6,80]{1,0:T(8,128)(2,1)} %param.28) | copy-start | bytes 2884
  22.3 12.3 %collective-permute-start.4 = (f32[36,8,128]{2,1,0:T(8,128)S(1)}, f32[36,8,128]{2,1,0:T(8,128)S(1)}, u32[]{:S(2)}, u32[]{:S(2)}) collective-permute-start(f32[36,8,128]{2,1,0:T(8,128)S(1)} %constant_dynamic-update-slice_fusion.same_ref), channel_id=1, source_target_pairs={{0,1},{1,2},{2,3},{3,4},{4,5},{5,6},{6,7},{8,9},{9,10},{10,11},{11... | collective-permute-start | bytes 442376 | tf_op jit(solution)/shard_map/ppermute | solution.py:431
  28.8 6.5 %collective-permute-start.5 = (f32[36,8,128]{2,1,0:T(8,128)S(1)}, f32[36,8,128]{2,1,0:T(8,128)S(1)}, u32[]{:S(2)}, u32[]{:S(2)}) collective-permute-start(f32[36,8,128]{2,1,0:T(8,128)S(1)} %constant_dynamic-update-slice_fusion.same_ref), channel_id=1, source_target_pairs={{1,0},{2,1},{3,2},{4,3},{5,4},{6,5},{7,6},{9,8},{10,9},{11,10},{12... | collective-permute-start | bytes 442376 | tf_op jit(solution)/shard_map/ppermute | solution.py:432
  30.9 4.4 %copy-start.9 = (bf16[80,64]{0,1:T(8,128)(2,1)S(1)}, bf16[80,64]{0,1:T(8,128)(2,1)}, u32[]{:S(2)}) copy-start(bf16[80,64]{0,1:T(8,128)(2,1)} %param.30) | copy-start | bytes 30724
  45.9 9.7 %copy-start.5 = (bf16[256,512]{1,0:T(8,128)(2,1)S(1)}, bf16[256,512]{1,0:T(8,128)(2,1)}, u32[]{:S(2)}) copy-start(bf16[256,512]{1,0:T(8,128)(2,1)} %constant.94.clone.alo_ref) | copy-start | bytes 786436
  45.9 9.7 %all-to-all-start = ((bf16[8,8,1024]{2,1,0:T(8,128)(2,1)}), bf16[8,8,1024]{2,1,0:T(8,128)(2,1)S(1)}, u32[]{:S(2)}, u32[]{:S(2)}) async-start(bf16[8,8,1024]{2,1,0:T(8,128)(2,1)} %shard_map.235.lat_ref), calls=%async_computation | async-start | bytes 262144 | tf_op jit(solution)/shard_map/all_to_all | solution.py:509
  50.4 5.2 %copy-start.4 = (bf16[256,512]{1,0:T(8,128)(2,1)S(1)}, bf16[256,512]{1,0:T(8,128)(2,1)}, u32[]{:S(2)}) copy-start(bf16[256,512]{1,0:T(8,128)(2,1)} %constant.93.clone.ahi_ref) | copy-start | bytes 786436
  57.0 25.7 %all-to-all-start.1 = ((bf16[256,2,128]{2,1,0:T(2,128)(2,1)}), bf16[256,2,128]{2,1,0:T(2,128)(2,1)S(1)}, u32[]{:S(2)}, u32[]{:S(2)}) async-start(bf16[256,2,128]{2,1,0:T(2,128)(2,1)} %bitcast.13), calls=%async_computation.1 | async-start | bytes 262144 | tf_op jit(solution)/shard_map/all_to_all | solution.py:512
  70.1 12.5 %copy-start.1 = (bf16[128,1024]{1,0:T(8,128)(2,1)S(1)}, bf16[128,1024]{1,0:T(8,128)(2,1)}, u32[]{:S(2)}) copy-start(bf16[128,1024]{1,0:T(8,128)(2,1)} %constant.96.clone.sel_ref) | copy-start | bytes 786436
  70.1 12.5 %copy-start.7 = (f32[16,1024]{1,0:T(8,128)S(1)}, f32[16,1024]{1,0:T(8,128)}, u32[]{:S(2)}) copy-start(f32[16,1024]{1,0:T(8,128)} %constant.97.clone.place_ref) | copy-start | bytes 196612
  70.2 12.5 %copy-start.8 = (f32[16,256]{1,0:T(8,128)S(1)}, f32[16,256]{1,0:T(8,128)}, u32[]{:S(2)}) copy-start(f32[16,256]{1,0:T(8,128)} %constant.95.clone.own_ref) | copy-start | bytes 49156
  70.2 12.5 %copy-start.10 = (bf16[8,16]{1,0:T(8,128)(2,1)S(1)}, bf16[8,16]{1,0:T(8,128)(2,1)}, u32[]{:S(2)}) copy-start(bf16[8,16]{1,0:T(8,128)(2,1)} %constant.98.clone.half_ref) | copy-start | bytes 772
  83.8 5.7 %copy-start.12 = (f32[128,256]{1,0:T(8,128)S(1)}, f32[128,256]{1,0:T(8,128)}, u32[]{:S(2)}) copy-start(f32[128,256]{1,0:T(8,128)} %constant.91.clone) | copy-start | bytes 393220
  83.8 5.7 %copy-start.13 = (f32[128,256]{1,0:T(8,128)S(1)}, f32[128,256]{1,0:T(8,128)}, u32[]{:S(2)}) copy-start(f32[128,256]{1,0:T(8,128)} %constant.92.clone) | copy-start | bytes 393220
  83.8 18.7 %all-to-all-start.2 = ((bf16[256,2,128]{2,1,0:T(2,128)(2,1)}), bf16[256,2,128]{2,1,0:T(2,128)(2,1)S(1)}, u32[]{:S(2)}, u32[]{:S(2)}) async-start(bf16[256,2,128]{2,1,0:T(2,128)(2,1)} %bitcast.23), calls=%async_computation.2 | async-start | bytes 262144 | tf_op jit(solution)/shard_map/all_to_all | solution.py:525
  89.5 13.0 %copy-start.2 = (bf16[512,256]{1,0:T(8,128)(2,1)S(1)}, bf16[512,256]{1,0:T(8,128)(2,1)}, u32[]{:S(2)}) copy-start(bf16[512,256]{1,0:T(8,128)(2,1)} %constant.100.clone.bs_ref) | copy-start | bytes 786436
  89.5 13.0 %copy-start.3 = (bf16[512,256]{1,0:T(8,128)(2,1)S(1)}, bf16[512,256]{1,0:T(8,128)(2,1)}, u32[]{:S(2)}) copy-start(bf16[512,256]{1,0:T(8,128)(2,1)} %constant.99.clone.bc_ref) | copy-start | bytes 786436
  89.6 13.0 %copy-start.6 = (bf16[256,256]{1,0:T(8,128)(2,1)S(1)}, bf16[256,256]{1,0:T(8,128)(2,1)}, u32[]{:S(2)}) copy-start(bf16[256,256]{1,0:T(8,128)(2,1)} %constant.101.clone.partner_ref) | copy-start | bytes 393220
  104.2 9.0 %all-to-all-start.3 = ((bf16[8,8,8,128]{3,2,1,0:T(8,128)(2,1)}), bf16[8,8,8,128]{3,2,1,0:T(8,128)(2,1)S(1)}, u32[]{:S(2)}, u32[]{:S(2)}) async-start(bf16[8,8,8,128]{3,2,1,0:T(8,128)(2,1)} %shard_map.238), calls=%async_computation.3 | async-start | bytes 262144 | tf_op jit(solution)/shard_map/all_to_all | solution.py:537
  107.9 0.7 copy-start.18
  (2 other events, 1.4 us)

commit v7 on v6

--- a/solution.py
+++ b/solution.py
@@ -181,7 +181,7 @@
     steps = tile_ref[8]
     ends = [tile_ref[t] for t in range(7)]
 
-    def gather(b):
+    def gather(b, after=(None,) * 6):
         lines = []
         for half in range(2):
             code = code_ref[pl.ds(pl.multiple_of(b * 16 + half * 8, 8), 8), :]
@@ -191,7 +191,7 @@
                 ((cell & 15).astype(f32) + y0) * (1.0 / GRID),
                 ((cell >> 7).astype(f32) + z0) * (1.0 / GRID),
             )
-            values = look_up(code, b * 2 + half)
+            values = look_up(code, b * 2 + half, after[half * 3 : half * 3 + 3])
             for c in range(6):
                 value = values[c]
                 if c < 3:
@@ -200,19 +200,26 @@
             lines += [turn[half, :, n, :] for n in range(8)]
         return jnp.concatenate(lines, axis=1)
 
-    def add(b, pair):
-        hidden = gelu_twice(dot(ki_ref[...], pair.astype(bf16))).astype(bf16)
-        hidden = gelu_twice(dot(km_ref[...], hidden))
+    def layers(pair):
+        first = gelu_twice(dot(ki_ref[...], pair.astype(bf16)))
+        return first, gelu_twice(dot(km_ref[...], first.astype(bf16)))
+
+    def add(b, hidden):
         for r in range(16):
             tile = sum((b * 16 + r >= end).astype(i32) for end in ends)
             acc_ref[tile] += hidden[:, r * 128 : r * 128 + 128]
 
     def step(b, pair):
-        following = gather(b + 1)
-        add(b, pair)
+        first, second = layers(pair)
+        after = (None,) + tuple(
+            h[0:8, n * 128 : n * 128 + 128]
+            for h, n in ((first, 2), (first, 8), (first, 14), (second, 4), (second, 9))
+        )
+        following = gather(b + 1, after)
+        add(b, second)
         return following
 
-    add(steps - 1, lax.fori_loop(0, steps - 1, step, gather(0)))
+    add(steps - 1, layers(lax.fori_loop(0, steps - 1, step, gather(0)))[1])
 
 
 def lane_gather(line, at):
@@ -236,9 +243,11 @@
     return [jnp.broadcast_to(unit[c : c + 1], (8, 128)) for c in range(6)]
 
 
-def pick_word(words, c, code, count):
+def pick_word(words, c, code, count, after=None):
     levels = (count - 1).bit_length()
     at = code & 127
+    if after is not None:
+        at = jnp.where(after > 3.0e38, 0, at)
     bits = [(code & (128 << n)) != 0 for n in range(levels)]
 
     def pick(lo, level):
@@ -288,11 +297,11 @@
     near_units = rows_of(unit_ref[...])
     acc_ref[...] = jnp.zeros(acc_ref.shape, f32)
 
-    def look_up(code, block):
+    def look_up(code, block, after):
         near = (code & 16383) >= 72 * 128
         values = [None] * 6
         for c in range(3):
-            word = jnp.where(near, near_ref[block, c], pick_word(words, c, code, 72))
+            word = jnp.where(near, near_ref[block, c], pick_word(words, c, code, 72, after[c]))
             upper = jnp.where(near, near_units[c], far_units[c])
             lower = jnp.where(near, near_units[c + 3], far_units[c + 3])
             values[c] = (lax.shift_right_logical(word, 16) - 32768).astype(f32) * upper

time: 116 us -> 117 us (level)
  no operation moved by 1% of the time
where the time goes in v7:
time: 117 us; the launch traced here: 116 us
  starting transfers between devices  45.1 us (39%)
  waiting for transfers between devices  40.5 us (35%)
  Pallas kernels  23.9 us (20%)
  local copies, waits for them, and re-layouts  5.12 us (4%)
    pallas_call x5, Pallas kernels, call(): pl.pallas_call(kernel, out_shape=jax.ShapeDtypeStruct(shape, dtype), in_s...  17.5 us
    ppermute x3, starting transfers between devices, beside(): lower = lax.ppermute(cells, axis, [(i, i + 1) for i in range(ends)])  14 us
    all_to_all x1, waiting for transfers between devices, layer(): lax.all_to_all(mixed.reshape(256, 2, 128), ALL, split_axis=0, concat_axis=0)  12.9 us
    all_to_all x1, starting transfers between devices, layer(): lax.all_to_all(partial.reshape(256, 2, 128), ALL, split_axis=0, concat_ax...  12.7 us
    all_to_all x1, waiting for transfers between devices, layer(): lax.all_to_all(partial.reshape(256, 2, 128), ALL, split_axis=0, concat_ax...  12.4 us
    all_to_all x1, starting transfers between devices, layer(): lax.all_to_all(mixed.reshape(256, 2, 128), ALL, split_axis=0, concat_axis=0)  5.64 us
    ppermute x3, waiting for transfers between devices, beside(): upper = lax.ppermute(cells, axis, [(i + 1, i) for i in range(ends)])  5.34 us
    all_to_all x1, waiting for transfers between devices, layer(): depth = lax.all_to_all(latent, GZ, split_axis=0, concat_axis=0)  5.22 us
  transfers between devices with their start and end apart: 10, of which 7 were waited for; matrix products, arithmetic and copies ran while one was open for 1% of the time, Pallas kernels for 6%

profile of v7, /device:TPU:1, one launch (start us, length us, event | category | flops | bytes accessed | tf_op | source)
XLA Modules:
  0.0 115.9 jit_solution(10642453882744967979)
XLA Ops:
  0.0 0.8 copy.44
  0.8 4.3 %collective-permute-start = (f32[4,8,128]{2,1,0:T(8,128)S(1)}, f32[4,8,128]{2,1,0:T(8,128)S(1)}, u32[]{:S(2)}, u32[]{:S(2)}) collective-permute-start(f32[4,8,128]{2,1,0:T(8,128)S(1)} %pad.8), channel_id=1, source_target_pairs={{0,32},{32,64},{64,96},{96,128},{128,160},{160,192},{192,224},{1,3... | collective-permute-start | bytes 49160 | tf_op jit(solution)/shard_map/ppermute | solution.py:440
  5.1 1.3 %collective-permute-start.1 = (f32[4,8,128]{2,1,0:T(8,128)S(1)}, f32[4,8,128]{2,1,0:T(8,128)S(1)}, u32[]{:S(2)}, u32[]{:S(2)}) collective-permute-start(f32[4,8,128]{2,1,0:T(8,128)S(1)} %pad.8), channel_id=1, source_target_pairs={{32,0},{64,32},{96,64},{128,96},{160,128},{192,160},{224,192},{33,... | collective-permute-start | bytes 49160 | tf_op jit(solution)/shard_map/ppermute | solution.py:441
  6.5 0.6 copy-done.23
  7.5 0.8 copy-done.14
  8.6 1.2 %collective-permute-done.1 = f32[4,8,128]{2,1,0:T(8,128)S(1)} collective-permute-done((f32[4,8,128]{2,1,0:T(8,128)S(1)}, f32[4,8,128]{2,1,0:T(8,128)S(1)}, u32[]{:S(2)}, u32[]{:S(2)}) %collective-permute-start.1) | collective-permute-done | bytes 16416 | tf_op jit(solution)/shard_map/ppermute | solution.py:441
  9.8 3.2 %collective-permute-start.2 = (f32[12,8,128]{2,1,0:T(8,128)S(1)}, f32[12,8,128]{2,1,0:T(8,128)S(1)}, u32[]{:S(2)}, u32[]{:S(2)}) collective-permute-start(f32[12,8,128]{2,1,0:T(8,128)S(1)} %pad_maximum_fusion.3), channel_id=1, source_target_pairs={{0,8},{8,16},{16,24},{1,9},{9,17},{17,25},{2,10},{10,18},{18,26},{... | collective-permute-start | bytes 147464 | tf_op jit(solution)/shard_map/ppermute | solution.py:440
  13.1 0.2 copy.35.nb_ref
  13.3 0.5 copy-done.16
  13.9 0.6 copy-done.17
  14.7 2.7 %sort.1 = (s32[288,128]{1,0:T(8,128)S(1)}, s32[8,1024]{1,0:T(8,128)S(1)}, f32[8,1024]{1,0:T(8,128)S(1)}, s32[9]{0:T(128)S(1)}) custom-call(s32[3]{0:T(128)S(1)} %pad_add_fusion.place_ref, s32[32,8,128]{2,1,0:T(8,128)S(1)} %copy.35.nb_ref, s32[8,128]{1,0:T(8,128)S(1)} %reshape.36.cnt_ref), custom_call_target="tpu_custom_call" | custom-call | tf_op jit(solution)/shard_map/sort/pallas_call | solution.py:414
  17.4 1.3 %collective-permute-start.3 = (f32[12,8,128]{2,1,0:T(8,128)S(1)}, f32[12,8,128]{2,1,0:T(8,128)S(1)}, u32[]{:S(2)}, u32[]{:S(2)}) collective-permute-start(f32[12,8,128]{2,1,0:T(8,128)S(1)} %pad_maximum_fusion.3), channel_id=1, source_target_pairs={{8,0},{16,8},{24,16},{9,1},{17,9},{25,17},{10,2},{18,10},{26,18},{... | collective-permute-start | bytes 147464 | tf_op jit(solution)/shard_map/ppermute | solution.py:441
  18.8 3.5 %collective-permute-done.3 = f32[12,8,128]{2,1,0:T(8,128)S(1)} collective-permute-done((f32[12,8,128]{2,1,0:T(8,128)S(1)}, f32[12,8,128]{2,1,0:T(8,128)S(1)}, u32[]{:S(2)}, u32[]{:S(2)}) %collective-permute-start.3) | collective-permute-done | bytes 49184 | tf_op jit(solution)/shard_map/ppermute | solution.py:441
  22.3 6.5 %collective-permute-start.4 = (f32[36,8,128]{2,1,0:T(8,128)S(1)}, f32[36,8,128]{2,1,0:T(8,128)S(1)}, u32[]{:S(2)}, u32[]{:S(2)}) collective-permute-start(f32[36,8,128]{2,1,0:T(8,128)S(1)} %constant_dynamic-update-slice_fusion.same_ref), channel_id=1, source_target_pairs={{0,1},{1,2},{2,3},{3,4},{4,5},{5,6},{6,7},{8,9},{9,10},{10,11},{11... | collective-permute-start | bytes 442376 | tf_op jit(solution)/shard_map/ppermute | solution.py:440
  28.8 1.9 %collective-permute-start.5 = (f32[36,8,128]{2,1,0:T(8,128)S(1)}, f32[36,8,128]{2,1,0:T(8,128)S(1)}, u32[]{:S(2)}, u32[]{:S(2)}) collective-permute-start(f32[36,8,128]{2,1,0:T(8,128)S(1)} %constant_dynamic-update-slice_fusion.same_ref), channel_id=1, source_target_pairs={{1,0},{2,1},{3,2},{4,3},{5,4},{6,5},{7,6},{9,8},{10,9},{11,10},{12... | collective-permute-start | bytes 442376 | tf_op jit(solution)/shard_map/ppermute | solution.py:441
  30.9 3.7 %near.1 = (s32[36,3,8,128]{3,2,1,0:T(8,128)S(1)}, f32[8,128]{1,0:T(8,128)S(1)}) custom-call(s32[9]{0:T(128)S(1)} %get-tuple-element.20.tile_ref, f32[36,8,128]{2,1,0:T(8,128)S(1)} %constant_dynamic-update-slice_fusion.same_ref, s32[288,128]{1,0:T(8,128)S(1)} %get-tuple-element.22.code_ref), custom_call_target="tpu_custom_call" | custom-call | tf_op jit(solution)/shard_map/near/pallas_call | solution.py:426
  34.6 0.6 collective-permute-done.5.above_ref
  35.2 11.1 %shard_map.235.lat_ref = bf16[8,8,1024]{2,1,0:T(8,128)(2,1)} custom-call(s32[3]{0:T(128)S(1)} %pad_add_fusion.place_ref, s32[9]{0:T(128)S(1)} %get-tuple-element.20.tile_ref, f32[36,8,128]{2,1,0:T(8,128)S(1)} %collective-permute-done.4.below_ref, f32[36,8,128]{2,1,0:T(8,128)S(1)} %collective-permute-done.5.above_ref, ...), custom_call_target="tpu_custom_call" | custom-call | tf_op jit(solution)/shard_map/pallas_call | solution.py:397
  46.3 4.5 %all-to-all-start = ((bf16[8,8,1024]{2,1,0:T(8,128)(2,1)}), bf16[8,8,1024]{2,1,0:T(8,128)(2,1)S(1)}, u32[]{:S(2)}, u32[]{:S(2)}) async-start(bf16[8,8,1024]{2,1,0:T(8,128)(2,1)} %shard_map.235.lat_ref), calls=%async_computation | async-start | bytes 262144 | tf_op jit(solution)/shard_map/all_to_all | solution.py:518
  50.8 5.2 %all-to-all-done.m_ref = bf16[8,8,1024]{2,1,0:T(8,128)(2,1)S(1)} async-done(((bf16[8,8,1024]{2,1,0:T(8,128)(2,1)}), bf16[8,8,1024]{2,1,0:T(8,128)(2,1)S(1)}, u32[]{:S(2)}, u32[]{:S(2)}) %all-to-all-start) | async-done | bytes 131104 | tf_op jit(solution)/shard_map/all_to_all | solution.py:518
  56.0 1.4 %shard_map.236 = bf16[512,128]{1,0:T(8,128)(2,1)} custom-call(bf16[8,8,1024]{2,1,0:T(8,128)(2,1)S(1)} %all-to-all-done.m_ref, bf16[256,512]{1,0:T(8,128)(2,1)S(1)} %copy-done.4, bf16[256,512]{1,0:T(8,128)(2,1)S(1)} %copy-done.5, bf16[256,256]{1,0:T(8,128)(2,1)S(1)} %fusion.whi_ref, bf16[256,256]{1,0:T(8,128)(2,1)S(1)} %subtract_convert_fusion.wlo_ref), custom_call_target="tpu_custom_call" | custom-call | tf_op jit(solution)/shard_map/pallas_call | solution.py:397
  57.4 12.7 %all-to-all-start.1 = ((bf16[256,2,128]{2,1,0:T(2,128)(2,1)}), bf16[256,2,128]{2,1,0:T(2,128)(2,1)S(1)}, u32[]{:S(2)}, u32[]{:S(2)}) async-start(bf16[256,2,128]{2,1,0:T(2,128)(2,1)} %bitcast.13), calls=%async_computation.1 | async-start | bytes 262144 | tf_op jit(solution)/shard_map/all_to_all | solution.py:521
  70.2 0.3 maximum_bitcast_fusion
  70.6 12.4 %all-to-all-done.1 = bf16[256,2,128]{2,1,0:T(2,128)(2,1)S(1)} async-done(((bf16[256,2,128]{2,1,0:T(2,128)(2,1)}), bf16[256,2,128]{2,1,0:T(2,128)(2,1)S(1)}, u32[]{:S(2)}, u32[]{:S(2)}) %all-to-all-start.1) | async-done | bytes 131104 | tf_op jit(solution)/shard_map/all_to_all | solution.py:521
  83.0 1.1 shard_map.237
  84.2 5.6 %all-to-all-start.2 = ((bf16[256,2,128]{2,1,0:T(2,128)(2,1)}), bf16[256,2,128]{2,1,0:T(2,128)(2,1)S(1)}, u32[]{:S(2)}, u32[]{:S(2)}) async-start(bf16[256,2,128]{2,1,0:T(2,128)(2,1)} %bitcast.23), calls=%async_computation.2 | async-start | bytes 262144 | tf_op jit(solution)/shard_map/all_to_all | solution.py:534
  90.0 12.9 %all-to-all-done.2 = bf16[256,2,128]{2,1,0:T(2,128)(2,1)S(1)} async-done(((bf16[256,2,128]{2,1,0:T(2,128)(2,1)}), bf16[256,2,128]{2,1,0:T(2,128)(2,1)S(1)}, u32[]{:S(2)}, u32[]{:S(2)}) %all-to-all-start.2) | async-done | bytes 131104 | tf_op jit(solution)/shard_map/all_to_all | solution.py:534
  102.9 1.6 %shard_map.238 = bf16[8,8,8,128]{3,2,1,0:T(8,128)(2,1)} custom-call(bf16[8,4,16,128]{3,2,1,0:T(8,128)(2,1)S(1)} %bitcast.44, bf16[256,256]{1,0:T(8,128)(2,1)S(1)} %pad_maximum_fusion.2.v_ref, bf16[512,256]{1,0:T(8,128)(2,1)S(1)} %copy-done.3, bf16[512,256]{1,0:T(8,128)(2,1)S(1)} %copy-done.2, bf16[256,256]{1,0:T(8,128)(2,1)S(1)} %copy-done.6), custom_call_target="tpu_custom_call" | custom-call | tf_op jit(solution)/shard_map/pallas_call | solution.py:397
  104.5 3.8 %all-to-all-start.3 = ((bf16[8,8,8,128]{3,2,1,0:T(8,128)(2,1)}), bf16[8,8,8,128]{3,2,1,0:T(8,128)(2,1)S(1)}, u32[]{:S(2)}, u32[]{:S(2)}) async-start(bf16[8,8,8,128]{3,2,1,0:T(8,128)(2,1)} %shard_map.238), calls=%async_computation.3 | async-start | bytes 262144 | tf_op jit(solution)/shard_map/all_to_all | solution.py:546
  108.3 0.7 copy-done.18
  109.0 4.5 %all-to-all-done.3.y_ref = bf16[8,8,8,128]{3,2,1,0:T(8,128)(2,1)S(1)} async-done(((bf16[8,8,8,128]{3,2,1,0:T(8,128)(2,1)}), bf16[8,8,8,128]{3,2,1,0:T(8,128)(2,1)S(1)}, u32[]{:S(2)}, u32[]{:S(2)}) %all-to-all-start.3) | async-done | bytes 131104 | tf_op jit(solution)/shard_map/all_to_all | solution.py:546
  113.6 2.3 %shard_map.239 = f32[128,8,64]{2,1,0:T(8,128)} custom-call(bf16[8,8,8,128]{3,2,1,0:T(8,128)(2,1)S(1)} %all-to-all-done.3.y_ref, bf16[8,8,1024]{2,1,0:T(8,128)(2,1)} %shard_map.235.lat_ref, bf16[128,64]{1,0:T(8,128)(2,1)S(1)} %pad_maximum_fusion.4.w_ref), custom_call_target="tpu_custom_call" | custom-call | tf_op jit(solution)/shard_map/pallas_call | solution.py:397
  (74 shorter events, 1.3 us)
Async XLA Ops:
  0.0 7.3 %copy-start = (bf16[2,2,2,4,64,64]{5,4,3,2,1,0:T(8,128)(2,1)S(1)}, bf16[2,2,2,4,64,64]{5,4,3,2,1,0:T(8,128)(2,1)}, u32[]{:S(2)}) copy-start(bf16[2,2,2,4,64,64]{5,4,3,2,1,0:T(8,128)(2,1)} %param.31) | copy-start | bytes 786436
  0.8 7.8 %collective-permute-start = (f32[4,8,128]{2,1,0:T(8,128)S(1)}, f32[4,8,128]{2,1,0:T(8,128)S(1)}, u32[]{:S(2)}, u32[]{:S(2)}) collective-permute-start(f32[4,8,128]{2,1,0:T(8,128)S(1)} %pad.8), channel_id=1, source_target_pairs={{0,32},{32,64},{64,96},{96,128},{128,160},{160,192},{192,224},{1,3... | collective-permute-start | bytes 49160 | tf_op jit(solution)/shard_map/ppermute | solution.py:440
  5.1 4.7 %collective-permute-start.1 = (f32[4,8,128]{2,1,0:T(8,128)S(1)}, f32[4,8,128]{2,1,0:T(8,128)S(1)}, u32[]{:S(2)}, u32[]{:S(2)}) collective-permute-start(f32[4,8,128]{2,1,0:T(8,128)S(1)} %pad.8), channel_id=1, source_target_pairs={{32,0},{64,32},{96,64},{128,96},{160,128},{192,160},{224,192},{33,... | collective-permute-start | bytes 49160 | tf_op jit(solution)/shard_map/ppermute | solution.py:441
  6.5 0.7 copy-start.22
  6.5 0.7 copy-start.20
  7.4 0.9 copy-start.14
  7.4 1.0 copy-start.15
  7.5 5.6 %copy-start.11 = (s32[1,8,16,8,32]{4,3,2,1,0:T(8,128)S(1)}, s32[1,8,16,8,32]{4,3,2,1,0:T(8,128)}, u32[]{:S(2)}) copy-start(s32[1,8,16,8,32]{4,3,2,1,0:T(8,128)} %param.26) | copy-start | bytes 393220
  9.8 8.9 %collective-permute-start.2 = (f32[12,8,128]{2,1,0:T(8,128)S(1)}, f32[12,8,128]{2,1,0:T(8,128)S(1)}, u32[]{:S(2)}, u32[]{:S(2)}) collective-permute-start(f32[12,8,128]{2,1,0:T(8,128)S(1)} %pad_maximum_fusion.3), channel_id=1, source_target_pairs={{0,8},{8,16},{16,24},{1,9},{9,17},{17,25},{2,10},{10,18},{18,26},{... | collective-permute-start | bytes 147464 | tf_op jit(solution)/shard_map/ppermute | solution.py:440
  13.1 0.8 copy-start.16
  13.9 0.7 copy-start.17
  17.4 4.8 %collective-permute-start.3 = (f32[12,8,128]{2,1,0:T(8,128)S(1)}, f32[12,8,128]{2,1,0:T(8,128)S(1)}, u32[]{:S(2)}, u32[]{:S(2)}) collective-permute-start(f32[12,8,128]{2,1,0:T(8,128)S(1)} %pad_maximum_fusion.3), channel_id=1, source_target_pairs={{8,0},{16,8},{24,16},{9,1},{17,9},{25,17},{10,2},{18,10},{26,18},{... | collective-permute-start | bytes 147464 | tf_op jit(solution)/shard_map/ppermute | solution.py:441
  22.3 8.4 %copy-start.19 = (bf16[6,80]{1,0:T(8,128)(2,1)S(1)}, bf16[6,80]{1,0:T(8,128)(2,1)}, u32[]{:S(2)}) copy-start(bf16[6,80]{1,0:T(8,128)(2,1)} %param.28) | copy-start | bytes 2884
  22.3 12.3 %collective-permute-start.4 = (f32[36,8,128]{2,1,0:T(8,128)S(1)}, f32[36,8,128]{2,1,0:T(8,128)S(1)}, u32[]{:S(2)}, u32[]{:S(2)}) collective-permute-start(f32[36,8,128]{2,1,0:T(8,128)S(1)} %constant_dynamic-update-slice_fusion.same_ref), channel_id=1, source_target_pairs={{0,1},{1,2},{2,3},{3,4},{4,5},{5,6},{6,7},{8,9},{9,10},{10,11},{11... | collective-permute-start | bytes 442376 | tf_op jit(solution)/shard_map/ppermute | solution.py:440
  28.8 6.5 %collective-permute-start.5 = (f32[36,8,128]{2,1,0:T(8,128)S(1)}, f32[36,8,128]{2,1,0:T(8,128)S(1)}, u32[]{:S(2)}, u32[]{:S(2)}) collective-permute-start(f32[36,8,128]{2,1,0:T(8,128)S(1)} %constant_dynamic-update-slice_fusion.same_ref), channel_id=1, source_target_pairs={{1,0},{2,1},{3,2},{4,3},{5,4},{6,5},{7,6},{9,8},{10,9},{11,10},{12... | collective-permute-start | bytes 442376 | tf_op jit(solution)/shard_map/ppermute | solution.py:441
  30.9 4.4 %copy-start.9 = (bf16[80,64]{0,1:T(8,128)(2,1)S(1)}, bf16[80,64]{0,1:T(8,128)(2,1)}, u32[]{:S(2)}) copy-start(bf16[80,64]{0,1:T(8,128)(2,1)} %param.30) | copy-start | bytes 30724
  46.3 9.7 %copy-start.5 = (bf16[256,512]{1,0:T(8,128)(2,1)S(1)}, bf16[256,512]{1,0:T(8,128)(2,1)}, u32[]{:S(2)}) copy-start(bf16[256,512]{1,0:T(8,128)(2,1)} %constant.94.clone.alo_ref) | copy-start | bytes 786436
  46.3 9.7 %all-to-all-start = ((bf16[8,8,1024]{2,1,0:T(8,128)(2,1)}), bf16[8,8,1024]{2,1,0:T(8,128)(2,1)S(1)}, u32[]{:S(2)}, u32[]{:S(2)}) async-start(bf16[8,8,1024]{2,1,0:T(8,128)(2,1)} %shard_map.235.lat_ref), calls=%async_computation | async-start | bytes 262144 | tf_op jit(solution)/shard_map/all_to_all | solution.py:518
  50.7 5.2 %copy-start.4 = (bf16[256,512]{1,0:T(8,128)(2,1)S(1)}, bf16[256,512]{1,0:T(8,128)(2,1)}, u32[]{:S(2)}) copy-start(bf16[256,512]{1,0:T(8,128)(2,1)} %constant.93.clone.ahi_ref) | copy-start | bytes 786436
  57.4 25.7 %all-to-all-start.1 = ((bf16[256,2,128]{2,1,0:T(2,128)(2,1)}), bf16[256,2,128]{2,1,0:T(2,128)(2,1)S(1)}, u32[]{:S(2)}, u32[]{:S(2)}) async-start(bf16[256,2,128]{2,1,0:T(2,128)(2,1)} %bitcast.13), calls=%async_computation.1 | async-start | bytes 262144 | tf_op jit(solution)/shard_map/all_to_all | solution.py:521
  70.5 12.5 %copy-start.1 = (bf16[128,1024]{1,0:T(8,128)(2,1)S(1)}, bf16[128,1024]{1,0:T(8,128)(2,1)}, u32[]{:S(2)}) copy-start(bf16[128,1024]{1,0:T(8,128)(2,1)} %constant.96.clone.sel_ref) | copy-start | bytes 786436
  70.5 12.5 %copy-start.7 = (f32[16,1024]{1,0:T(8,128)S(1)}, f32[16,1024]{1,0:T(8,128)}, u32[]{:S(2)}) copy-start(f32[16,1024]{1,0:T(8,128)} %constant.97.clone.place_ref) | copy-start | bytes 196612
  70.5 12.5 %copy-start.8 = (f32[16,256]{1,0:T(8,128)S(1)}, f32[16,256]{1,0:T(8,128)}, u32[]{:S(2)}) copy-start(f32[16,256]{1,0:T(8,128)} %constant.95.clone.own_ref) | copy-start | bytes 49156
  70.6 12.5 %copy-start.10 = (bf16[8,16]{1,0:T(8,128)(2,1)S(1)}, bf16[8,16]{1,0:T(8,128)(2,1)}, u32[]{:S(2)}) copy-start(bf16[8,16]{1,0:T(8,128)(2,1)} %constant.98.clone.half_ref) | copy-start | bytes 772
  84.2 5.7 %copy-start.12 = (f32[128,256]{1,0:T(8,128)S(1)}, f32[128,256]{1,0:T(8,128)}, u32[]{:S(2)}) copy-start(f32[128,256]{1,0:T(8,128)} %constant.91.clone) | copy-start | bytes 393220
  84.2 5.7 %copy-start.13 = (f32[128,256]{1,0:T(8,128)S(1)}, f32[128,256]{1,0:T(8,128)}, u32[]{:S(2)}) copy-start(f32[128,256]{1,0:T(8,128)} %constant.92.clone) | copy-start | bytes 393220
  84.2 18.7 %all-to-all-start.2 = ((bf16[256,2,128]{2,1,0:T(2,128)(2,1)}), bf16[256,2,128]{2,1,0:T(2,128)(2,1)S(1)}, u32[]{:S(2)}, u32[]{:S(2)}) async-start(bf16[256,2,128]{2,1,0:T(2,128)(2,1)} %bitcast.23), calls=%async_computation.2 | async-start | bytes 262144 | tf_op jit(solution)/shard_map/all_to_all | solution.py:534
  89.9 13.0 %copy-start.2 = (bf16[512,256]{1,0:T(8,128)(2,1)S(1)}, bf16[512,256]{1,0:T(8,128)(2,1)}, u32[]{:S(2)}) copy-start(bf16[512,256]{1,0:T(8,128)(2,1)} %constant.100.clone.bs_ref) | copy-start | bytes 786436
  89.9 13.0 %copy-start.3 = (bf16[512,256]{1,0:T(8,128)(2,1)S(1)}, bf16[512,256]{1,0:T(8,128)(2,1)}, u32[]{:S(2)}) copy-start(bf16[512,256]{1,0:T(8,128)(2,1)} %constant.99.clone.bc_ref) | copy-start | bytes 786436
  89.9 13.0 %copy-start.6 = (bf16[256,256]{1,0:T(8,128)(2,1)S(1)}, bf16[256,256]{1,0:T(8,128)(2,1)}, u32[]{:S(2)}) copy-start(bf16[256,256]{1,0:T(8,128)(2,1)} %constant.101.clone.partner_ref) | copy-start | bytes 393220
  104.5 9.0 %all-to-all-start.3 = ((bf16[8,8,8,128]{3,2,1,0:T(8,128)(2,1)}), bf16[8,8,8,128]{3,2,1,0:T(8,128)(2,1)S(1)}, u32[]{:S(2)}, u32[]{:S(2)}) async-start(bf16[8,8,8,128]{3,2,1,0:T(8,128)(2,1)} %shard_map.238), calls=%async_computation.3 | async-start | bytes 262144 | tf_op jit(solution)/shard_map/all_to_all | solution.py:546
  108.3 0.7 copy-start.18
  (2 other events, 1.4 us)

commit v8 on v6

--- a/solution.py
+++ b/solution.py
@@ -220,20 +220,19 @@
 
 
 def packed(parts, words):
-    most = jnp.zeros((8, 128), f32)
+    most = jnp.zeros((24, 128), f32)
     for part in parts:
         most = jnp.maximum(most, jnp.max(jnp.abs(part[...]), axis=0))
     most = jnp.maximum(jnp.max(most, axis=1, keepdims=True), 1e-30)
-    scale = jnp.broadcast_to(32767.0 / most, (8, 128))
-    unit = jnp.broadcast_to(most * (1.0 / 32767.0), (8, 128))
-    for n in range(36 * len(parts)):
-        q = (parts[n // 36][n % 36] * scale + 32768.5).astype(i32)
-        words[n] = (q << 16) | pltpu.roll(q, 5, 0)
-    return unit
-
-
-def rows_of(unit):
-    return [jnp.broadcast_to(unit[c : c + 1], (8, 128)) for c in range(6)]
+    place = jnp.broadcast_to(jnp.max(most[0:12], axis=0, keepdims=True), (12, 128))
+    normal = jnp.broadcast_to(jnp.max(most[12:24], axis=0, keepdims=True), (12, 128))
+    upper, lower = 32767.0 / place, 32767.0 / normal
+    for n in range(9 * len(parts)):
+        part = parts[n // 9]
+        p = (part[n % 9, 0:12] * upper + 32768.5).astype(i32)
+        q = (part[n % 9, 12:24] * lower + 32768.5).astype(i32)
+        words[n] = (p << 16) | q
+    return place[0:8] * (1.0 / 32767.0), normal[0:8] * (1.0 / 32767.0)
 
 
 def pick_word(words, c, code, count):
@@ -245,7 +244,8 @@
         if lo >= count:
             return None
         if level == 0:
-            return lane_gather(words[lo, c : c + 1, :], at)
+            row = c * 4 + lo % 4
+            return lane_gather(words[lo // 4, row : row + 1, :], at)
         first = pick(lo, level - 1)
         second = pick(lo + (1 << (level - 1)), level - 1)
         return first if second is None else jnp.where(bits[level - 1], second, first)
@@ -254,7 +254,7 @@
 
 
 def near_kernel(tile_ref, same_ref, code_ref, out_ref, unit_ref, words):
-    unit_ref[...] = packed((same_ref,), words)
+    unit_ref[0], unit_ref[1] = packed((same_ref,), words)
 
     def step(b, carry):
         for half in range(2):
@@ -284,17 +284,17 @@
     turn,
     acc_ref,
 ):
-    far_units = rows_of(packed((below_ref, above_ref), words))
-    near_units = rows_of(unit_ref[...])
+    far_place, far_normal = packed((below_ref, above_ref), words)
+    near_place, near_normal = unit_ref[0], unit_ref[1]
     acc_ref[...] = jnp.zeros(acc_ref.shape, f32)
 
     def look_up(code, block):
         near = (code & 16383) >= 72 * 128
+        upper = jnp.where(near, near_place, far_place)
+        lower = jnp.where(near, near_normal, far_normal)
         values = [None] * 6
         for c in range(3):
             word = jnp.where(near, near_ref[block, c], pick_word(words, c, code, 72))
-            upper = jnp.where(near, near_units[c], far_units[c])
-            lower = jnp.where(near, near_units[c + 3], far_units[c + 3])
             values[c] = (lax.shift_right_logical(word, 16) - 32768).astype(f32) * upper
             values[c + 3] = ((word & 65535) - 32768).astype(f32) * lower
         return values
@@ -413,13 +413,13 @@
 
 
 def near_words(tiles, same, code):
-    shapes = (((ROWS // 8, 3, 8, 128), i32), ((8, 128), f32))
+    shapes = (((ROWS // 8, 3, 8, 128), i32), ((2, 8, 128), f32))
     return pl.pallas_call(
         near_kernel,
         out_shape=[jax.ShapeDtypeStruct(*s) for s in shapes],
         in_specs=[SMEM, VMEM, VMEM],
         out_specs=[VMEM] * 2,
-        scratch_shapes=[pltpu.VMEM((36, 8, 128), i32)],
+        scratch_shapes=[pltpu.VMEM((9, 12, 128), i32)],
         compiler_params=pltpu.CompilerParams(vmem_limit_bytes=48 * 1024 * 1024),
         name="near",
     )(tiles, same, code)
@@ -444,7 +444,7 @@
     gz = lax.axis_index(GZ)
     place = jnp.stack([gx, gy, gz]).astype(i32)
 
-    own = jnp.pad(point_data[0].reshape(6, 4, 128).transpose(1, 0, 2), ((0, 0), (0, 2), (0, 0)))
+    own = point_data.reshape(1, 24, 128)
     near = neighbours[0].transpose(3, 2, 0, 1).reshape(NB, 8, 128)
     valid = counts[0].transpose(2, 0, 1).reshape(8, 128)
     ki = jnp.pad(kernel_in.T, ((0, 0), (0, 2)))
@@ -474,7 +474,7 @@
         km,
         kernel_out.T,
         scratch=(
-            pltpu.VMEM((72, 8, 128), i32),
+            pltpu.VMEM((18, 12, 128), i32),
             pltpu.VMEM((2, 8, 8, 128), f32),
             pltpu.VMEM((8, 80, 128), f32),
         ),

time: 116 us -> 117 us (level)
  starting transfers between devices: 45.1 us -> 46.5 us
    all_to_all x1, starting transfers between devices: 12.7 us -> 14 us  [layer(): lax.all_to_all(partial.reshape(256, 2, 128), ALL, split_axis=0, concat_ax...]
  transfers between devices with their start and end apart: 10 -> 10, of which waited for: 7 -> 7; matrix products, arithmetic and copies ran while one was open for 1% -> 2% of each run, Pallas kernels for 6% -> 6%
where the time goes in v8:
time: 117 us; the launch traced here: 116 us
  starting transfers between devices  46.5 us (40%)
  waiting for transfers between devices  39.4 us (34%)
  Pallas kernels  23.7 us (20%)
  local copies, waits for them, and re-layouts  5.14 us (4%)
    pallas_call x5, Pallas kernels, call(): pl.pallas_call(kernel, out_shape=jax.ShapeDtypeStruct(shape, dtype), in_s...  17.3 us
    all_to_all x1, starting transfers between devices, layer(): lax.all_to_all(partial.reshape(256, 2, 128), ALL, split_axis=0, concat_ax...  14 us
    ppermute x3, starting transfers between devices, beside(): lower = lax.ppermute(cells, axis, [(i, i + 1) for i in range(ends)])  13.9 us
    all_to_all x1, waiting for transfers between devices, layer(): lax.all_to_all(mixed.reshape(256, 2, 128), ALL, split_axis=0, concat_axis=0)  12.9 us
    all_to_all x1, waiting for transfers between devices, layer(): lax.all_to_all(partial.reshape(256, 2, 128), ALL, split_axis=0, concat_ax...  12.4 us
    all_to_all x1, starting transfers between devices, layer(): lax.all_to_all(mixed.reshape(256, 2, 128), ALL, split_axis=0, concat_axis=0)  5.64 us
    all_to_all x1, waiting for transfers between devices, layer(): depth = lax.all_to_all(latent, GZ, split_axis=0, concat_axis=0)  5.22 us
    all_to_all x1, starting transfers between devices, layer(): depth = lax.all_to_all(latent, GZ, split_axis=0, concat_axis=0)  4.72 us
  transfers between devices with their start and end apart: 10, of which 7 were waited for; matrix products, arithmetic and copies ran while one was open for 2% of the time, Pallas kernels for 6%

profile of v8, /device:TPU:1, one launch (start us, length us, event | category | flops | bytes accessed | tf_op | source)
XLA Modules:
  0.0 116.0 jit_solution(10350841074067120089)
XLA Ops:
  0.0 4.5 %collective-permute-start = (f32[1,24,128]{2,1,0:T(8,128)}, f32[1,24,128]{2,1,0:T(8,128)S(1)}, u32[]{:S(2)}, u32[]{:S(2)}) collective-permute-start(f32[1,24,128]{2,1,0:T(8,128)} %bitcast.45), channel_id=1, source_target_pairs={{0,32},{32,64},{64,96},{96,128},{128,160},{160,192},{192,224},{1,3... | collective-permute-start | bytes 36872 | tf_op jit(solution)/shard_map/ppermute | solution.py:431
  4.5 1.3 %collective-permute-start.1 = (f32[1,24,128]{2,1,0:T(8,128)}, f32[1,24,128]{2,1,0:T(8,128)S(1)}, u32[]{:S(2)}, u32[]{:S(2)}) collective-permute-start(f32[1,24,128]{2,1,0:T(8,128)} %bitcast.46), channel_id=1, source_target_pairs={{32,0},{64,32},{96,64},{128,96},{160,128},{192,160},{224,192},{33,... | collective-permute-start | bytes 36872 | tf_op jit(solution)/shard_map/ppermute | solution.py:432
  5.8 0.8 copy.36
  6.7 0.6 copy-done.21
  7.7 0.8 copy-done.14
  8.8 0.6 collective-permute-done.1
  9.5 3.2 %collective-permute-start.2 = (f32[3,24,128]{2,1,0:T(8,128)S(1)}, f32[3,24,128]{2,1,0:T(8,128)S(1)}, u32[]{:S(2)}, u32[]{:S(2)}) collective-permute-start(f32[3,24,128]{2,1,0:T(8,128)S(1)} %pad_maximum_fusion.3), channel_id=1, source_target_pairs={{0,8},{8,16},{16,24},{1,9},{9,17},{17,25},{2,10},{10,18},{18,26},{... | collective-permute-start | bytes 110600 | tf_op jit(solution)/shard_map/ppermute | solution.py:431
  12.7 0.2 copy.34.nb_ref
  13.0 0.5 copy-done.17
  13.6 0.6 copy-done.19
  14.3 2.7 %sort.1 = (s32[288,128]{1,0:T(8,128)S(1)}, s32[8,1024]{1,0:T(8,128)S(1)}, f32[8,1024]{1,0:T(8,128)S(1)}, s32[9]{0:T(128)S(1)}) custom-call(s32[3]{0:T(128)S(1)} %pad_add_fusion.place_ref, s32[32,8,128]{2,1,0:T(8,128)S(1)} %copy.34.nb_ref, s32[8,128]{1,0:T(8,128)S(1)} %reshape.40.cnt_ref), custom_call_target="tpu_custom_call" | custom-call | tf_op jit(solution)/shard_map/sort/pallas_call | solution.py:405
  17.0 1.3 %collective-permute-start.3 = (f32[3,24,128]{2,1,0:T(8,128)S(1)}, f32[3,24,128]{2,1,0:T(8,128)S(1)}, u32[]{:S(2)}, u32[]{:S(2)}) collective-permute-start(f32[3,24,128]{2,1,0:T(8,128)S(1)} %pad_maximum_fusion.3), channel_id=1, source_target_pairs={{8,0},{16,8},{24,16},{9,1},{17,9},{25,17},{10,2},{18,10},{26,18},{... | collective-permute-start | bytes 110600 | tf_op jit(solution)/shard_map/ppermute | solution.py:432
  18.4 3.3 %collective-permute-done.3 = f32[3,24,128]{2,1,0:T(8,128)S(1)} collective-permute-done((f32[3,24,128]{2,1,0:T(8,128)S(1)}, f32[3,24,128]{2,1,0:T(8,128)S(1)}, u32[]{:S(2)}, u32[]{:S(2)}) %collective-permute-start.3) | collective-permute-done | bytes 36896 | tf_op jit(solution)/shard_map/ppermute | solution.py:432
  21.8 6.2 %collective-permute-start.4 = (f32[9,24,128]{2,1,0:T(8,128)S(1)}, f32[9,24,128]{2,1,0:T(8,128)S(1)}, u32[]{:S(2)}, u32[]{:S(2)}) collective-permute-start(f32[9,24,128]{2,1,0:T(8,128)S(1)} %constant_dynamic-update-slice_fusion.same_ref), channel_id=1, source_target_pairs={{0,1},{1,2},{2,3},{3,4},{4,5},{5,6},{6,7},{8,9},{9,10},{10,11},{11... | collective-permute-start | bytes 331784 | tf_op jit(solution)/shard_map/ppermute | solution.py:431
  28.0 1.9 %collective-permute-start.5 = (f32[9,24,128]{2,1,0:T(8,128)S(1)}, f32[9,24,128]{2,1,0:T(8,128)S(1)}, u32[]{:S(2)}, u32[]{:S(2)}) collective-permute-start(f32[9,24,128]{2,1,0:T(8,128)S(1)} %constant_dynamic-update-slice_fusion.same_ref), channel_id=1, source_target_pairs={{1,0},{2,1},{3,2},{4,3},{5,4},{6,5},{7,6},{9,8},{10,9},{11,10},{12... | collective-permute-start | bytes 331784 | tf_op jit(solution)/shard_map/ppermute | solution.py:432
  29.9 3.7 %near.1 = (s32[36,3,8,128]{3,2,1,0:T(8,128)S(1)}, f32[2,8,128]{2,1,0:T(8,128)S(1)}) custom-call(s32[9]{0:T(128)S(1)} %get-tuple-element.20.tile_ref, f32[9,24,128]{2,1,0:T(8,128)S(1)} %constant_dynamic-update-slice_fusion.same_ref, s32[288,128]{1,0:T(8,128)S(1)} %get-tuple-element.22.code_ref), custom_call_target="tpu_custom_call" | custom-call | tf_op jit(solution)/shard_map/near/pallas_call | solution.py:417
  33.7 0.4 collective-permute-done.5.above_ref
  34.1 10.9 %shard_map.235.lat_ref = bf16[8,8,1024]{2,1,0:T(8,128)(2,1)} custom-call(s32[3]{0:T(128)S(1)} %pad_add_fusion.place_ref, s32[9]{0:T(128)S(1)} %get-tuple-element.20.tile_ref, f32[9,24,128]{2,1,0:T(8,128)S(1)} %collective-permute-done.4.below_ref, f32[9,24,128]{2,1,0:T(8,128)S(1)} %collective-permute-done.5.above_ref, ...), custom_call_target="tpu_custom_call" | custom-call | tf_op jit(solution)/shard_map/pallas_call | solution.py:388
  44.9 4.7 %all-to-all-start = ((bf16[8,8,1024]{2,1,0:T(8,128)(2,1)}), bf16[8,8,1024]{2,1,0:T(8,128)(2,1)S(1)}, u32[]{:S(2)}, u32[]{:S(2)}) async-start(bf16[8,8,1024]{2,1,0:T(8,128)(2,1)} %shard_map.235.lat_ref), calls=%async_computation | async-start | bytes 262144 | tf_op jit(solution)/shard_map/all_to_all | solution.py:509
  49.7 5.2 %all-to-all-done.m_ref = bf16[8,8,1024]{2,1,0:T(8,128)(2,1)S(1)} async-done(((bf16[8,8,1024]{2,1,0:T(8,128)(2,1)}), bf16[8,8,1024]{2,1,0:T(8,128)(2,1)S(1)}, u32[]{:S(2)}, u32[]{:S(2)}) %all-to-all-start) | async-done | bytes 131104 | tf_op jit(solution)/shard_map/all_to_all | solution.py:509
  54.9 1.4 %shard_map.236 = bf16[512,128]{1,0:T(8,128)(2,1)} custom-call(bf16[8,8,1024]{2,1,0:T(8,128)(2,1)S(1)} %all-to-all-done.m_ref, bf16[256,512]{1,0:T(8,128)(2,1)S(1)} %copy-done.4, bf16[256,512]{1,0:T(8,128)(2,1)S(1)} %copy-done.5, bf16[256,256]{1,0:T(8,128)(2,1)S(1)} %fusion.whi_ref, bf16[256,256]{1,0:T(8,128)(2,1)S(1)} %subtract_convert_fusion.wlo_ref), custom_call_target="tpu_custom_call" | custom-call | tf_op jit(solution)/shard_map/pallas_call | solution.py:388
  56.3 14.0 %all-to-all-start.1 = ((bf16[256,2,128]{2,1,0:T(2,128)(2,1)}), bf16[256,2,128]{2,1,0:T(2,128)(2,1)S(1)}, u32[]{:S(2)}, u32[]{:S(2)}) async-start(bf16[256,2,128]{2,1,0:T(2,128)(2,1)} %bitcast.12), calls=%async_computation.1 | async-start | bytes 262144 | tf_op jit(solution)/shard_map/all_to_all | solution.py:512
  70.3 0.3 maximum_bitcast_fusion
  70.7 12.4 %all-to-all-done.1 = bf16[256,2,128]{2,1,0:T(2,128)(2,1)S(1)} async-done(((bf16[256,2,128]{2,1,0:T(2,128)(2,1)}), bf16[256,2,128]{2,1,0:T(2,128)(2,1)S(1)}, u32[]{:S(2)}, u32[]{:S(2)}) %all-to-all-start.1) | async-done | bytes 131104 | tf_op jit(solution)/shard_map/all_to_all | solution.py:512
  83.2 1.1 shard_map.237
  84.3 5.6 %all-to-all-start.2 = ((bf16[256,2,128]{2,1,0:T(2,128)(2,1)}), bf16[256,2,128]{2,1,0:T(2,128)(2,1)S(1)}, u32[]{:S(2)}, u32[]{:S(2)}) async-start(bf16[256,2,128]{2,1,0:T(2,128)(2,1)} %bitcast.22), calls=%async_computation.2 | async-start | bytes 262144 | tf_op jit(solution)/shard_map/all_to_all | solution.py:525
  90.1 12.9 %all-to-all-done.2 = bf16[256,2,128]{2,1,0:T(2,128)(2,1)S(1)} async-done(((bf16[256,2,128]{2,1,0:T(2,128)(2,1)}), bf16[256,2,128]{2,1,0:T(2,128)(2,1)S(1)}, u32[]{:S(2)}, u32[]{:S(2)}) %all-to-all-start.2) | async-done | bytes 131104 | tf_op jit(solution)/shard_map/all_to_all | solution.py:525
  103.1 1.6 %shard_map.238 = bf16[8,8,8,128]{3,2,1,0:T(8,128)(2,1)} custom-call(bf16[8,4,16,128]{3,2,1,0:T(8,128)(2,1)S(1)} %bitcast.41, bf16[256,256]{1,0:T(8,128)(2,1)S(1)} %pad_maximum_fusion.2.v_ref, bf16[512,256]{1,0:T(8,128)(2,1)S(1)} %copy-done.2, bf16[512,256]{1,0:T(8,128)(2,1)S(1)} %copy-done.3, bf16[256,256]{1,0:T(8,128)(2,1)S(1)} %copy-done.6), custom_call_target="tpu_custom_call" | custom-call | tf_op jit(solution)/shard_map/pallas_call | solution.py:388
  104.7 3.8 %all-to-all-start.3 = ((bf16[8,8,8,128]{3,2,1,0:T(8,128)(2,1)}), bf16[8,8,8,128]{3,2,1,0:T(8,128)(2,1)S(1)}, u32[]{:S(2)}, u32[]{:S(2)}) async-start(bf16[8,8,8,128]{3,2,1,0:T(8,128)(2,1)} %shard_map.238), calls=%async_computation.3 | async-start | bytes 262144 | tf_op jit(solution)/shard_map/all_to_all | solution.py:537
  108.5 0.7 copy-done.18
  109.2 4.5 %all-to-all-done.3.y_ref = bf16[8,8,8,128]{3,2,1,0:T(8,128)(2,1)S(1)} async-done(((bf16[8,8,8,128]{3,2,1,0:T(8,128)(2,1)}), bf16[8,8,8,128]{3,2,1,0:T(8,128)(2,1)S(1)}, u32[]{:S(2)}, u32[]{:S(2)}) %all-to-all-start.3) | async-done | bytes 131104 | tf_op jit(solution)/shard_map/all_to_all | solution.py:537
  113.7 2.3 %shard_map.239 = f32[128,8,64]{2,1,0:T(8,128)} custom-call(bf16[8,8,8,128]{3,2,1,0:T(8,128)(2,1)S(1)} %all-to-all-done.3.y_ref, bf16[8,8,1024]{2,1,0:T(8,128)(2,1)} %shard_map.235.lat_ref, bf16[128,64]{1,0:T(8,128)(2,1)S(1)} %pad_maximum_fusion.4.w_ref), custom_call_target="tpu_custom_call" | custom-call | tf_op jit(solution)/shard_map/pallas_call | solution.py:388
  (72 shorter events, 1.3 us)
Async XLA Ops:
  0.0 7.5 %copy-start = (bf16[2,2,2,4,64,64]{5,4,3,2,1,0:T(8,128)(2,1)S(1)}, bf16[2,2,2,4,64,64]{5,4,3,2,1,0:T(8,128)(2,1)}, u32[]{:S(2)}) copy-start(bf16[2,2,2,4,64,64]{5,4,3,2,1,0:T(8,128)(2,1)} %param.31) | copy-start | bytes 786436
  0.0 8.8 %collective-permute-start = (f32[1,24,128]{2,1,0:T(8,128)}, f32[1,24,128]{2,1,0:T(8,128)S(1)}, u32[]{:S(2)}, u32[]{:S(2)}) collective-permute-start(f32[1,24,128]{2,1,0:T(8,128)} %bitcast.45), channel_id=1, source_target_pairs={{0,32},{32,64},{64,96},{96,128},{128,160},{160,192},{192,224},{1,3... | collective-permute-start | bytes 36872 | tf_op jit(solution)/shard_map/ppermute | solution.py:431
  4.5 4.8 %collective-permute-start.1 = (f32[1,24,128]{2,1,0:T(8,128)}, f32[1,24,128]{2,1,0:T(8,128)S(1)}, u32[]{:S(2)}, u32[]{:S(2)}) collective-permute-start(f32[1,24,128]{2,1,0:T(8,128)} %bitcast.46), channel_id=1, source_target_pairs={{32,0},{64,32},{96,64},{128,96},{160,128},{192,160},{224,192},{33,... | collective-permute-start | bytes 36872 | tf_op jit(solution)/shard_map/ppermute | solution.py:432
  5.8 0.9 copy-start.23
  6.7 0.7 copy-start.22
  6.7 0.7 copy-start.20
  7.6 0.9 copy-start.14
  7.6 1.0 copy-start.15
  7.7 5.0 %copy-start.11 = (s32[1,8,16,8,32]{4,3,2,1,0:T(8,128)S(1)}, s32[1,8,16,8,32]{4,3,2,1,0:T(8,128)}, u32[]{:S(2)}) copy-start(s32[1,8,16,8,32]{4,3,2,1,0:T(8,128)} %param.26) | copy-start | bytes 393220
  8.7 0.7 copy-start.16
  9.5 8.9 %collective-permute-start.2 = (f32[3,24,128]{2,1,0:T(8,128)S(1)}, f32[3,24,128]{2,1,0:T(8,128)S(1)}, u32[]{:S(2)}, u32[]{:S(2)}) collective-permute-start(f32[3,24,128]{2,1,0:T(8,128)S(1)} %pad_maximum_fusion.3), channel_id=1, source_target_pairs={{0,8},{8,16},{16,24},{1,9},{9,17},{17,25},{2,10},{10,18},{18,26},{... | collective-permute-start | bytes 110600 | tf_op jit(solution)/shard_map/ppermute | solution.py:431
  12.7 0.8 copy-start.17
  17.0 4.7 %collective-permute-start.3 = (f32[3,24,128]{2,1,0:T(8,128)S(1)}, f32[3,24,128]{2,1,0:T(8,128)S(1)}, u32[]{:S(2)}, u32[]{:S(2)}) collective-permute-start(f32[3,24,128]{2,1,0:T(8,128)S(1)} %pad_maximum_fusion.3), channel_id=1, source_target_pairs={{8,0},{16,8},{24,16},{9,1},{17,9},{25,17},{10,2},{18,10},{26,18},{... | collective-permute-start | bytes 110600 | tf_op jit(solution)/shard_map/ppermute | solution.py:432
  21.8 11.9 %collective-permute-start.4 = (f32[9,24,128]{2,1,0:T(8,128)S(1)}, f32[9,24,128]{2,1,0:T(8,128)S(1)}, u32[]{:S(2)}, u32[]{:S(2)}) collective-permute-start(f32[9,24,128]{2,1,0:T(8,128)S(1)} %constant_dynamic-update-slice_fusion.same_ref), channel_id=1, source_target_pairs={{0,1},{1,2},{2,3},{3,4},{4,5},{5,6},{6,7},{8,9},{9,10},{10,11},{11... | collective-permute-start | bytes 331784 | tf_op jit(solution)/shard_map/ppermute | solution.py:431
  28.0 6.1 %collective-permute-start.5 = (f32[9,24,128]{2,1,0:T(8,128)S(1)}, f32[9,24,128]{2,1,0:T(8,128)S(1)}, u32[]{:S(2)}, u32[]{:S(2)}) collective-permute-start(f32[9,24,128]{2,1,0:T(8,128)S(1)} %constant_dynamic-update-slice_fusion.same_ref), channel_id=1, source_target_pairs={{1,0},{2,1},{3,2},{4,3},{5,4},{6,5},{7,6},{9,8},{10,9},{11,10},{12... | collective-permute-start | bytes 331784 | tf_op jit(solution)/shard_map/ppermute | solution.py:432
  29.9 4.1 %copy-start.8 = (bf16[80,64]{0,1:T(8,128)(2,1)S(1)}, bf16[80,64]{0,1:T(8,128)(2,1)}, u32[]{:S(2)}) copy-start(bf16[80,64]{0,1:T(8,128)(2,1)} %param.30) | copy-start | bytes 30724
  44.9 10.0 %copy-start.5 = (bf16[256,512]{1,0:T(8,128)(2,1)S(1)}, bf16[256,512]{1,0:T(8,128)(2,1)}, u32[]{:S(2)}) copy-start(bf16[256,512]{1,0:T(8,128)(2,1)} %constant.92.clone.alo_ref) | copy-start | bytes 786436
  44.9 10.0 %all-to-all-start = ((bf16[8,8,1024]{2,1,0:T(8,128)(2,1)}), bf16[8,8,1024]{2,1,0:T(8,128)(2,1)S(1)}, u32[]{:S(2)}, u32[]{:S(2)}) async-start(bf16[8,8,1024]{2,1,0:T(8,128)(2,1)} %shard_map.235.lat_ref), calls=%async_computation | async-start | bytes 262144 | tf_op jit(solution)/shard_map/all_to_all | solution.py:509
  49.7 5.2 %copy-start.4 = (bf16[256,512]{1,0:T(8,128)(2,1)S(1)}, bf16[256,512]{1,0:T(8,128)(2,1)}, u32[]{:S(2)}) copy-start(bf16[256,512]{1,0:T(8,128)(2,1)} %constant.91.clone.ahi_ref) | copy-start | bytes 786436
  56.3 26.9 %all-to-all-start.1 = ((bf16[256,2,128]{2,1,0:T(2,128)(2,1)}), bf16[256,2,128]{2,1,0:T(2,128)(2,1)S(1)}, u32[]{:S(2)}, u32[]{:S(2)}) async-start(bf16[256,2,128]{2,1,0:T(2,128)(2,1)} %bitcast.12), calls=%async_computation.1 | async-start | bytes 262144 | tf_op jit(solution)/shard_map/all_to_all | solution.py:512
  70.6 12.5 %copy-start.1 = (bf16[128,1024]{1,0:T(8,128)(2,1)S(1)}, bf16[128,1024]{1,0:T(8,128)(2,1)}, u32[]{:S(2)}) copy-start(bf16[128,1024]{1,0:T(8,128)(2,1)} %constant.94.clone.sel_ref) | copy-start | bytes 786436
  70.7 12.5 %copy-start.7 = (f32[16,1024]{1,0:T(8,128)S(1)}, f32[16,1024]{1,0:T(8,128)}, u32[]{:S(2)}) copy-start(f32[16,1024]{1,0:T(8,128)} %constant.95.clone.place_ref) | copy-start | bytes 196612
  70.7 12.5 %copy-start.9 = (f32[16,256]{1,0:T(8,128)S(1)}, f32[16,256]{1,0:T(8,128)}, u32[]{:S(2)}) copy-start(f32[16,256]{1,0:T(8,128)} %constant.93.clone.own_ref) | copy-start | bytes 49156
  70.7 12.4 %copy-start.10 = (bf16[8,16]{1,0:T(8,128)(2,1)S(1)}, bf16[8,16]{1,0:T(8,128)(2,1)}, u32[]{:S(2)}) copy-start(bf16[8,16]{1,0:T(8,128)(2,1)} %constant.96.clone.half_ref) | copy-start | bytes 772
  84.3 5.7 %copy-start.12 = (f32[128,256]{1,0:T(8,128)S(1)}, f32[128,256]{1,0:T(8,128)}, u32[]{:S(2)}) copy-start(f32[128,256]{1,0:T(8,128)} %constant.89.clone) | copy-start | bytes 393220
  84.3 5.7 %copy-start.13 = (f32[128,256]{1,0:T(8,128)S(1)}, f32[128,256]{1,0:T(8,128)}, u32[]{:S(2)}) copy-start(f32[128,256]{1,0:T(8,128)} %constant.90.clone) | copy-start | bytes 393220
  84.3 18.7 %all-to-all-start.2 = ((bf16[256,2,128]{2,1,0:T(2,128)(2,1)}), bf16[256,2,128]{2,1,0:T(2,128)(2,1)S(1)}, u32[]{:S(2)}, u32[]{:S(2)}) async-start(bf16[256,2,128]{2,1,0:T(2,128)(2,1)} %bitcast.22), calls=%async_computation.2 | async-start | bytes 262144 | tf_op jit(solution)/shard_map/all_to_all | solution.py:525
  90.0 13.0 %copy-start.2 = (bf16[512,256]{1,0:T(8,128)(2,1)S(1)}, bf16[512,256]{1,0:T(8,128)(2,1)}, u32[]{:S(2)}) copy-start(bf16[512,256]{1,0:T(8,128)(2,1)} %constant.97.clone.bc_ref) | copy-start | bytes 786436
  90.0 13.0 %copy-start.3 = (bf16[512,256]{1,0:T(8,128)(2,1)S(1)}, bf16[512,256]{1,0:T(8,128)(2,1)}, u32[]{:S(2)}) copy-start(bf16[512,256]{1,0:T(8,128)(2,1)} %constant.98.clone.bs_ref) | copy-start | bytes 786436
  90.1 13.0 %copy-start.6 = (bf16[256,256]{1,0:T(8,128)(2,1)S(1)}, bf16[256,256]{1,0:T(8,128)(2,1)}, u32[]{:S(2)}) copy-start(bf16[256,256]{1,0:T(8,128)(2,1)} %constant.99.clone.partner_ref) | copy-start | bytes 393220
  104.7 9.0 %all-to-all-start.3 = ((bf16[8,8,8,128]{3,2,1,0:T(8,128)(2,1)}), bf16[8,8,8,128]{3,2,1,0:T(8,128)(2,1)S(1)}, u32[]{:S(2)}, u32[]{:S(2)}) async-start(bf16[8,8,8,128]{3,2,1,0:T(8,128)(2,1)} %shard_map.238), calls=%async_computation.3 | async-start | bytes 262144 | tf_op jit(solution)/shard_map/all_to_all | solution.py:537
  108.4 0.7 copy-start.18
  (2 other events, 1.4 us)

commit v9 on v8

--- a/solution.py
+++ b/solution.py
@@ -276,14 +276,20 @@
     unit_ref,
     rank_ref,
     scnt_ref,
+    kernel_in_ref,
+    kernel_mid_ref,
+    ko_ref,
+    out_ref,
     ki_ref,
     km_ref,
-    ko_ref,
-    out_ref,
     words,
     turn,
     acc_ref,
 ):
+    ki = jnp.concatenate([kernel_in_ref[...].astype(f32), jnp.zeros((2, 80), f32)], axis=0)
+    ki_ref[...] = jnp.concatenate([ki, jnp.zeros((8, 48), f32)], axis=1).T[0:80].astype(bf16)
+    km = jnp.concatenate([kernel_mid_ref[...].astype(f32) * 0.5, jnp.zeros((80, 48), f32)], axis=1)
+    km_ref[...] = km.T[0:80].astype(bf16)
     far_place, far_normal = packed((below_ref, above_ref), words)
     near_place, near_normal = unit_ref[0], unit_ref[1]
     acc_ref[...] = jnp.zeros(acc_ref.shape, f32)
@@ -447,8 +453,6 @@
     own = point_data.reshape(1, 24, 128)
     near = neighbours[0].transpose(3, 2, 0, 1).reshape(NB, 8, 128)
     valid = counts[0].transpose(2, 0, 1).reshape(8, 128)
-    ki = jnp.pad(kernel_in.T, ((0, 0), (0, 2)))
-    km = kernel_mid.T * jnp.bfloat16(0.5)
 
     line = jnp.concatenate(beside(own, "gx"), axis=0)
     plane = jnp.concatenate(beside(line, "gy"), axis=0)
@@ -470,10 +474,12 @@
         units,
         rank,
         sorted_counts,
-        ki,
-        km,
+        kernel_in,
+        kernel_mid,
         kernel_out.T,
         scratch=(
+            pltpu.VMEM((80, 8), bf16),
+            pltpu.VMEM((80, 80), bf16),
             pltpu.VMEM((18, 12, 128), i32),
             pltpu.VMEM((2, 8, 8, 128), f32),
             pltpu.VMEM((8, 80, 128), f32),
@@ -481,6 +487,7 @@
         smem=2,
     )
 
+    latent, spectral, gx, gy = lax.optimization_barrier((latent, spectral, gx, gy))
     (ffi, ffj), (ifi, ifj), xl, yl = plane_tables()
     local = angle(1, ffi[:, None] * xl[None, :] + ffj[:, None] * yl[None, :])
     phase = ((jnp.asarray(ffi, i32) * 8 * gx + jnp.asarray(ffj, i32) * 16 * gy) % GRID).astype(f32)

time: 117 us -> 116 us (level)
  waiting for transfers between devices: 39.4 us -> 37.8 us
    all_to_all x1, waiting for transfers between devices: 5.22 us -> 3.12 us  [layer(): depth = lax.all_to_all(latent, GZ, split_axis=0, concat_axis=0)]
    unnamed x54 -> x52, local copies, waits for them, and re-layouts: 4.58 us -> 3.07 us
where the time goes in v9:
time: 116 us; the launch traced here: 115 us
  starting transfers between devices  47.5 us (41%)
  waiting for transfers between devices  37.8 us (33%)
  Pallas kernels  23.7 us (20%)
  local copies, waits for them, and re-layouts  4.64 us (4%)
    pallas_call x5, Pallas kernels, call(): pl.pallas_call(kernel, out_shape=jax.ShapeDtypeStruct(shape, dtype), in_s...  17.2 us
    all_to_all x1, starting transfers between devices, layer(): lax.all_to_all(partial.reshape(256, 2, 128), ALL, split_axis=0, concat_ax...  14.5 us
    ppermute x3, starting transfers between devices, beside(): lower = lax.ppermute(cells, axis, [(i, i + 1) for i in range(ends)])  14.4 us
    all_to_all x1, waiting for transfers between devices, layer(): lax.all_to_all(mixed.reshape(256, 2, 128), ALL, split_axis=0, concat_axis=0)  12.9 us
    all_to_all x1, waiting for transfers between devices, layer(): lax.all_to_all(partial.reshape(256, 2, 128), ALL, split_axis=0, concat_ax...  12.4 us
    all_to_all x1, starting transfers between devices, layer(): lax.all_to_all(mixed.reshape(256, 2, 128), ALL, split_axis=0, concat_axis=0)  5.64 us
    all_to_all x1, starting transfers between devices, layer(): depth = lax.all_to_all(latent, GZ, split_axis=0, concat_axis=0)  4.68 us
    ppermute x3, starting transfers between devices, beside(): upper = lax.ppermute(cells, axis, [(i + 1, i) for i in range(ends)])  4.62 us
  transfers between devices with their start and end apart: 10, of which 7 were waited for; matrix products, arithmetic and copies ran while one was open for 2% of the time, Pallas kernels for 6%

profile of v9, /device:TPU:1, one launch (start us, length us, event | category | flops | bytes accessed | tf_op | source)
XLA Modules:
  0.0 114.8 jit_solution(3983860041457003609)
XLA Ops:
  0.0 1.4 %collective-permute-start.1 = (f32[1,24,128]{2,1,0:T(8,128)}, f32[1,24,128]{2,1,0:T(8,128)S(1)}, u32[]{:S(2)}, u32[]{:S(2)}) collective-permute-start(f32[1,24,128]{2,1,0:T(8,128)} %bitcast.41), channel_id=1, source_target_pairs={{32,0},{64,32},{96,64},{128,96},{160,128},{192,160},{224,192},{33,... | collective-permute-start | bytes 36872 | tf_op jit(solution)/shard_map/ppermute | solution.py:438
  1.4 5.0 %collective-permute-start = (f32[1,24,128]{2,1,0:T(8,128)}, f32[1,24,128]{2,1,0:T(8,128)S(1)}, u32[]{:S(2)}, u32[]{:S(2)}) collective-permute-start(f32[1,24,128]{2,1,0:T(8,128)} %bitcast.42), channel_id=1, source_target_pairs={{0,32},{32,64},{64,96},{96,128},{128,160},{160,192},{192,224},{1,3... | collective-permute-start | bytes 36872 | tf_op jit(solution)/shard_map/ppermute | solution.py:437
  6.4 1.0 collective-permute-done
  7.4 3.2 %collective-permute-start.2 = (f32[3,24,128]{2,1,0:T(8,128)S(1)}, f32[3,24,128]{2,1,0:T(8,128)S(1)}, u32[]{:S(2)}, u32[]{:S(2)}) collective-permute-start(f32[3,24,128]{2,1,0:T(8,128)S(1)} %pad_maximum_fusion.3), channel_id=1, source_target_pairs={{0,8},{8,16},{16,24},{1,9},{9,17},{17,25},{2,10},{10,18},{18,26},{... | collective-permute-start | bytes 110600 | tf_op jit(solution)/shard_map/ppermute | solution.py:437
  10.7 1.2 %copy.32.nb_ref = s32[32,8,128]{2,1,0:T(8,128)S(1)} copy(s32[32,8,128]{0,1,2:T(8,128)} %bitcast.40) | data formatting | bytes 262144 | tf_op jit(solution)/shard_map/reshape | solution.py:454
  12.1 2.7 %sort.1 = (s32[288,128]{1,0:T(8,128)S(1)}, s32[8,1024]{1,0:T(8,128)S(1)}, f32[8,1024]{1,0:T(8,128)S(1)}, s32[9]{0:T(128)S(1)}) custom-call(s32[3]{0:T(128)S(1)} %pad_add_fusion.place_ref, s32[32,8,128]{2,1,0:T(8,128)S(1)} %copy.32.nb_ref, s32[8,128]{1,0:T(8,128)S(1)} %reshape.40.cnt_ref), custom_call_target="tpu_custom_call" | custom-call | tf_op jit(solution)/shard_map/sort/pallas_call | solution.py:411
  14.8 1.3 %collective-permute-start.3 = (f32[3,24,128]{2,1,0:T(8,128)S(1)}, f32[3,24,128]{2,1,0:T(8,128)S(1)}, u32[]{:S(2)}, u32[]{:S(2)}) collective-permute-start(f32[3,24,128]{2,1,0:T(8,128)S(1)} %pad_maximum_fusion.3), channel_id=1, source_target_pairs={{8,0},{16,8},{24,16},{9,1},{17,9},{25,17},{10,2},{18,10},{26,18},{... | collective-permute-start | bytes 110600 | tf_op jit(solution)/shard_map/ppermute | solution.py:438
  16.2 3.3 %collective-permute-done.3 = f32[3,24,128]{2,1,0:T(8,128)S(1)} collective-permute-done((f32[3,24,128]{2,1,0:T(8,128)S(1)}, f32[3,24,128]{2,1,0:T(8,128)S(1)}, u32[]{:S(2)}, u32[]{:S(2)}) %collective-permute-start.3) | collective-permute-done | bytes 36896 | tf_op jit(solution)/shard_map/ppermute | solution.py:438
  19.5 6.2 %collective-permute-start.4 = (f32[9,24,128]{2,1,0:T(8,128)S(1)}, f32[9,24,128]{2,1,0:T(8,128)S(1)}, u32[]{:S(2)}, u32[]{:S(2)}) collective-permute-start(f32[9,24,128]{2,1,0:T(8,128)S(1)} %constant_dynamic-update-slice_fusion.same_ref), channel_id=1, source_target_pairs={{0,1},{1,2},{2,3},{3,4},{4,5},{5,6},{6,7},{8,9},{9,10},{10,11},{11... | collective-permute-start | bytes 331784 | tf_op jit(solution)/shard_map/ppermute | solution.py:437
  25.7 1.9 %collective-permute-start.5 = (f32[9,24,128]{2,1,0:T(8,128)S(1)}, f32[9,24,128]{2,1,0:T(8,128)S(1)}, u32[]{:S(2)}, u32[]{:S(2)}) collective-permute-start(f32[9,24,128]{2,1,0:T(8,128)S(1)} %constant_dynamic-update-slice_fusion.same_ref), channel_id=1, source_target_pairs={{1,0},{2,1},{3,2},{4,3},{5,4},{6,5},{7,6},{9,8},{10,9},{11,10},{12... | collective-permute-start | bytes 331784 | tf_op jit(solution)/shard_map/ppermute | solution.py:438
  27.6 3.7 %near.1 = (s32[36,3,8,128]{3,2,1,0:T(8,128)S(1)}, f32[2,8,128]{2,1,0:T(8,128)S(1)}) custom-call(s32[9]{0:T(128)S(1)} %get-tuple-element.24.tile_ref, f32[9,24,128]{2,1,0:T(8,128)S(1)} %constant_dynamic-update-slice_fusion.same_ref, s32[288,128]{1,0:T(8,128)S(1)} %get-tuple-element.26.code_ref), custom_call_target="tpu_custom_call" | custom-call | tf_op jit(solution)/shard_map/near/pallas_call | solution.py:423
  31.4 0.4 collective-permute-done.5.above_ref
  31.8 0.7 copy-done.11
  32.5 10.8 %shard_map.235.lat_ref = bf16[8,8,1024]{2,1,0:T(8,128)(2,1)} custom-call(s32[3]{0:T(128)S(1)} %pad_add_fusion.place_ref, s32[9]{0:T(128)S(1)} %get-tuple-element.24.tile_ref, f32[9,24,128]{2,1,0:T(8,128)S(1)} %collective-permute-done.4.below_ref, f32[9,24,128]{2,1,0:T(8,128)S(1)} %collective-permute-done.5.above_ref, ...), custom_call_target="tpu_custom_call" | custom-call | tf_op jit(solution)/shard_map/pallas_call | solution.py:394
  43.3 4.7 %all-to-all-start = ((bf16[8,8,1024]{2,1,0:T(8,128)(2,1)}), bf16[8,8,1024]{2,1,0:T(8,128)(2,1)S(1)}, u32[]{:S(2)}, u32[]{:S(2)}) async-start(bf16[8,8,1024]{2,1,0:T(8,128)(2,1)} %shard_map.235.lat_ref), calls=%async_computation | async-start | bytes 262144 | tf_op jit(solution)/shard_map/all_to_all | solution.py:516
  48.0 0.7 copy-done.20
  48.8 0.1 copy_bitcast_fusion
  49.0 0.8 copy-done.15
  49.9 0.1 multiply_subtract_fusion
  50.1 3.1 %all-to-all-done.m_ref = bf16[8,8,1024]{2,1,0:T(8,128)(2,1)S(1)} async-done(((bf16[8,8,1024]{2,1,0:T(8,128)(2,1)}), bf16[8,8,1024]{2,1,0:T(8,128)(2,1)S(1)}, u32[]{:S(2)}, u32[]{:S(2)}) %all-to-all-start) | async-done | bytes 131104 | tf_op jit(solution)/shard_map/all_to_all | solution.py:516
  53.2 1.4 %shard_map.236 = bf16[512,128]{1,0:T(8,128)(2,1)} custom-call(bf16[8,8,1024]{2,1,0:T(8,128)(2,1)S(1)} %all-to-all-done.m_ref, bf16[256,512]{1,0:T(8,128)(2,1)S(1)} %copy-done.4, bf16[256,512]{1,0:T(8,128)(2,1)S(1)} %copy-done.5, bf16[256,256]{1,0:T(8,128)(2,1)S(1)} %fusion.whi_ref, bf16[256,256]{1,0:T(8,128)(2,1)S(1)} %subtract_convert_fusion.wlo_ref), custom_call_target="tpu_custom_call" | custom-call | tf_op jit(solution)/shard_map/pallas_call | solution.py:394
  54.6 14.5 %all-to-all-start.1 = ((bf16[256,2,128]{2,1,0:T(2,128)(2,1)}), bf16[256,2,128]{2,1,0:T(2,128)(2,1)S(1)}, u32[]{:S(2)}, u32[]{:S(2)}) async-start(bf16[256,2,128]{2,1,0:T(2,128)(2,1)} %bitcast.10), calls=%async_computation.1 | async-start | bytes 262144 | tf_op jit(solution)/shard_map/all_to_all | solution.py:519
  69.1 0.3 maximum_bitcast_fusion
  69.6 12.4 %all-to-all-done.1 = bf16[256,2,128]{2,1,0:T(2,128)(2,1)S(1)} async-done(((bf16[256,2,128]{2,1,0:T(2,128)(2,1)}), bf16[256,2,128]{2,1,0:T(2,128)(2,1)S(1)}, u32[]{:S(2)}, u32[]{:S(2)}) %all-to-all-start.1) | async-done | bytes 131104 | tf_op jit(solution)/shard_map/all_to_all | solution.py:519
  82.0 1.1 shard_map.237
  83.1 5.6 %all-to-all-start.2 = ((bf16[256,2,128]{2,1,0:T(2,128)(2,1)}), bf16[256,2,128]{2,1,0:T(2,128)(2,1)S(1)}, u32[]{:S(2)}, u32[]{:S(2)}) async-start(bf16[256,2,128]{2,1,0:T(2,128)(2,1)} %bitcast.20), calls=%async_computation.2 | async-start | bytes 262144 | tf_op jit(solution)/shard_map/all_to_all | solution.py:532
  88.9 12.9 %all-to-all-done.2 = bf16[256,2,128]{2,1,0:T(2,128)(2,1)S(1)} async-done(((bf16[256,2,128]{2,1,0:T(2,128)(2,1)}), bf16[256,2,128]{2,1,0:T(2,128)(2,1)S(1)}, u32[]{:S(2)}, u32[]{:S(2)}) %all-to-all-start.2) | async-done | bytes 131104 | tf_op jit(solution)/shard_map/all_to_all | solution.py:532
  101.9 1.6 %shard_map.238 = bf16[8,8,8,128]{3,2,1,0:T(8,128)(2,1)} custom-call(bf16[8,4,16,128]{3,2,1,0:T(8,128)(2,1)S(1)} %bitcast.38, bf16[256,256]{1,0:T(8,128)(2,1)S(1)} %pad_maximum_fusion.2.v_ref, bf16[512,256]{1,0:T(8,128)(2,1)S(1)} %copy-done.2, bf16[512,256]{1,0:T(8,128)(2,1)S(1)} %copy-done.3, bf16[256,256]{1,0:T(8,128)(2,1)S(1)} %copy-done.6), custom_call_target="tpu_custom_call" | custom-call | tf_op jit(solution)/shard_map/pallas_call | solution.py:394
  103.5 3.8 %all-to-all-start.3 = ((bf16[8,8,8,128]{3,2,1,0:T(8,128)(2,1)}), bf16[8,8,8,128]{3,2,1,0:T(8,128)(2,1)S(1)}, u32[]{:S(2)}, u32[]{:S(2)}) async-start(bf16[8,8,8,128]{3,2,1,0:T(8,128)(2,1)} %shard_map.238), calls=%async_computation.3 | async-start | bytes 262144 | tf_op jit(solution)/shard_map/all_to_all | solution.py:544
  107.3 0.7 copy-done.19
  108.0 4.5 %all-to-all-done.3.y_ref = bf16[8,8,8,128]{3,2,1,0:T(8,128)(2,1)S(1)} async-done(((bf16[8,8,8,128]{3,2,1,0:T(8,128)(2,1)}), bf16[8,8,8,128]{3,2,1,0:T(8,128)(2,1)S(1)}, u32[]{:S(2)}, u32[]{:S(2)}) %all-to-all-start.3) | async-done | bytes 131104 | tf_op jit(solution)/shard_map/all_to_all | solution.py:544
  112.5 2.3 %shard_map.239 = f32[128,8,64]{2,1,0:T(8,128)} custom-call(bf16[8,8,8,128]{3,2,1,0:T(8,128)(2,1)S(1)} %all-to-all-done.3.y_ref, bf16[8,8,1024]{2,1,0:T(8,128)(2,1)} %shard_map.235.lat_ref, bf16[128,64]{1,0:T(8,128)(2,1)S(1)} %pad_maximum_fusion.4.w_ref), custom_call_target="tpu_custom_call" | custom-call | tf_op jit(solution)/shard_map/pallas_call | solution.py:394
  (68 shorter events, 0.7 us)
Async XLA Ops:
  0.0 48.8 %copy-start = (bf16[2,2,2,4,64,64]{5,4,3,2,1,0:T(8,128)(2,1)S(1)}, bf16[2,2,2,4,64,64]{5,4,3,2,1,0:T(8,128)(2,1)}, u32[]{:S(2)}) copy-start(bf16[2,2,2,4,64,64]{5,4,3,2,1,0:T(8,128)(2,1)} %param.31) | copy-start | bytes 786436
  0.0 6.4 %collective-permute-start.1 = (f32[1,24,128]{2,1,0:T(8,128)}, f32[1,24,128]{2,1,0:T(8,128)S(1)}, u32[]{:S(2)}, u32[]{:S(2)}) collective-permute-start(f32[1,24,128]{2,1,0:T(8,128)} %bitcast.41), channel_id=1, source_target_pairs={{32,0},{64,32},{96,64},{128,96},{160,128},{192,160},{224,192},{33,... | collective-permute-start | bytes 36872 | tf_op jit(solution)/shard_map/ppermute | solution.py:438
  1.4 6.0 %collective-permute-start = (f32[1,24,128]{2,1,0:T(8,128)}, f32[1,24,128]{2,1,0:T(8,128)S(1)}, u32[]{:S(2)}, u32[]{:S(2)}) collective-permute-start(f32[1,24,128]{2,1,0:T(8,128)} %bitcast.42), channel_id=1, source_target_pairs={{0,32},{32,64},{64,96},{96,128},{128,160},{160,192},{192,224},{1,3... | collective-permute-start | bytes 36872 | tf_op jit(solution)/shard_map/ppermute | solution.py:437
  6.4 1.0 copy-start.17
  7.4 8.7 %collective-permute-start.2 = (f32[3,24,128]{2,1,0:T(8,128)S(1)}, f32[3,24,128]{2,1,0:T(8,128)S(1)}, u32[]{:S(2)}, u32[]{:S(2)}) collective-permute-start(f32[3,24,128]{2,1,0:T(8,128)S(1)} %pad_maximum_fusion.3), channel_id=1, source_target_pairs={{0,8},{8,16},{16,24},{1,9},{9,17},{17,25},{2,10},{10,18},{18,26},{... | collective-permute-start | bytes 110600 | tf_op jit(solution)/shard_map/ppermute | solution.py:437
  10.7 1.2 %copy-start.18 = (s32[1,8,16,8]{2,3,1,0:T(8,128)S(1)}, s32[1,8,16,8]{2,3,1,0:T(8,128)}, u32[]{:S(2)}) copy-start(s32[1,8,16,8]{2,3,1,0:T(8,128)} %param.27) | copy-start | bytes 12292
  14.8 4.7 %collective-permute-start.3 = (f32[3,24,128]{2,1,0:T(8,128)S(1)}, f32[3,24,128]{2,1,0:T(8,128)S(1)}, u32[]{:S(2)}, u32[]{:S(2)}) collective-permute-start(f32[3,24,128]{2,1,0:T(8,128)S(1)} %pad_maximum_fusion.3), channel_id=1, source_target_pairs={{8,0},{16,8},{24,16},{9,1},{17,9},{25,17},{10,2},{18,10},{26,18},{... | collective-permute-start | bytes 110600 | tf_op jit(solution)/shard_map/ppermute | solution.py:438
  19.5 12.3 %copy-start.8 = (bf16[80,80]{1,0:T(8,128)(2,1)S(1)}, bf16[80,80]{1,0:T(8,128)(2,1)}, u32[]{:S(2)}) copy-start(bf16[80,80]{1,0:T(8,128)(2,1)} %kernel_mid_ref.1) | copy-start | bytes 38404
  19.5 11.8 %collective-permute-start.4 = (f32[9,24,128]{2,1,0:T(8,128)S(1)}, f32[9,24,128]{2,1,0:T(8,128)S(1)}, u32[]{:S(2)}, u32[]{:S(2)}) collective-permute-start(f32[9,24,128]{2,1,0:T(8,128)S(1)} %constant_dynamic-update-slice_fusion.same_ref), channel_id=1, source_target_pairs={{0,1},{1,2},{2,3},{3,4},{4,5},{5,6},{6,7},{8,9},{9,10},{10,11},{11... | collective-permute-start | bytes 331784 | tf_op jit(solution)/shard_map/ppermute | solution.py:437
  25.7 6.1 %collective-permute-start.5 = (f32[9,24,128]{2,1,0:T(8,128)S(1)}, f32[9,24,128]{2,1,0:T(8,128)S(1)}, u32[]{:S(2)}, u32[]{:S(2)}) collective-permute-start(f32[9,24,128]{2,1,0:T(8,128)S(1)} %constant_dynamic-update-slice_fusion.same_ref), channel_id=1, source_target_pairs={{1,0},{2,1},{3,2},{4,3},{5,4},{6,5},{7,6},{9,8},{10,9},{11,10},{12... | collective-permute-start | bytes 331784 | tf_op jit(solution)/shard_map/ppermute | solution.py:438
  27.6 4.1 %copy-start.9 = (bf16[80,64]{0,1:T(8,128)(2,1)S(1)}, bf16[80,64]{0,1:T(8,128)(2,1)}, u32[]{:S(2)}) copy-start(bf16[80,64]{0,1:T(8,128)(2,1)} %param.30) | copy-start | bytes 30724
  43.3 4.7 %copy-start.21 = (s32[256]{0:T(256)S(1)}, s32[256]{0:T(256)}, u32[]{:S(2)}) copy-start(s32[256]{0:T(256)} %constant.82.clone) | copy-start | bytes 3076
  43.3 4.7 %copy-start.22 = (s32[256]{0:T(256)S(1)}, s32[256]{0:T(256)}, u32[]{:S(2)}) copy-start(s32[256]{0:T(256)} %constant.79.clone) | copy-start | bytes 3076
  43.3 4.7 %copy-start.23 = (s32[256]{0:T(256)S(1)}, s32[256]{0:T(256)}, u32[]{:S(2)}) copy-start(s32[256]{0:T(256)} %constant.78.clone) | copy-start | bytes 3076
  43.3 9.9 %all-to-all-start = ((bf16[8,8,1024]{2,1,0:T(8,128)(2,1)}), bf16[8,8,1024]{2,1,0:T(8,128)(2,1)S(1)}, u32[]{:S(2)}, u32[]{:S(2)}) async-start(bf16[8,8,1024]{2,1,0:T(8,128)(2,1)} %shard_map.235.lat_ref), calls=%async_computation | async-start | bytes 262144 | tf_op jit(solution)/shard_map/all_to_all | solution.py:516
  48.9 0.9 copy-start.15
  48.9 1.0 copy-start.16
  50.0 3.2 %copy-start.5 = (bf16[256,512]{1,0:T(8,128)(2,1)S(1)}, bf16[256,512]{1,0:T(8,128)(2,1)}, u32[]{:S(2)}) copy-start(bf16[256,512]{1,0:T(8,128)(2,1)} %constant.87.clone.alo_ref) | copy-start | bytes 786436
  50.0 3.2 %copy-start.4 = (bf16[256,512]{1,0:T(8,128)(2,1)S(1)}, bf16[256,512]{1,0:T(8,128)(2,1)}, u32[]{:S(2)}) copy-start(bf16[256,512]{1,0:T(8,128)(2,1)} %constant.86.clone.ahi_ref) | copy-start | bytes 786436
  54.6 27.4 %all-to-all-start.1 = ((bf16[256,2,128]{2,1,0:T(2,128)(2,1)}), bf16[256,2,128]{2,1,0:T(2,128)(2,1)S(1)}, u32[]{:S(2)}, u32[]{:S(2)}) async-start(bf16[256,2,128]{2,1,0:T(2,128)(2,1)} %bitcast.10), calls=%async_computation.1 | async-start | bytes 262144 | tf_op jit(solution)/shard_map/all_to_all | solution.py:519
  69.5 12.5 %copy-start.1 = (bf16[128,1024]{1,0:T(8,128)(2,1)S(1)}, bf16[128,1024]{1,0:T(8,128)(2,1)}, u32[]{:S(2)}) copy-start(bf16[128,1024]{1,0:T(8,128)(2,1)} %constant.89.clone.sel_ref) | copy-start | bytes 786436
  69.5 12.5 %copy-start.7 = (f32[16,1024]{1,0:T(8,128)S(1)}, f32[16,1024]{1,0:T(8,128)}, u32[]{:S(2)}) copy-start(f32[16,1024]{1,0:T(8,128)} %constant.90.clone.place_ref) | copy-start | bytes 196612
  69.5 12.5 %copy-start.10 = (f32[16,256]{1,0:T(8,128)S(1)}, f32[16,256]{1,0:T(8,128)}, u32[]{:S(2)}) copy-start(f32[16,256]{1,0:T(8,128)} %constant.88.clone.own_ref) | copy-start | bytes 49156
  69.5 12.4 %copy-start.12 = (bf16[8,16]{1,0:T(8,128)(2,1)S(1)}, bf16[8,16]{1,0:T(8,128)(2,1)}, u32[]{:S(2)}) copy-start(bf16[8,16]{1,0:T(8,128)(2,1)} %constant.91.clone.half_ref) | copy-start | bytes 772
  83.1 5.7 %copy-start.13 = (f32[128,256]{1,0:T(8,128)S(1)}, f32[128,256]{1,0:T(8,128)}, u32[]{:S(2)}) copy-start(f32[128,256]{1,0:T(8,128)} %constant.85.clone) | copy-start | bytes 393220
  83.1 5.7 %copy-start.14 = (f32[128,256]{1,0:T(8,128)S(1)}, f32[128,256]{1,0:T(8,128)}, u32[]{:S(2)}) copy-start(f32[128,256]{1,0:T(8,128)} %constant.84.clone) | copy-start | bytes 393220
  83.1 18.7 %all-to-all-start.2 = ((bf16[256,2,128]{2,1,0:T(2,128)(2,1)}), bf16[256,2,128]{2,1,0:T(2,128)(2,1)S(1)}, u32[]{:S(2)}, u32[]{:S(2)}) async-start(bf16[256,2,128]{2,1,0:T(2,128)(2,1)} %bitcast.20), calls=%async_computation.2 | async-start | bytes 262144 | tf_op jit(solution)/shard_map/all_to_all | solution.py:532
  88.8 13.0 %copy-start.2 = (bf16[512,256]{1,0:T(8,128)(2,1)S(1)}, bf16[512,256]{1,0:T(8,128)(2,1)}, u32[]{:S(2)}) copy-start(bf16[512,256]{1,0:T(8,128)(2,1)} %constant.92.clone.bc_ref) | copy-start | bytes 786436
  88.8 13.0 %copy-start.3 = (bf16[512,256]{1,0:T(8,128)(2,1)S(1)}, bf16[512,256]{1,0:T(8,128)(2,1)}, u32[]{:S(2)}) copy-start(bf16[512,256]{1,0:T(8,128)(2,1)} %constant.93.clone.bs_ref) | copy-start | bytes 786436
  88.9 13.0 %copy-start.6 = (bf16[256,256]{1,0:T(8,128)(2,1)S(1)}, bf16[256,256]{1,0:T(8,128)(2,1)}, u32[]{:S(2)}) copy-start(bf16[256,256]{1,0:T(8,128)(2,1)} %constant.94.clone.partner_ref) | copy-start | bytes 393220
  103.5 9.0 %all-to-all-start.3 = ((bf16[8,8,8,128]{3,2,1,0:T(8,128)(2,1)}), bf16[8,8,8,128]{3,2,1,0:T(8,128)(2,1)S(1)}, u32[]{:S(2)}, u32[]{:S(2)}) async-start(bf16[8,8,8,128]{3,2,1,0:T(8,128)(2,1)} %shard_map.238), calls=%async_computation.3 | async-start | bytes 262144 | tf_op jit(solution)/shard_map/all_to_all | solution.py:544
  107.3 0.7 copy-start.19
  (2 other events, 1.4 us)

commit v10 on v8

--- a/solution.py
+++ b/solution.py
@@ -122,7 +122,13 @@
     return jnp.where(r == rank, 1.0, 0.0).astype(bf16)
 
 
-def sort_kernel(place_ref, nb_ref, cnt_ref, code_ref, rank_ref, scnt_ref, tile_ref):
+def sort_kernel(
+    place_ref, nb_ref, cnt_ref, kernel_in_ref, kernel_mid_ref, code_ref, rank_ref, scnt_ref, ki_ref, km_ref, tile_ref
+):
+    ki = jnp.concatenate([kernel_in_ref[...].astype(f32), jnp.zeros((2, 80), f32)], axis=0)
+    ki_ref[...] = jnp.concatenate([ki, jnp.zeros((8, 48), f32)], axis=1).T[0:80].astype(bf16)
+    km = jnp.concatenate([kernel_mid_ref[...].astype(f32) * 0.5, jnp.zeros((80, 48), f32)], axis=1)
+    km_ref[...] = km.T[0:80].astype(bf16)
     px, py, pz = place_ref[0], place_ref[1], place_ref[2]
     j = nb_ref[...]
     owner = j >> 9
@@ -395,21 +401,23 @@
     )(*args)
 
 
-def sorted_nodes(place, near, valid):
+def sorted_nodes(place, near, valid, kernel_in, kernel_mid):
     shapes = (
         ((ROWS, 128), i32),
         ((8, 1024), i32),
         ((8, 1024), f32),
+        ((80, 8), bf16),
+        ((80, 80), bf16),
         ((9,), i32),
     )
     return pl.pallas_call(
         sort_kernel,
         out_shape=[jax.ShapeDtypeStruct(*s) for s in shapes],
-        in_specs=[SMEM, VMEM, VMEM],
-        out_specs=[VMEM] * 3 + [SMEM],
+        in_specs=[SMEM] + [VMEM] * 4,
+        out_specs=[VMEM] * 5 + [SMEM],
         compiler_params=pltpu.CompilerParams(vmem_limit_bytes=48 * 1024 * 1024),
         name="sort",
-    )(place, near, valid)
+    )(place, near, valid, kernel_in, kernel_mid)
 
 
 def near_words(tiles, same, code):
@@ -447,14 +455,12 @@
     own = point_data.reshape(1, 24, 128)
     near = neighbours[0].transpose(3, 2, 0, 1).reshape(NB, 8, 128)
     valid = counts[0].transpose(2, 0, 1).reshape(8, 128)
-    ki = jnp.pad(kernel_in.T, ((0, 0), (0, 2)))
-    km = kernel_mid.T * jnp.bfloat16(0.5)
 
     line = jnp.concatenate(beside(own, "gx"), axis=0)
     plane = jnp.concatenate(beside(line, "gy"), axis=0)
-    tables = sorted_nodes(place, near, valid)
+    tables = sorted_nodes(place, near, valid, kernel_in, kernel_mid)
     plane, tables = lax.optimization_barrier((plane, tables))
-    code, rank, sorted_counts, tiles = tables
+    code, rank, sorted_counts, ki, km, tiles = tables
     below, same, above = beside(plane, GZ)
     words, units = near_words(tiles, same, code)
     latent = call(
@@ -481,6 +487,7 @@
         smem=2,
     )
 
+    latent, spectral, gx, gy = lax.optimization_barrier((latent, spectral, gx, gy))
     (ffi, ffj), (ifi, ifj), xl, yl = plane_tables()
     local = angle(1, ffi[:, None] * xl[None, :] + ffj[:, None] * yl[None, :])
     phase = ((jnp.asarray(ffi, i32) * 8 * gx + jnp.asarray(ffj, i32) * 16 * gy) % GRID).astype(f32)

time: 117 us -> 115 us (0.983)
  waiting for transfers between devices: 39.4 us -> 37.8 us
    all_to_all x1, waiting for transfers between devices: 5.22 us -> 3.12 us  [layer(): depth = lax.all_to_all(latent, GZ, split_axis=0, concat_axis=0)]
    unnamed x54 -> x52, local copies, waits for them, and re-layouts: 4.58 us -> 3.03 us
where the time goes in v10:
time: 115 us
  starting transfers between devices  47.4 us (41%)
  waiting for transfers between devices  37.8 us (33%)
  Pallas kernels  23.7 us (21%)
  local copies, waits for them, and re-layouts  4.6 us (4%)
    pallas_call x5, Pallas kernels, call(): pl.pallas_call(kernel, out_shape=jax.ShapeDtypeStruct(shape, dtype), in_s...  17.3 us
    all_to_all x1, starting transfers between devices, layer(): lax.all_to_all(partial.reshape(256, 2, 128), ALL, split_axis=0, concat_ax...  14.5 us
    ppermute x3, starting transfers between devices, beside(): lower = lax.ppermute(cells, axis, [(i, i + 1) for i in range(ends)])  14.2 us
    all_to_all x1, waiting for transfers between devices, layer(): lax.all_to_all(mixed.reshape(256, 2, 128), ALL, split_axis=0, concat_axis=0)  12.9 us
    all_to_all x1, waiting for transfers between devices, layer(): lax.all_to_all(partial.reshape(256, 2, 128), ALL, split_axis=0, concat_ax...  12.4 us
    all_to_all x1, starting transfers between devices, layer(): lax.all_to_all(mixed.reshape(256, 2, 128), ALL, split_axis=0, concat_axis=0)  5.64 us
    all_to_all x1, starting transfers between devices, layer(): depth = lax.all_to_all(latent, GZ, split_axis=0, concat_axis=0)  4.69 us
    ppermute x3, starting transfers between devices, beside(): upper = lax.ppermute(cells, axis, [(i + 1, i) for i in range(ends)])  4.62 us
  transfers between devices with their start and end apart: 10, of which 7 were waited for; matrix products, arithmetic and copies ran while one was open for 2% of the time, Pallas kernels for 6%

profile of v10, /device:TPU:1, one launch (start us, length us, event | category | flops | bytes accessed | tf_op | source)
XLA Modules:
  0.0 114.7 jit_solution(3161621276086504334)
XLA Ops:
  0.0 1.4 %collective-permute-start.1 = (f32[1,24,128]{2,1,0:T(8,128)}, f32[1,24,128]{2,1,0:T(8,128)S(1)}, u32[]{:S(2)}, u32[]{:S(2)}) collective-permute-start(f32[1,24,128]{2,1,0:T(8,128)} %bitcast.41), channel_id=1, source_target_pairs={{32,0},{64,32},{96,64},{128,96},{160,128},{192,160},{224,192},{33,... | collective-permute-start | bytes 36872 | tf_op jit(solution)/shard_map/ppermute | solution.py:440
  1.4 5.0 %collective-permute-start = (f32[1,24,128]{2,1,0:T(8,128)}, f32[1,24,128]{2,1,0:T(8,128)S(1)}, u32[]{:S(2)}, u32[]{:S(2)}) collective-permute-start(f32[1,24,128]{2,1,0:T(8,128)} %bitcast.42), channel_id=1, source_target_pairs={{0,32},{32,64},{64,96},{96,128},{128,160},{160,192},{192,224},{1,3... | collective-permute-start | bytes 36872 | tf_op jit(solution)/shard_map/ppermute | solution.py:439
  6.4 1.0 collective-permute-done
  7.4 3.2 %collective-permute-start.2 = (f32[3,24,128]{2,1,0:T(8,128)S(1)}, f32[3,24,128]{2,1,0:T(8,128)S(1)}, u32[]{:S(2)}, u32[]{:S(2)}) collective-permute-start(f32[3,24,128]{2,1,0:T(8,128)S(1)} %pad_maximum_fusion.3), channel_id=1, source_target_pairs={{0,8},{8,16},{16,24},{1,9},{9,17},{17,25},{2,10},{10,18},{18,26},{... | collective-permute-start | bytes 110600 | tf_op jit(solution)/shard_map/ppermute | solution.py:439
  10.7 1.2 %copy.32.nb_ref = s32[32,8,128]{2,1,0:T(8,128)S(1)} copy(s32[32,8,128]{0,1,2:T(8,128)} %bitcast.40) | data formatting | bytes 262144 | tf_op jit(solution)/shard_map/reshape | solution.py:456
  12.1 0.6 copy-done.8
  12.7 2.7 %sort.1 = (s32[288,128]{1,0:T(8,128)S(1)}, s32[8,1024]{1,0:T(8,128)S(1)}, f32[8,1024]{1,0:T(8,128)S(1)}, bf16[80,8]{1,0:T(8,128)(2,1)S(1)}, bf16[80,80]{1,0:T(8,128)(2,1)S(1)}, /*index=5*/s32[9]{0:T(128)S(1)}) custom-call(s32[3]{0:T(128)S(1)} %pad_add_fusion.place_ref, s32[32,8,128]{2,1,0:T(8,128)S(1)} %copy.32.nb_ref, s32[8,128]{1,0:T(8,128)S(1)} %reshape.40.cnt_ref, ...), custom_call_target="tpu_custom_call" | custom-call | tf_op jit(solution)/shard_map/sort/pallas_call | solution.py:413
  15.5 1.3 %collective-permute-start.3 = (f32[3,24,128]{2,1,0:T(8,128)S(1)}, f32[3,24,128]{2,1,0:T(8,128)S(1)}, u32[]{:S(2)}, u32[]{:S(2)}) collective-permute-start(f32[3,24,128]{2,1,0:T(8,128)S(1)} %pad_maximum_fusion.3), channel_id=1, source_target_pairs={{8,0},{16,8},{24,16},{9,1},{17,9},{25,17},{10,2},{18,10},{26,18},{... | collective-permute-start | bytes 110600 | tf_op jit(solution)/shard_map/ppermute | solution.py:440
  16.8 3.3 %collective-permute-done.3 = f32[3,24,128]{2,1,0:T(8,128)S(1)} collective-permute-done((f32[3,24,128]{2,1,0:T(8,128)S(1)}, f32[3,24,128]{2,1,0:T(8,128)S(1)}, u32[]{:S(2)}, u32[]{:S(2)}) %collective-permute-start.3) | collective-permute-done | bytes 36896 | tf_op jit(solution)/shard_map/ppermute | solution.py:440
  20.2 6.0 %collective-permute-start.4 = (f32[9,24,128]{2,1,0:T(8,128)S(1)}, f32[9,24,128]{2,1,0:T(8,128)S(1)}, u32[]{:S(2)}, u32[]{:S(2)}) collective-permute-start(f32[9,24,128]{2,1,0:T(8,128)S(1)} %constant_dynamic-update-slice_fusion.same_ref), channel_id=1, source_target_pairs={{0,1},{1,2},{2,3},{3,4},{4,5},{5,6},{6,7},{8,9},{9,10},{10,11},{11... | collective-permute-start | bytes 331784 | tf_op jit(solution)/shard_map/ppermute | solution.py:439
  26.2 1.9 %collective-permute-start.5 = (f32[9,24,128]{2,1,0:T(8,128)S(1)}, f32[9,24,128]{2,1,0:T(8,128)S(1)}, u32[]{:S(2)}, u32[]{:S(2)}) collective-permute-start(f32[9,24,128]{2,1,0:T(8,128)S(1)} %constant_dynamic-update-slice_fusion.same_ref), channel_id=1, source_target_pairs={{1,0},{2,1},{3,2},{4,3},{5,4},{6,5},{7,6},{9,8},{10,9},{11,10},{12... | collective-permute-start | bytes 331784 | tf_op jit(solution)/shard_map/ppermute | solution.py:440
  28.2 3.7 %near.1 = (s32[36,3,8,128]{3,2,1,0:T(8,128)S(1)}, f32[2,8,128]{2,1,0:T(8,128)S(1)}) custom-call(s32[9]{0:T(128)S(1)} %get-tuple-element.30.tile_ref, f32[9,24,128]{2,1,0:T(8,128)S(1)} %constant_dynamic-update-slice_fusion.same_ref, s32[288,128]{1,0:T(8,128)S(1)} %get-tuple-element.32.code_ref), custom_call_target="tpu_custom_call" | custom-call | tf_op jit(solution)/shard_map/near/pallas_call | solution.py:425
  31.9 0.4 collective-permute-done.5.above_ref
  32.3 10.9 %shard_map.235.lat_ref = bf16[8,8,1024]{2,1,0:T(8,128)(2,1)} custom-call(s32[3]{0:T(128)S(1)} %pad_add_fusion.place_ref, s32[9]{0:T(128)S(1)} %get-tuple-element.30.tile_ref, f32[9,24,128]{2,1,0:T(8,128)S(1)} %collective-permute-done.4.below_ref, f32[9,24,128]{2,1,0:T(8,128)S(1)} %collective-permute-done.5.above_ref, ...), custom_call_target="tpu_custom_call" | custom-call | tf_op jit(solution)/shard_map/pallas_call | solution.py:394
  43.2 4.7 %all-to-all-start = ((bf16[8,8,1024]{2,1,0:T(8,128)(2,1)}), bf16[8,8,1024]{2,1,0:T(8,128)(2,1)S(1)}, u32[]{:S(2)}, u32[]{:S(2)}) async-start(bf16[8,8,1024]{2,1,0:T(8,128)(2,1)} %shard_map.235.lat_ref), calls=%async_computation | async-start | bytes 262144 | tf_op jit(solution)/shard_map/all_to_all | solution.py:516
  47.9 0.7 copy-done.20
  48.7 0.1 copy_bitcast_fusion
  48.9 0.8 copy-done.15
  49.8 0.1 multiply_subtract_fusion
  50.0 3.1 %all-to-all-done.m_ref = bf16[8,8,1024]{2,1,0:T(8,128)(2,1)S(1)} async-done(((bf16[8,8,1024]{2,1,0:T(8,128)(2,1)}), bf16[8,8,1024]{2,1,0:T(8,128)(2,1)S(1)}, u32[]{:S(2)}, u32[]{:S(2)}) %all-to-all-start) | async-done | bytes 131104 | tf_op jit(solution)/shard_map/all_to_all | solution.py:516
  53.1 1.4 %shard_map.236 = bf16[512,128]{1,0:T(8,128)(2,1)} custom-call(bf16[8,8,1024]{2,1,0:T(8,128)(2,1)S(1)} %all-to-all-done.m_ref, bf16[256,512]{1,0:T(8,128)(2,1)S(1)} %copy-done.4, bf16[256,512]{1,0:T(8,128)(2,1)S(1)} %copy-done.5, bf16[256,256]{1,0:T(8,128)(2,1)S(1)} %fusion.whi_ref, bf16[256,256]{1,0:T(8,128)(2,1)S(1)} %subtract_convert_fusion.wlo_ref), custom_call_target="tpu_custom_call" | custom-call | tf_op jit(solution)/shard_map/pallas_call | solution.py:394
  54.5 14.5 %all-to-all-start.1 = ((bf16[256,2,128]{2,1,0:T(2,128)(2,1)}), bf16[256,2,128]{2,1,0:T(2,128)(2,1)S(1)}, u32[]{:S(2)}, u32[]{:S(2)}) async-start(bf16[256,2,128]{2,1,0:T(2,128)(2,1)} %bitcast.10), calls=%async_computation.1 | async-start | bytes 262144 | tf_op jit(solution)/shard_map/all_to_all | solution.py:519
  69.0 0.3 maximum_bitcast_fusion
  69.5 12.4 %all-to-all-done.1 = bf16[256,2,128]{2,1,0:T(2,128)(2,1)S(1)} async-done(((bf16[256,2,128]{2,1,0:T(2,128)(2,1)}), bf16[256,2,128]{2,1,0:T(2,128)(2,1)S(1)}, u32[]{:S(2)}, u32[]{:S(2)}) %all-to-all-start.1) | async-done | bytes 131104 | tf_op jit(solution)/shard_map/all_to_all | solution.py:519
  81.9 1.1 shard_map.237
  83.0 5.6 %all-to-all-start.2 = ((bf16[256,2,128]{2,1,0:T(2,128)(2,1)}), bf16[256,2,128]{2,1,0:T(2,128)(2,1)S(1)}, u32[]{:S(2)}, u32[]{:S(2)}) async-start(bf16[256,2,128]{2,1,0:T(2,128)(2,1)} %bitcast.20), calls=%async_computation.2 | async-start | bytes 262144 | tf_op jit(solution)/shard_map/all_to_all | solution.py:532
  88.8 12.9 %all-to-all-done.2 = bf16[256,2,128]{2,1,0:T(2,128)(2,1)S(1)} async-done(((bf16[256,2,128]{2,1,0:T(2,128)(2,1)}), bf16[256,2,128]{2,1,0:T(2,128)(2,1)S(1)}, u32[]{:S(2)}, u32[]{:S(2)}) %all-to-all-start.2) | async-done | bytes 131104 | tf_op jit(solution)/shard_map/all_to_all | solution.py:532
  101.8 1.6 %shard_map.238 = bf16[8,8,8,128]{3,2,1,0:T(8,128)(2,1)} custom-call(bf16[8,4,16,128]{3,2,1,0:T(8,128)(2,1)S(1)} %bitcast.38, bf16[256,256]{1,0:T(8,128)(2,1)S(1)} %pad_maximum_fusion.2.v_ref, bf16[512,256]{1,0:T(8,128)(2,1)S(1)} %copy-done.2, bf16[512,256]{1,0:T(8,128)(2,1)S(1)} %copy-done.3, bf16[256,256]{1,0:T(8,128)(2,1)S(1)} %copy-done.6), custom_call_target="tpu_custom_call" | custom-call | tf_op jit(solution)/shard_map/pallas_call | solution.py:394
  103.4 3.8 %all-to-all-start.3 = ((bf16[8,8,8,128]{3,2,1,0:T(8,128)(2,1)}), bf16[8,8,8,128]{3,2,1,0:T(8,128)(2,1)S(1)}, u32[]{:S(2)}, u32[]{:S(2)}) async-start(bf16[8,8,8,128]{3,2,1,0:T(8,128)(2,1)} %shard_map.238), calls=%async_computation.3 | async-start | bytes 262144 | tf_op jit(solution)/shard_map/all_to_all | solution.py:544
  107.2 0.7 copy-done.19
  107.9 4.5 %all-to-all-done.3.y_ref = bf16[8,8,8,128]{3,2,1,0:T(8,128)(2,1)S(1)} async-done(((bf16[8,8,8,128]{3,2,1,0:T(8,128)(2,1)}), bf16[8,8,8,128]{3,2,1,0:T(8,128)(2,1)S(1)}, u32[]{:S(2)}, u32[]{:S(2)}) %all-to-all-start.3) | async-done | bytes 131104 | tf_op jit(solution)/shard_map/all_to_all | solution.py:544
  112.4 2.3 %shard_map.239 = f32[128,8,64]{2,1,0:T(8,128)} custom-call(bf16[8,8,8,128]{3,2,1,0:T(8,128)(2,1)S(1)} %all-to-all-done.3.y_ref, bf16[8,8,1024]{2,1,0:T(8,128)(2,1)} %shard_map.235.lat_ref, bf16[128,64]{1,0:T(8,128)(2,1)S(1)} %pad_maximum_fusion.4.w_ref), custom_call_target="tpu_custom_call" | custom-call | tf_op jit(solution)/shard_map/pallas_call | solution.py:394
  (68 shorter events, 0.7 us)
Async XLA Ops:
  0.0 48.7 %copy-start = (bf16[2,2,2,4,64,64]{5,4,3,2,1,0:T(8,128)(2,1)S(1)}, bf16[2,2,2,4,64,64]{5,4,3,2,1,0:T(8,128)(2,1)}, u32[]{:S(2)}) copy-start(bf16[2,2,2,4,64,64]{5,4,3,2,1,0:T(8,128)(2,1)} %param.31) | copy-start | bytes 786436
  0.0 6.4 %collective-permute-start.1 = (f32[1,24,128]{2,1,0:T(8,128)}, f32[1,24,128]{2,1,0:T(8,128)S(1)}, u32[]{:S(2)}, u32[]{:S(2)}) collective-permute-start(f32[1,24,128]{2,1,0:T(8,128)} %bitcast.41), channel_id=1, source_target_pairs={{32,0},{64,32},{96,64},{128,96},{160,128},{192,160},{224,192},{33,... | collective-permute-start | bytes 36872 | tf_op jit(solution)/shard_map/ppermute | solution.py:440
  1.4 6.0 %collective-permute-start = (f32[1,24,128]{2,1,0:T(8,128)}, f32[1,24,128]{2,1,0:T(8,128)S(1)}, u32[]{:S(2)}, u32[]{:S(2)}) collective-permute-start(f32[1,24,128]{2,1,0:T(8,128)} %bitcast.42), channel_id=1, source_target_pairs={{0,32},{32,64},{64,96},{96,128},{128,160},{160,192},{192,224},{1,3... | collective-permute-start | bytes 36872 | tf_op jit(solution)/shard_map/ppermute | solution.py:439
  6.4 1.0 copy-start.17
  7.4 9.3 %collective-permute-start.2 = (f32[3,24,128]{2,1,0:T(8,128)S(1)}, f32[3,24,128]{2,1,0:T(8,128)S(1)}, u32[]{:S(2)}, u32[]{:S(2)}) collective-permute-start(f32[3,24,128]{2,1,0:T(8,128)S(1)} %pad_maximum_fusion.3), channel_id=1, source_target_pairs={{0,8},{8,16},{16,24},{1,9},{9,17},{17,25},{2,10},{10,18},{18,26},{... | collective-permute-start | bytes 110600 | tf_op jit(solution)/shard_map/ppermute | solution.py:439
  10.7 1.2 %copy-start.18 = (s32[1,8,16,8]{2,3,1,0:T(8,128)S(1)}, s32[1,8,16,8]{2,3,1,0:T(8,128)}, u32[]{:S(2)}) copy-start(s32[1,8,16,8]{2,3,1,0:T(8,128)} %param.27) | copy-start | bytes 12292
  12.0 0.7 copy-start.8
  12.0 0.7 copy-start.11
  15.5 4.7 %collective-permute-start.3 = (f32[3,24,128]{2,1,0:T(8,128)S(1)}, f32[3,24,128]{2,1,0:T(8,128)S(1)}, u32[]{:S(2)}, u32[]{:S(2)}) collective-permute-start(f32[3,24,128]{2,1,0:T(8,128)S(1)} %pad_maximum_fusion.3), channel_id=1, source_target_pairs={{8,0},{16,8},{24,16},{9,1},{17,9},{25,17},{10,2},{18,10},{26,18},{... | collective-permute-start | bytes 110600 | tf_op jit(solution)/shard_map/ppermute | solution.py:440
  20.2 11.7 %collective-permute-start.4 = (f32[9,24,128]{2,1,0:T(8,128)S(1)}, f32[9,24,128]{2,1,0:T(8,128)S(1)}, u32[]{:S(2)}, u32[]{:S(2)}) collective-permute-start(f32[9,24,128]{2,1,0:T(8,128)S(1)} %constant_dynamic-update-slice_fusion.same_ref), channel_id=1, source_target_pairs={{0,1},{1,2},{2,3},{3,4},{4,5},{5,6},{6,7},{8,9},{9,10},{10,11},{11... | collective-permute-start | bytes 331784 | tf_op jit(solution)/shard_map/ppermute | solution.py:439
  26.2 6.1 %collective-permute-start.5 = (f32[9,24,128]{2,1,0:T(8,128)S(1)}, f32[9,24,128]{2,1,0:T(8,128)S(1)}, u32[]{:S(2)}, u32[]{:S(2)}) collective-permute-start(f32[9,24,128]{2,1,0:T(8,128)S(1)} %constant_dynamic-update-slice_fusion.same_ref), channel_id=1, source_target_pairs={{1,0},{2,1},{3,2},{4,3},{5,4},{6,5},{7,6},{9,8},{10,9},{11,10},{12... | collective-permute-start | bytes 331784 | tf_op jit(solution)/shard_map/ppermute | solution.py:440
  28.2 4.1 %copy-start.9 = (bf16[80,64]{0,1:T(8,128)(2,1)S(1)}, bf16[80,64]{0,1:T(8,128)(2,1)}, u32[]{:S(2)}) copy-start(bf16[80,64]{0,1:T(8,128)(2,1)} %param.30) | copy-start | bytes 30724
  43.2 4.7 %copy-start.21 = (s32[256]{0:T(256)S(1)}, s32[256]{0:T(256)}, u32[]{:S(2)}) copy-start(s32[256]{0:T(256)} %constant.82.clone) | copy-start | bytes 3076
  43.2 4.7 %copy-start.22 = (s32[256]{0:T(256)S(1)}, s32[256]{0:T(256)}, u32[]{:S(2)}) copy-start(s32[256]{0:T(256)} %constant.79.clone) | copy-start | bytes 3076
  43.2 4.7 %copy-start.23 = (s32[256]{0:T(256)S(1)}, s32[256]{0:T(256)}, u32[]{:S(2)}) copy-start(s32[256]{0:T(256)} %constant.78.clone) | copy-start | bytes 3076
  43.2 9.9 %all-to-all-start = ((bf16[8,8,1024]{2,1,0:T(8,128)(2,1)}), bf16[8,8,1024]{2,1,0:T(8,128)(2,1)S(1)}, u32[]{:S(2)}, u32[]{:S(2)}) async-start(bf16[8,8,1024]{2,1,0:T(8,128)(2,1)} %shard_map.235.lat_ref), calls=%async_computation | async-start | bytes 262144 | tf_op jit(solution)/shard_map/all_to_all | solution.py:516
  48.8 0.9 copy-start.15
  48.8 1.0 copy-start.16
  49.9 3.2 %copy-start.5 = (bf16[256,512]{1,0:T(8,128)(2,1)S(1)}, bf16[256,512]{1,0:T(8,128)(2,1)}, u32[]{:S(2)}) copy-start(bf16[256,512]{1,0:T(8,128)(2,1)} %constant.87.clone.alo_ref) | copy-start | bytes 786436
  50.0 3.2 %copy-start.4 = (bf16[256,512]{1,0:T(8,128)(2,1)S(1)}, bf16[256,512]{1,0:T(8,128)(2,1)}, u32[]{:S(2)}) copy-start(bf16[256,512]{1,0:T(8,128)(2,1)} %constant.86.clone.ahi_ref) | copy-start | bytes 786436
  54.5 27.4 %all-to-all-start.1 = ((bf16[256,2,128]{2,1,0:T(2,128)(2,1)}), bf16[256,2,128]{2,1,0:T(2,128)(2,1)S(1)}, u32[]{:S(2)}, u32[]{:S(2)}) async-start(bf16[256,2,128]{2,1,0:T(2,128)(2,1)} %bitcast.10), calls=%async_computation.1 | async-start | bytes 262144 | tf_op jit(solution)/shard_map/all_to_all | solution.py:519
  69.4 12.5 %copy-start.1 = (bf16[128,1024]{1,0:T(8,128)(2,1)S(1)}, bf16[128,1024]{1,0:T(8,128)(2,1)}, u32[]{:S(2)}) copy-start(bf16[128,1024]{1,0:T(8,128)(2,1)} %constant.89.clone.sel_ref) | copy-start | bytes 786436
  69.4 12.5 %copy-start.7 = (f32[16,1024]{1,0:T(8,128)S(1)}, f32[16,1024]{1,0:T(8,128)}, u32[]{:S(2)}) copy-start(f32[16,1024]{1,0:T(8,128)} %constant.90.clone.place_ref) | copy-start | bytes 196612
  69.4 12.5 %copy-start.10 = (f32[16,256]{1,0:T(8,128)S(1)}, f32[16,256]{1,0:T(8,128)}, u32[]{:S(2)}) copy-start(f32[16,256]{1,0:T(8,128)} %constant.88.clone.own_ref) | copy-start | bytes 49156
  69.5 12.4 %copy-start.12 = (bf16[8,16]{1,0:T(8,128)(2,1)S(1)}, bf16[8,16]{1,0:T(8,128)(2,1)}, u32[]{:S(2)}) copy-start(bf16[8,16]{1,0:T(8,128)(2,1)} %constant.91.clone.half_ref) | copy-start | bytes 772
  83.0 5.7 %copy-start.13 = (f32[128,256]{1,0:T(8,128)S(1)}, f32[128,256]{1,0:T(8,128)}, u32[]{:S(2)}) copy-start(f32[128,256]{1,0:T(8,128)} %constant.85.clone) | copy-start | bytes 393220
  83.0 5.7 %copy-start.14 = (f32[128,256]{1,0:T(8,128)S(1)}, f32[128,256]{1,0:T(8,128)}, u32[]{:S(2)}) copy-start(f32[128,256]{1,0:T(8,128)} %constant.84.clone) | copy-start | bytes 393220
  83.0 18.7 %all-to-all-start.2 = ((bf16[256,2,128]{2,1,0:T(2,128)(2,1)}), bf16[256,2,128]{2,1,0:T(2,128)(2,1)S(1)}, u32[]{:S(2)}, u32[]{:S(2)}) async-start(bf16[256,2,128]{2,1,0:T(2,128)(2,1)} %bitcast.20), calls=%async_computation.2 | async-start | bytes 262144 | tf_op jit(solution)/shard_map/all_to_all | solution.py:532
  88.7 13.0 %copy-start.2 = (bf16[512,256]{1,0:T(8,128)(2,1)S(1)}, bf16[512,256]{1,0:T(8,128)(2,1)}, u32[]{:S(2)}) copy-start(bf16[512,256]{1,0:T(8,128)(2,1)} %constant.92.clone.bc_ref) | copy-start | bytes 786436
  88.7 13.0 %copy-start.3 = (bf16[512,256]{1,0:T(8,128)(2,1)S(1)}, bf16[512,256]{1,0:T(8,128)(2,1)}, u32[]{:S(2)}) copy-start(bf16[512,256]{1,0:T(8,128)(2,1)} %constant.93.clone.bs_ref) | copy-start | bytes 786436
  88.8 13.0 %copy-start.6 = (bf16[256,256]{1,0:T(8,128)(2,1)S(1)}, bf16[256,256]{1,0:T(8,128)(2,1)}, u32[]{:S(2)}) copy-start(bf16[256,256]{1,0:T(8,128)(2,1)} %constant.94.clone.partner_ref) | copy-start | bytes 393220
  103.4 9.0 %all-to-all-start.3 = ((bf16[8,8,8,128]{3,2,1,0:T(8,128)(2,1)}), bf16[8,8,8,128]{3,2,1,0:T(8,128)(2,1)S(1)}, u32[]{:S(2)}, u32[]{:S(2)}) async-start(bf16[8,8,8,128]{3,2,1,0:T(8,128)(2,1)} %shard_map.238), calls=%async_computation.3 | async-start | bytes 262144 | tf_op jit(solution)/shard_map/all_to_all | solution.py:544
  (2 other events, 1.4 us)

commit v11 on v10

--- a/solution.py
+++ b/solution.py
@@ -178,7 +178,7 @@
     tile_ref[8] = (end + 15) >> 4
 
 
-def pair_sums(place_ref, tile_ref, code_ref, look_up, ki_ref, km_ref, turn, acc_ref):
+def pair_sums(place_ref, tile_ref, code_ref, look_up, ki_ref, km_ref, turn, acc_refs):
     px, py, pz = place_ref[0], place_ref[1], place_ref[2]
     x0 = px.astype(f32) * 8.0 + 0.5
     y0 = py.astype(f32) * 16.0 + 0.5
@@ -211,7 +211,7 @@
         hidden = gelu_twice(dot(km_ref[...], hidden))
         for r in range(16):
             tile = sum((b * 16 + r >= end).astype(i32) for end in ends)
-            acc_ref[tile] += hidden[:, r * 128 : r * 128 + 128]
+            acc_refs[r % 2][tile] += hidden[:, r * 128 : r * 128 + 128]
 
     def step(b, pair):
         following = gather(b + 1)
@@ -288,11 +288,13 @@
     out_ref,
     words,
     turn,
-    acc_ref,
+    even_ref,
+    odd_ref,
 ):
     far_place, far_normal = packed((below_ref, above_ref), words)
     near_place, near_normal = unit_ref[0], unit_ref[1]
-    acc_ref[...] = jnp.zeros(acc_ref.shape, f32)
+    for ref in (even_ref, odd_ref):
+        ref[...] = jnp.zeros(ref.shape, f32)
 
     def look_up(code, block):
         near = (code & 16383) >= 72 * 128
@@ -305,8 +307,8 @@
             values[c + 3] = ((word & 65535) - 32768).astype(f32) * lower
         return values
 
-    pair_sums(place_ref, tile_ref, code_ref, look_up, ki_ref, km_ref, turn, acc_ref)
-    mean = jnp.concatenate([acc_ref[t] for t in range(8)], axis=1) * (0.5 / scnt_ref[0:1])
+    pair_sums(place_ref, tile_ref, code_ref, look_up, ki_ref, km_ref, turn, (even_ref, odd_ref))
+    mean = jnp.concatenate([even_ref[t] + odd_ref[t] for t in range(8)], axis=1) * (0.5 / scnt_ref[0:1])
     upper = mean.astype(bf16)
     lower = (mean - upper.astype(f32)).astype(bf16)
     latent = (dot(ko_ref[...], upper) + dot(ko_ref[...], lower)).astype(bf16)
@@ -483,6 +485,7 @@
             pltpu.VMEM((18, 12, 128), i32),
             pltpu.VMEM((2, 8, 8, 128), f32),
             pltpu.VMEM((8, 80, 128), f32),
+            pltpu.VMEM((8, 80, 128), f32),
         ),
         smem=2,
     )

time: 115 us -> 114 us (level)
  no operation moved by 1% of the time
where the time goes in v11:
time: 114 us
  starting transfers between devices  47.4 us (42%)
  waiting for transfers between devices  37.8 us (33%)
  Pallas kernels  22.8 us (20%)
  local copies, waits for them, and re-layouts  4.6 us (4%)
    pallas_call x5, Pallas kernels, call(): pl.pallas_call(kernel, out_shape=jax.ShapeDtypeStruct(shape, dtype), in_s...  16.3 us
    all_to_all x1, starting transfers between devices, layer(): lax.all_to_all(partial.reshape(256, 2, 128), ALL, split_axis=0, concat_ax...  14.5 us
    ppermute x3, starting transfers between devices, beside(): lower = lax.ppermute(cells, axis, [(i, i + 1) for i in range(ends)])  14.2 us
    all_to_all x1, waiting for transfers between devices, layer(): lax.all_to_all(mixed.reshape(256, 2, 128), ALL, split_axis=0, concat_axis=0)  12.9 us
    all_to_all x1, waiting for transfers between devices, layer(): lax.all_to_all(partial.reshape(256, 2, 128), ALL, split_axis=0, concat_ax...  12.4 us
    all_to_all x1, starting transfers between devices, layer(): lax.all_to_all(mixed.reshape(256, 2, 128), ALL, split_axis=0, concat_axis=0)  5.64 us
    all_to_all x1, starting transfers between devices, layer(): depth = lax.all_to_all(latent, GZ, split_axis=0, concat_axis=0)  4.68 us
    ppermute x3, starting transfers between devices, beside(): upper = lax.ppermute(cells, axis, [(i + 1, i) for i in range(ends)])  4.62 us
  transfers between devices with their start and end apart: 10, of which 7 were waited for; matrix products, arithmetic and copies ran while one was open for 2% of the time, Pallas kernels for 6%

profile of v11, /device:TPU:1, one launch (start us, length us, event | category | flops | bytes accessed | tf_op | source)
XLA Modules:
  0.0 113.8 jit_solution(8929428572393228283)
XLA Ops:
  0.0 1.4 %collective-permute-start.1 = (f32[1,24,128]{2,1,0:T(8,128)}, f32[1,24,128]{2,1,0:T(8,128)S(1)}, u32[]{:S(2)}, u32[]{:S(2)}) collective-permute-start(f32[1,24,128]{2,1,0:T(8,128)} %bitcast.41), channel_id=1, source_target_pairs={{32,0},{64,32},{96,64},{128,96},{160,128},{192,160},{224,192},{33,... | collective-permute-start | bytes 36872 | tf_op jit(solution)/shard_map/ppermute | solution.py:442
  1.4 5.0 %collective-permute-start = (f32[1,24,128]{2,1,0:T(8,128)}, f32[1,24,128]{2,1,0:T(8,128)S(1)}, u32[]{:S(2)}, u32[]{:S(2)}) collective-permute-start(f32[1,24,128]{2,1,0:T(8,128)} %bitcast.42), channel_id=1, source_target_pairs={{0,32},{32,64},{64,96},{96,128},{128,160},{160,192},{192,224},{1,3... | collective-permute-start | bytes 36872 | tf_op jit(solution)/shard_map/ppermute | solution.py:441
  6.4 1.0 collective-permute-done
  7.4 3.2 %collective-permute-start.2 = (f32[3,24,128]{2,1,0:T(8,128)S(1)}, f32[3,24,128]{2,1,0:T(8,128)S(1)}, u32[]{:S(2)}, u32[]{:S(2)}) collective-permute-start(f32[3,24,128]{2,1,0:T(8,128)S(1)} %pad_maximum_fusion.3), channel_id=1, source_target_pairs={{0,8},{8,16},{16,24},{1,9},{9,17},{17,25},{2,10},{10,18},{18,26},{... | collective-permute-start | bytes 110600 | tf_op jit(solution)/shard_map/ppermute | solution.py:441
  10.7 1.2 %copy.32.nb_ref = s32[32,8,128]{2,1,0:T(8,128)S(1)} copy(s32[32,8,128]{0,1,2:T(8,128)} %bitcast.40) | data formatting | bytes 262144 | tf_op jit(solution)/shard_map/reshape | solution.py:458
  12.1 0.6 copy-done.8
  12.7 2.7 %sort.1 = (s32[288,128]{1,0:T(8,128)S(1)}, s32[8,1024]{1,0:T(8,128)S(1)}, f32[8,1024]{1,0:T(8,128)S(1)}, bf16[80,8]{1,0:T(8,128)(2,1)S(1)}, bf16[80,80]{1,0:T(8,128)(2,1)S(1)}, /*index=5*/s32[9]{0:T(128)S(1)}) custom-call(s32[3]{0:T(128)S(1)} %pad_add_fusion.place_ref, s32[32,8,128]{2,1,0:T(8,128)S(1)} %copy.32.nb_ref, s32[8,128]{1,0:T(8,128)S(1)} %reshape.40.cnt_ref, ...), custom_call_target="tpu_custom_call" | custom-call | tf_op jit(solution)/shard_map/sort/pallas_call | solution.py:415
  15.5 1.3 %collective-permute-start.3 = (f32[3,24,128]{2,1,0:T(8,128)S(1)}, f32[3,24,128]{2,1,0:T(8,128)S(1)}, u32[]{:S(2)}, u32[]{:S(2)}) collective-permute-start(f32[3,24,128]{2,1,0:T(8,128)S(1)} %pad_maximum_fusion.3), channel_id=1, source_target_pairs={{8,0},{16,8},{24,16},{9,1},{17,9},{25,17},{10,2},{18,10},{26,18},{... | collective-permute-start | bytes 110600 | tf_op jit(solution)/shard_map/ppermute | solution.py:442
  16.8 3.3 %collective-permute-done.3 = f32[3,24,128]{2,1,0:T(8,128)S(1)} collective-permute-done((f32[3,24,128]{2,1,0:T(8,128)S(1)}, f32[3,24,128]{2,1,0:T(8,128)S(1)}, u32[]{:S(2)}, u32[]{:S(2)}) %collective-permute-start.3) | collective-permute-done | bytes 36896 | tf_op jit(solution)/shard_map/ppermute | solution.py:442
  20.2 6.0 %collective-permute-start.4 = (f32[9,24,128]{2,1,0:T(8,128)S(1)}, f32[9,24,128]{2,1,0:T(8,128)S(1)}, u32[]{:S(2)}, u32[]{:S(2)}) collective-permute-start(f32[9,24,128]{2,1,0:T(8,128)S(1)} %constant_dynamic-update-slice_fusion.same_ref), channel_id=1, source_target_pairs={{0,1},{1,2},{2,3},{3,4},{4,5},{5,6},{6,7},{8,9},{9,10},{10,11},{11... | collective-permute-start | bytes 331784 | tf_op jit(solution)/shard_map/ppermute | solution.py:441
  26.2 1.9 %collective-permute-start.5 = (f32[9,24,128]{2,1,0:T(8,128)S(1)}, f32[9,24,128]{2,1,0:T(8,128)S(1)}, u32[]{:S(2)}, u32[]{:S(2)}) collective-permute-start(f32[9,24,128]{2,1,0:T(8,128)S(1)} %constant_dynamic-update-slice_fusion.same_ref), channel_id=1, source_target_pairs={{1,0},{2,1},{3,2},{4,3},{5,4},{6,5},{7,6},{9,8},{10,9},{11,10},{12... | collective-permute-start | bytes 331784 | tf_op jit(solution)/shard_map/ppermute | solution.py:442
  28.2 3.7 %near.1 = (s32[36,3,8,128]{3,2,1,0:T(8,128)S(1)}, f32[2,8,128]{2,1,0:T(8,128)S(1)}) custom-call(s32[9]{0:T(128)S(1)} %get-tuple-element.30.tile_ref, f32[9,24,128]{2,1,0:T(8,128)S(1)} %constant_dynamic-update-slice_fusion.same_ref, s32[288,128]{1,0:T(8,128)S(1)} %get-tuple-element.32.code_ref), custom_call_target="tpu_custom_call" | custom-call | tf_op jit(solution)/shard_map/near/pallas_call | solution.py:427
  31.9 0.4 collective-permute-done.5.above_ref
  32.3 9.9 %shard_map.235.lat_ref = bf16[8,8,1024]{2,1,0:T(8,128)(2,1)} custom-call(s32[3]{0:T(128)S(1)} %pad_add_fusion.place_ref, s32[9]{0:T(128)S(1)} %get-tuple-element.30.tile_ref, f32[9,24,128]{2,1,0:T(8,128)S(1)} %collective-permute-done.4.below_ref, f32[9,24,128]{2,1,0:T(8,128)S(1)} %collective-permute-done.5.above_ref, ...), custom_call_target="tpu_custom_call" | custom-call | tf_op jit(solution)/shard_map/pallas_call | solution.py:396
  42.2 4.7 %all-to-all-start = ((bf16[8,8,1024]{2,1,0:T(8,128)(2,1)}), bf16[8,8,1024]{2,1,0:T(8,128)(2,1)S(1)}, u32[]{:S(2)}, u32[]{:S(2)}) async-start(bf16[8,8,1024]{2,1,0:T(8,128)(2,1)} %shard_map.235.lat_ref), calls=%async_computation | async-start | bytes 262144 | tf_op jit(solution)/shard_map/all_to_all | solution.py:519
  46.9 0.7 copy-done.20
  47.7 0.1 copy_bitcast_fusion
  47.9 0.8 copy-done.15
  48.8 0.1 multiply_subtract_fusion
  49.0 3.1 %all-to-all-done.m_ref = bf16[8,8,1024]{2,1,0:T(8,128)(2,1)S(1)} async-done(((bf16[8,8,1024]{2,1,0:T(8,128)(2,1)}), bf16[8,8,1024]{2,1,0:T(8,128)(2,1)S(1)}, u32[]{:S(2)}, u32[]{:S(2)}) %all-to-all-start) | async-done | bytes 131104 | tf_op jit(solution)/shard_map/all_to_all | solution.py:519
  52.2 1.4 %shard_map.236 = bf16[512,128]{1,0:T(8,128)(2,1)} custom-call(bf16[8,8,1024]{2,1,0:T(8,128)(2,1)S(1)} %all-to-all-done.m_ref, bf16[256,512]{1,0:T(8,128)(2,1)S(1)} %copy-done.4, bf16[256,512]{1,0:T(8,128)(2,1)S(1)} %copy-done.5, bf16[256,256]{1,0:T(8,128)(2,1)S(1)} %fusion.whi_ref, bf16[256,256]{1,0:T(8,128)(2,1)S(1)} %subtract_convert_fusion.wlo_ref), custom_call_target="tpu_custom_call" | custom-call | tf_op jit(solution)/shard_map/pallas_call | solution.py:396
  53.5 14.5 %all-to-all-start.1 = ((bf16[256,2,128]{2,1,0:T(2,128)(2,1)}), bf16[256,2,128]{2,1,0:T(2,128)(2,1)S(1)}, u32[]{:S(2)}, u32[]{:S(2)}) async-start(bf16[256,2,128]{2,1,0:T(2,128)(2,1)} %bitcast.10), calls=%async_computation.1 | async-start | bytes 262144 | tf_op jit(solution)/shard_map/all_to_all | solution.py:522
  68.1 0.3 maximum_bitcast_fusion
  68.5 12.4 %all-to-all-done.1 = bf16[256,2,128]{2,1,0:T(2,128)(2,1)S(1)} async-done(((bf16[256,2,128]{2,1,0:T(2,128)(2,1)}), bf16[256,2,128]{2,1,0:T(2,128)(2,1)S(1)}, u32[]{:S(2)}, u32[]{:S(2)}) %all-to-all-start.1) | async-done | bytes 131104 | tf_op jit(solution)/shard_map/all_to_all | solution.py:522
  81.0 1.1 shard_map.237
  82.1 5.6 %all-to-all-start.2 = ((bf16[256,2,128]{2,1,0:T(2,128)(2,1)}), bf16[256,2,128]{2,1,0:T(2,128)(2,1)S(1)}, u32[]{:S(2)}, u32[]{:S(2)}) async-start(bf16[256,2,128]{2,1,0:T(2,128)(2,1)} %bitcast.20), calls=%async_computation.2 | async-start | bytes 262144 | tf_op jit(solution)/shard_map/all_to_all | solution.py:535
  87.9 12.9 %all-to-all-done.2 = bf16[256,2,128]{2,1,0:T(2,128)(2,1)S(1)} async-done(((bf16[256,2,128]{2,1,0:T(2,128)(2,1)}), bf16[256,2,128]{2,1,0:T(2,128)(2,1)S(1)}, u32[]{:S(2)}, u32[]{:S(2)}) %all-to-all-start.2) | async-done | bytes 131104 | tf_op jit(solution)/shard_map/all_to_all | solution.py:535
  100.8 1.6 %shard_map.238 = bf16[8,8,8,128]{3,2,1,0:T(8,128)(2,1)} custom-call(bf16[8,4,16,128]{3,2,1,0:T(8,128)(2,1)S(1)} %bitcast.38, bf16[256,256]{1,0:T(8,128)(2,1)S(1)} %pad_maximum_fusion.2.v_ref, bf16[512,256]{1,0:T(8,128)(2,1)S(1)} %copy-done.2, bf16[512,256]{1,0:T(8,128)(2,1)S(1)} %copy-done.3, bf16[256,256]{1,0:T(8,128)(2,1)S(1)} %copy-done.6), custom_call_target="tpu_custom_call" | custom-call | tf_op jit(solution)/shard_map/pallas_call | solution.py:396
  102.4 3.8 %all-to-all-start.3 = ((bf16[8,8,8,128]{3,2,1,0:T(8,128)(2,1)}), bf16[8,8,8,128]{3,2,1,0:T(8,128)(2,1)S(1)}, u32[]{:S(2)}, u32[]{:S(2)}) async-start(bf16[8,8,8,128]{3,2,1,0:T(8,128)(2,1)} %shard_map.238), calls=%async_computation.3 | async-start | bytes 262144 | tf_op jit(solution)/shard_map/all_to_all | solution.py:547
  106.2 0.7 copy-done.19
  106.9 4.5 %all-to-all-done.3.y_ref = bf16[8,8,8,128]{3,2,1,0:T(8,128)(2,1)S(1)} async-done(((bf16[8,8,8,128]{3,2,1,0:T(8,128)(2,1)}), bf16[8,8,8,128]{3,2,1,0:T(8,128)(2,1)S(1)}, u32[]{:S(2)}, u32[]{:S(2)}) %all-to-all-start.3) | async-done | bytes 131104 | tf_op jit(solution)/shard_map/all_to_all | solution.py:547
  111.5 2.3 %shard_map.239 = f32[128,8,64]{2,1,0:T(8,128)} custom-call(bf16[8,8,8,128]{3,2,1,0:T(8,128)(2,1)S(1)} %all-to-all-done.3.y_ref, bf16[8,8,1024]{2,1,0:T(8,128)(2,1)} %shard_map.235.lat_ref, bf16[128,64]{1,0:T(8,128)(2,1)S(1)} %pad_maximum_fusion.4.w_ref), custom_call_target="tpu_custom_call" | custom-call | tf_op jit(solution)/shard_map/pallas_call | solution.py:396
  (68 shorter events, 0.7 us)
Async XLA Ops:
  0.0 47.7 %copy-start = (bf16[2,2,2,4,64,64]{5,4,3,2,1,0:T(8,128)(2,1)S(1)}, bf16[2,2,2,4,64,64]{5,4,3,2,1,0:T(8,128)(2,1)}, u32[]{:S(2)}) copy-start(bf16[2,2,2,4,64,64]{5,4,3,2,1,0:T(8,128)(2,1)} %param.31) | copy-start | bytes 786436
  0.0 6.4 %collective-permute-start.1 = (f32[1,24,128]{2,1,0:T(8,128)}, f32[1,24,128]{2,1,0:T(8,128)S(1)}, u32[]{:S(2)}, u32[]{:S(2)}) collective-permute-start(f32[1,24,128]{2,1,0:T(8,128)} %bitcast.41), channel_id=1, source_target_pairs={{32,0},{64,32},{96,64},{128,96},{160,128},{192,160},{224,192},{33,... | collective-permute-start | bytes 36872 | tf_op jit(solution)/shard_map/ppermute | solution.py:442
  1.4 6.0 %collective-permute-start = (f32[1,24,128]{2,1,0:T(8,128)}, f32[1,24,128]{2,1,0:T(8,128)S(1)}, u32[]{:S(2)}, u32[]{:S(2)}) collective-permute-start(f32[1,24,128]{2,1,0:T(8,128)} %bitcast.42), channel_id=1, source_target_pairs={{0,32},{32,64},{64,96},{96,128},{128,160},{160,192},{192,224},{1,3... | collective-permute-start | bytes 36872 | tf_op jit(solution)/shard_map/ppermute | solution.py:441
  6.4 1.0 copy-start.17
  7.4 9.3 %collective-permute-start.2 = (f32[3,24,128]{2,1,0:T(8,128)S(1)}, f32[3,24,128]{2,1,0:T(8,128)S(1)}, u32[]{:S(2)}, u32[]{:S(2)}) collective-permute-start(f32[3,24,128]{2,1,0:T(8,128)S(1)} %pad_maximum_fusion.3), channel_id=1, source_target_pairs={{0,8},{8,16},{16,24},{1,9},{9,17},{17,25},{2,10},{10,18},{18,26},{... | collective-permute-start | bytes 110600 | tf_op jit(solution)/shard_map/ppermute | solution.py:441
  10.7 1.2 %copy-start.18 = (s32[1,8,16,8]{2,3,1,0:T(8,128)S(1)}, s32[1,8,16,8]{2,3,1,0:T(8,128)}, u32[]{:S(2)}) copy-start(s32[1,8,16,8]{2,3,1,0:T(8,128)} %param.27) | copy-start | bytes 12292
  12.0 0.7 copy-start.8
  12.0 0.7 copy-start.11
  15.5 4.7 %collective-permute-start.3 = (f32[3,24,128]{2,1,0:T(8,128)S(1)}, f32[3,24,128]{2,1,0:T(8,128)S(1)}, u32[]{:S(2)}, u32[]{:S(2)}) collective-permute-start(f32[3,24,128]{2,1,0:T(8,128)S(1)} %pad_maximum_fusion.3), channel_id=1, source_target_pairs={{8,0},{16,8},{24,16},{9,1},{17,9},{25,17},{10,2},{18,10},{26,18},{... | collective-permute-start | bytes 110600 | tf_op jit(solution)/shard_map/ppermute | solution.py:442
  20.2 11.7 %collective-permute-start.4 = (f32[9,24,128]{2,1,0:T(8,128)S(1)}, f32[9,24,128]{2,1,0:T(8,128)S(1)}, u32[]{:S(2)}, u32[]{:S(2)}) collective-permute-start(f32[9,24,128]{2,1,0:T(8,128)S(1)} %constant_dynamic-update-slice_fusion.same_ref), channel_id=1, source_target_pairs={{0,1},{1,2},{2,3},{3,4},{4,5},{5,6},{6,7},{8,9},{9,10},{10,11},{11... | collective-permute-start | bytes 331784 | tf_op jit(solution)/shard_map/ppermute | solution.py:441
  26.2 6.1 %collective-permute-start.5 = (f32[9,24,128]{2,1,0:T(8,128)S(1)}, f32[9,24,128]{2,1,0:T(8,128)S(1)}, u32[]{:S(2)}, u32[]{:S(2)}) collective-permute-start(f32[9,24,128]{2,1,0:T(8,128)S(1)} %constant_dynamic-update-slice_fusion.same_ref), channel_id=1, source_target_pairs={{1,0},{2,1},{3,2},{4,3},{5,4},{6,5},{7,6},{9,8},{10,9},{11,10},{12... | collective-permute-start | bytes 331784 | tf_op jit(solution)/shard_map/ppermute | solution.py:442
  28.2 4.1 %copy-start.9 = (bf16[80,64]{0,1:T(8,128)(2,1)S(1)}, bf16[80,64]{0,1:T(8,128)(2,1)}, u32[]{:S(2)}) copy-start(bf16[80,64]{0,1:T(8,128)(2,1)} %param.30) | copy-start | bytes 30724
  42.2 4.7 %copy-start.21 = (s32[256]{0:T(256)S(1)}, s32[256]{0:T(256)}, u32[]{:S(2)}) copy-start(s32[256]{0:T(256)} %constant.82.clone) | copy-start | bytes 3076
  42.2 4.7 %copy-start.22 = (s32[256]{0:T(256)S(1)}, s32[256]{0:T(256)}, u32[]{:S(2)}) copy-start(s32[256]{0:T(256)} %constant.79.clone) | copy-start | bytes 3076
  42.2 4.7 %copy-start.23 = (s32[256]{0:T(256)S(1)}, s32[256]{0:T(256)}, u32[]{:S(2)}) copy-start(s32[256]{0:T(256)} %constant.78.clone) | copy-start | bytes 3076
  42.2 9.9 %all-to-all-start = ((bf16[8,8,1024]{2,1,0:T(8,128)(2,1)}), bf16[8,8,1024]{2,1,0:T(8,128)(2,1)S(1)}, u32[]{:S(2)}, u32[]{:S(2)}) async-start(bf16[8,8,1024]{2,1,0:T(8,128)(2,1)} %shard_map.235.lat_ref), calls=%async_computation | async-start | bytes 262144 | tf_op jit(solution)/shard_map/all_to_all | solution.py:519
  47.9 0.9 copy-start.15
  47.9 1.0 copy-start.16
  49.0 3.2 %copy-start.5 = (bf16[256,512]{1,0:T(8,128)(2,1)S(1)}, bf16[256,512]{1,0:T(8,128)(2,1)}, u32[]{:S(2)}) copy-start(bf16[256,512]{1,0:T(8,128)(2,1)} %constant.87.clone.alo_ref) | copy-start | bytes 786436
  49.0 3.2 %copy-start.4 = (bf16[256,512]{1,0:T(8,128)(2,1)S(1)}, bf16[256,512]{1,0:T(8,128)(2,1)}, u32[]{:S(2)}) copy-start(bf16[256,512]{1,0:T(8,128)(2,1)} %constant.86.clone.ahi_ref) | copy-start | bytes 786436
  53.5 27.4 %all-to-all-start.1 = ((bf16[256,2,128]{2,1,0:T(2,128)(2,1)}), bf16[256,2,128]{2,1,0:T(2,128)(2,1)S(1)}, u32[]{:S(2)}, u32[]{:S(2)}) async-start(bf16[256,2,128]{2,1,0:T(2,128)(2,1)} %bitcast.10), calls=%async_computation.1 | async-start | bytes 262144 | tf_op jit(solution)/shard_map/all_to_all | solution.py:522
  68.4 12.5 %copy-start.1 = (bf16[128,1024]{1,0:T(8,128)(2,1)S(1)}, bf16[128,1024]{1,0:T(8,128)(2,1)}, u32[]{:S(2)}) copy-start(bf16[128,1024]{1,0:T(8,128)(2,1)} %constant.89.clone.sel_ref) | copy-start | bytes 786436
  68.4 12.5 %copy-start.7 = (f32[16,1024]{1,0:T(8,128)S(1)}, f32[16,1024]{1,0:T(8,128)}, u32[]{:S(2)}) copy-start(f32[16,1024]{1,0:T(8,128)} %constant.90.clone.place_ref) | copy-start | bytes 196612
  68.4 12.5 %copy-start.10 = (f32[16,256]{1,0:T(8,128)S(1)}, f32[16,256]{1,0:T(8,128)}, u32[]{:S(2)}) copy-start(f32[16,256]{1,0:T(8,128)} %constant.88.clone.own_ref) | copy-start | bytes 49156
  68.5 12.4 %copy-start.12 = (bf16[8,16]{1,0:T(8,128)(2,1)S(1)}, bf16[8,16]{1,0:T(8,128)(2,1)}, u32[]{:S(2)}) copy-start(bf16[8,16]{1,0:T(8,128)(2,1)} %constant.91.clone.half_ref) | copy-start | bytes 772
  82.1 5.7 %copy-start.13 = (f32[128,256]{1,0:T(8,128)S(1)}, f32[128,256]{1,0:T(8,128)}, u32[]{:S(2)}) copy-start(f32[128,256]{1,0:T(8,128)} %constant.85.clone) | copy-start | bytes 393220
  82.1 5.7 %copy-start.14 = (f32[128,256]{1,0:T(8,128)S(1)}, f32[128,256]{1,0:T(8,128)}, u32[]{:S(2)}) copy-start(f32[128,256]{1,0:T(8,128)} %constant.84.clone) | copy-start | bytes 393220
  82.1 18.7 %all-to-all-start.2 = ((bf16[256,2,128]{2,1,0:T(2,128)(2,1)}), bf16[256,2,128]{2,1,0:T(2,128)(2,1)S(1)}, u32[]{:S(2)}, u32[]{:S(2)}) async-start(bf16[256,2,128]{2,1,0:T(2,128)(2,1)} %bitcast.20), calls=%async_computation.2 | async-start | bytes 262144 | tf_op jit(solution)/shard_map/all_to_all | solution.py:535
  87.8 13.0 %copy-start.2 = (bf16[512,256]{1,0:T(8,128)(2,1)S(1)}, bf16[512,256]{1,0:T(8,128)(2,1)}, u32[]{:S(2)}) copy-start(bf16[512,256]{1,0:T(8,128)(2,1)} %constant.92.clone.bc_ref) | copy-start | bytes 786436
  87.8 13.0 %copy-start.3 = (bf16[512,256]{1,0:T(8,128)(2,1)S(1)}, bf16[512,256]{1,0:T(8,128)(2,1)}, u32[]{:S(2)}) copy-start(bf16[512,256]{1,0:T(8,128)(2,1)} %constant.93.clone.bs_ref) | copy-start | bytes 786436
  87.8 13.0 %copy-start.6 = (bf16[256,256]{1,0:T(8,128)(2,1)S(1)}, bf16[256,256]{1,0:T(8,128)(2,1)}, u32[]{:S(2)}) copy-start(bf16[256,256]{1,0:T(8,128)(2,1)} %constant.94.clone.partner_ref) | copy-start | bytes 393220
  102.4 9.0 %all-to-all-start.3 = ((bf16[8,8,8,128]{3,2,1,0:T(8,128)(2,1)}), bf16[8,8,8,128]{3,2,1,0:T(8,128)(2,1)S(1)}, u32[]{:S(2)}, u32[]{:S(2)}) async-start(bf16[8,8,8,128]{3,2,1,0:T(8,128)(2,1)} %shard_map.238), calls=%async_computation.3 | async-start | bytes 262144 | tf_op jit(solution)/shard_map/all_to_all | solution.py:547
  (2 other events, 1.4 us)
